TPU v7x, 32 devices: a whole 2x2x4 slice. The times are simulated.
32 devices in a mesh: kv: 8 (over z, x), mlp: 4 (over y, core).
Axes of the slice: x: 2, y: 2, z: 4, core: 2. Of those that a mesh axis runs over, the one named last changes fastest.
Arguments:
- queries: bfloat16 [384, 4096], P('kv', 'mlp')
- root_cache: bfloat16 [8, 4096, 2048], P('kv', None, 'mlp')
- mid_cache: bfloat16 [16, 2048, 2048], P('kv', None, 'mlp')
- leaf_cache: bfloat16 [32, 1024, 2048], P('kv', None, 'mlp')
- token_leaf: int32 [384], replicated, may hold values from 0 to 31, as said below
- leaf_parent: int32 [32], replicated, may hold values from 0 to 15, as said below
- mid_parent: int32 [16], replicated, may hold values from 0 to 7, as said below
- root_len: int32 [8], replicated, may hold values from 256 to 4096, as said below
- mid_len: int32 [16], replicated, may hold values from 128 to 2048, as said below
- leaf_len: int32 [32], replicated, may hold values from 64 to 1024, as said below
- root_slot: int32 [8], replicated, may hold values from 0 to 7, each once
- mid_slot: int32 [16], replicated, may hold values from 0 to 15, each once
- leaf_slot: int32 [32], replicated, may hold values from 0 to 31, each once
- stream: bfloat16 [384, 4096], P('kv', 'mlp')
- out_weight: bfloat16 [4096, 4096], P('mlp'), may hold values from -0.09375 to 0.09375
- norm_gain: float32 [4096], P('mlp'), may hold values from 0.1 to 1.9
- gate_weight: bfloat16 [4096, 14336], P('mlp', 'kv'), may hold values from -0.09375 to 0.09375
- up_weight: bfloat16 [4096, 14336], P('mlp', 'kv'), may hold values from -0.09375 to 0.09375
- down_weight: bfloat16 [14336, 4096], P('kv', 'mlp'), may hold values from -0.046875 to 0.046875
Outputs:
- attended: bfloat16 [384, 4096], P('kv', 'mlp')
- mixed: bfloat16 [384, 4096], P('kv', 'mlp')
Inputs may be any that keep to these rules, and one draw needn't show every extreme that they name: `token_leaf`: never falls; the tokens of one leaf are contiguous, 8 to 16 of them, and some leaf has exactly 16. `leaf_parent`: never falls; every mid node has 1 to 3 leaves; no mid node has more than 48 tokens beneath it, and one has exactly 48. `mid_parent`: never falls; every root has 1 to 3 mid nodes; no root has more than 144 tokens beneath it, and one has exactly 144. `root_len`: some root has exactly 4096. `mid_len`: some mid node has exactly 2048. `leaf_len`: some leaf has exactly 1024.
All inputs are finite; a program needn't handle non-finite values.
Results may differ from a plain program's by a relative error of at most 0.022.
Values may be sent and summed in bfloat16 or wider, within the bound.
No kernel may reach another device: no remote copies, remote signals or barrier semaphores. Data moves between devices by JAX's collectives and lax.ppermute only.
A program may use at most 128 MiB of HBM per device.

v0:
```python
import math

import jax
import jax.numpy as jnp
from jax import lax
from jax.sharding import PartitionSpec as P

D = 4096
HEAD = 128
QLEAF = 16
QMID = 48
QROOT = 144


LOWEST = -1e30
EPSILON = 1e-05


def tree_counts(token_leaf, leaf_parent, mid_parent, root_total):
    leaf_ids = jnp.arange(leaf_parent.shape[0], dtype=jnp.int32)
    leaf_count = jnp.sum((token_leaf[None, :] == leaf_ids[:, None]).astype(jnp.int32), axis=1)
    mid_ids = jnp.arange(mid_parent.shape[0], dtype=jnp.int32)
    mid_count = jnp.sum(
        jnp.where(leaf_parent[None, :] == mid_ids[:, None], leaf_count[None, :], 0), axis=1
    )
    root_ids = jnp.arange(root_total, dtype=jnp.int32)
    root_count = jnp.sum(
        jnp.where(mid_parent[None, :] == root_ids[:, None], mid_count[None, :], 0), axis=1
    )
    counts = (root_count, mid_count, leaf_count)
    return (tuple(before(level_count) for level_count in counts), counts)


def before(level_count):
    ids = jnp.arange(level_count.shape[0], dtype=jnp.int32)
    return jnp.sum(jnp.where(ids[None, :] < ids[:, None], level_count[None, :], 0), axis=1)


def slot_nodes(slot_map, wanted):
    node_ids = jnp.arange(slot_map.shape[0], dtype=jnp.int32)
    matches = slot_map[None, :] == wanted[:, None]
    return jnp.sum(jnp.where(matches, node_ids[None, :], 0), axis=1)


def lookup(values, wanted):
    table_ids = jnp.arange(values.shape[0], dtype=jnp.int32)
    matches = table_ids[None, :] == wanted[:, None]
    return jnp.sum(jnp.where(matches, values[None, :], 0), axis=1)


def attend(query_rows, cache, lengths):
    slot_total, row_count, row_width = query_rows.shape
    key_span = cache.shape[1]
    kv_count = cache.shape[2] // (2 * HEAD)
    group_size = row_width // (kv_count * HEAD)
    grouped = query_rows.reshape(slot_total, row_count, kv_count, group_size, HEAD)
    paired = cache.reshape(slot_total, key_span, kv_count, 2, HEAD)
    block_len = min(512, key_span)
    block_total = (jnp.max(lengths) + block_len - 1) // block_len
    score_scale = 1.0 / math.sqrt(HEAD)

    def visit_block(block_index, carry):
        peak_score, weight_sum, partial_out = carry
        key_piece = lax.dynamic_slice_in_dim(paired, block_index * block_len, block_len, 1)
        scores = (
            jnp.einsum(
                "srkgd,sjkd->srkgj",
                grouped,
                key_piece[:, :, :, 0, :],
                preferred_element_type=jnp.float32,
            )
            * score_scale
        )
        position = block_index * block_len + jnp.arange(block_len, dtype=jnp.int32)
        live_keys = (position[None, :] < lengths[:, None])[:, None, None, None, :]
        scores = jnp.where(live_keys, scores, LOWEST)
        new_peak = jnp.maximum(peak_score, jnp.max(scores, axis=-1))
        weights = jnp.where(live_keys, jnp.exp(scores - new_peak[..., None]), 0.0)
        carry_factor = jnp.exp(peak_score - new_peak)
        weight_sum = weight_sum * carry_factor + jnp.sum(weights, axis=-1)
        partial_out = partial_out * carry_factor[..., None] + jnp.einsum(
            "srkgj,sjkd->srkgd",
            weights.astype(jnp.bfloat16),
            key_piece[:, :, :, 1, :],
            preferred_element_type=jnp.float32,
        )
        return (new_peak, weight_sum, partial_out)

    initial = (
        jnp.full((slot_total, row_count, kv_count, group_size), LOWEST, jnp.float32),
        jnp.zeros((slot_total, row_count, kv_count, group_size), jnp.float32),
        jnp.zeros((slot_total, row_count, kv_count, group_size, HEAD), jnp.float32),
    )
    peak_score, weight_sum, partial_out = lax.fori_loop(0, block_total, visit_block, initial)
    head_count = kv_count * group_size
    return (
        peak_score.reshape(slot_total, row_count, head_count),
        weight_sum.reshape(slot_total, row_count, head_count),
        partial_out.reshape(slot_total, row_count, head_count, HEAD),
    )


def merge_into(running, part, first_row, row_count, capacity):
    run_peak, run_sum, run_out = running
    part_peak, part_sum, part_out = part
    window = jnp.minimum(first_row, run_peak.shape[0] - capacity)
    positions = window + jnp.arange(capacity, dtype=jnp.int32)
    live_rows = ((positions >= first_row) & (positions < first_row + row_count))[:, None]
    old_peak = lax.dynamic_slice_in_dim(run_peak, window, capacity, 0)
    old_sum = lax.dynamic_slice_in_dim(run_sum, window, capacity, 0)
    old_out = lax.dynamic_slice_in_dim(run_out, window, capacity, 0)
    new_peak = jnp.where(live_rows, jnp.maximum(old_peak, part_peak), old_peak)
    carry_factor = jnp.exp(old_peak - new_peak)
    take_factor = jnp.where(live_rows, jnp.exp(part_peak - new_peak), 0.0)
    new_sum = old_sum * carry_factor + part_sum * take_factor
    new_out = old_out * carry_factor[..., None] + part_out * take_factor[..., None]
    return (
        lax.dynamic_update_slice_in_dim(run_peak, new_peak, window, 0),
        lax.dynamic_update_slice_in_dim(run_sum, new_sum, window, 0),
        lax.dynamic_update_slice_in_dim(run_out, new_out, window, 0),
    )


def run_slots(running, everyone, cache_stack, lengths, node_starts, node_counts, capacity):
    slot_total = cache_stack.shape[0]
    windows = jnp.minimum(node_starts, everyone.shape[0] - capacity)
    query_rows = jnp.stack(
        [
            lax.dynamic_slice_in_dim(everyone, windows[member], capacity, 0)
            for member in range(slot_total)
        ]
    )
    part_peak, part_sum, part_out = attend(query_rows, cache_stack, lengths)
    for member in range(slot_total):
        running = merge_into(
            running,
            (part_peak[member], part_sum[member], part_out[member]),
            node_starts[member],
            node_counts[member],
            capacity,
        )
    return running


def shards(
    queries,
    root_cache,
    mid_cache,
    leaf_cache,
    token_leaf,
    leaf_parent,
    mid_parent,
    root_len,
    mid_len,
    leaf_len,
    root_slot,
    mid_slot,
    leaf_slot,
    stream,
    out_weight,
    norm_gain,
    gate_weight,
    up_weight,
    down_weight,
):
    own_rows = queries.shape[0]
    owner_index = lax.axis_index("kv")
    everyone = lax.all_gather(queries, "kv", axis=0, tiled=True)
    total_rows = everyone.shape[0]
    head_count = queries.shape[1] // HEAD
    starts, counts = tree_counts(token_leaf, leaf_parent, mid_parent, root_len.shape[0])
    running = (
        jnp.full((total_rows, head_count), LOWEST, jnp.float32),
        jnp.zeros((total_rows, head_count), jnp.float32),
        jnp.zeros((total_rows, head_count, HEAD), jnp.float32),
    )
    node_ids = slot_nodes(root_slot, owner_index[None])
    running = run_slots(
        running,
        everyone,
        root_cache,
        lookup(root_len, node_ids),
        lookup(starts[0], node_ids),
        lookup(counts[0], node_ids),
        QROOT,
    )
    mid_local = mid_cache.shape[0]
    mid_wanted = owner_index * mid_local + jnp.arange(mid_local, dtype=jnp.int32)
    mid_nodes = slot_nodes(mid_slot, mid_wanted)
    running = run_slots(
        running,
        everyone,
        mid_cache,
        lookup(mid_len, mid_nodes),
        lookup(starts[1], mid_nodes),
        lookup(counts[1], mid_nodes),
        QMID,
    )
    leaf_local = leaf_cache.shape[0]
    leaf_wanted = owner_index * leaf_local + jnp.arange(leaf_local, dtype=jnp.int32)
    leaf_nodes = slot_nodes(leaf_slot, leaf_wanted)
    running = run_slots(
        running,
        everyone,
        leaf_cache,
        lookup(leaf_len, leaf_nodes),
        lookup(starts[2], leaf_nodes),
        lookup(counts[2], leaf_nodes),
        QLEAF,
    )
    kv_total = total_rows // own_rows
    filled = running[1] > 0.0
    safe_sum = jnp.where(filled, running[1], 1.0)
    part_out = (running[2] / safe_sum[..., None]).astype(jnp.bfloat16)
    part_lse = jnp.where(filled, running[0] + jnp.log(safe_sum), LOWEST)
    every_out = lax.all_to_all(
        part_out.reshape(kv_total, own_rows, head_count * HEAD), "kv", 0, 0
    ).reshape(kv_total, own_rows, head_count, HEAD)
    every_lse = lax.all_to_all(part_lse.reshape(kv_total, own_rows, head_count), "kv", 0, 0)
    share = jnp.exp(every_lse - jnp.max(every_lse, axis=0))
    attended = (
        (
            jnp.sum(every_out.astype(jnp.float32) * share[..., None], axis=0)
            / jnp.sum(share, axis=0)[..., None]
        )
        .reshape(own_rows, head_count * HEAD)
        .astype(jnp.bfloat16)
    )
    mlp_total = lax.axis_size("mlp")
    own_width = stream.shape[1]
    projected = lax.dot_general(
        attended, out_weight, (((1,), (0,)), ((), ())), preferred_element_type=jnp.float32
    ).astype(jnp.bfloat16)
    projected = projected.reshape(own_rows, mlp_total, own_width).transpose(1, 0, 2)
    projected = jnp.sum(lax.all_to_all(projected, "mlp", 0, 0).astype(jnp.float32), axis=0)
    residual = (stream.astype(jnp.float32) + projected).astype(jnp.bfloat16)
    widened = lax.optimization_barrier(residual).astype(jnp.float32)
    square_sum = lax.psum(jnp.sum(widened * widened, axis=1), "mlp")
    row_scale = lax.all_gather(lax.rsqrt(square_sum / D + EPSILON), "kv", axis=0, tiled=True)
    scaled = lax.all_gather((widened * norm_gain).astype(jnp.bfloat16), "kv", axis=0, tiled=True)
    gate_up = jnp.concatenate([gate_weight, up_weight], axis=1)
    unit_count = gate_weight.shape[1]
    gate_up_sum = jnp.dot(scaled, gate_up, preferred_element_type=jnp.float32)
    share_rows = halve(
        (gate_up_sum * row_scale[:, None]).astype(jnp.bfloat16), "mlp", mlp_total
    )
    share_rows = share_rows.astype(jnp.float32)
    hidden = (jax.nn.silu(share_rows[:, :unit_count]) * share_rows[:, unit_count:]).astype(
        jnp.bfloat16
    )
    hidden = double(hidden, "mlp", mlp_total)
    partial_mixed = jnp.dot(hidden, down_weight, preferred_element_type=jnp.float32)
    partial_mixed = partial_mixed.astype(jnp.bfloat16).reshape(kv_total, own_rows, own_width)
    mixed = jnp.sum(lax.all_to_all(partial_mixed, "kv", 0, 0).astype(jnp.float32), axis=0)
    return (attended, mixed.astype(jnp.bfloat16))


def halve(rows, axis_name, axis_total):
    place = lax.axis_index(axis_name)
    step = 1
    while step < axis_total:
        half = rows.shape[0] // 2
        side = (place // step) % 2
        keep = lax.dynamic_slice_in_dim(rows, side * half, half, 0)
        send = lax.dynamic_slice_in_dim(rows, (1 - side) * half, half, 0)
        got = lax.ppermute(send, axis_name, [(j, j ^ step) for j in range(axis_total)])
        rows = (keep.astype(jnp.float32) + got.astype(jnp.float32)).astype(jnp.bfloat16)
        step *= 2
    return rows


def double(rows, axis_name, axis_total):
    place = lax.axis_index(axis_name)
    step = axis_total // 2
    while step > 0:
        got = lax.ppermute(rows, axis_name, [(j, j ^ step) for j in range(axis_total)])
        low = (place // step) % 2 == 0
        rows = jnp.where(
            low, jnp.concatenate([rows, got], axis=0), jnp.concatenate([got, rows], axis=0)
        )
        step //= 2
    return rows


def solution(mesh):
    in_specs = (
        P("kv", "mlp"),
        P("kv", None, "mlp"),
        P("kv", None, "mlp"),
        P("kv", None, "mlp"),
        P(),
        P(),
        P(),
        P(),
        P(),
        P(),
        P(),
        P(),
        P(),
        P("kv", "mlp"),
        P("mlp", None),
        P("mlp"),
        P("mlp", "kv"),
        P("mlp", "kv"),
        P("kv", "mlp"),
    )
    out_specs = (P("kv", "mlp"), P("kv", "mlp"))
    return jax.shard_map(shards, mesh=mesh, in_specs=in_specs, out_specs=out_specs, check_vma=False)
```

profile of v0, /device:TPU:0, one launch (start us, length us, event | category | flops | bytes accessed | tf_op | source)
XLA Modules:
  0.0 344.7 jit_solution(7223671233065496885)
XLA Ops:
  0.6 1.3 fusion.93
  1.9 2.0 select_reduce_fusion.12
  7.1 1.3 select_reduce_fusion.13
  9.1 0.8 fusion.92
  9.9 0.9 select_reduce_fusion.10
  17.4 0.8 select_reduce_fusion.8
  18.3 0.9 select_reduce_fusion.6
  29.3 6.5 %copy.90 = bf16[1,4096,512]{1,2,0:T(8,128)(2,1)} copy(bf16[1,4096,512]{2,1,0:T(8,128)(2,1)} %param.26) | data formatting | bytes 8388608 | tf_op args[1]
  35.8 33.8 %all_gather.9 = bf16[384,1024]{1,0:T(8,128)(2,1)S(1)} all-gather(bf16[48,1024]{1,0:T(8,128)(2,1)S(1)} %copy-done.3), channel_id=1, replica_groups=mesh['kv'=8,'mlp'=4] {'kv'}, dimensions={0}, use_global_device_ids=true | all-gather | bytes 884736 | tf_op jit(solution)/shard_map/all_gather | solution.py:168
  70.0 0.9 broadcast_in_dim.414
  70.8 17.7 %while.42 = (s32[]{:T(128)}, f32[1,144,2,4]{1,3,2,0:T(4,128)S(1)}, f32[1,144,2,4]{1,3,2,0:T(4,128)S(1)}, f32[1,144,2,4,128]{4,1,3,2,0:T(8,128)}, s32[]{:T(128)},...) while((s32[]{:T(128)}, f32[1,144,2,4]{1,3,2,0:T(4,128)S(1)}, ...), condition=%wide.region_11.12_spmd, body=%wide.region_8.11_spmd.sunk | while | flops 309956992 | bytes 9160403 | solution.py:94
  71.5 1.6 bitcast_reduce_fusion.5
  74.0 2.8 fusion.132
  77.4 1.6 bitcast_reduce_fusion.5
  79.8 2.8 fusion.132
  83.3 1.6 bitcast_reduce_fusion.5
  85.7 2.8 fusion.132
  90.3 6.3 %copy.96 = bf16[2,2048,512]{1,2,0:T(8,128)(2,1)} copy(bf16[2,2048,512]{2,1,0:T(8,128)(2,1)} %param.27) | data formatting | bytes 8388608 | tf_op args[2]
  98.4 3.7 %while.43 = (s32[]{:T(128)}, f32[2,48,2,4]{1,3,2,0:T(4,128)S(1)}, f32[2,48,2,4]{1,3,2,0:T(4,128)S(1)}, f32[2,48,2,4,128]{4,1,3,2,0:T(8,128)S(1)}, s32[]{:T(128)}...) while((s32[]{:T(128)}, f32[2,48,2,4]{1,3,2,0:T(4,128)S(1)}, ...), condition=%wide.region_21.22_spmd, body=%wide.region_18.21_spmd.sunk | while | flops 205065216 | bytes 6807767 | solution.py:94
  98.5 1.5 bitcast_reduce_fusion.6
  100.5 1.6 fusion.136
  107.5 6.3 %copy.105 = bf16[4,1024,512]{1,2,0:T(8,128)(2,1)} copy(bf16[4,1024,512]{2,1,0:T(8,128)(2,1)} %param.28) | data formatting | bytes 8388608 | tf_op args[3]
  116.7 7.9 %while.44 = (s32[]{:T(128)}, f32[4,16,2,4]{1,3,2,0:T(4,128)S(1)}, f32[4,16,2,4]{1,3,2,0:T(4,128)S(1)}, f32[4,16,2,4,128]{4,1,3,2,0:T(8,128)S(1)}, s32[]{:T(128)}...) while((s32[]{:T(128)}, f32[4,16,2,4]{1,3,2,0:T(4,128)S(1)}, ...), condition=%wide.region_31.32_spmd, body=%wide.region_28.31_spmd.sunk | while | flops 136711680 | bytes 5943519 | solution.py:94
  116.8 1.6 fusion.139
  118.8 1.8 fusion.141
  120.7 1.6 fusion.139
  122.7 1.8 fusion.141
  136.0 38.6 %all-to-all-start.1 = ((f32[8,1,384]{2,1,0:T(1,128)}), f32[8,1,384]{2,1,0:T(1,128)S(1)}, u32[]{:S(2)}, u32[]{:S(2)}) async-start(f32[8,1,384]{2,1,0:T(1,128)} %reshape.380), calls=%async_computation.1 | async-start | bytes 24576 | tf_op jit(solution)/shard_map/all_to_all | solution.py:219
  177.7 1.2 reshape.365
  178.9 2.4 all-to-all-done.1
  181.3 4.2 %all-to-all-start = ((bf16[8,48,1024]{2,1,0:T(8,128)(2,1)}), bf16[8,48,1024]{2,1,0:T(8,128)(2,1)}, u32[]{:S(2)}, u32[]{:S(2)}) async-start(bf16[8,48,1024]{2,1,0:T(8,128)(2,1)} %reshape.365), calls=%async_computation | async-start | bytes 1572864 | tf_op jit(solution)/shard_map/all_to_all | solution.py:216
  187.7 11.3 %all-to-all-done = bf16[8,48,1024]{2,1,0:T(8,128)(2,1)} async-done(((bf16[8,48,1024]{2,1,0:T(8,128)(2,1)}), bf16[8,48,1024]{2,1,0:T(8,128)(2,1)}, u32[]{:S(2)}, u32[]{:S(2)}) %all-to-all-start) | async-done | bytes 786464 | tf_op jit(solution)/shard_map/all_to_all | solution.py:216
  199.0 1.4 multiply_reduce_fusion
  200.6 5.0 %convolution_convert_fusion = bf16[48,4096]{1,0:T(8,128)(2,1)S(1)} fusion(bf16[48,1024]{1,0:T(8,128)(2,1)S(1)} %fusion.67, bf16[1024,4096]{1,0:T(8,128)(2,1)} %param.39), kind=kOutput, calls=%fused_computation.77 | convolution fusion | flops 402849792 | bytes 8880128 | tf_op jit(solution)/shard_map/dot_general | solution.py:231
  206.4 3.5 %all-to-all-start.2 = ((bf16[4,48,1024]{2,1,0:T(8,128)(2,1)}), bf16[4,48,1024]{2,1,0:T(8,128)(2,1)S(1)}, u32[]{:S(2)}, u32[]{:S(2)}) async-start(bf16[4,48,1024]{2,1,0:T(8,128)(2,1)} %bitcast.195), calls=%async_computation.2 | async-start | bytes 786432 | tf_op jit(solution)/shard_map/all_to_all | solution.py:235
  211.1 6.1 %all-to-all-done.2 = bf16[4,48,1024]{2,1,0:T(8,128)(2,1)S(1)} async-done(((bf16[4,48,1024]{2,1,0:T(8,128)(2,1)}), bf16[4,48,1024]{2,1,0:T(8,128)(2,1)S(1)}, u32[]{:S(2)}, u32[]{:S(2)}) %all-to-all-start.2) | async-done | bytes 393248 | tf_op jit(solution)/shard_map/all_to_all | solution.py:235
  217.5 32.1 %all_gather.10 = bf16[384,1024]{1,0:T(8,128)(2,1)S(1)} all-gather(bf16[48,1024]{1,0:T(8,128)(2,1)S(1)} %get-tuple-element.326), channel_id=1, replica_groups=mesh['kv'=8,'mlp'=4] {'kv'}, dimensions={0}, use_global_device_ids=true | all-gather | bytes 884736 | tf_op jit(solution)/shard_map/all_gather | solution.py:240
  249.6 5.7 %psum.7 = f32[48]{0:T(128)S(1)} all-reduce(f32[48]{0:T(128)S(1)} %get-tuple-element.325), channel_id=1, replica_groups=mesh['kv'=8,'mlp'=4] {'mlp'}, use_global_device_ids=true, to_apply=%region_37.38 | all-reduce | flops 48 | bytes 384 | tf_op jit(solution)/shard_map/psum | solution.py:238
  255.5 19.4 %all-reduce = f32[384]{0:T(512)S(1)} all-reduce(f32[384]{0:T(512)S(1)} %rsqrt_dynamic-update-slice_fusion), channel_id=1, replica_groups=mesh['kv'=8,'mlp'=4] {'kv'}, use_global_device_ids=true, to_apply=%add | all-reduce | flops 384 | bytes 3072
  274.9 6.2 %fusion.52 = bf16[384,3584]{1,0:T(8,128)(2,1)S(1)} fusion(bf16[384,1024]{1,0:T(8,128)(2,1)S(1)} %all_gather.10, bf16[1024,1792]{1,0:T(8,128)(2,1)} %param.42, bf16[1024,1792]{1,0:T(8,128)(2,1)} %param.41, f32[384]{0:T(512)S(1)} %all-reduce), kind=kOutput, calls=%fused_computation.76 | convolution fusion | flops 2836004864 | bytes 10880512 | tf_op jit(solution)/shard_map/dot_general | solution.py:243
  281.1 1.5 copy-done
  282.9 3.1 collective-permute-done
  285.9 1.7 add_convert_fusion
  288.0 17.2 %collective-permute-done.1 = bf16[96,3584]{1,0:T(8,128)(2,1)S(1)} collective-permute-done((bf16[96,3584]{1,0:T(8,128)(2,1)S(1)}, bf16[96,3584]{1,0:T(8,128)(2,1)S(1)}, u32[]{:S(2)}, u32[]{:S(2)}) %collective-permute-start.1) | collective-permute-done | bytes 688160 | tf_op jit(solution)/shard_map/ppermute | solution.py:266
  305.9 9.0 %collective-permute-done.2 = bf16[96,1792]{1,0:T(8,128)(2,1)S(1)} collective-permute-done((bf16[96,1792]{1,0:T(8,128)(2,1)S(1)}, bf16[96,1792]{1,0:T(8,128)(2,1)S(1)}, u32[]{:S(2)}, u32[]{:S(2)}) %collective-permute-start.2) | collective-permute-done | bytes 344096 | tf_op jit(solution)/shard_map/ppermute | solution.py:276
  315.1 2.1 collective-permute-done.3
  317.2 3.6 %convolution_convert_fusion.1 = bf16[384,1024]{1,0:T(8,128)(2,1)S(1)} fusion(bf16[1792,1024]{1,0:T(8,128)(2,1)} %param.43, bf16[192,1792]{1,0:T(8,128)(2,1)S(1)} %collective-permute-done.3, bf16[192,1792]{1,0:T(8,128)(2,1)S(1)} %maximum_select_fusion.2, pred[]{:T(512)S(6)} %eq.96), kind=kOutput, calls=%fused_computation.81 | convolution fusion | flops 1415872512 | bytes 5832705 | tf_op jit(solution)/shard_map/dot_general | solution.py:252
  320.9 23.1 %all_to_all.20 = bf16[8,48,1024]{2,1,0:T(8,128)(2,1)S(1)} all-to-all(bf16[8,48,1024]{2,1,0:T(8,128)(2,1)S(1)} %bitcast.302), channel_id=1, replica_groups=mesh['kv'=8,'mlp'=4] {'kv'}, dimensions={0} | all-to-all | bytes 1572864 | tf_op jit(solution)/shard_map/all_to_all | solution.py:254
  (177 shorter events, 32.5 us)
Async XLA Ops:
  29.3 6.5 %copy-start.3 = (bf16[48,1024]{1,0:T(8,128)(2,1)S(1)}, bf16[48,1024]{1,0:T(8,128)(2,1)}, u32[]{:S(2)}) copy-start(bf16[48,1024]{1,0:T(8,128)(2,1)} %param.25) | copy-start | bytes 294916
  124.5 51.5 %copy-start.1 = (f32[1,144,2,4,128]{4,1,3,2,0:T(8,128)S(1)}, f32[1,144,2,4,128]{4,1,3,2,0:T(8,128)}, u32[]{:S(2)}) copy-start(f32[1,144,2,4,128]{4,1,3,2,0:T(8,128)} %get-tuple-element.138) | copy-start | bytes 1769476
  136.0 45.3 %all-to-all-start.1 = ((f32[8,1,384]{2,1,0:T(1,128)}), f32[8,1,384]{2,1,0:T(1,128)S(1)}, u32[]{:S(2)}, u32[]{:S(2)}) async-start(f32[8,1,384]{2,1,0:T(1,128)} %reshape.380), calls=%async_computation.1 | async-start | bytes 24576 | tf_op jit(solution)/shard_map/all_to_all | solution.py:219
  181.3 17.7 %all-to-all-start = ((bf16[8,48,1024]{2,1,0:T(8,128)(2,1)}), bf16[8,48,1024]{2,1,0:T(8,128)(2,1)}, u32[]{:S(2)}, u32[]{:S(2)}) async-start(bf16[8,48,1024]{2,1,0:T(8,128)(2,1)} %reshape.365), calls=%async_computation | async-start | bytes 1572864 | tf_op jit(solution)/shard_map/all_to_all | solution.py:216
  200.5 5.1 %copy-start.2 = (bf16[48,1024]{1,0:T(8,128)(2,1)}, bf16[48,1024]{1,0:T(8,128)(2,1)S(1)}, u32[]{:S(2)}) copy-start(bf16[48,1024]{1,0:T(8,128)(2,1)S(1)} %fusion.67) | copy-start | bytes 294916
  200.5 9.3 %copy-start.6 = (u32[32]{0:T(128)S(1)}, u32[32]{0:T(128)}, u32[]{:S(2)}) copy-start(u32[32]{0:T(128)} %constant.191) | copy-start | bytes 388
  200.6 16.7 %copy-start.4 = (bf16[48,1024]{1,0:T(8,128)(2,1)S(1)}, bf16[48,1024]{1,0:T(8,128)(2,1)}, u32[]{:S(2)}) copy-start(bf16[48,1024]{1,0:T(8,128)(2,1)} %param.38) | copy-start | bytes 294916
  205.6 11.8 %copy-start.5 = (f32[1024]{0:T(1024)S(1)}, f32[1024]{0:T(1024)}, u32[]{:S(2)}) copy-start(f32[1024]{0:T(1024)} %param.40) | copy-start | bytes 12292
  206.4 10.9 %all-to-all-start.2 = ((bf16[4,48,1024]{2,1,0:T(8,128)(2,1)}), bf16[4,48,1024]{2,1,0:T(8,128)(2,1)S(1)}, u32[]{:S(2)}, u32[]{:S(2)}) async-start(bf16[4,48,1024]{2,1,0:T(8,128)(2,1)} %bitcast.195), calls=%async_computation.2 | async-start | bytes 786432 | tf_op jit(solution)/shard_map/all_to_all | solution.py:235
  281.1 1.6 copy-start
  282.7 3.2 collective-permute-start
  287.6 17.5 %collective-permute-start.1 = (bf16[96,3584]{1,0:T(8,128)(2,1)S(1)}, bf16[96,3584]{1,0:T(8,128)(2,1)S(1)}, u32[]{:S(2)}, u32[]{:S(2)}) collective-permute-start(bf16[96,3584]{1,0:T(8,128)(2,1)S(1)} %constant_dynamic-slice_fusion.16), channel_id=1, source_target_pairs={{0,2},{1,3},{2,0},{3,1},{4,6},{5,7},{6,4},{7,5},{8,10},{9,11},{10,... | collective-permute-start | bytes 2064392 | tf_op jit(solution)/shard_map/ppermute | solution.py:266
  305.6 9.3 %collective-permute-start.2 = (bf16[96,1792]{1,0:T(8,128)(2,1)S(1)}, bf16[96,1792]{1,0:T(8,128)(2,1)S(1)}, u32[]{:S(2)}, u32[]{:S(2)}) collective-permute-start(bf16[96,1792]{1,0:T(8,128)(2,1)S(1)} %fusion.62), channel_id=1, source_target_pairs={{0,2},{1,3},{2,0},{3,1},{4,6},{5,7},{6,4},{7,5},{8,10},{9,11},{10,... | collective-permute-start | bytes 1032200 | tf_op jit(solution)/shard_map/ppermute | solution.py:276
  315.0 2.2 collective-permute-start.3
where the time goes:
time: 346 us; the launch traced here: 345 us
  blocking collectives  114 us (33%)
  waiting for transfers between devices  51.1 us (15%)
  starting transfers between devices  47.1 us (14%)
  matrix products  37.8 us (11%)
  local copies, waits for them, and re-layouts  35.3 us (10%)
  other arithmetic  30.1 us (9%)
  between operations  28.7 us (8%)
    all_to_all x1, starting transfers between devices, shards(): lax.all_to_all(part_lse.reshape(kv_total, own_rows, head_count), 'kv', 0, 0)  38.6 us
    all_gather x1, blocking collectives, shards(): everyone = lax.all_gather(queries, 'kv', axis=0, tiled=True)  33.8 us
    all_gather x1, blocking collectives, shards(): lax.all_gather((widened * norm_gain).astype(jnp.bfloat16), 'kv', axis=0,...  32.1 us
    all_to_all x1, blocking collectives, shards(): lax.all_to_all(partial_mixed, 'kv', 0, 0).astype(jnp.float32)  23.1 us
    unnamed x21, local copies, waits for them, and re-layouts  22 us
    ppermute x2, waiting for transfers between devices, halve(): lax.ppermute(send, axis_name, [(j, j ^ step) for j in range(axis_total)])  20.3 us
    unnamed x1, blocking collectives  19.4 us
    dot_general x6, matrix products, visit_block(): jnp.einsum('srkgj,sjkd->srkgd', weights.astype(jnp.bfloat16), key_piece[:...  13.4 us
  transfers between devices with their start and end apart: 7, of which 7 were waited for; matrix products, arithmetic and copies ran while one was open for 2% of the time, Pallas kernels for 0%

commit v1 on v0

v1 whole, which is shorter than its diff:
```python
import math

import jax
import jax.numpy as jnp
from jax import lax
from jax.experimental import pallas as pl
from jax.experimental.pallas import tpu as pltpu
from jax.sharding import PartitionSpec as P

D = 4096
HEAD = 128
QLEAF = 16
QMID = 48
QROOT = 144


LOWEST = -1e30
EPSILON = 1e-05
ALIGN = 16
BLOCK = 512


def count_below(sorted_values, bounds):
    return jnp.sum((sorted_values[None, :] < bounds[:, None]).astype(jnp.int32), axis=1)


def slot_nodes(slot_map, lengths, wanted):
    node_ids = jnp.arange(slot_map.shape[0], dtype=jnp.int32)
    matches = slot_map[None, :] == wanted[:, None]
    nodes = jnp.sum(jnp.where(matches, node_ids[None, :], 0), axis=1)
    return nodes, jnp.sum(jnp.where(matches, lengths[None, :], 0), axis=1)


def own_nodes(owner, local_counts, tree, lengths, slots):
    token_leaf, leaf_parent, mid_parent = tree
    picked = [
        slot_nodes(slot_map, level_len, owner * local + jnp.arange(local, dtype=jnp.int32))
        for slot_map, level_len, local in zip(slots, lengths, local_counts)
    ]
    edges = jnp.concatenate([picked[0][0], picked[0][0] + 1])
    edges = jnp.concatenate([count_below(mid_parent, edges), picked[1][0], picked[1][0] + 1])
    edges = jnp.concatenate([count_below(leaf_parent, edges), picked[2][0], picked[2][0] + 1])
    edges = count_below(token_leaf, edges)
    first, last, place = [], [], 0
    for local in local_counts:
        first.append(edges[place : place + local])
        last.append(edges[place + local : place + 2 * local])
        place += 2 * local
    return jnp.stack(
        [
            jnp.concatenate(first),
            jnp.concatenate(last),
            jnp.concatenate([level_len for _, level_len in picked]),
        ]
    ).astype(jnp.int32)


def tree_attention(query_parts, caches, nodes, owner):
    part_total = len(query_parts)
    own_rows, width = query_parts[0].shape
    total_rows = part_total * own_rows
    kv_count = caches[0].shape[2] // (2 * HEAD)
    head_count = width // HEAD
    group_size = head_count // kv_count
    score_scale = 1.0 / math.sqrt(HEAD)
    levels = []
    for cache, capacity in zip(caches, (QROOT, QMID, QLEAF)):
        levels.append((cache.shape[0], cache.shape[1], min(capacity + ALIGN, total_rows)))

    def kernel(nodes_ref, owner_ref, *refs):
        query_refs = refs[:part_total]
        cache_refs = refs[part_total : part_total + 3]
        out_ref, all_rows, run_out, run_lse, acc, peak, total = refs[part_total + 3 :]
        me = owner_ref[0]
        for part in range(part_total):
            row = pl.multiple_of((me ^ part) * own_rows, ALIGN)
            all_rows[pl.ds(row, own_rows), :] = query_refs[part][...]
        run_out[...] = jnp.zeros_like(run_out)
        run_lse[...] = jnp.full_like(run_lse, LOWEST)
        node = 0
        for (slot_total, span, rows), cache_ref in zip(levels, cache_refs):
            lanes = rows * group_size
            block = min(BLOCK, span)
            for member in range(slot_total):
                low, high, length = nodes_ref[0, node], nodes_ref[1, node], nodes_ref[2, node]
                node += 1
                window = jnp.minimum(low - lax.rem(low, ALIGN), total_rows - rows)
                window = pl.multiple_of(window, ALIGN)
                for kv_head in range(kv_count):
                    columns = [
                        (kv_head * group_size + h) * HEAD for h in range(group_size)
                    ]
                    grouped = jnp.concatenate(
                        [all_rows[pl.ds(window, rows), c : c + HEAD] for c in columns], axis=0
                    )
                    acc[:, :lanes] = jnp.zeros((HEAD, lanes), jnp.float32)
                    peak[:, :lanes] = jnp.full((1, lanes), LOWEST, jnp.float32)
                    total[:, :lanes] = jnp.zeros((1, lanes), jnp.float32)

                    def visit(index, carry, masked):
                        at = pl.multiple_of(index * block, block)
                        keys = cache_ref[
                            member, pl.ds(at, block), 2 * kv_head * HEAD : (2 * kv_head + 1) * HEAD
                        ]
                        values = cache_ref[
                            member,
                            pl.ds(at, block),
                            (2 * kv_head + 1) * HEAD : (2 * kv_head + 2) * HEAD,
                        ]
                        scores = lax.dot_general(
                            keys,
                            grouped,
                            (((1,), (1,)), ((), ())),
                            preferred_element_type=jnp.float32,
                        )
                        if masked:
                            position = at + lax.broadcasted_iota(jnp.int32, (block, lanes), 0)
                            scores = jnp.where(position < length, scores, LOWEST)
                        old_peak = peak[:, :lanes]
                        new_peak = jnp.maximum(old_peak, jnp.max(scores, axis=0, keepdims=True))
                        weights = jnp.exp((scores - new_peak) * score_scale)
                        fade = jnp.exp((old_peak - new_peak) * score_scale)
                        peak[:, :lanes] = new_peak
                        total[:, :lanes] = total[:, :lanes] * fade + jnp.sum(
                            weights, axis=0, keepdims=True
                        )
                        acc[:, :lanes] = acc[:, :lanes] * fade + lax.dot_general(
                            values,
                            weights.astype(jnp.bfloat16),
                            (((0,), (0,)), ((), ())),
                            preferred_element_type=jnp.float32,
                        )
                        return carry

                    whole = lax.div(length, block)
                    lax.fori_loop(0, whole, lambda i, c: visit(i, c, False), 0)

                    @pl.when(whole * block < length)
                    def _():
                        visit(whole, 0, True)

                    weight_sum = total[:, :lanes]
                    part_out = (acc[:, :lanes] / weight_sum).T
                    part_lse = jnp.broadcast_to(
                        peak[:, :lanes] * score_scale + jnp.log(weight_sum), (HEAD, lanes)
                    ).T
                    position = window + lax.broadcasted_iota(jnp.int32, (rows, HEAD), 0)
                    live = (position >= low) & (position < high)
                    for h, c in enumerate(columns):
                        here = (pl.ds(window, rows), slice(c, c + HEAD))
                        old_lse, old_out = run_lse[here], run_out[here]
                        add_lse = part_lse[h * rows : (h + 1) * rows]
                        add_out = part_out[h * rows : (h + 1) * rows]
                        best = jnp.maximum(old_lse, add_lse)
                        old_share = jnp.exp(old_lse - best)
                        add_share = jnp.exp(add_lse - best)
                        share = old_share + add_share
                        run_out[here] = jnp.where(
                            live, (old_out * old_share + add_out * add_share) / share, old_out
                        )
                        run_lse[here] = jnp.where(live, best + jnp.log(share), old_lse)
        lane = lax.broadcasted_iota(jnp.int32, (own_rows, HEAD), 1)
        for part in range(part_total):
            at = part * own_rows
            out_ref[part, :, :width] = run_out[at : at + own_rows, :].astype(jnp.bfloat16)
            lse = jnp.zeros((own_rows, HEAD), jnp.float32)
            for h in range(head_count):
                piece = run_lse[at : at + own_rows, h * HEAD : (h + 1) * HEAD]
                lse = jnp.where(lax.rem(lane, head_count) == h, piece, lse)
            first = lse.astype(jnp.bfloat16)
            rest = lse - first.astype(jnp.float32)
            second = rest.astype(jnp.bfloat16)
            third = rest - second.astype(jnp.float32)
            field = lax.div(lane, head_count)
            packed = jnp.where(
                field == 0,
                first.astype(jnp.float32),
                jnp.where(
                    field == 1,
                    second.astype(jnp.float32),
                    jnp.where(field == 2, third, 0.0),
                ),
            )
            out_ref[part, :, width:] = packed.astype(jnp.bfloat16)

    most = max(rows for _, _, rows in levels) * group_size
    vmem = pl.BlockSpec(memory_space=pltpu.VMEM)
    smem = pl.BlockSpec(memory_space=pltpu.SMEM)
    return pl.pallas_call(
        kernel,
        out_shape=jax.ShapeDtypeStruct((part_total, own_rows, width + HEAD), jnp.bfloat16),
        in_specs=[smem, smem] + [vmem] * (part_total + 3),
        out_specs=vmem,
        scratch_shapes=[
            pltpu.VMEM((total_rows, width), jnp.bfloat16),
            pltpu.VMEM((total_rows, width), jnp.float32),
            pltpu.VMEM((total_rows, width), jnp.float32),
            pltpu.VMEM((HEAD, most), jnp.float32),
            pltpu.VMEM((1, most), jnp.float32),
            pltpu.VMEM((1, most), jnp.float32),
        ],
        compiler_params=pltpu.CompilerParams(vmem_limit_bytes=48 << 20),
        name="tree_attention",
    )(nodes, owner[None], *query_parts, *caches)


def swap(value, axis_name, mask):
    axis_total = lax.axis_size(axis_name)
    return lax.ppermute(value, axis_name, [(j, j ^ mask) for j in range(axis_total)])


def gather_parts(value, axis_name):
    parts = [value] * lax.axis_size(axis_name)
    for mask in range(len(parts) - 2, 0, -2):
        parts[mask] = swap(value, axis_name, mask)
    for mask in [0] + list(range(len(parts) - 2, 0, -2)):
        parts[mask + 1] = swap(parts[mask], axis_name, 1)
    return parts


def scatter_sum(parts, axis_name):
    wide = jnp.float32
    evens = list(range(len(parts) - 2, -1, -2))
    pairs = {
        mask: parts[mask].astype(wide) + swap(parts[mask + 1], axis_name, 1).astype(wide)
        for mask in evens
    }
    summed = pairs[0]
    for mask in evens[:-1]:
        summed = summed + swap(pairs[mask].astype(jnp.bfloat16), axis_name, mask).astype(wide)
    return summed


def shards(
    queries,
    root_cache,
    mid_cache,
    leaf_cache,
    token_leaf,
    leaf_parent,
    mid_parent,
    root_len,
    mid_len,
    leaf_len,
    root_slot,
    mid_slot,
    leaf_slot,
    stream,
    out_weight,
    norm_gain,
    gate_weight,
    up_weight,
    down_weight,
):
    own_rows, width = queries.shape
    head_count = width // HEAD
    owner = lax.axis_index("kv").astype(jnp.int32)
    caches = (root_cache, mid_cache, leaf_cache)
    nodes = own_nodes(
        owner,
        [cache.shape[0] for cache in caches],
        (token_leaf, leaf_parent, mid_parent),
        (root_len, mid_len, leaf_len),
        (root_slot, mid_slot, leaf_slot),
    )
    parts = tree_attention(gather_parts(queries, "kv"), caches, nodes, owner)
    every = lax.all_to_all(parts, "kv", 0, 0)
    fields = every[:, :, width : width + 3 * head_count].astype(jnp.float32)
    every_lse = (
        fields[:, :, :head_count]
        + fields[:, :, head_count : 2 * head_count]
        + fields[:, :, 2 * head_count :]
    )
    every_out = every[:, :, :width].reshape(-1, own_rows, head_count, HEAD)
    share = jnp.exp(every_lse - jnp.max(every_lse, axis=0))
    attended = (
        (
            jnp.sum(every_out.astype(jnp.float32) * share[..., None], axis=0)
            / jnp.sum(share, axis=0)[..., None]
        )
        .reshape(own_rows, width)
        .astype(jnp.bfloat16)
    )
    mlp_total = lax.axis_size("mlp")
    own_width = stream.shape[1]
    projected = lax.dot_general(
        attended, out_weight, (((1,), (0,)), ((), ())), preferred_element_type=jnp.float32
    ).astype(jnp.bfloat16)
    projected = projected.reshape(own_rows, mlp_total, own_width).transpose(1, 0, 2)
    projected = jnp.sum(lax.all_to_all(projected, "mlp", 0, 0).astype(jnp.float32), axis=0)
    residual = (stream.astype(jnp.float32) + projected).astype(jnp.bfloat16)
    widened = lax.optimization_barrier(residual).astype(jnp.float32)
    square_sum = jnp.sum(widened * widened, axis=1)
    square_parts = gather_parts(square_sum[None, :], "kv")
    scaled = jnp.concatenate(
        gather_parts((widened * norm_gain).astype(jnp.bfloat16), "kv"), axis=0
    )
    gate_up = jnp.concatenate([gate_weight, up_weight], axis=1)
    unit_count = gate_weight.shape[1]
    gate_up_sum = jnp.dot(scaled, gate_up, preferred_element_type=jnp.float32)
    share_rows = halve(gate_up_sum.astype(jnp.bfloat16), "mlp", mlp_total)
    every_square = jnp.concatenate(square_parts, axis=1).reshape(-1)
    every_square = jnp.sum(lax.all_gather(every_square, "mlp"), axis=0)
    row_scale = halve_place(lax.rsqrt(every_square / D + EPSILON), "mlp", mlp_total)
    share_rows = share_rows.astype(jnp.float32) * row_scale[:, None]
    hidden = (jax.nn.silu(share_rows[:, :unit_count]) * share_rows[:, unit_count:]).astype(
        jnp.bfloat16
    )
    hidden = double(hidden, "mlp", mlp_total)
    partial_mixed = jnp.dot(hidden, down_weight, preferred_element_type=jnp.float32)
    partial_mixed = partial_mixed.astype(jnp.bfloat16)
    mixed = scatter_sum(jnp.split(partial_mixed, lax.axis_size("kv"), axis=0), "kv")
    return (attended, mixed.astype(jnp.bfloat16))


def halve_place(rows, axis_name, axis_total):
    place = lax.axis_index(axis_name)
    step = 1
    while step < axis_total:
        half = rows.shape[0] // 2
        rows = lax.dynamic_slice_in_dim(rows, ((place // step) % 2) * half, half, 0)
        step *= 2
    return rows


def halve(rows, axis_name, axis_total):
    place = lax.axis_index(axis_name)
    step = 1
    while step < axis_total:
        half = rows.shape[0] // 2
        side = (place // step) % 2
        keep = lax.dynamic_slice_in_dim(rows, side * half, half, 0)
        send = lax.dynamic_slice_in_dim(rows, (1 - side) * half, half, 0)
        got = lax.ppermute(send, axis_name, [(j, j ^ step) for j in range(axis_total)])
        rows = (keep.astype(jnp.float32) + got.astype(jnp.float32)).astype(jnp.bfloat16)
        step *= 2
    return rows


def double(rows, axis_name, axis_total):
    place = lax.axis_index(axis_name)
    step = axis_total // 2
    while step > 0:
        got = lax.ppermute(rows, axis_name, [(j, j ^ step) for j in range(axis_total)])
        low = (place // step) % 2 == 0
        rows = jnp.where(
            low, jnp.concatenate([rows, got], axis=0), jnp.concatenate([got, rows], axis=0)
        )
        step //= 2
    return rows


def solution(mesh):
    in_specs = (
        P("kv", "mlp"),
        P("kv", None, "mlp"),
        P("kv", None, "mlp"),
        P("kv", None, "mlp"),
        P(),
        P(),
        P(),
        P(),
        P(),
        P(),
        P(),
        P(),
        P(),
        P("kv", "mlp"),
        P("mlp", None),
        P("mlp"),
        P("mlp", "kv"),
        P("mlp", "kv"),
        P("kv", "mlp"),
    )
    out_specs = (P("kv", "mlp"), P("kv", "mlp"))
    return jax.shard_map(shards, mesh=mesh, in_specs=in_specs, out_specs=out_specs, check_vma=False)
```

time: 346 us -> 189 us (0.55)
  blocking collectives: 114 us -> 50 us
  local copies, waits for them, and re-layouts: 35.3 us -> 7.61 us
  between operations: 28.7 us -> 1.69 us
  matrix products: 37.8 us -> 14.8 us
  Pallas kernels: 0 us -> 19.1 us
  other arithmetic: 30.1 us -> 13.6 us
  starting transfers between devices: 47.1 us -> 36.6 us
  waiting for transfers between devices: 51.1 us -> 42.7 us
    all_gather x2 -> x1, blocking collectives: 66 us -> 6.44 us  [shards(): every_square = jnp.sum(lax.all_gather(every_square, 'mlp'), axis=0)]
    all_to_all x3 -> x0, starting transfers between devices: 46.3 us -> none  [the longest x1 38.6 us: shards(): lax.all_to_all(part_lse.reshape(kv_total, own_rows, head_count), 'kv', 0, 0)]
    ppermute x0 -> x28, starting transfers between devices: none -> 35 us  [swap(): lax.ppermute(value, axis_name, [(j, j ^ mask) for j in range(axis_total)])]
    ppermute x0 -> x28, waiting for transfers between devices: none -> 27.9 us  [swap(): lax.ppermute(value, axis_name, [(j, j ^ mask) for j in range(axis_total)])]
    dot_general x12 -> x0, matrix products: 23 us -> none  [the longest x6 13.4 us: visit_block(): jnp.einsum('srkgj,sjkd->srkgd', weights.astype(jnp.bfloat16), key_piece[:...]
    all_to_all x1 -> x2, blocking collectives: 23.1 us -> 43.5 us  [the longest x1 33.5 us: shards(): every = lax.all_to_all(parts, 'kv', 0, 0)]
    all_to_all x3 -> x0, waiting for transfers between devices: 19.8 us -> none  [the longest x1 11.3 us: shards(): lax.all_to_all(part_out.reshape(kv_total, own_rows, head_count * HEAD), '...]
    unnamed x1 -> x0, blocking collectives: 19.4 us -> none
  transfers between devices with their start and end apart: 7 -> 32, of which waited for: 7 -> 19; matrix products, arithmetic and copies ran while one was open for 2% -> 5% of each run, Pallas kernels for 0% -> 0%
where the time goes in v1:
time: 189 us; the launch traced here: 186 us
  blocking collectives  50 us (26%)
  waiting for transfers between devices  42.7 us (23%)
  starting transfers between devices  36.6 us (19%)
  Pallas kernels  19.1 us (10%)
  matrix products  14.8 us (8%)
  other arithmetic  13.6 us (7%)
  local copies, waits for them, and re-layouts  7.61 us (4%)
    ppermute x28, starting transfers between devices, swap(): lax.ppermute(value, axis_name, [(j, j ^ mask) for j in range(axis_total)])  35 us
    all_to_all x1, blocking collectives, shards(): every = lax.all_to_all(parts, 'kv', 0, 0)  33.5 us
    ppermute x28, waiting for transfers between devices, swap(): lax.ppermute(value, axis_name, [(j, j ^ mask) for j in range(axis_total)])  27.9 us
    pallas_call x1, Pallas kernels, tree_attention(): pl.pallas_call(kernel, out_shape=jax.ShapeDtypeStruct((part_total, own_ro...  19.1 us
    ppermute x2, waiting for transfers between devices, double(): lax.ppermute(rows, axis_name, [(j, j ^ step) for j in range(axis_total)])  11.7 us
    all_to_all x1, blocking collectives, shards(): lax.all_to_all(projected, 'mlp', 0, 0).astype(jnp.float32)  10 us
    all_gather x1, blocking collectives, shards(): every_square = jnp.sum(lax.all_gather(every_square, 'mlp'), axis=0)  6.44 us
    dot_general x1, matrix products, shards(): gate_up_sum = jnp.dot(scaled, gate_up, preferred_element_type=jnp.float32)  6.16 us
  transfers between devices with their start and end apart: 32, of which 19 were waited for; matrix products, arithmetic and copies ran while one was open for 5% of the time, Pallas kernels for 0%

profile of v1, /device:TPU:0, one launch (start us, length us, event | category | flops | bytes accessed | tf_op | source)
XLA Modules:
  0.0 186.1 jit_solution(9722159078981527288)
XLA Ops:
  0.6 3.1 %collective-permute-start.1 = (bf16[48,1024]{1,0:T(8,128)(2,1)}, bf16[48,1024]{1,0:T(8,128)(2,1)S(1)}, u32[]{:S(2)}, u32[]{:S(2)}) collective-permute-start(bf16[48,1024]{1,0:T(8,128)(2,1)} %refs_0_.1), channel_id=1, source_target_pairs={{0,8},{4,12},{8,0},{12,4},{16,24},{20,28},{24,16},{28,20},{1,9},{5... | collective-permute-start | bytes 294920 | tf_op jit(solution)/shard_map/ppermute | solution.py:209
  3.7 2.6 %collective-permute-start.3 = (bf16[48,1024]{1,0:T(8,128)(2,1)}, bf16[48,1024]{1,0:T(8,128)(2,1)S(1)}, u32[]{:S(2)}, u32[]{:S(2)}) collective-permute-start(bf16[48,1024]{1,0:T(8,128)(2,1)} %refs_0_.1), channel_id=1, source_target_pairs={{0,16},{4,20},{8,24},{12,28},{16,0},{20,4},{24,8},{28,12},{1,17},{... | collective-permute-start | bytes 294920 | tf_op jit(solution)/shard_map/ppermute | solution.py:209
  6.3 1.7 collective-permute-start
  8.0 1.3 fusion.22
  16.0 1.4 add_bitcast_fusion
  18.4 1.7 collective-permute-start.4
  20.5 3.2 %collective-permute-done.2.refs_3_ = bf16[48,1024]{1,0:T(8,128)(2,1)S(1)} collective-permute-done((bf16[48,1024]{1,0:T(8,128)(2,1)S(1)}, bf16[48,1024]{1,0:T(8,128)(2,1)S(1)}, u32[]{:S(2)}, u32[]{:S(2)}) %collective-permute-start.2) | collective-permute-done | bytes 98336 | tf_op jit(solution)/shard_map/ppermute | solution.py:209
  23.7 1.1 collective-permute-done.4.refs_5_
  24.7 1.1 collective-permute-done.6.refs_7_
  25.8 2.2 %copy-done = bf16[1,4096,512]{2,1,0:T(8,128)(2,1)S(1)} copy-done((bf16[1,4096,512]{2,1,0:T(8,128)(2,1)S(1)}, bf16[1,4096,512]{2,1,0:T(8,128)(2,1)}, u32[]{:S(2)}) %copy-start) | copy-done | bytes 4194328
  28.9 19.1 %tree_attention.1 = bf16[8,48,1152]{2,1,0:T(8,128)(2,1)S(1)} custom-call(s32[3,7]{1,0:T(4,128)S(1)} %pad_add_fusion.nodes_ref, s32[1]{0:T(128)} %bitcast.5.owner_ref, bf16[48,1024]{1,0:T(8,128)(2,1)S(1)} %copy-done.1, bf16[48,1024]{1,0:T(8,128)(2,1)S(1)} %collective-permute-done.refs_1_, bf16[48,1024]{1,0:T(8,128)(2,1)S(1)} %collective-permute-done.1.refs_2_, ...), custom_call_target="tpu_custom_call" | custom-call | tf_op jit(solution)/shard_map/tree_attention/pallas_call | solution.py:189
  48.0 33.5 %all_to_all.10 = bf16[8,48,1152]{2,1,0:T(8,128)(2,1)S(1)} all-to-all(bf16[8,48,1152]{2,1,0:T(8,128)(2,1)S(1)} %tree_attention.1), channel_id=1, replica_groups=mesh['kv'=8,'mlp'=4] {'kv'}, dimensions={0} | all-to-all | bytes 1769472 | tf_op jit(solution)/shard_map/all_to_all | solution.py:267
  83.5 1.4 multiply_reduce_fusion
  85.1 5.0 %convolution_convert_fusion = bf16[48,4096]{1,0:T(8,128)(2,1)S(1)} fusion(bf16[48,1024]{1,0:T(8,128)(2,1)S(1)} %fusion.16, bf16[1024,4096]{1,0:T(8,128)(2,1)} %param.33), kind=kOutput, calls=%fused_computation.5 | convolution fusion | flops 402849792 | bytes 8880128 | tf_op jit(solution)/shard_map/dot_general | solution.py:286
  90.2 10.0 %all_to_all.11 = bf16[4,48,1024]{2,1,0:T(8,128)(2,1)S(1)} all-to-all(bf16[4,48,1024]{2,1,0:T(8,128)(2,1)S(1)} %bitcast.29), channel_id=1, replica_groups=mesh['kv'=8,'mlp'=4] {'mlp'}, dimensions={0} | all-to-all | bytes 786432 | tf_op jit(solution)/shard_map/all_to_all | solution.py:290
  101.3 1.2 collective-permute-start.10
  102.4 2.4 %collective-permute-start.12 = (bf16[48,1024]{1,0:T(8,128)(2,1)S(1)}, bf16[48,1024]{1,0:T(8,128)(2,1)S(1)}, u32[]{:S(2)}, u32[]{:S(2)}) collective-permute-start(bf16[48,1024]{1,0:T(8,128)(2,1)S(1)} %get-tuple-element.9), channel_id=1, source_target_pairs={{0,24},{4,28},{8,16},{12,20},{16,8},{20,12},{24,0},{28,4},{1,25},{... | collective-permute-start | bytes 294920 | tf_op jit(solution)/shard_map/ppermute | solution.py:209
  106.9 4.5 %collective-permute-done.10 = bf16[48,1024]{1,0:T(8,128)(2,1)S(1)} collective-permute-done((bf16[48,1024]{1,0:T(8,128)(2,1)S(1)}, bf16[48,1024]{1,0:T(8,128)(2,1)S(1)}, u32[]{:S(2)}, u32[]{:S(2)}) %collective-permute-start.10) | collective-permute-done | bytes 98336 | tf_op jit(solution)/shard_map/ppermute | solution.py:209
  111.8 1.5 collective-permute-start.13
  113.4 2.5 %collective-permute-done.11 = bf16[48,1024]{1,0:T(8,128)(2,1)S(1)} collective-permute-done((bf16[48,1024]{1,0:T(8,128)(2,1)S(1)}, bf16[48,1024]{1,0:T(8,128)(2,1)S(1)}, u32[]{:S(2)}, u32[]{:S(2)}) %collective-permute-start.11) | collective-permute-done | bytes 98336 | tf_op jit(solution)/shard_map/ppermute | solution.py:209
  116.0 1.0 collective-permute-done.13
  117.0 6.2 %fusion.4 = bf16[384,3584]{1,0:T(8,128)(2,1)S(1)} fusion(bf16[384,1024]{1,0:T(8,128)(2,1)S(1)} %constant_dynamic-update-slice_fusion, bf16[1024,1792]{1,0:T(8,128)(2,1)} %param.36, bf16[1024,1792]{1,0:T(8,128)(2,1)} %param.35), kind=kOutput, calls=%fused_computation.4 | convolution fusion | flops 2834628608 | bytes 10878976 | tf_op jit(solution)/shard_map/dot_general | solution.py:300
  123.2 1.5 copy-done.3
  125.0 3.1 %collective-permute-done.14 = bf16[192,3584]{1,0:T(8,128)(2,1)S(1)} collective-permute-done((bf16[192,3584]{1,0:T(8,128)(2,1)S(1)}, bf16[192,3584]{1,0:T(8,128)(2,1)S(1)}, u32[]{:S(2)}, u32[]{:S(2)}) %collective-permute-start.14) | collective-permute-done | bytes 1376288 | tf_op jit(solution)/shard_map/ppermute | solution.py:334
  128.0 1.7 add_convert_fusion
  131.4 1.4 collective-permute-start.19
  132.8 2.3 %collective-permute-start.21 = (f32[1,48]{1,0:T(1,128)S(1)}, f32[1,48]{1,0:T(1,128)S(1)}, u32[]{:S(2)}, u32[]{:S(2)}) collective-permute-start(f32[1,48]{1,0:T(1,128)S(1)} %bitcast.35), channel_id=1, source_target_pairs={{0,24},{4,28},{8,16},{12,20},{16,8},{20,12},{24,0},{28,4},{1,25},{... | collective-permute-start | bytes 584 | tf_op jit(solution)/shard_map/ppermute | solution.py:209
  135.1 1.0 collective-permute-start.16
  136.0 1.0 collective-permute-start.18
  137.1 1.0 collective-permute-start.20
  138.1 1.0 collective-permute-start.22
  139.6 1.1 collective-permute-done.20
  140.6 1.0 collective-permute-done.22
  141.8 6.4 %all-gather = f32[4,1,384]{2,1,0:T(1,128)S(1)} all-gather(f32[1,1,384]{2,1,0:T(1,128)S(1)} %bitcast.32), channel_id=1, replica_groups=mesh['kv'=8,'mlp'=4] {'mlp'}, dimensions={0}, use_global_device_ids=true | all-gather | bytes 7680 | tf_op jit(solution)/shard_map/all_gather | solution.py:303
  149.5 9.6 %collective-permute-done.23 = bf16[96,1792]{1,0:T(8,128)(2,1)S(1)} collective-permute-done((bf16[96,1792]{1,0:T(8,128)(2,1)S(1)}, bf16[96,1792]{1,0:T(8,128)(2,1)S(1)}, u32[]{:S(2)}, u32[]{:S(2)}) %collective-permute-start.23) | collective-permute-done | bytes 344096 | tf_op jit(solution)/shard_map/ppermute | solution.py:344
  159.3 2.1 %collective-permute-done.24 = bf16[192,1792]{1,0:T(8,128)(2,1)S(1)} collective-permute-done((bf16[192,1792]{1,0:T(8,128)(2,1)S(1)}, bf16[192,1792]{1,0:T(8,128)(2,1)S(1)}, u32[]{:S(2)}, u32[]{:S(2)}) %collective-permute-start.24) | collective-permute-done | bytes 688160 | tf_op jit(solution)/shard_map/ppermute | solution.py:344
  161.4 3.6 %convolution_convert_fusion.1 = bf16[384,1024]{1,0:T(8,128)(2,1)S(1)} fusion(bf16[1792,1024]{1,0:T(8,128)(2,1)} %param.37, bf16[192,1792]{1,0:T(8,128)(2,1)S(1)} %collective-permute-done.24, bf16[192,1792]{1,0:T(8,128)(2,1)S(1)} %maximum_select_fusion.2, pred[]{:T(512)S(6)} %eq.56), kind=kOutput, calls=%fused_computation.8 | convolution fusion | flops 1415872512 | bytes 5832705 | tf_op jit(solution)/shard_map/dot_general | solution.py:310
  165.1 1.0 collective-permute-start.26
  166.1 1.0 collective-permute-start.28
  167.2 1.0 collective-permute-start.30
  168.2 1.0 collective-permute-start.25
  169.2 1.6 collective-permute-done.26
  170.8 2.1 %collective-permute-done.28 = bf16[48,1024]{1,0:T(8,128)(2,1)S(1)} collective-permute-done((bf16[48,1024]{1,0:T(8,128)(2,1)S(1)}, bf16[48,1024]{1,0:T(8,128)(2,1)S(1)}, u32[]{:S(2)}, u32[]{:S(2)}) %collective-permute-start.28) | collective-permute-done | bytes 98336 | tf_op jit(solution)/shard_map/ppermute | solution.py:209
  172.9 2.1 %collective-permute-done.30 = bf16[48,1024]{1,0:T(8,128)(2,1)S(1)} collective-permute-done((bf16[48,1024]{1,0:T(8,128)(2,1)S(1)}, bf16[48,1024]{1,0:T(8,128)(2,1)S(1)}, u32[]{:S(2)}, u32[]{:S(2)}) %collective-permute-start.30) | collective-permute-done | bytes 98336 | tf_op jit(solution)/shard_map/ppermute | solution.py:209
  175.1 1.5 collective-permute-start.27
  177.2 2.3 %collective-permute-start.31 = (bf16[48,1024]{1,0:T(8,128)(2,1)S(1)}, bf16[48,1024]{1,0:T(8,128)(2,1)S(1)}, u32[]{:S(2)}, u32[]{:S(2)}) collective-permute-start(bf16[48,1024]{1,0:T(8,128)(2,1)S(1)} %get-tuple-element.17), channel_id=1, source_target_pairs={{0,8},{4,12},{8,0},{12,4},{16,24},{20,28},{24,16},{28,20},{1,9},{5... | collective-permute-start | bytes 294920 | tf_op jit(solution)/shard_map/ppermute | solution.py:209
  179.6 2.8 %collective-permute-done.27 = bf16[48,1024]{1,0:T(8,128)(2,1)S(1)} collective-permute-done((bf16[48,1024]{1,0:T(8,128)(2,1)S(1)}, bf16[48,1024]{1,0:T(8,128)(2,1)S(1)}, u32[]{:S(2)}, u32[]{:S(2)}) %collective-permute-start.27) | collective-permute-done | bytes 98336 | tf_op jit(solution)/shard_map/ppermute | solution.py:209
  182.4 3.1 %collective-permute-done.29 = bf16[48,1024]{1,0:T(8,128)(2,1)S(1)} collective-permute-done((bf16[48,1024]{1,0:T(8,128)(2,1)S(1)}, bf16[48,1024]{1,0:T(8,128)(2,1)S(1)}, u32[]{:S(2)}, u32[]{:S(2)}) %collective-permute-start.29) | collective-permute-done | bytes 98336 | tf_op jit(solution)/shard_map/ppermute | solution.py:209
  (89 shorter events, 19.4 us)
Async XLA Ops:
  0.6 17.4 %collective-permute-start.1 = (bf16[48,1024]{1,0:T(8,128)(2,1)}, bf16[48,1024]{1,0:T(8,128)(2,1)S(1)}, u32[]{:S(2)}, u32[]{:S(2)}) collective-permute-start(bf16[48,1024]{1,0:T(8,128)(2,1)} %refs_0_.1), channel_id=1, source_target_pairs={{0,8},{4,12},{8,0},{12,4},{16,24},{20,28},{24,16},{28,20},{1,9},{5... | collective-permute-start | bytes 294920 | tf_op jit(solution)/shard_map/ppermute | solution.py:209
  3.7 14.7 %collective-permute-start.3 = (bf16[48,1024]{1,0:T(8,128)(2,1)}, bf16[48,1024]{1,0:T(8,128)(2,1)S(1)}, u32[]{:S(2)}, u32[]{:S(2)}) collective-permute-start(bf16[48,1024]{1,0:T(8,128)(2,1)} %refs_0_.1), channel_id=1, source_target_pairs={{0,16},{4,20},{8,24},{12,28},{16,0},{20,4},{24,8},{28,12},{1,17},{... | collective-permute-start | bytes 294920 | tf_op jit(solution)/shard_map/ppermute | solution.py:209
  6.3 13.8 %collective-permute-start.5 = (bf16[48,1024]{1,0:T(8,128)(2,1)}, bf16[48,1024]{1,0:T(8,128)(2,1)S(1)}, u32[]{:S(2)}, u32[]{:S(2)}) collective-permute-start(bf16[48,1024]{1,0:T(8,128)(2,1)} %refs_0_.1), channel_id=1, source_target_pairs={{0,24},{4,28},{8,16},{12,20},{16,8},{20,12},{24,0},{28,4},{1,25},{... | collective-permute-start | bytes 294920 | tf_op jit(solution)/shard_map/ppermute | solution.py:209
  6.3 14.1 %collective-permute-start = (bf16[48,1024]{1,0:T(8,128)(2,1)}, bf16[48,1024]{1,0:T(8,128)(2,1)S(1)}, u32[]{:S(2)}, u32[]{:S(2)}) collective-permute-start(bf16[48,1024]{1,0:T(8,128)(2,1)} %refs_0_.1), channel_id=1, source_target_pairs={{0,4},{4,0},{8,12},{12,8},{16,20},{20,16},{24,28},{28,24},{1,5},{5... | collective-permute-start | bytes 294920 | tf_op jit(solution)/shard_map/ppermute | solution.py:209
  18.1 5.6 %collective-permute-start.2 = (bf16[48,1024]{1,0:T(8,128)(2,1)S(1)}, bf16[48,1024]{1,0:T(8,128)(2,1)S(1)}, u32[]{:S(2)}, u32[]{:S(2)}) collective-permute-start(bf16[48,1024]{1,0:T(8,128)(2,1)S(1)} %collective-permute-done.1.refs_2_), channel_id=1, source_target_pairs={{0,4},{4,0},{8,12},{12,8},{16,20},{20,16},{24,28},{28,24},{1,5},{5... | collective-permute-start | bytes 294920 | tf_op jit(solution)/shard_map/ppermute | solution.py:209
  18.4 6.3 %collective-permute-start.4 = (bf16[48,1024]{1,0:T(8,128)(2,1)S(1)}, bf16[48,1024]{1,0:T(8,128)(2,1)S(1)}, u32[]{:S(2)}, u32[]{:S(2)}) collective-permute-start(bf16[48,1024]{1,0:T(8,128)(2,1)S(1)} %collective-permute-done.3.refs_4_), channel_id=1, source_target_pairs={{0,4},{4,0},{8,12},{12,8},{16,20},{20,16},{24,28},{28,24},{1,5},{5... | collective-permute-start | bytes 294920 | tf_op jit(solution)/shard_map/ppermute | solution.py:209
  20.1 5.7 %collective-permute-start.6 = (bf16[48,1024]{1,0:T(8,128)(2,1)S(1)}, bf16[48,1024]{1,0:T(8,128)(2,1)S(1)}, u32[]{:S(2)}, u32[]{:S(2)}) collective-permute-start(bf16[48,1024]{1,0:T(8,128)(2,1)S(1)} %collective-permute-done.5.refs_6_), channel_id=1, source_target_pairs={{0,4},{4,0},{8,12},{12,8},{16,20},{20,16},{24,28},{28,24},{1,5},{5... | collective-permute-start | bytes 294920 | tf_op jit(solution)/shard_map/ppermute | solution.py:209
  25.8 2.2 %copy-start = (bf16[1,4096,512]{2,1,0:T(8,128)(2,1)S(1)}, bf16[1,4096,512]{2,1,0:T(8,128)(2,1)}, u32[]{:S(2)}) copy-start(bf16[1,4096,512]{2,1,0:T(8,128)(2,1)} %refs_8_.1) | copy-start | bytes 12582916
  28.0 0.9 copy-start.1
  81.5 0.9 copy-start.2
  85.1 5.1 %copy-start.4 = (bf16[48,1024]{1,0:T(8,128)(2,1)}, bf16[48,1024]{1,0:T(8,128)(2,1)S(1)}, u32[]{:S(2)}) copy-start(bf16[48,1024]{1,0:T(8,128)(2,1)S(1)} %fusion.16) | copy-start | bytes 294916
  85.1 15.2 %copy-start.5 = (bf16[48,1024]{1,0:T(8,128)(2,1)S(1)}, bf16[48,1024]{1,0:T(8,128)(2,1)}, u32[]{:S(2)}) copy-start(bf16[48,1024]{1,0:T(8,128)(2,1)} %param.32) | copy-start | bytes 294916
  85.1 15.2 %copy-start.6 = (f32[1024]{0:T(1024)S(1)}, f32[1024]{0:T(1024)}, u32[]{:S(2)}) copy-start(f32[1024]{0:T(1024)} %param.34) | copy-start | bytes 12292
  100.4 5.7 %collective-permute-start.8 = (bf16[48,1024]{1,0:T(8,128)(2,1)S(1)}, bf16[48,1024]{1,0:T(8,128)(2,1)S(1)}, u32[]{:S(2)}, u32[]{:S(2)}) collective-permute-start(bf16[48,1024]{1,0:T(8,128)(2,1)S(1)} %get-tuple-element.9), channel_id=1, source_target_pairs={{0,8},{4,12},{8,0},{12,4},{16,24},{20,28},{24,16},{28,20},{1,9},{5... | collective-permute-start | bytes 294920 | tf_op jit(solution)/shard_map/ppermute | solution.py:209
  101.3 10.1 %collective-permute-start.10 = (bf16[48,1024]{1,0:T(8,128)(2,1)S(1)}, bf16[48,1024]{1,0:T(8,128)(2,1)S(1)}, u32[]{:S(2)}, u32[]{:S(2)}) collective-permute-start(bf16[48,1024]{1,0:T(8,128)(2,1)S(1)} %get-tuple-element.9), channel_id=1, source_target_pairs={{0,16},{4,20},{8,24},{12,28},{16,0},{20,4},{24,8},{28,12},{1,17},{... | collective-permute-start | bytes 294920 | tf_op jit(solution)/shard_map/ppermute | solution.py:209
  102.4 9.4 %collective-permute-start.12 = (bf16[48,1024]{1,0:T(8,128)(2,1)S(1)}, bf16[48,1024]{1,0:T(8,128)(2,1)S(1)}, u32[]{:S(2)}, u32[]{:S(2)}) collective-permute-start(bf16[48,1024]{1,0:T(8,128)(2,1)S(1)} %get-tuple-element.9), channel_id=1, source_target_pairs={{0,24},{4,28},{8,16},{12,20},{16,8},{20,12},{24,0},{28,4},{1,25},{... | collective-permute-start | bytes 294920 | tf_op jit(solution)/shard_map/ppermute | solution.py:209
  104.8 8.5 %collective-permute-start.7 = (bf16[48,1024]{1,0:T(8,128)(2,1)S(1)}, bf16[48,1024]{1,0:T(8,128)(2,1)S(1)}, u32[]{:S(2)}, u32[]{:S(2)}) collective-permute-start(bf16[48,1024]{1,0:T(8,128)(2,1)S(1)} %get-tuple-element.9), channel_id=1, source_target_pairs={{0,4},{4,0},{8,12},{12,8},{16,20},{20,16},{24,28},{28,24},{1,5},{5... | collective-permute-start | bytes 294920 | tf_op jit(solution)/shard_map/ppermute | solution.py:209
  106.1 7.3 %collective-permute-start.9 = (bf16[48,1024]{1,0:T(8,128)(2,1)S(1)}, bf16[48,1024]{1,0:T(8,128)(2,1)S(1)}, u32[]{:S(2)}, u32[]{:S(2)}) collective-permute-start(bf16[48,1024]{1,0:T(8,128)(2,1)S(1)} %collective-permute-done.8), channel_id=1, source_target_pairs={{0,4},{4,0},{8,12},{12,8},{16,20},{20,16},{24,28},{28,24},{1,5},{5... | collective-permute-start | bytes 294920 | tf_op jit(solution)/shard_map/ppermute | solution.py:209
  111.3 4.6 %collective-permute-start.11 = (bf16[48,1024]{1,0:T(8,128)(2,1)S(1)}, bf16[48,1024]{1,0:T(8,128)(2,1)S(1)}, u32[]{:S(2)}, u32[]{:S(2)}) collective-permute-start(bf16[48,1024]{1,0:T(8,128)(2,1)S(1)} %collective-permute-done.10), channel_id=1, source_target_pairs={{0,4},{4,0},{8,12},{12,8},{16,20},{20,16},{24,28},{28,24},{1,5},{5... | collective-permute-start | bytes 294920 | tf_op jit(solution)/shard_map/ppermute | solution.py:209
  111.8 5.2 %collective-permute-start.13 = (bf16[48,1024]{1,0:T(8,128)(2,1)S(1)}, bf16[48,1024]{1,0:T(8,128)(2,1)S(1)}, u32[]{:S(2)}, u32[]{:S(2)}) collective-permute-start(bf16[48,1024]{1,0:T(8,128)(2,1)S(1)} %collective-permute-done.12), channel_id=1, source_target_pairs={{0,4},{4,0},{8,12},{12,8},{16,20},{20,16},{24,28},{28,24},{1,5},{5... | collective-permute-start | bytes 294920 | tf_op jit(solution)/shard_map/ppermute | solution.py:209
  123.2 1.5 copy-start.3
  124.8 3.2 %collective-permute-start.14 = (bf16[192,3584]{1,0:T(8,128)(2,1)S(1)}, bf16[192,3584]{1,0:T(8,128)(2,1)S(1)}, u32[]{:S(2)}, u32[]{:S(2)}) collective-permute-start(bf16[192,3584]{1,0:T(8,128)(2,1)S(1)} %constant_dynamic-slice_fusion.1), channel_id=1, source_target_pairs={{0,1},{1,0},{2,3},{3,2},{4,5},{5,4},{6,7},{7,6},{8,9},{9,8},{10,11... | collective-permute-start | bytes 4128776 | tf_op jit(solution)/shard_map/ppermute | solution.py:334
  129.7 18.6 %collective-permute-start.15 = (bf16[96,3584]{1,0:T(8,128)(2,1)S(1)}, bf16[96,3584]{1,0:T(8,128)(2,1)S(1)}, u32[]{:S(2)}, u32[]{:S(2)}) collective-permute-start(bf16[96,3584]{1,0:T(8,128)(2,1)S(1)} %constant_dynamic-slice_fusion), channel_id=1, source_target_pairs={{0,2},{1,3},{2,0},{3,1},{4,6},{5,7},{6,4},{7,5},{8,10},{9,11},{10,... | collective-permute-start | bytes 2064392 | tf_op jit(solution)/shard_map/ppermute | solution.py:334
  130.6 5.4 %collective-permute-start.17 = (f32[1,48]{1,0:T(1,128)S(1)}, f32[1,48]{1,0:T(1,128)S(1)}, u32[]{:S(2)}, u32[]{:S(2)}) collective-permute-start(f32[1,48]{1,0:T(1,128)S(1)} %bitcast.33), channel_id=1, source_target_pairs={{0,8},{4,12},{8,0},{12,4},{16,24},{20,28},{24,16},{28,20},{1,9},{5... | collective-permute-start | bytes 584 | tf_op jit(solution)/shard_map/ppermute | solution.py:209
  131.4 5.7 %collective-permute-start.19 = (f32[1,48]{1,0:T(1,128)S(1)}, f32[1,48]{1,0:T(1,128)S(1)}, u32[]{:S(2)}, u32[]{:S(2)}) collective-permute-start(f32[1,48]{1,0:T(1,128)S(1)} %bitcast.34), channel_id=1, source_target_pairs={{0,16},{4,20},{8,24},{12,28},{16,0},{20,4},{24,8},{28,12},{1,17},{... | collective-permute-start | bytes 584 | tf_op jit(solution)/shard_map/ppermute | solution.py:209
  132.8 5.3 %collective-permute-start.21 = (f32[1,48]{1,0:T(1,128)S(1)}, f32[1,48]{1,0:T(1,128)S(1)}, u32[]{:S(2)}, u32[]{:S(2)}) collective-permute-start(f32[1,48]{1,0:T(1,128)S(1)} %bitcast.35), channel_id=1, source_target_pairs={{0,24},{4,28},{8,16},{12,20},{16,8},{20,12},{24,0},{28,4},{1,25},{... | collective-permute-start | bytes 584 | tf_op jit(solution)/shard_map/ppermute | solution.py:209
  135.1 4.1 %collective-permute-start.16 = (f32[1,48]{1,0:T(1,128)S(1)}, f32[1,48]{1,0:T(1,128)S(1)}, u32[]{:S(2)}, u32[]{:S(2)}) collective-permute-start(f32[1,48]{1,0:T(1,128)S(1)} %bitcast.36), channel_id=1, source_target_pairs={{0,4},{4,0},{8,12},{12,8},{16,20},{20,16},{24,28},{28,24},{1,5},{5... | collective-permute-start | bytes 584 | tf_op jit(solution)/shard_map/ppermute | solution.py:209
  136.0 3.5 %collective-permute-start.18 = (f32[1,48]{1,0:T(1,128)S(1)}, f32[1,48]{1,0:T(1,128)S(1)}, u32[]{:S(2)}, u32[]{:S(2)}) collective-permute-start(f32[1,48]{1,0:T(1,128)S(1)} %collective-permute-done.17), channel_id=1, source_target_pairs={{0,4},{4,0},{8,12},{12,8},{16,20},{20,16},{24,28},{28,24},{1,5},{5... | collective-permute-start | bytes 584 | tf_op jit(solution)/shard_map/ppermute | solution.py:209
  137.1 3.5 %collective-permute-start.20 = (f32[1,48]{1,0:T(1,128)S(1)}, f32[1,48]{1,0:T(1,128)S(1)}, u32[]{:S(2)}, u32[]{:S(2)}) collective-permute-start(f32[1,48]{1,0:T(1,128)S(1)} %collective-permute-done.19), channel_id=1, source_target_pairs={{0,4},{4,0},{8,12},{12,8},{16,20},{20,16},{24,28},{28,24},{1,5},{5... | collective-permute-start | bytes 584 | tf_op jit(solution)/shard_map/ppermute | solution.py:209
  138.1 3.5 %collective-permute-start.22 = (f32[1,48]{1,0:T(1,128)S(1)}, f32[1,48]{1,0:T(1,128)S(1)}, u32[]{:S(2)}, u32[]{:S(2)}) collective-permute-start(f32[1,48]{1,0:T(1,128)S(1)} %collective-permute-done.21), channel_id=1, source_target_pairs={{0,4},{4,0},{8,12},{12,8},{16,20},{20,16},{24,28},{28,24},{1,5},{5... | collective-permute-start | bytes 584 | tf_op jit(solution)/shard_map/ppermute | solution.py:209
  148.8 10.3 %collective-permute-start.23 = (bf16[96,1792]{1,0:T(8,128)(2,1)S(1)}, bf16[96,1792]{1,0:T(8,128)(2,1)S(1)}, u32[]{:S(2)}, u32[]{:S(2)}) collective-permute-start(bf16[96,1792]{1,0:T(8,128)(2,1)S(1)} %fusion.13), channel_id=1, source_target_pairs={{0,2},{1,3},{2,0},{3,1},{4,6},{5,7},{6,4},{7,5},{8,10},{9,11},{10,... | collective-permute-start | bytes 1032200 | tf_op jit(solution)/shard_map/ppermute | solution.py:344
  159.2 2.2 %collective-permute-start.24 = (bf16[192,1792]{1,0:T(8,128)(2,1)S(1)}, bf16[192,1792]{1,0:T(8,128)(2,1)S(1)}, u32[]{:S(2)}, u32[]{:S(2)}) collective-permute-start(bf16[192,1792]{1,0:T(8,128)(2,1)S(1)} %maximum_select_fusion.2), channel_id=1, source_target_pairs={{0,1},{1,0},{2,3},{3,2},{4,5},{5,4},{6,7},{7,6},{8,9},{9,8},{10,11... | collective-permute-start | bytes 2064392 | tf_op jit(solution)/shard_map/ppermute | solution.py:344
  165.1 5.7 %collective-permute-start.26 = (bf16[48,1024]{1,0:T(8,128)(2,1)S(1)}, bf16[48,1024]{1,0:T(8,128)(2,1)S(1)}, u32[]{:S(2)}, u32[]{:S(2)}) collective-permute-start(bf16[48,1024]{1,0:T(8,128)(2,1)S(1)} %get-tuple-element.15), channel_id=1, source_target_pairs={{0,4},{4,0},{8,12},{12,8},{16,20},{20,16},{24,28},{28,24},{1,5},{5... | collective-permute-start | bytes 294920 | tf_op jit(solution)/shard_map/ppermute | solution.py:209
  166.1 6.8 %collective-permute-start.28 = (bf16[48,1024]{1,0:T(8,128)(2,1)S(1)}, bf16[48,1024]{1,0:T(8,128)(2,1)S(1)}, u32[]{:S(2)}, u32[]{:S(2)}) collective-permute-start(bf16[48,1024]{1,0:T(8,128)(2,1)S(1)} %get-tuple-element.14), channel_id=1, source_target_pairs={{0,4},{4,0},{8,12},{12,8},{16,20},{20,16},{24,28},{28,24},{1,5},{5... | collective-permute-start | bytes 294920 | tf_op jit(solution)/shard_map/ppermute | solution.py:209
  167.2 7.8 %collective-permute-start.30 = (bf16[48,1024]{1,0:T(8,128)(2,1)S(1)}, bf16[48,1024]{1,0:T(8,128)(2,1)S(1)}, u32[]{:S(2)}, u32[]{:S(2)}) collective-permute-start(bf16[48,1024]{1,0:T(8,128)(2,1)S(1)} %get-tuple-element.13), channel_id=1, source_target_pairs={{0,4},{4,0},{8,12},{12,8},{16,20},{20,16},{24,28},{28,24},{1,5},{5... | collective-permute-start | bytes 294920 | tf_op jit(solution)/shard_map/ppermute | solution.py:209
  168.2 11.4 %collective-permute-start.25 = (bf16[48,1024]{1,0:T(8,128)(2,1)S(1)}, bf16[48,1024]{1,0:T(8,128)(2,1)S(1)}, u32[]{:S(2)}, u32[]{:S(2)}) collective-permute-start(bf16[48,1024]{1,0:T(8,128)(2,1)S(1)} %get-tuple-element.12), channel_id=1, source_target_pairs={{0,4},{4,0},{8,12},{12,8},{16,20},{20,16},{24,28},{28,24},{1,5},{5... | collective-permute-start | bytes 294920 | tf_op jit(solution)/shard_map/ppermute | solution.py:209
  175.1 7.3 %collective-permute-start.27 = (bf16[48,1024]{1,0:T(8,128)(2,1)S(1)}, bf16[48,1024]{1,0:T(8,128)(2,1)S(1)}, u32[]{:S(2)}, u32[]{:S(2)}) collective-permute-start(bf16[48,1024]{1,0:T(8,128)(2,1)S(1)} %get-tuple-element.16), channel_id=1, source_target_pairs={{0,24},{4,28},{8,16},{12,20},{16,8},{20,12},{24,0},{28,4},{1,25},{... | collective-permute-start | bytes 294920 | tf_op jit(solution)/shard_map/ppermute | solution.py:209
  176.6 8.8 %collective-permute-start.29 = (bf16[48,1024]{1,0:T(8,128)(2,1)S(1)}, bf16[48,1024]{1,0:T(8,128)(2,1)S(1)}, u32[]{:S(2)}, u32[]{:S(2)}) collective-permute-start(bf16[48,1024]{1,0:T(8,128)(2,1)S(1)} %get-tuple-element.18), channel_id=1, source_target_pairs={{0,16},{4,20},{8,24},{12,28},{16,0},{20,4},{24,8},{28,12},{1,17},{... | collective-permute-start | bytes 294920 | tf_op jit(solution)/shard_map/ppermute | solution.py:209
  177.2 8.2 %collective-permute-start.31 = (bf16[48,1024]{1,0:T(8,128)(2,1)S(1)}, bf16[48,1024]{1,0:T(8,128)(2,1)S(1)}, u32[]{:S(2)}, u32[]{:S(2)}) collective-permute-start(bf16[48,1024]{1,0:T(8,128)(2,1)S(1)} %get-tuple-element.17), channel_id=1, source_target_pairs={{0,8},{4,12},{8,0},{12,4},{16,24},{20,28},{24,16},{28,20},{1,9},{5... | collective-permute-start | bytes 294920 | tf_op jit(solution)/shard_map/ppermute | solution.py:209

commit v2 on v1

--- a/solution.py
+++ b/solution.py
@@ -20,48 +20,66 @@
 BLOCK = 512
 
 
-def count_below(sorted_values, bounds):
-    return jnp.sum((sorted_values[None, :] < bounds[:, None]).astype(jnp.int32), axis=1)
-
-
-def slot_nodes(slot_map, lengths, wanted):
-    node_ids = jnp.arange(slot_map.shape[0], dtype=jnp.int32)
-    matches = slot_map[None, :] == wanted[:, None]
-    nodes = jnp.sum(jnp.where(matches, node_ids[None, :], 0), axis=1)
-    return nodes, jnp.sum(jnp.where(matches, lengths[None, :], 0), axis=1)
-
-
 def own_nodes(owner, local_counts, tree, lengths, slots):
     token_leaf, leaf_parent, mid_parent = tree
-    picked = [
-        slot_nodes(slot_map, level_len, owner * local + jnp.arange(local, dtype=jnp.int32))
-        for slot_map, level_len, local in zip(slots, lengths, local_counts)
-    ]
-    edges = jnp.concatenate([picked[0][0], picked[0][0] + 1])
-    edges = jnp.concatenate([count_below(mid_parent, edges), picked[1][0], picked[1][0] + 1])
-    edges = jnp.concatenate([count_below(leaf_parent, edges), picked[2][0], picked[2][0] + 1])
-    edges = count_below(token_leaf, edges)
-    first, last, place = [], [], 0
-    for local in local_counts:
-        first.append(edges[place : place + local])
-        last.append(edges[place + local : place + 2 * local])
-        place += 2 * local
-    return jnp.stack(
-        [
-            jnp.concatenate(first),
-            jnp.concatenate(last),
-            jnp.concatenate([level_len for _, level_len in picked]),
-        ]
-    ).astype(jnp.int32)
-
-
-def tree_attention(query_parts, caches, nodes, owner):
+    node_total = sum(local_counts)
+
+    def kernel(owner_ref, token_ref, leaf_up, mid_up, *refs):
+        len_refs, slot_refs, out_ref = refs[:3], refs[3:6], refs[6]
+
+        def find(slot_ref, len_ref, local):
+            base = owner_ref[0] * local
+
+            def step(j, found):
+                at, size = slot_ref[j] - base, len_ref[j]
+                return tuple(
+                    (jnp.where(at == k, j, node), jnp.where(at == k, size, length))
+                    for k, (node, length) in enumerate(found)
+                )
+
+            zero = jnp.int32(0)
+            return lax.fori_loop(0, slot_ref.shape[0], step, ((zero, zero),) * local)
+
+        def below(parent_ref, edges):
+            def step(j, counted):
+                parent = parent_ref[j]
+                return tuple(
+                    c + jnp.where(parent < edge, 1, 0) for c, edge in zip(counted, edges)
+                )
+
+            return lax.fori_loop(0, parent_ref.shape[0], step, (jnp.int32(0),) * len(edges))
+
+        picked = [find(*level) for level in zip(slot_refs, len_refs, local_counts)]
+        edges = ()
+        for level, parent_ref in enumerate((mid_up, leaf_up, None)):
+            for node, _ in picked[level]:
+                edges += (node, node + 1)
+            if parent_ref is not None:
+                edges = below(parent_ref, edges)
+        tokens = token_ref[...]
+        sizes = [length for level in picked for _, length in level]
+        for k in range(node_total):
+            for side in range(2):
+                under = jnp.where(tokens < edges[2 * k + side], 1.0, 0.0)
+                out_ref[side, k] = jnp.sum(under).astype(jnp.int32)
+            out_ref[2, k] = sizes[k]
+
+    smem = pl.BlockSpec(memory_space=pltpu.SMEM)
+    vmem = pl.BlockSpec(memory_space=pltpu.VMEM)
+    return pl.pallas_call(
+        kernel,
+        out_shape=jax.ShapeDtypeStruct((3, node_total), jnp.int32),
+        in_specs=[smem, vmem] + [smem] * 8,
+        out_specs=smem,
+        name="own_nodes",
+    )(owner[None], token_leaf.reshape(-1, HEAD), leaf_parent, mid_parent, *lengths, *slots)
+
+
+def tree_attention(query_parts, caches, nodes, owner, kv_head):
     part_total = len(query_parts)
     own_rows, width = query_parts[0].shape
     total_rows = part_total * own_rows
-    kv_count = caches[0].shape[2] // (2 * HEAD)
-    head_count = width // HEAD
-    group_size = head_count // kv_count
+    group_size = width // HEAD
     score_scale = 1.0 / math.sqrt(HEAD)
     levels = []
     for cache, capacity in zip(caches, (QROOT, QMID, QLEAF)):
@@ -86,10 +104,8 @@
                 node += 1
                 window = jnp.minimum(low - lax.rem(low, ALIGN), total_rows - rows)
                 window = pl.multiple_of(window, ALIGN)
-                for kv_head in range(kv_count):
-                    columns = [
-                        (kv_head * group_size + h) * HEAD for h in range(group_size)
-                    ]
+                columns = [h * HEAD for h in range(group_size)]
+                if True:
                     grouped = jnp.concatenate(
                         [all_rows[pl.ds(window, rows), c : c + HEAD] for c in columns], axis=0
                     )
@@ -164,14 +180,14 @@
             at = part * own_rows
             out_ref[part, :, :width] = run_out[at : at + own_rows, :].astype(jnp.bfloat16)
             lse = jnp.zeros((own_rows, HEAD), jnp.float32)
-            for h in range(head_count):
+            for h in range(group_size):
                 piece = run_lse[at : at + own_rows, h * HEAD : (h + 1) * HEAD]
-                lse = jnp.where(lax.rem(lane, head_count) == h, piece, lse)
+                lse = jnp.where(lax.rem(lane, group_size) == h, piece, lse)
             first = lse.astype(jnp.bfloat16)
             rest = lse - first.astype(jnp.float32)
             second = rest.astype(jnp.bfloat16)
             third = rest - second.astype(jnp.float32)
-            field = lax.div(lane, head_count)
+            field = lax.div(lane, group_size)
             packed = jnp.where(
                 field == 0,
                 first.astype(jnp.float32),
@@ -202,6 +218,21 @@
         compiler_params=pltpu.CompilerParams(vmem_limit_bytes=48 << 20),
         name="tree_attention",
     )(nodes, owner[None], *query_parts, *caches)
+
+
+def combine(every, group_size):
+    width = group_size * HEAD
+    fields = every[:, :, width : width + 3 * group_size].astype(jnp.float32)
+    every_lse = (
+        fields[:, :, :group_size]
+        + fields[:, :, group_size : 2 * group_size]
+        + fields[:, :, 2 * group_size :]
+    )
+    every_out = every[:, :, :width].reshape(every.shape[0], every.shape[1], group_size, HEAD)
+    share = jnp.exp(every_lse - jnp.max(every_lse, axis=0))
+    summed = jnp.sum(every_out.astype(jnp.float32) * share[..., None], axis=0)
+    summed = summed / jnp.sum(share, axis=0)[..., None]
+    return summed.reshape(every.shape[1], width).astype(jnp.bfloat16)
 
 
 def swap(value, axis_name, mask):
@@ -253,7 +284,6 @@
     down_weight,
 ):
     own_rows, width = queries.shape
-    head_count = width // HEAD
     owner = lax.axis_index("kv").astype(jnp.int32)
     caches = (root_cache, mid_cache, leaf_cache)
     nodes = own_nodes(
@@ -263,45 +293,42 @@
         (root_len, mid_len, leaf_len),
         (root_slot, mid_slot, leaf_slot),
     )
-    parts = tree_attention(gather_parts(queries, "kv"), caches, nodes, owner)
-    every = lax.all_to_all(parts, "kv", 0, 0)
-    fields = every[:, :, width : width + 3 * head_count].astype(jnp.float32)
-    every_lse = (
-        fields[:, :, :head_count]
-        + fields[:, :, head_count : 2 * head_count]
-        + fields[:, :, 2 * head_count :]
-    )
-    every_out = every[:, :, :width].reshape(-1, own_rows, head_count, HEAD)
-    share = jnp.exp(every_lse - jnp.max(every_lse, axis=0))
-    attended = (
-        (
-            jnp.sum(every_out.astype(jnp.float32) * share[..., None], axis=0)
-            / jnp.sum(share, axis=0)[..., None]
+    kv_count = root_cache.shape[2] // (2 * HEAD)
+    group_width = width // kv_count
+    group_size = group_width // HEAD
+    gathered = [
+        gather_parts(queries[:, k * group_width : (k + 1) * group_width], "kv")
+        for k in range(kv_count)
+    ]
+    attended, projected = [], 0.0
+    for k in range(kv_count):
+        parts = tree_attention(gathered[k], caches, nodes, owner, k)
+        attended.append(combine(lax.all_to_all(parts, "kv", 0, 0), group_size))
+        projected = projected + jnp.dot(
+            attended[k],
+            out_weight[k * group_width : (k + 1) * group_width],
+            preferred_element_type=jnp.float32,
         )
-        .reshape(own_rows, width)
-        .astype(jnp.bfloat16)
-    )
+    attended = jnp.concatenate(attended, axis=1)
     mlp_total = lax.axis_size("mlp")
     own_width = stream.shape[1]
-    projected = lax.dot_general(
-        attended, out_weight, (((1,), (0,)), ((), ())), preferred_element_type=jnp.float32
-    ).astype(jnp.bfloat16)
+    projected = projected.astype(jnp.bfloat16)
     projected = projected.reshape(own_rows, mlp_total, own_width).transpose(1, 0, 2)
     projected = jnp.sum(lax.all_to_all(projected, "mlp", 0, 0).astype(jnp.float32), axis=0)
     residual = (stream.astype(jnp.float32) + projected).astype(jnp.bfloat16)
-    widened = lax.optimization_barrier(residual).astype(jnp.float32)
-    square_sum = jnp.sum(widened * widened, axis=1)
-    square_parts = gather_parts(square_sum[None, :], "kv")
-    scaled = jnp.concatenate(
-        gather_parts((widened * norm_gain).astype(jnp.bfloat16), "kv"), axis=0
-    )
+    rows = jnp.concatenate(gather_parts(residual, "kv"), axis=0)
+    widened = lax.optimization_barrier(rows).astype(jnp.float32)
+    squares = jnp.sum(widened * widened, axis=1)[None, :]
+    step = 1
+    while step < mlp_total:
+        squares = squares + swap(squares, "mlp", step)
+        step *= 2
+    scaled = (widened * norm_gain).astype(jnp.bfloat16)
     gate_up = jnp.concatenate([gate_weight, up_weight], axis=1)
     unit_count = gate_weight.shape[1]
     gate_up_sum = jnp.dot(scaled, gate_up, preferred_element_type=jnp.float32)
     share_rows = halve(gate_up_sum.astype(jnp.bfloat16), "mlp", mlp_total)
-    every_square = jnp.concatenate(square_parts, axis=1).reshape(-1)
-    every_square = jnp.sum(lax.all_gather(every_square, "mlp"), axis=0)
-    row_scale = halve_place(lax.rsqrt(every_square / D + EPSILON), "mlp", mlp_total)
+    row_scale = halve_place(lax.rsqrt(squares[0] / D + EPSILON), "mlp", mlp_total)
     share_rows = share_rows.astype(jnp.float32) * row_scale[:, None]
     hidden = (jax.nn.silu(share_rows[:, :unit_count]) * share_rows[:, unit_count:]).astype(
         jnp.bfloat16

time: 189 us -> 200 us (1.058)
  blocking collectives: 50 us -> 10 us
  waiting for transfers between devices: 42.7 us -> 70 us
  starting transfers between devices: 36.6 us -> 56.1 us
  Pallas kernels: 19.1 us -> 31 us
  other arithmetic: 13.6 us -> 5.54 us
    all_to_all x1 -> x0, blocking collectives: 33.5 us -> none  [shards(): every = lax.all_to_all(parts, 'kv', 0, 0)]
    ppermute x28 -> x30, waiting for transfers between devices: 27.9 us -> 45.9 us  [swap(): lax.ppermute(value, axis_name, [(j, j ^ mask) for j in range(axis_total)])]
    all_to_all x0 -> x2, starting transfers between devices: none -> 15.1 us  [shards(): attended.append(combine(lax.all_to_all(parts, 'kv', 0, 0), group_size))]
    all_to_all x0 -> x2, waiting for transfers between devices: none -> 10.4 us  [shards(): attended.append(combine(lax.all_to_all(parts, 'kv', 0, 0), group_size))]
    pallas_call x1 -> x2, Pallas kernels: 19.1 us -> 27.9 us  [tree_attention(): pl.pallas_call(kernel, out_shape=jax.ShapeDtypeStruct((part_total, own_ro...]
    all_gather x1 -> x0, blocking collectives: 6.44 us -> none  [shards(): every_square = jnp.sum(lax.all_gather(every_square, 'mlp'), axis=0)]
    reduce_sum x10 -> x4, other arithmetic: 7.35 us -> 1.34 us  [the longest x1 0.89 us: combine(): summed = summed / jnp.sum(share, axis=0)[..., None]]
    ppermute x28 -> x30, starting transfers between devices: 35 us -> 39.1 us  [swap(): lax.ppermute(value, axis_name, [(j, j ^ mask) for j in range(axis_total)])]
  transfers between devices with their start and end apart: 32 -> 36, of which waited for: 19 -> 20; matrix products, arithmetic and copies ran while one was open for 5% -> 1% of each run, Pallas kernels for 0% -> 9%
where the time goes in v2:
time: 200 us; the launch traced here: 199 us
  waiting for transfers between devices  70 us (35%)
  starting transfers between devices  56.1 us (28%)
  Pallas kernels  31 us (16%)
  matrix products  15.9 us (8%)
  blocking collectives  10 us (5%)
  local copies, waits for them, and re-layouts  9.49 us (5%)
  other arithmetic  5.54 us (3%)
    ppermute x30, waiting for transfers between devices, swap(): lax.ppermute(value, axis_name, [(j, j ^ mask) for j in range(axis_total)])  45.9 us
    ppermute x30, starting transfers between devices, swap(): lax.ppermute(value, axis_name, [(j, j ^ mask) for j in range(axis_total)])  39.1 us
    pallas_call x2, Pallas kernels, tree_attention(): pl.pallas_call(kernel, out_shape=jax.ShapeDtypeStruct((part_total, own_ro...  27.9 us
    all_to_all x2, starting transfers between devices, shards(): attended.append(combine(lax.all_to_all(parts, 'kv', 0, 0), group_size))  15.1 us
    ppermute x2, waiting for transfers between devices, double(): lax.ppermute(rows, axis_name, [(j, j ^ step) for j in range(axis_total)])  10.6 us
    all_to_all x2, waiting for transfers between devices, shards(): attended.append(combine(lax.all_to_all(parts, 'kv', 0, 0), group_size))  10.4 us
    all_to_all x1, blocking collectives, shards(): lax.all_to_all(projected, 'mlp', 0, 0).astype(jnp.float32)  10 us
    unnamed x30, local copies, waits for them, and re-layouts  6.68 us
  transfers between devices with their start and end apart: 36, of which 20 were waited for; matrix products, arithmetic and copies ran while one was open for 1% of the time, Pallas kernels for 9%

profile of v2, /device:TPU:0, one launch (start us, length us, event | category | flops | bytes accessed | tf_op | source)
XLA Modules:
  0.0 199.1 jit_solution(2624192226883300595)
XLA Ops:
  1.5 4.1 %collective-permute-start.10 = (bf16[48,512]{1,0:T(8,128)(2,1)S(1)}, bf16[48,512]{1,0:T(8,128)(2,1)S(1)}, u32[]{:S(2)}, u32[]{:S(2)}) collective-permute-start(bf16[48,512]{1,0:T(8,128)(2,1)S(1)} %get-tuple-element.16.refs_0_), channel_id=1, source_target_pairs={{0,16},{4,20},{8,24},{12,28},{16,0},{20,4},{24,8},{28,12},{1,17},{... | collective-permute-start | bytes 147464 | tf_op jit(solution)/shard_map/ppermute | solution.py:240
  5.5 1.3 collective-permute-start.12
  7.1 1.5 collective-permute-start.7
  8.6 1.2 collective-permute-start.11
  9.8 1.7 collective-permute-done.12.refs_6_
  11.5 1.5 collective-permute-start.13
  13.5 3.0 %own_nodes.1.nodes_ref = s32[3,7]{1,0:T(4,128)} custom-call(s32[1]{0:T(128)} %bitcast.owner_ref, s32[3,128]{1,0:T(4,128)} %bitcast.28, s32[32]{0:T(128)} %leaf_up.1, s32[16]{0:T(128)} %mid_up.1, s32[8]{0:T(128)} %refs_0_.1, s32[16]{0:T(128)} %refs_1_.1, s32[32]{0:T(128)} %refs_2_.1, s32[8]{0:T(128)} %refs_3_.1, s32[16]{0:T(128)} %refs_4_.1, s32[32]{0:T(128)} %refs_5_.1), custom_call_target="tpu_custom_call" | custom-call | tf_op jit(solution)/shard_map/own_nodes/pallas_call | solution.py:69
  17.1 2.2 %copy-done = bf16[1,4096,512]{2,1,0:T(8,128)(2,1)S(1)} copy-done((bf16[1,4096,512]{2,1,0:T(8,128)(2,1)S(1)}, bf16[1,4096,512]{2,1,0:T(8,128)(2,1)}, u32[]{:S(2)}) %copy-start) | copy-done | bytes 4194328
  20.0 13.9 %tree_attention.3 = bf16[8,48,640]{2,1,0:T(8,128)(2,1)} custom-call(s32[3,7]{1,0:T(4,128)S(1)} %copy-done.2, s32[1]{0:T(128)} %bitcast.owner_ref, bf16[48,512]{1,0:T(8,128)(2,1)S(1)} %get-tuple-element.16.refs_0_, bf16[48,512]{1,0:T(8,128)(2,1)S(1)} %collective-permute-done.7.refs_1_, bf16[48,512]{1,0:T(8,128)(2,1)S(1)} %collective-permute-done.8.refs_2_, ...), custom_call_target="tpu_custom_call" | custom-call | tf_op jit(solution)/shard_map/tree_attention/pallas_call | solution.py:205
  33.8 8.6 %all-to-all-start.1 = ((bf16[8,48,640]{2,1,0:T(8,128)(2,1)}), bf16[8,48,640]{2,1,0:T(8,128)(2,1)S(1)}, u32[]{:S(2)}, u32[]{:S(2)}) async-start(bf16[8,48,640]{2,1,0:T(8,128)(2,1)} %tree_attention.3), calls=%async_computation.1 | async-start | bytes 983040 | tf_op jit(solution)/shard_map/all_to_all | solution.py:306
  42.4 2.0 %collective-permute-start.1 = (bf16[48,512]{1,0:T(8,128)(2,1)S(1)}, bf16[48,512]{1,0:T(8,128)(2,1)S(1)}, u32[]{:S(2)}, u32[]{:S(2)}) collective-permute-start(bf16[48,512]{1,0:T(8,128)(2,1)S(1)} %get-tuple-element.15.refs_0_), channel_id=1, source_target_pairs={{0,8},{4,12},{8,0},{12,4},{16,24},{20,28},{24,16},{28,20},{1,9},{5... | collective-permute-start | bytes 147464 | tf_op jit(solution)/shard_map/ppermute | solution.py:240
  44.4 2.4 %collective-permute-start.3 = (bf16[48,512]{1,0:T(8,128)(2,1)S(1)}, bf16[48,512]{1,0:T(8,128)(2,1)S(1)}, u32[]{:S(2)}, u32[]{:S(2)}) collective-permute-start(bf16[48,512]{1,0:T(8,128)(2,1)S(1)} %get-tuple-element.15.refs_0_), channel_id=1, source_target_pairs={{0,16},{4,20},{8,24},{12,28},{16,0},{20,4},{24,8},{28,12},{1,17},{... | collective-permute-start | bytes 147464 | tf_op jit(solution)/shard_map/ppermute | solution.py:240
  46.8 2.0 %collective-permute-start = (bf16[48,512]{1,0:T(8,128)(2,1)S(1)}, bf16[48,512]{1,0:T(8,128)(2,1)S(1)}, u32[]{:S(2)}, u32[]{:S(2)}) collective-permute-start(bf16[48,512]{1,0:T(8,128)(2,1)S(1)} %get-tuple-element.15.refs_0_), channel_id=1, source_target_pairs={{0,4},{4,0},{8,12},{12,8},{16,20},{20,16},{24,28},{28,24},{1,5},{5... | collective-permute-start | bytes 147464 | tf_op jit(solution)/shard_map/ppermute | solution.py:240
  49.5 1.7 collective-permute-start.2
  51.2 5.6 %collective-permute-done.3.refs_4_ = bf16[48,512]{1,0:T(8,128)(2,1)S(1)} collective-permute-done((bf16[48,512]{1,0:T(8,128)(2,1)S(1)}, bf16[48,512]{1,0:T(8,128)(2,1)S(1)}, u32[]{:S(2)}, u32[]{:S(2)}) %collective-permute-start.3) | collective-permute-done | bytes 49184 | tf_op jit(solution)/shard_map/ppermute | solution.py:240
  56.8 1.5 collective-permute-start.4
  58.8 2.1 %collective-permute-done.4.refs_5_ = bf16[48,512]{1,0:T(8,128)(2,1)S(1)} collective-permute-done((bf16[48,512]{1,0:T(8,128)(2,1)S(1)}, bf16[48,512]{1,0:T(8,128)(2,1)S(1)}, u32[]{:S(2)}, u32[]{:S(2)}) %collective-permute-start.4) | collective-permute-done | bytes 49184 | tf_op jit(solution)/shard_map/ppermute | solution.py:240
  60.9 1.5 collective-permute-done.6.refs_7_
  62.3 2.2 %copy-done.1 = bf16[1,4096,512]{2,1,0:T(8,128)(2,1)S(1)} copy-done((bf16[1,4096,512]{2,1,0:T(8,128)(2,1)S(1)}, bf16[1,4096,512]{2,1,0:T(8,128)(2,1)}, u32[]{:S(2)}) %copy-start.1) | copy-done | bytes 4194328
  64.5 14.1 %tree_attention.2 = bf16[8,48,640]{2,1,0:T(8,128)(2,1)} custom-call(s32[3,7]{1,0:T(4,128)S(1)} %copy-done.3, s32[1]{0:T(128)} %bitcast.owner_ref, bf16[48,512]{1,0:T(8,128)(2,1)S(1)} %get-tuple-element.15.refs_0_, bf16[48,512]{1,0:T(8,128)(2,1)S(1)} %collective-permute-done.refs_1_, bf16[48,512]{1,0:T(8,128)(2,1)S(1)} %collective-permute-done.1.refs_2_, ...), custom_call_target="tpu_custom_call" | custom-call | tf_op jit(solution)/shard_map/tree_attention/pallas_call | solution.py:205
  78.6 6.6 %all-to-all-start = ((bf16[8,48,640]{2,1,0:T(8,128)(2,1)}), bf16[8,48,640]{2,1,0:T(8,128)(2,1)S(1)}, u32[]{:S(2)}, u32[]{:S(2)}) async-start(bf16[8,48,640]{2,1,0:T(8,128)(2,1)} %tree_attention.2), calls=%async_computation | async-start | bytes 983040 | tf_op jit(solution)/shard_map/all_to_all | solution.py:306
  85.3 10.4 %all-to-all-done = bf16[8,48,640]{2,1,0:T(8,128)(2,1)S(1)} async-done(((bf16[8,48,640]{2,1,0:T(8,128)(2,1)}), bf16[8,48,640]{2,1,0:T(8,128)(2,1)S(1)}, u32[]{:S(2)}, u32[]{:S(2)}) %all-to-all-start) | async-done | bytes 491552 | tf_op jit(solution)/shard_map/all_to_all | solution.py:306
  98.7 3.0 %fusion.9 = f32[48,4096]{1,0:T(8,128)S(1)} fusion(bf16[48,512]{1,0:T(8,128)(2,1)S(1)} %fusion.23, bf16[1024,4096]{1,0:T(8,128)(2,1)} %param.33), kind=kOutput, calls=%fused_computation.8 | convolution fusion | flops 201326592 | bytes 5029888 | tf_op jit(solution)/shard_map/dot_general | solution.py:307
  102.0 3.1 %fusion.7 = bf16[48,4096]{1,0:T(8,128)(2,1)S(1)} fusion(f32[48,4096]{1,0:T(8,128)S(1)} %fusion.9, bf16[48,512]{1,0:T(8,128)(2,1)S(1)} %fusion.22, bf16[1024,4096]{1,0:T(8,128)(2,1)} %param.33), kind=kOutput, calls=%fused_computation.6 | convolution fusion | flops 201719808 | bytes 5423104 | tf_op jit(solution)/shard_map/dot_general | solution.py:307
  105.2 10.0 %all_to_all.15 = bf16[4,48,1024]{2,1,0:T(8,128)(2,1)S(1)} all-to-all(bf16[4,48,1024]{2,1,0:T(8,128)(2,1)S(1)} %bitcast.24), channel_id=1, replica_groups=mesh['kv'=8,'mlp'=4] {'mlp'}, dimensions={0} | all-to-all | bytes 786432 | tf_op jit(solution)/shard_map/all_to_all | solution.py:317
  117.1 2.6 %collective-permute-start.19 = (bf16[48,1024]{1,0:T(8,128)(2,1)S(1)}, bf16[48,1024]{1,0:T(8,128)(2,1)S(1)}, u32[]{:S(2)}, u32[]{:S(2)}) collective-permute-start(bf16[48,1024]{1,0:T(8,128)(2,1)S(1)} %get-tuple-element.3), channel_id=1, source_target_pairs={{0,24},{4,28},{8,16},{12,20},{16,8},{20,12},{24,0},{28,4},{1,25},{... | collective-permute-start | bytes 294920 | tf_op jit(solution)/shard_map/ppermute | solution.py:240
  119.7 1.5 collective-permute-start.14
  122.0 4.2 %collective-permute-done.17 = bf16[48,1024]{1,0:T(8,128)(2,1)S(1)} collective-permute-done((bf16[48,1024]{1,0:T(8,128)(2,1)S(1)}, bf16[48,1024]{1,0:T(8,128)(2,1)S(1)}, u32[]{:S(2)}, u32[]{:S(2)}) %collective-permute-start.17) | collective-permute-done | bytes 98336 | tf_op jit(solution)/shard_map/ppermute | solution.py:240
  128.3 2.5 %collective-permute-done.18 = bf16[48,1024]{1,0:T(8,128)(2,1)S(1)} collective-permute-done((bf16[48,1024]{1,0:T(8,128)(2,1)S(1)}, bf16[48,1024]{1,0:T(8,128)(2,1)S(1)}, u32[]{:S(2)}, u32[]{:S(2)}) %collective-permute-start.18) | collective-permute-done | bytes 98336 | tf_op jit(solution)/shard_map/ppermute | solution.py:240
  131.9 6.2 %fusion.4 = bf16[384,3584]{1,0:T(8,128)(2,1)S(1)} fusion(bf16[1024,1792]{1,0:T(8,128)(2,1)} %param.36, bf16[1024,1792]{1,0:T(8,128)(2,1)} %param.35, bf16[384,1024]{1,0:T(8,128)(2,1)S(1)} %constant_dynamic-update-slice_fusion, f32[1024]{0:T(1024)S(1)} %copy-done.11), kind=kOutput, calls=%fused_computation.4 | convolution fusion | flops 2835808256 | bytes 10883072 | tf_op jit(solution)/shard_map/dot_general | solution.py:329
  138.1 1.5 copy-done.4
  139.8 3.1 %collective-permute-done.21 = bf16[192,3584]{1,0:T(8,128)(2,1)S(1)} collective-permute-done((bf16[192,3584]{1,0:T(8,128)(2,1)S(1)}, bf16[192,3584]{1,0:T(8,128)(2,1)S(1)}, u32[]{:S(2)}, u32[]{:S(2)}) %collective-permute-start.21) | collective-permute-done | bytes 1376288 | tf_op jit(solution)/shard_map/ppermute | solution.py:361
  142.9 1.7 add_convert_fusion
  145.8 1.1 collective-permute-done.23
  146.9 1.2 collective-permute-start.24
  148.2 14.1 %collective-permute-done.24 = f32[1,384]{1,0:T(1,128)S(1)} collective-permute-done((f32[1,384]{1,0:T(1,128)S(1)}, f32[1,384]{1,0:T(1,128)S(1)}, u32[]{:S(2)}, u32[]{:S(2)}) %collective-permute-start.24) | collective-permute-done | bytes 1568 | tf_op jit(solution)/shard_map/ppermute | solution.py:240
  163.6 8.5 %collective-permute-done.25 = bf16[96,1792]{1,0:T(8,128)(2,1)S(1)} collective-permute-done((bf16[96,1792]{1,0:T(8,128)(2,1)S(1)}, bf16[96,1792]{1,0:T(8,128)(2,1)S(1)}, u32[]{:S(2)}, u32[]{:S(2)}) %collective-permute-start.25) | collective-permute-done | bytes 344096 | tf_op jit(solution)/shard_map/ppermute | solution.py:371
  172.3 2.1 %collective-permute-done.26 = bf16[192,1792]{1,0:T(8,128)(2,1)S(1)} collective-permute-done((bf16[192,1792]{1,0:T(8,128)(2,1)S(1)}, bf16[192,1792]{1,0:T(8,128)(2,1)S(1)}, u32[]{:S(2)}, u32[]{:S(2)}) %collective-permute-start.26) | collective-permute-done | bytes 688160 | tf_op jit(solution)/shard_map/ppermute | solution.py:371
  174.4 3.6 %convolution_convert_fusion = bf16[384,1024]{1,0:T(8,128)(2,1)S(1)} fusion(bf16[1792,1024]{1,0:T(8,128)(2,1)} %param.37, bf16[192,1792]{1,0:T(8,128)(2,1)S(1)} %collective-permute-done.26, bf16[192,1792]{1,0:T(8,128)(2,1)S(1)} %maximum_select_fusion.2, pred[]{:T(512)S(6)} %eq.13), kind=kOutput, calls=%fused_computation.15 | convolution fusion | flops 1415872512 | bytes 5832705 | tf_op jit(solution)/shard_map/dot_general | solution.py:337
  178.1 1.1 collective-permute-start.28
  180.1 1.0 collective-permute-start.32
  182.2 1.6 collective-permute-done.28
  183.8 2.1 %collective-permute-done.30 = bf16[48,1024]{1,0:T(8,128)(2,1)S(1)} collective-permute-done((bf16[48,1024]{1,0:T(8,128)(2,1)S(1)}, bf16[48,1024]{1,0:T(8,128)(2,1)S(1)}, u32[]{:S(2)}, u32[]{:S(2)}) %collective-permute-start.30) | collective-permute-done | bytes 98336 | tf_op jit(solution)/shard_map/ppermute | solution.py:240
  185.9 2.1 %collective-permute-done.32 = bf16[48,1024]{1,0:T(8,128)(2,1)S(1)} collective-permute-done((bf16[48,1024]{1,0:T(8,128)(2,1)S(1)}, bf16[48,1024]{1,0:T(8,128)(2,1)S(1)}, u32[]{:S(2)}, u32[]{:S(2)}) %collective-permute-start.32) | collective-permute-done | bytes 98336 | tf_op jit(solution)/shard_map/ppermute | solution.py:240
  188.1 1.6 collective-permute-start.29
  190.1 2.4 %collective-permute-start.33 = (bf16[48,1024]{1,0:T(8,128)(2,1)S(1)}, bf16[48,1024]{1,0:T(8,128)(2,1)S(1)}, u32[]{:S(2)}, u32[]{:S(2)}) collective-permute-start(bf16[48,1024]{1,0:T(8,128)(2,1)S(1)} %get-tuple-element.13), channel_id=1, source_target_pairs={{0,8},{4,12},{8,0},{12,4},{16,24},{20,28},{24,16},{28,20},{1,9},{5... | collective-permute-start | bytes 294920 | tf_op jit(solution)/shard_map/ppermute | solution.py:240
  193.2 2.1 %collective-permute-done.29 = bf16[48,1024]{1,0:T(8,128)(2,1)S(1)} collective-permute-done((bf16[48,1024]{1,0:T(8,128)(2,1)S(1)}, bf16[48,1024]{1,0:T(8,128)(2,1)S(1)}, u32[]{:S(2)}, u32[]{:S(2)}) %collective-permute-start.29) | collective-permute-done | bytes 98336 | tf_op jit(solution)/shard_map/ppermute | solution.py:240
  195.3 3.1 %collective-permute-done.31 = bf16[48,1024]{1,0:T(8,128)(2,1)S(1)} collective-permute-done((bf16[48,1024]{1,0:T(8,128)(2,1)S(1)}, bf16[48,1024]{1,0:T(8,128)(2,1)S(1)}, u32[]{:S(2)}, u32[]{:S(2)}) %collective-permute-start.31) | collective-permute-done | bytes 98336 | tf_op jit(solution)/shard_map/ppermute | solution.py:240
  (96 shorter events, 20.1 us)
Async XLA Ops:
  1.5 7.2 %collective-permute-start.10 = (bf16[48,512]{1,0:T(8,128)(2,1)S(1)}, bf16[48,512]{1,0:T(8,128)(2,1)S(1)}, u32[]{:S(2)}, u32[]{:S(2)}) collective-permute-start(bf16[48,512]{1,0:T(8,128)(2,1)S(1)} %get-tuple-element.16.refs_0_), channel_id=1, source_target_pairs={{0,16},{4,20},{8,24},{12,28},{16,0},{20,4},{24,8},{28,12},{1,17},{... | collective-permute-start | bytes 147464 | tf_op jit(solution)/shard_map/ppermute | solution.py:240
  5.5 6.0 %collective-permute-start.12 = (bf16[48,512]{1,0:T(8,128)(2,1)S(1)}, bf16[48,512]{1,0:T(8,128)(2,1)S(1)}, u32[]{:S(2)}, u32[]{:S(2)}) collective-permute-start(bf16[48,512]{1,0:T(8,128)(2,1)S(1)} %get-tuple-element.16.refs_0_), channel_id=1, source_target_pairs={{0,24},{4,28},{8,16},{12,20},{16,8},{20,12},{24,0},{28,4},{1,25},{... | collective-permute-start | bytes 147464 | tf_op jit(solution)/shard_map/ppermute | solution.py:240
  6.9 6.1 %collective-permute-start.8 = (bf16[48,512]{1,0:T(8,128)(2,1)S(1)}, bf16[48,512]{1,0:T(8,128)(2,1)S(1)}, u32[]{:S(2)}, u32[]{:S(2)}) collective-permute-start(bf16[48,512]{1,0:T(8,128)(2,1)S(1)} %get-tuple-element.16.refs_0_), channel_id=1, source_target_pairs={{0,8},{4,12},{8,0},{12,4},{16,24},{20,28},{24,16},{28,20},{1,9},{5... | collective-permute-start | bytes 147464 | tf_op jit(solution)/shard_map/ppermute | solution.py:240
  7.1 9.5 %collective-permute-start.7 = (bf16[48,512]{1,0:T(8,128)(2,1)S(1)}, bf16[48,512]{1,0:T(8,128)(2,1)S(1)}, u32[]{:S(2)}, u32[]{:S(2)}) collective-permute-start(bf16[48,512]{1,0:T(8,128)(2,1)S(1)} %get-tuple-element.16.refs_0_), channel_id=1, source_target_pairs={{0,4},{4,0},{8,12},{12,8},{16,20},{20,16},{24,28},{28,24},{1,5},{5... | collective-permute-start | bytes 147464 | tf_op jit(solution)/shard_map/ppermute | solution.py:240
  8.6 8.0 %collective-permute-start.11 = (bf16[48,512]{1,0:T(8,128)(2,1)S(1)}, bf16[48,512]{1,0:T(8,128)(2,1)S(1)}, u32[]{:S(2)}, u32[]{:S(2)}) collective-permute-start(bf16[48,512]{1,0:T(8,128)(2,1)S(1)} %collective-permute-done.10.refs_4_), channel_id=1, source_target_pairs={{0,4},{4,0},{8,12},{12,8},{16,20},{20,16},{24,28},{28,24},{1,5},{5... | collective-permute-start | bytes 147464 | tf_op jit(solution)/shard_map/ppermute | solution.py:240
  11.5 5.1 %collective-permute-start.13 = (bf16[48,512]{1,0:T(8,128)(2,1)S(1)}, bf16[48,512]{1,0:T(8,128)(2,1)S(1)}, u32[]{:S(2)}, u32[]{:S(2)}) collective-permute-start(bf16[48,512]{1,0:T(8,128)(2,1)S(1)} %collective-permute-done.12.refs_6_), channel_id=1, source_target_pairs={{0,4},{4,0},{8,12},{12,8},{16,20},{20,16},{24,28},{28,24},{1,5},{5... | collective-permute-start | bytes 147464 | tf_op jit(solution)/shard_map/ppermute | solution.py:240
  13.0 4.1 %collective-permute-start.9 = (bf16[48,512]{1,0:T(8,128)(2,1)S(1)}, bf16[48,512]{1,0:T(8,128)(2,1)S(1)}, u32[]{:S(2)}, u32[]{:S(2)}) collective-permute-start(bf16[48,512]{1,0:T(8,128)(2,1)S(1)} %collective-permute-done.8.refs_2_), channel_id=1, source_target_pairs={{0,4},{4,0},{8,12},{12,8},{16,20},{20,16},{24,28},{28,24},{1,5},{5... | collective-permute-start | bytes 147464 | tf_op jit(solution)/shard_map/ppermute | solution.py:240
  17.1 2.2 %copy-start = (bf16[1,4096,512]{2,1,0:T(8,128)(2,1)S(1)}, bf16[1,4096,512]{2,1,0:T(8,128)(2,1)}, u32[]{:S(2)}) copy-start(bf16[1,4096,512]{2,1,0:T(8,128)(2,1)} %refs_8_.3) | copy-start | bytes 12582916
  19.3 0.7 copy-start.2
  20.0 42.4 %copy-start.3 = (s32[3,7]{1,0:T(4,128)S(1)}, s32[3,7]{1,0:T(4,128)}, u32[]{:S(2)}) copy-start(s32[3,7]{1,0:T(4,128)} %own_nodes.1.nodes_ref) | copy-start | bytes 256
  33.8 44.7 %all-to-all-start.1 = ((bf16[8,48,640]{2,1,0:T(8,128)(2,1)}), bf16[8,48,640]{2,1,0:T(8,128)(2,1)S(1)}, u32[]{:S(2)}, u32[]{:S(2)}) async-start(bf16[8,48,640]{2,1,0:T(8,128)(2,1)} %tree_attention.3), calls=%async_computation.1 | async-start | bytes 983040 | tf_op jit(solution)/shard_map/all_to_all | solution.py:306
  42.4 7.2 %collective-permute-start.1 = (bf16[48,512]{1,0:T(8,128)(2,1)S(1)}, bf16[48,512]{1,0:T(8,128)(2,1)S(1)}, u32[]{:S(2)}, u32[]{:S(2)}) collective-permute-start(bf16[48,512]{1,0:T(8,128)(2,1)S(1)} %get-tuple-element.15.refs_0_), channel_id=1, source_target_pairs={{0,8},{4,12},{8,0},{12,4},{16,24},{20,28},{24,16},{28,20},{1,9},{5... | collective-permute-start | bytes 147464 | tf_op jit(solution)/shard_map/ppermute | solution.py:240
  44.4 12.4 %collective-permute-start.3 = (bf16[48,512]{1,0:T(8,128)(2,1)S(1)}, bf16[48,512]{1,0:T(8,128)(2,1)S(1)}, u32[]{:S(2)}, u32[]{:S(2)}) collective-permute-start(bf16[48,512]{1,0:T(8,128)(2,1)S(1)} %get-tuple-element.15.refs_0_), channel_id=1, source_target_pairs={{0,16},{4,20},{8,24},{12,28},{16,0},{20,4},{24,8},{28,12},{1,17},{... | collective-permute-start | bytes 147464 | tf_op jit(solution)/shard_map/ppermute | solution.py:240
  46.8 11.5 %collective-permute-start.5 = (bf16[48,512]{1,0:T(8,128)(2,1)S(1)}, bf16[48,512]{1,0:T(8,128)(2,1)S(1)}, u32[]{:S(2)}, u32[]{:S(2)}) collective-permute-start(bf16[48,512]{1,0:T(8,128)(2,1)S(1)} %get-tuple-element.15.refs_0_), channel_id=1, source_target_pairs={{0,24},{4,28},{8,16},{12,20},{16,8},{20,12},{24,0},{28,4},{1,25},{... | collective-permute-start | bytes 147464 | tf_op jit(solution)/shard_map/ppermute | solution.py:240
  46.8 12.0 %collective-permute-start = (bf16[48,512]{1,0:T(8,128)(2,1)S(1)}, bf16[48,512]{1,0:T(8,128)(2,1)S(1)}, u32[]{:S(2)}, u32[]{:S(2)}) collective-permute-start(bf16[48,512]{1,0:T(8,128)(2,1)S(1)} %get-tuple-element.15.refs_0_), channel_id=1, source_target_pairs={{0,4},{4,0},{8,12},{12,8},{16,20},{20,16},{24,28},{28,24},{1,5},{5... | collective-permute-start | bytes 147464 | tf_op jit(solution)/shard_map/ppermute | solution.py:240
  49.5 9.3 %collective-permute-start.2 = (bf16[48,512]{1,0:T(8,128)(2,1)S(1)}, bf16[48,512]{1,0:T(8,128)(2,1)S(1)}, u32[]{:S(2)}, u32[]{:S(2)}) collective-permute-start(bf16[48,512]{1,0:T(8,128)(2,1)S(1)} %collective-permute-done.1.refs_2_), channel_id=1, source_target_pairs={{0,4},{4,0},{8,12},{12,8},{16,20},{20,16},{24,28},{28,24},{1,5},{5... | collective-permute-start | bytes 147464 | tf_op jit(solution)/shard_map/ppermute | solution.py:240
  56.8 4.1 %collective-permute-start.4 = (bf16[48,512]{1,0:T(8,128)(2,1)S(1)}, bf16[48,512]{1,0:T(8,128)(2,1)S(1)}, u32[]{:S(2)}, u32[]{:S(2)}) collective-permute-start(bf16[48,512]{1,0:T(8,128)(2,1)S(1)} %collective-permute-done.3.refs_4_), channel_id=1, source_target_pairs={{0,4},{4,0},{8,12},{12,8},{16,20},{20,16},{24,28},{28,24},{1,5},{5... | collective-permute-start | bytes 147464 | tf_op jit(solution)/shard_map/ppermute | solution.py:240
  58.2 4.1 %collective-permute-start.6 = (bf16[48,512]{1,0:T(8,128)(2,1)S(1)}, bf16[48,512]{1,0:T(8,128)(2,1)S(1)}, u32[]{:S(2)}, u32[]{:S(2)}) collective-permute-start(bf16[48,512]{1,0:T(8,128)(2,1)S(1)} %collective-permute-done.5.refs_6_), channel_id=1, source_target_pairs={{0,4},{4,0},{8,12},{12,8},{16,20},{20,16},{24,28},{28,24},{1,5},{5... | collective-permute-start | bytes 147464 | tf_op jit(solution)/shard_map/ppermute | solution.py:240
  62.3 2.2 %copy-start.1 = (bf16[1,4096,512]{2,1,0:T(8,128)(2,1)S(1)}, bf16[1,4096,512]{2,1,0:T(8,128)(2,1)}, u32[]{:S(2)}) copy-start(bf16[1,4096,512]{2,1,0:T(8,128)(2,1)} %refs_8_.3) | copy-start | bytes 12582916
  78.6 17.1 %all-to-all-start = ((bf16[8,48,640]{2,1,0:T(8,128)(2,1)}), bf16[8,48,640]{2,1,0:T(8,128)(2,1)S(1)}, u32[]{:S(2)}, u32[]{:S(2)}) async-start(bf16[8,48,640]{2,1,0:T(8,128)(2,1)} %tree_attention.2), calls=%async_computation | async-start | bytes 983040 | tf_op jit(solution)/shard_map/all_to_all | solution.py:306
  98.7 3.2 %copy-start.5 = (bf16[48,512]{1,0:T(8,128)(2,1)}, bf16[48,512]{1,0:T(8,128)(2,1)S(1)}, u32[]{:S(2)}) copy-start(bf16[48,512]{1,0:T(8,128)(2,1)S(1)} %fusion.23) | copy-start | bytes 147460
  98.7 3.2 %copy-start.10 = (f32[48,4]{1,0:T(8,128)S(1)}, f32[48,4]{1,0:T(8,128)}, u32[]{:S(2)}) copy-start(f32[48,4]{1,0:T(8,128)} %get-tuple-element.17) | copy-start | bytes 2308
  102.0 3.2 %copy-start.7 = (bf16[48,512]{1,0:T(8,128)(2,1)}, bf16[48,512]{1,0:T(8,128)(2,1)S(1)}, u32[]{:S(2)}) copy-start(bf16[48,512]{1,0:T(8,128)(2,1)S(1)} %fusion.22) | copy-start | bytes 147460
  102.0 13.2 %copy-start.9 = (bf16[48,1024]{1,0:T(8,128)(2,1)S(1)}, bf16[48,1024]{1,0:T(8,128)(2,1)}, u32[]{:S(2)}) copy-start(bf16[48,1024]{1,0:T(8,128)(2,1)} %param.32) | copy-start | bytes 294916
  105.1 26.8 %copy-start.11 = (f32[1024]{0:T(1024)S(1)}, f32[1024]{0:T(1024)}, u32[]{:S(2)}) copy-start(f32[1024]{0:T(1024)} %param.34) | copy-start | bytes 12292
  115.3 5.9 %collective-permute-start.15 = (bf16[48,1024]{1,0:T(8,128)(2,1)S(1)}, bf16[48,1024]{1,0:T(8,128)(2,1)S(1)}, u32[]{:S(2)}, u32[]{:S(2)}) collective-permute-start(bf16[48,1024]{1,0:T(8,128)(2,1)S(1)} %get-tuple-element.3), channel_id=1, source_target_pairs={{0,8},{4,12},{8,0},{12,4},{16,24},{20,28},{24,16},{28,20},{1,9},{5... | collective-permute-start | bytes 294920 | tf_op jit(solution)/shard_map/ppermute | solution.py:240
  116.2 10.1 %collective-permute-start.17 = (bf16[48,1024]{1,0:T(8,128)(2,1)S(1)}, bf16[48,1024]{1,0:T(8,128)(2,1)S(1)}, u32[]{:S(2)}, u32[]{:S(2)}) collective-permute-start(bf16[48,1024]{1,0:T(8,128)(2,1)S(1)} %get-tuple-element.3), channel_id=1, source_target_pairs={{0,16},{4,20},{8,24},{12,28},{16,0},{20,4},{24,8},{28,12},{1,17},{... | collective-permute-start | bytes 294920 | tf_op jit(solution)/shard_map/ppermute | solution.py:240
  117.1 10.2 %collective-permute-start.19 = (bf16[48,1024]{1,0:T(8,128)(2,1)S(1)}, bf16[48,1024]{1,0:T(8,128)(2,1)S(1)}, u32[]{:S(2)}, u32[]{:S(2)}) collective-permute-start(bf16[48,1024]{1,0:T(8,128)(2,1)S(1)} %get-tuple-element.3), channel_id=1, source_target_pairs={{0,24},{4,28},{8,16},{12,20},{16,8},{20,12},{24,0},{28,4},{1,25},{... | collective-permute-start | bytes 294920 | tf_op jit(solution)/shard_map/ppermute | solution.py:240
  119.7 8.5 %collective-permute-start.14 = (bf16[48,1024]{1,0:T(8,128)(2,1)S(1)}, bf16[48,1024]{1,0:T(8,128)(2,1)S(1)}, u32[]{:S(2)}, u32[]{:S(2)}) collective-permute-start(bf16[48,1024]{1,0:T(8,128)(2,1)S(1)} %get-tuple-element.3), channel_id=1, source_target_pairs={{0,4},{4,0},{8,12},{12,8},{16,20},{20,16},{24,28},{28,24},{1,5},{5... | collective-permute-start | bytes 294920 | tf_op jit(solution)/shard_map/ppermute | solution.py:240
  121.2 7.1 %collective-permute-start.16 = (bf16[48,1024]{1,0:T(8,128)(2,1)S(1)}, bf16[48,1024]{1,0:T(8,128)(2,1)S(1)}, u32[]{:S(2)}, u32[]{:S(2)}) collective-permute-start(bf16[48,1024]{1,0:T(8,128)(2,1)S(1)} %collective-permute-done.15), channel_id=1, source_target_pairs={{0,4},{4,0},{8,12},{12,8},{16,20},{20,16},{24,28},{28,24},{1,5},{5... | collective-permute-start | bytes 294920 | tf_op jit(solution)/shard_map/ppermute | solution.py:240
  126.2 4.6 %collective-permute-start.18 = (bf16[48,1024]{1,0:T(8,128)(2,1)S(1)}, bf16[48,1024]{1,0:T(8,128)(2,1)S(1)}, u32[]{:S(2)}, u32[]{:S(2)}) collective-permute-start(bf16[48,1024]{1,0:T(8,128)(2,1)S(1)} %collective-permute-done.17), channel_id=1, source_target_pairs={{0,4},{4,0},{8,12},{12,8},{16,20},{20,16},{24,28},{28,24},{1,5},{5... | collective-permute-start | bytes 294920 | tf_op jit(solution)/shard_map/ppermute | solution.py:240
  127.3 4.6 %collective-permute-start.20 = (bf16[48,1024]{1,0:T(8,128)(2,1)S(1)}, bf16[48,1024]{1,0:T(8,128)(2,1)S(1)}, u32[]{:S(2)}, u32[]{:S(2)}) collective-permute-start(bf16[48,1024]{1,0:T(8,128)(2,1)S(1)} %collective-permute-done.19), channel_id=1, source_target_pairs={{0,4},{4,0},{8,12},{12,8},{16,20},{20,16},{24,28},{28,24},{1,5},{5... | collective-permute-start | bytes 294920 | tf_op jit(solution)/shard_map/ppermute | solution.py:240
  138.1 1.5 copy-start.4
  139.7 3.2 %collective-permute-start.21 = (bf16[192,3584]{1,0:T(8,128)(2,1)S(1)}, bf16[192,3584]{1,0:T(8,128)(2,1)S(1)}, u32[]{:S(2)}, u32[]{:S(2)}) collective-permute-start(bf16[192,3584]{1,0:T(8,128)(2,1)S(1)} %constant_dynamic-slice_fusion.3), channel_id=1, source_target_pairs={{0,1},{1,0},{2,3},{3,2},{4,5},{5,4},{6,7},{7,6},{8,9},{9,8},{10,11... | collective-permute-start | bytes 4128776 | tf_op jit(solution)/shard_map/ppermute | solution.py:361
  144.6 17.7 %collective-permute-start.22 = (bf16[96,3584]{1,0:T(8,128)(2,1)S(1)}, bf16[96,3584]{1,0:T(8,128)(2,1)S(1)}, u32[]{:S(2)}, u32[]{:S(2)}) collective-permute-start(bf16[96,3584]{1,0:T(8,128)(2,1)S(1)} %constant_dynamic-slice_fusion.2), channel_id=1, source_target_pairs={{0,2},{1,3},{2,0},{3,1},{4,6},{5,7},{6,4},{7,5},{8,10},{9,11},{10,... | collective-permute-start | bytes 2064392 | tf_op jit(solution)/shard_map/ppermute | solution.py:361
  145.7 1.2 collective-permute-start.23
  146.9 15.3 %collective-permute-start.24 = (f32[1,384]{1,0:T(1,128)S(1)}, f32[1,384]{1,0:T(1,128)S(1)}, u32[]{:S(2)}, u32[]{:S(2)}) collective-permute-start(f32[1,384]{1,0:T(1,128)S(1)} %reshape_add_fusion), channel_id=1, source_target_pairs={{0,2},{1,3},{2,0},{3,1},{4,6},{5,7},{6,4},{7,5},{8,10},{9,11},{10,... | collective-permute-start | bytes 4616 | tf_op jit(solution)/shard_map/ppermute | solution.py:240
  162.7 9.3 %collective-permute-start.25 = (bf16[96,1792]{1,0:T(8,128)(2,1)S(1)}, bf16[96,1792]{1,0:T(8,128)(2,1)S(1)}, u32[]{:S(2)}, u32[]{:S(2)}) collective-permute-start(bf16[96,1792]{1,0:T(8,128)(2,1)S(1)} %fusion.21), channel_id=1, source_target_pairs={{0,2},{1,3},{2,0},{3,1},{4,6},{5,7},{6,4},{7,5},{8,10},{9,11},{10,... | collective-permute-start | bytes 1032200 | tf_op jit(solution)/shard_map/ppermute | solution.py:371
  172.2 2.2 %collective-permute-start.26 = (bf16[192,1792]{1,0:T(8,128)(2,1)S(1)}, bf16[192,1792]{1,0:T(8,128)(2,1)S(1)}, u32[]{:S(2)}, u32[]{:S(2)}) collective-permute-start(bf16[192,1792]{1,0:T(8,128)(2,1)S(1)} %maximum_select_fusion.2), channel_id=1, source_target_pairs={{0,1},{1,0},{2,3},{3,2},{4,5},{5,4},{6,7},{7,6},{8,9},{9,8},{10,11... | collective-permute-start | bytes 2064392 | tf_op jit(solution)/shard_map/ppermute | solution.py:371
  172.3 20.3 %copy-start.6 = (bf16[48,512]{1,0:T(8,128)(2,1)S(1)}, bf16[48,512]{1,0:T(8,128)(2,1)}, u32[]{:S(2)}) copy-start(bf16[48,512]{1,0:T(8,128)(2,1)} %copy-done.5) | copy-start | bytes 147460
  172.3 20.2 %copy-start.8 = (bf16[48,512]{1,0:T(8,128)(2,1)S(1)}, bf16[48,512]{1,0:T(8,128)(2,1)}, u32[]{:S(2)}) copy-start(bf16[48,512]{1,0:T(8,128)(2,1)} %copy-done.7) | copy-start | bytes 147460
  178.1 5.7 %collective-permute-start.28 = (bf16[48,1024]{1,0:T(8,128)(2,1)S(1)}, bf16[48,1024]{1,0:T(8,128)(2,1)S(1)}, u32[]{:S(2)}, u32[]{:S(2)}) collective-permute-start(bf16[48,1024]{1,0:T(8,128)(2,1)S(1)} %get-tuple-element.11), channel_id=1, source_target_pairs={{0,4},{4,0},{8,12},{12,8},{16,20},{20,16},{24,28},{28,24},{1,5},{5... | collective-permute-start | bytes 294920 | tf_op jit(solution)/shard_map/ppermute | solution.py:240
  179.2 6.7 %collective-permute-start.30 = (bf16[48,1024]{1,0:T(8,128)(2,1)S(1)}, bf16[48,1024]{1,0:T(8,128)(2,1)S(1)}, u32[]{:S(2)}, u32[]{:S(2)}) collective-permute-start(bf16[48,1024]{1,0:T(8,128)(2,1)S(1)} %get-tuple-element.10), channel_id=1, source_target_pairs={{0,4},{4,0},{8,12},{12,8},{16,20},{20,16},{24,28},{28,24},{1,5},{5... | collective-permute-start | bytes 294920 | tf_op jit(solution)/shard_map/ppermute | solution.py:240
  180.1 7.8 %collective-permute-start.32 = (bf16[48,1024]{1,0:T(8,128)(2,1)S(1)}, bf16[48,1024]{1,0:T(8,128)(2,1)S(1)}, u32[]{:S(2)}, u32[]{:S(2)}) collective-permute-start(bf16[48,1024]{1,0:T(8,128)(2,1)S(1)} %get-tuple-element.9), channel_id=1, source_target_pairs={{0,4},{4,0},{8,12},{12,8},{16,20},{20,16},{24,28},{28,24},{1,5},{5... | collective-permute-start | bytes 294920 | tf_op jit(solution)/shard_map/ppermute | solution.py:240
  181.2 12.0 %collective-permute-start.27 = (bf16[48,1024]{1,0:T(8,128)(2,1)S(1)}, bf16[48,1024]{1,0:T(8,128)(2,1)S(1)}, u32[]{:S(2)}, u32[]{:S(2)}) collective-permute-start(bf16[48,1024]{1,0:T(8,128)(2,1)S(1)} %get-tuple-element.8), channel_id=1, source_target_pairs={{0,4},{4,0},{8,12},{12,8},{16,20},{20,16},{24,28},{28,24},{1,5},{5... | collective-permute-start | bytes 294920 | tf_op jit(solution)/shard_map/ppermute | solution.py:240
  188.1 7.2 %collective-permute-start.29 = (bf16[48,1024]{1,0:T(8,128)(2,1)S(1)}, bf16[48,1024]{1,0:T(8,128)(2,1)S(1)}, u32[]{:S(2)}, u32[]{:S(2)}) collective-permute-start(bf16[48,1024]{1,0:T(8,128)(2,1)S(1)} %get-tuple-element.12), channel_id=1, source_target_pairs={{0,24},{4,28},{8,16},{12,20},{16,8},{20,12},{24,0},{28,4},{1,25},{... | collective-permute-start | bytes 294920 | tf_op jit(solution)/shard_map/ppermute | solution.py:240
  189.7 8.7 %collective-permute-start.31 = (bf16[48,1024]{1,0:T(8,128)(2,1)S(1)}, bf16[48,1024]{1,0:T(8,128)(2,1)S(1)}, u32[]{:S(2)}, u32[]{:S(2)}) collective-permute-start(bf16[48,1024]{1,0:T(8,128)(2,1)S(1)} %get-tuple-element.14), channel_id=1, source_target_pairs={{0,16},{4,20},{8,24},{12,28},{16,0},{20,4},{24,8},{28,12},{1,17},{... | collective-permute-start | bytes 294920 | tf_op jit(solution)/shard_map/ppermute | solution.py:240
  190.1 8.2 %collective-permute-start.33 = (bf16[48,1024]{1,0:T(8,128)(2,1)S(1)}, bf16[48,1024]{1,0:T(8,128)(2,1)S(1)}, u32[]{:S(2)}, u32[]{:S(2)}) collective-permute-start(bf16[48,1024]{1,0:T(8,128)(2,1)S(1)} %get-tuple-element.13), channel_id=1, source_target_pairs={{0,8},{4,12},{8,0},{12,4},{16,24},{20,28},{24,16},{28,20},{1,9},{5... | collective-permute-start | bytes 294920 | tf_op jit(solution)/shard_map/ppermute | solution.py:240

commit v3 on v2

v3 whole, which is shorter than its diff:
```python
import math

import jax
import jax.numpy as jnp
from jax import lax
from jax.experimental import pallas as pl
from jax.experimental.pallas import tpu as pltpu
from jax.sharding import PartitionSpec as P

D = 4096
HEAD = 128
QLEAF = 16
QMID = 48
QROOT = 144


LOWEST = -1e30
EPSILON = 1e-05
ALIGN = 16
BLOCK = 512


def own_nodes(owner, local_counts, tree, lengths, slots):
    token_leaf, leaf_parent, mid_parent = tree
    node_total = sum(local_counts)

    def kernel(owner_ref, token_ref, leaf_up, mid_up, *refs):
        len_refs, slot_refs, out_ref = refs[:3], refs[3:6], refs[6]

        def find(slot_ref, len_ref, local):
            base = owner_ref[0] * local

            def step(j, found):
                at, size = slot_ref[j] - base, len_ref[j]
                return tuple(
                    (jnp.where(at == k, j, node), jnp.where(at == k, size, length))
                    for k, (node, length) in enumerate(found)
                )

            zero = jnp.int32(0)
            return lax.fori_loop(0, slot_ref.shape[0], step, ((zero, zero),) * local)

        def below(parent_ref, edges):
            def step(j, counted):
                parent = parent_ref[j]
                return tuple(
                    c + jnp.where(parent < edge, 1, 0) for c, edge in zip(counted, edges)
                )

            return lax.fori_loop(0, parent_ref.shape[0], step, (jnp.int32(0),) * len(edges))

        picked = [find(*level) for level in zip(slot_refs, len_refs, local_counts)]
        edges = ()
        for level, parent_ref in enumerate((mid_up, leaf_up, None)):
            for node, _ in picked[level]:
                edges += (node, node + 1)
            if parent_ref is not None:
                edges = below(parent_ref, edges)
        tokens = token_ref[...]
        sizes = [length for level in picked for _, length in level]
        for k in range(node_total):
            for side in range(2):
                under = jnp.where(tokens < edges[2 * k + side], 1.0, 0.0)
                out_ref[side, k] = jnp.sum(under).astype(jnp.int32)
            out_ref[2, k] = sizes[k]

    smem = pl.BlockSpec(memory_space=pltpu.SMEM)
    vmem = pl.BlockSpec(memory_space=pltpu.VMEM)
    return pl.pallas_call(
        kernel,
        out_shape=jax.ShapeDtypeStruct((3, node_total), jnp.int32),
        in_specs=[smem, vmem] + [smem] * 8,
        out_specs=smem,
        name="own_nodes",
    )(owner[None], token_leaf.reshape(-1, HEAD), leaf_parent, mid_parent, *lengths, *slots)


def tree_attention(query_parts, caches, nodes, owner, kv_head):
    part_total = len(query_parts)
    own_rows = query_parts[0].shape[0]
    total_rows = part_total * own_rows
    width = query_parts[0].shape[1] // (caches[0].shape[2] // (2 * HEAD))
    group_size = width // HEAD
    score_scale = 1.0 / math.sqrt(HEAD)
    levels = []
    for cache, capacity in zip(caches, (QROOT, QMID, QLEAF)):
        levels.append((cache.shape[0], cache.shape[1], min(capacity + ALIGN, total_rows)))

    def kernel(nodes_ref, owner_ref, *refs):
        query_refs = refs[:part_total]
        cache_refs = refs[part_total : part_total + 3]
        out_ref, all_rows, run_out, run_lse, acc, peak, total = refs[part_total + 3 :]
        me = owner_ref[0]
        for part in range(part_total):
            row = pl.multiple_of((me ^ part) * own_rows, ALIGN)
            all_rows[pl.ds(row, own_rows), :] = query_refs[part][
                :, kv_head * width : (kv_head + 1) * width
            ]
        run_out[...] = jnp.zeros_like(run_out)
        run_lse[...] = jnp.full_like(run_lse, LOWEST)
        node = 0
        for (slot_total, span, rows), cache_ref in zip(levels, cache_refs):
            lanes = rows * group_size
            block = min(BLOCK, span)
            for member in range(slot_total):
                low, high, length = nodes_ref[0, node], nodes_ref[1, node], nodes_ref[2, node]
                node += 1
                window = jnp.minimum(low - lax.rem(low, ALIGN), total_rows - rows)
                window = pl.multiple_of(window, ALIGN)
                columns = [h * HEAD for h in range(group_size)]
                grouped = jnp.concatenate(
                    [all_rows[pl.ds(window, rows), c : c + HEAD] for c in columns], axis=0
                )
                acc[:, :lanes] = jnp.zeros((HEAD, lanes), jnp.float32)
                peak[:, :lanes] = jnp.full((1, lanes), LOWEST, jnp.float32)
                total[:, :lanes] = jnp.zeros((1, lanes), jnp.float32)

                def visit(index, carry, masked):
                    at = pl.multiple_of(index * block, block)
                    keys = cache_ref[
                        member, pl.ds(at, block), 2 * kv_head * HEAD : (2 * kv_head + 1) * HEAD
                    ]
                    values = cache_ref[
                        member,
                        pl.ds(at, block),
                        (2 * kv_head + 1) * HEAD : (2 * kv_head + 2) * HEAD,
                    ]
                    scores = lax.dot_general(
                        keys,
                        grouped,
                        (((1,), (1,)), ((), ())),
                        preferred_element_type=jnp.float32,
                    )
                    if masked:
                        position = at + lax.broadcasted_iota(jnp.int32, (block, lanes), 0)
                        scores = jnp.where(position < length, scores, LOWEST)
                    old_peak = peak[:, :lanes]
                    new_peak = jnp.maximum(old_peak, jnp.max(scores, axis=0, keepdims=True))
                    weights = jnp.exp((scores - new_peak) * score_scale)
                    fade = jnp.exp((old_peak - new_peak) * score_scale)
                    peak[:, :lanes] = new_peak
                    total[:, :lanes] = total[:, :lanes] * fade + jnp.sum(
                        weights, axis=0, keepdims=True
                    )
                    acc[:, :lanes] = acc[:, :lanes] * fade + lax.dot_general(
                        values,
                        weights.astype(jnp.bfloat16),
                        (((0,), (0,)), ((), ())),
                        preferred_element_type=jnp.float32,
                    )
                    return carry

                whole = lax.div(length, block)
                lax.fori_loop(0, whole, lambda i, c: visit(i, c, False), 0)

                @pl.when(whole * block < length)
                def _():
                    visit(whole, 0, True)

                weight_sum = total[:, :lanes]
                part_out = (acc[:, :lanes] / weight_sum).T
                part_lse = jnp.broadcast_to(
                    peak[:, :lanes] * score_scale + jnp.log(weight_sum), (HEAD, lanes)
                ).T
                position = window + lax.broadcasted_iota(jnp.int32, (rows, HEAD), 0)
                live = (position >= low) & (position < high)
                for h, c in enumerate(columns):
                    here = (pl.ds(window, rows), slice(c, c + HEAD))
                    old_lse, old_out = run_lse[here], run_out[here]
                    add_lse = part_lse[h * rows : (h + 1) * rows]
                    add_out = part_out[h * rows : (h + 1) * rows]
                    best = jnp.maximum(old_lse, add_lse)
                    old_share = jnp.exp(old_lse - best)
                    add_share = jnp.exp(add_lse - best)
                    share = old_share + add_share
                    run_out[here] = jnp.where(
                        live, (old_out * old_share + add_out * add_share) / share, old_out
                    )
                    run_lse[here] = jnp.where(live, best + jnp.log(share), old_lse)
        lane = lax.broadcasted_iota(jnp.int32, (own_rows, HEAD), 1)
        for part in range(part_total):
            at = part * own_rows
            out_ref[part, :, :width] = run_out[at : at + own_rows, :].astype(jnp.bfloat16)
            lse = jnp.zeros((own_rows, HEAD), jnp.float32)
            for h in range(group_size):
                piece = run_lse[at : at + own_rows, h * HEAD : (h + 1) * HEAD]
                lse = jnp.where(lax.rem(lane, group_size) == h, piece, lse)
            first = lse.astype(jnp.bfloat16)
            rest = lse - first.astype(jnp.float32)
            second = rest.astype(jnp.bfloat16)
            third = rest - second.astype(jnp.float32)
            field = lax.div(lane, group_size)
            packed = jnp.where(
                field == 0,
                first.astype(jnp.float32),
                jnp.where(
                    field == 1,
                    second.astype(jnp.float32),
                    jnp.where(field == 2, third, 0.0),
                ),
            )
            out_ref[part, :, width:] = packed.astype(jnp.bfloat16)

    most = max(rows for _, _, rows in levels) * group_size
    vmem = pl.BlockSpec(memory_space=pltpu.VMEM)
    smem = pl.BlockSpec(memory_space=pltpu.SMEM)
    return pl.pallas_call(
        kernel,
        out_shape=jax.ShapeDtypeStruct((part_total, own_rows, width + HEAD), jnp.bfloat16),
        in_specs=[smem, smem] + [vmem] * (part_total + 3),
        out_specs=vmem,
        scratch_shapes=[
            pltpu.VMEM((total_rows, width), jnp.bfloat16),
            pltpu.VMEM((total_rows, width), jnp.float32),
            pltpu.VMEM((total_rows, width), jnp.float32),
            pltpu.VMEM((HEAD, most), jnp.float32),
            pltpu.VMEM((1, most), jnp.float32),
            pltpu.VMEM((1, most), jnp.float32),
        ],
        compiler_params=pltpu.CompilerParams(vmem_limit_bytes=48 << 20),
        name="tree_attention",
    )(nodes, owner[None], *query_parts, *caches)


def combine_project(every, weight, row_start, added, place, own_width):
    part_total, own_rows, wide = every.shape
    width = wide - HEAD
    group_size = width // HEAD
    block_total = weight.shape[1] // own_width
    last = added is not None or width == weight.shape[0]
    kind = jnp.bfloat16 if last else jnp.float32

    def kernel(place_ref, every_ref, weight_ref, *refs):
        added_refs = refs[:block_total] if added is not None else (None,) * block_total
        attended_ref, *block_refs = refs[len(refs) - 1 - block_total :]
        lse = []
        for part in range(part_total):
            terms = every_ref[part, :, width:].astype(jnp.float32)
            lse.append(
                terms
                + pltpu.roll(terms, HEAD - group_size, 1)
                + pltpu.roll(terms, HEAD - 2 * group_size, 1)
            )
        best = lse[0]
        for one in lse[1:]:
            best = jnp.maximum(best, one)
        share = [jnp.exp(one - best) for one in lse]
        whole = share[0]
        for one in share[1:]:
            whole = whole + one
        for h in range(group_size):
            summed = jnp.zeros((own_rows, HEAD), jnp.float32)
            for part in range(part_total):
                summed = summed + (
                    every_ref[part, :, h * HEAD : (h + 1) * HEAD].astype(jnp.float32)
                    * share[part][:, h : h + 1]
                )
            attended_ref[:, h * HEAD : (h + 1) * HEAD] = (summed / whole[:, h : h + 1]).astype(
                jnp.bfloat16
            )
        for block in range(block_total):
            at = pl.multiple_of((place_ref[0] ^ block) * own_width, HEAD)
            product = jnp.dot(
                attended_ref[...],
                weight_ref[row_start : row_start + width, pl.ds(at, own_width)],
                preferred_element_type=jnp.float32,
            )
            if added is not None:
                product = product + added_refs[block][...]
            block_refs[block][...] = product.astype(kind)

    vmem = pl.BlockSpec(memory_space=pltpu.VMEM)
    outs = pl.pallas_call(
        kernel,
        out_shape=[jax.ShapeDtypeStruct((own_rows, width), jnp.bfloat16)]
        + [jax.ShapeDtypeStruct((own_rows, own_width), kind)] * block_total,
        in_specs=[pl.BlockSpec(memory_space=pltpu.SMEM)]
        + [vmem] * (2 + (block_total if added is not None else 0)),
        out_specs=[vmem] * (1 + block_total),
        compiler_params=pltpu.CompilerParams(vmem_limit_bytes=48 << 20),
        name="combine_project",
    )(place[None], every, weight, *(added or ()))
    return outs[0], outs[1:]


def split_terms(value):
    first = value.astype(jnp.bfloat16).astype(jnp.float32)
    second = (value - first).astype(jnp.bfloat16).astype(jnp.float32)
    lane = lax.broadcasted_iota(jnp.int32, value.shape, 1)
    third = jnp.where(lane == 2, value - first - second, 0.0)
    return jnp.where(lane == 0, first, jnp.where(lane == 1, second, third)).astype(jnp.bfloat16)


def gate_up_rows(parts, norm_gain, gate_weight, up_weight, spot, group_total):
    own_rows, features = parts[0].shape
    rows = own_rows * len(parts)
    half = rows // 2
    each = len(parts) // group_total
    units = gate_weight.shape[1]

    def kernel(spot_ref, gain_ref, gate_ref, up_ref, *refs):
        part_refs = refs[: len(parts)]
        keep_ref, send_ref, scaled, squares = refs[len(parts) :]
        for index, part_ref in enumerate(part_refs):
            at = ((index // each) ^ spot_ref[0]) * each + index % each
            here = pl.ds(pl.multiple_of(at * own_rows, ALIGN), own_rows)
            wide = part_ref[...].astype(jnp.float32)
            scaled[here, :] = (wide * gain_ref[...]).astype(jnp.bfloat16)
            squares[here, :] = jnp.broadcast_to(
                jnp.sum(wide * wide, axis=1, keepdims=True), (own_rows, HEAD)
            )
        for column, weight_ref in ((0, gate_ref), (units, up_ref)):
            product = jnp.dot(
                scaled[...], weight_ref[...], preferred_element_type=jnp.float32
            ).astype(jnp.bfloat16)
            keep_ref[:, column : column + units] = product[:half]
            send_ref[:, column : column + units] = product[half:]
        terms = split_terms(squares[...])
        keep_ref[:, 2 * units :] = terms[:half]
        send_ref[:, 2 * units :] = terms[half:]

    vmem = pl.BlockSpec(memory_space=pltpu.VMEM)
    return pl.pallas_call(
        kernel,
        out_shape=[jax.ShapeDtypeStruct((half, 2 * units + HEAD), jnp.bfloat16)] * 2,
        in_specs=[pl.BlockSpec(memory_space=pltpu.SMEM)] + [vmem] * (3 + len(parts)),
        out_specs=[vmem, vmem],
        scratch_shapes=[
            pltpu.VMEM((rows, features), jnp.bfloat16),
            pltpu.VMEM((rows, HEAD), jnp.float32),
        ],
        compiler_params=pltpu.CompilerParams(vmem_limit_bytes=48 << 20),
        name="gate_up",
    )(spot[None], norm_gain[None, :], gate_weight, up_weight, *parts)


def add_halves(keep, got, units):
    half = keep.shape[0] // 2

    def kernel(keep_ref, got_ref, next_ref, send_ref):
        for ref, at in ((next_ref, 0), (send_ref, half)):
            here = pl.ds(at, half)
            ref[:, : 2 * units] = (
                keep_ref[here, : 2 * units].astype(jnp.float32)
                + got_ref[here, : 2 * units].astype(jnp.float32)
            ).astype(jnp.bfloat16)
            terms = keep_ref[here, 2 * units :].astype(jnp.float32)
            terms = terms + got_ref[here, 2 * units :].astype(jnp.float32)
            total = jnp.sum(terms, axis=1, keepdims=True)
            ref[:, 2 * units :] = split_terms(jnp.broadcast_to(total, (half, HEAD)))

    vmem = pl.BlockSpec(memory_space=pltpu.VMEM)
    return pl.pallas_call(
        kernel,
        out_shape=[jax.ShapeDtypeStruct((half, keep.shape[1]), jnp.bfloat16)] * 2,
        in_specs=[vmem, vmem],
        out_specs=[vmem, vmem],
        compiler_params=pltpu.CompilerParams(vmem_limit_bytes=48 << 20),
        name="add_halves",
    )(keep, got)


def gated(keep, got, units):
    def kernel(keep_ref, got_ref, out_ref):
        summed = keep_ref[...].astype(jnp.float32) + got_ref[...].astype(jnp.float32)
        square = jnp.sum(summed[:, 2 * units :], axis=1, keepdims=True)
        scale = lax.rsqrt(square / D + EPSILON)
        gate = summed[:, :units] * scale
        up = summed[:, units : 2 * units] * scale
        out_ref[...] = (gate / (1.0 + jnp.exp(-gate)) * up).astype(jnp.bfloat16)

    vmem = pl.BlockSpec(memory_space=pltpu.VMEM)
    return pl.pallas_call(
        kernel,
        out_shape=jax.ShapeDtypeStruct((keep.shape[0], units), jnp.bfloat16),
        in_specs=[vmem, vmem],
        out_specs=vmem,
        compiler_params=pltpu.CompilerParams(vmem_limit_bytes=48 << 20),
        name="gated",
    )(keep, got)


def down_rows(pieces, down_weight, spot, part_count, own_rows, group_total):
    rows = part_count * own_rows
    each = part_count // group_total
    units, features = down_weight.shape

    def kernel(spot_ref, weight_ref, *refs):
        piece_refs = refs[: len(pieces)]
        out_refs = refs[len(pieces) : len(pieces) + part_count]
        hidden, product = refs[len(pieces) + part_count :]
        at = 0
        for piece_ref in piece_refs:
            hidden[at : at + piece_ref.shape[0], :] = piece_ref[...]
            at += piece_ref.shape[0]
        product[...] = jnp.dot(
            hidden[...], weight_ref[...], preferred_element_type=jnp.float32
        )
        for index, out_ref in enumerate(out_refs):
            at = ((index // each) ^ spot_ref[0]) * each + index % each
            here = pl.ds(pl.multiple_of(at * own_rows, ALIGN), own_rows)
            out_ref[...] = product[here, :].astype(jnp.bfloat16)

    vmem = pl.BlockSpec(memory_space=pltpu.VMEM)
    return pl.pallas_call(
        kernel,
        out_shape=[jax.ShapeDtypeStruct((own_rows, features), jnp.bfloat16)] * part_count,
        in_specs=[pl.BlockSpec(memory_space=pltpu.SMEM)] + [vmem] * (1 + len(pieces)),
        out_specs=[vmem] * part_count,
        scratch_shapes=[
            pltpu.VMEM((rows, units), jnp.bfloat16),
            pltpu.VMEM((rows, features), jnp.float32),
        ],
        compiler_params=pltpu.CompilerParams(vmem_limit_bytes=48 << 20),
        name="down",
    )(spot[None], down_weight, *pieces)


def swap(value, axis_name, mask):
    axis_total = lax.axis_size(axis_name)
    return lax.ppermute(value, axis_name, [(j, j ^ mask) for j in range(axis_total)])


def gather_parts(value, axis_name):
    parts = [value] * lax.axis_size(axis_name)
    for mask in range(len(parts) - 2, 0, -2):
        parts[mask] = swap(value, axis_name, mask)
    for mask in [0] + list(range(len(parts) - 2, 0, -2)):
        parts[mask + 1] = swap(parts[mask], axis_name, 1)
    return parts


def scatter_sum(parts, axis_name):
    wide = jnp.float32
    evens = sorted((mask for mask in parts if mask % 2 == 0), reverse=True)
    got = {mask: swap(parts[mask + 1], axis_name, 1) for mask in evens}
    summed = 0.0
    for mask in evens:
        pair = parts[mask].astype(wide) + got[mask].astype(wide)
        if mask:
            pair = swap(pair.astype(jnp.bfloat16), axis_name, mask).astype(wide)
        summed = summed + pair
    return summed


def shards(
    queries,
    root_cache,
    mid_cache,
    leaf_cache,
    token_leaf,
    leaf_parent,
    mid_parent,
    root_len,
    mid_len,
    leaf_len,
    root_slot,
    mid_slot,
    leaf_slot,
    stream,
    out_weight,
    norm_gain,
    gate_weight,
    up_weight,
    down_weight,
):
    own_rows, width = queries.shape
    owner = lax.axis_index("kv").astype(jnp.int32)
    caches = (root_cache, mid_cache, leaf_cache)
    nodes = own_nodes(
        owner,
        [cache.shape[0] for cache in caches],
        (token_leaf, leaf_parent, mid_parent),
        (root_len, mid_len, leaf_len),
        (root_slot, mid_slot, leaf_slot),
    )
    kv_count = root_cache.shape[2] // (2 * HEAD)
    group_width = width // kv_count
    mlp_total = lax.axis_size("mlp")
    mlp_place = lax.axis_index("mlp").astype(jnp.int32)
    own_width = stream.shape[1]
    query_parts = gather_parts(queries, "kv")
    attended, blocks = [], None
    for k in range(kv_count):
        parts = tree_attention(query_parts, caches, nodes, owner, k)
        every = lax.all_to_all(parts, "kv", 0, 0)
        one, blocks = combine_project(
            every, out_weight, k * group_width, blocks, mlp_place, own_width
        )
        attended.append(one)
    projected = scatter_sum(dict(enumerate(blocks)), "mlp")
    residual = (stream.astype(jnp.float32) + projected).astype(jnp.bfloat16)
    steps = [1 << bit for bit in range(mlp_total.bit_length() - 1)]
    spot = jnp.int32(0)
    for step in steps:
        spot = 2 * spot + (mlp_place // step) % 2
    units = gate_weight.shape[1]
    row_parts = gather_parts(residual, "kv")
    chunks = [
        [mask for mask in range(len(row_parts)) if (mask // 2) % 2 == side] for side in range(2)
    ]
    mixed = 0.0
    for masks in chunks:
        keep, send = gate_up_rows(
            [row_parts[mask] for mask in masks],
            norm_gain,
            gate_weight,
            up_weight,
            spot,
            mlp_total,
        )
        for step in steps[:-1]:
            keep, send = add_halves(keep, swap(send, "mlp", step), units)
        pieces = [gated(keep, swap(send, "mlp", steps[-1]), units)]
        for step in reversed(steps):
            held = pieces[0] if len(pieces) == 1 else jnp.concatenate(pieces, axis=0)
            pieces.append(swap(held, "mlp", step))
        outs = down_rows(pieces, down_weight, spot, len(masks), own_rows, mlp_total)
        mixed = mixed + scatter_sum(dict(zip(masks, outs)), "kv")
    return (jnp.concatenate(attended, axis=1), mixed.astype(jnp.bfloat16))


def solution(mesh):
    in_specs = (
        P("kv", "mlp"),
        P("kv", None, "mlp"),
        P("kv", None, "mlp"),
        P("kv", None, "mlp"),
        P(),
        P(),
        P(),
        P(),
        P(),
        P(),
        P(),
        P(),
        P(),
        P("kv", "mlp"),
        P("mlp", None),
        P("mlp"),
        P("mlp", "kv"),
        P("mlp", "kv"),
        P("kv", "mlp"),
    )
    out_specs = (P("kv", "mlp"), P("kv", "mlp"))
    return jax.shard_map(shards, mesh=mesh, in_specs=in_specs, out_specs=out_specs, check_vma=False)
```

time: 200 us -> 169 us (0.84); the launches traced: 199 us -> 170 us
  Pallas kernels: 31 us -> 48.5 us
  matrix products: 15.9 us -> 0 us
  waiting for transfers between devices: 70 us -> 56.7 us
  blocking collectives: 10 us -> 0 us
  other arithmetic: 5.54 us -> 1.57 us
    pallas_call x0 -> x10, Pallas kernels: none -> 19.8 us  [the longest x2 9.25 us: combine_project(): pl.pallas_call(kernel, out_shape=[jax.ShapeDtypeStruct((own_rows, width),...]
    dot_general x4 -> x0, matrix products: 15.9 us -> none  [the longest x1 6.17 us: shards(): gate_up_sum = jnp.dot(scaled, gate_up, preferred_element_type=jnp.float32)]
    ppermute x4 -> x0, waiting for transfers between devices: 13.6 us -> none  [the longest x2 10.6 us: double(): lax.ppermute(rows, axis_name, [(j, j ^ step) for j in range(axis_total)])]
    all_to_all x1 -> x0, blocking collectives: 10 us -> none  [shards(): lax.all_to_all(projected, 'mlp', 0, 0).astype(jnp.float32)]
    all_to_all x2, starting transfers between devices: 15.1 us -> 20.9 us  [shards(): every = lax.all_to_all(parts, 'kv', 0, 0)]
    ppermute x30 -> x32, starting transfers between devices: 39.1 us -> 33.7 us  [swap(): lax.ppermute(value, axis_name, [(j, j ^ mask) for j in range(axis_total)])]
    ppermute x30 -> x32, waiting for transfers between devices: 45.9 us -> 51.3 us  [swap(): lax.ppermute(value, axis_name, [(j, j ^ mask) for j in range(axis_total)])]
    all_to_all x2, waiting for transfers between devices: 10.4 us -> 5.32 us  [shards(): every = lax.all_to_all(parts, 'kv', 0, 0)]
  transfers between devices with their start and end apart: 36 -> 34, of which waited for: 20 -> 20; matrix products, arithmetic and copies ran while one was open for 1% -> 0% of each run, Pallas kernels for 9% -> 18%
where the time goes in v3:
time: 169 us; the launch traced here: 170 us
  waiting for transfers between devices  56.7 us (34%)
  starting transfers between devices  54.7 us (32%)
  Pallas kernels  48.5 us (29%)
  local copies, waits for them, and re-layouts  8 us (5%)
    ppermute x32, waiting for transfers between devices, swap(): lax.ppermute(value, axis_name, [(j, j ^ mask) for j in range(axis_total)])  51.3 us
    ppermute x32, starting transfers between devices, swap(): lax.ppermute(value, axis_name, [(j, j ^ mask) for j in range(axis_total)])  33.7 us
    pallas_call x2, Pallas kernels, tree_attention(): pl.pallas_call(kernel, out_shape=jax.ShapeDtypeStruct((part_total, own_ro...  25.6 us
    all_to_all x2, starting transfers between devices, shards(): every = lax.all_to_all(parts, 'kv', 0, 0)  20.9 us
    pallas_call x2, Pallas kernels, combine_project(): pl.pallas_call(kernel, out_shape=[jax.ShapeDtypeStruct((own_rows, width),...  9.25 us
    unnamed x20, local copies, waits for them, and re-layouts  8 us
    pallas_call x2, Pallas kernels, gate_up_rows(): pl.pallas_call(kernel, out_shape=[jax.ShapeDtypeStruct((half, 2 * units +...  7.47 us
    all_to_all x2, waiting for transfers between devices, shards(): every = lax.all_to_all(parts, 'kv', 0, 0)  5.32 us
  transfers between devices with their start and end apart: 34, of which 20 were waited for; matrix products, arithmetic and copies ran while one was open for 0% of the time, Pallas kernels for 18%

profile of v3, /device:TPU:0, one launch (start us, length us, event | category | flops | bytes accessed | tf_op | source)
XLA Modules:
  0.0 170.3 jit_solution(10576278467692836203)
XLA Ops:
  0.6 3.1 %collective-permute-start.1 = (bf16[48,1024]{1,0:T(8,128)(2,1)}, bf16[48,1024]{1,0:T(8,128)(2,1)S(1)}, u32[]{:S(2)}, u32[]{:S(2)}) collective-permute-start(bf16[48,1024]{1,0:T(8,128)(2,1)} %refs_0_.5), channel_id=1, source_target_pairs={{0,8},{4,12},{8,0},{12,4},{16,24},{20,28},{24,16},{28,20},{1,9},{5... | collective-permute-start | bytes 294920 | tf_op jit(solution)/shard_map/ppermute | solution.py:421
  3.7 2.6 %collective-permute-start.3 = (bf16[48,1024]{1,0:T(8,128)(2,1)}, bf16[48,1024]{1,0:T(8,128)(2,1)S(1)}, u32[]{:S(2)}, u32[]{:S(2)}) collective-permute-start(bf16[48,1024]{1,0:T(8,128)(2,1)} %refs_0_.5), channel_id=1, source_target_pairs={{0,16},{4,20},{8,24},{12,28},{16,0},{20,4},{24,8},{28,12},{1,17},{... | collective-permute-start | bytes 294920 | tf_op jit(solution)/shard_map/ppermute | solution.py:421
  6.3 1.7 %collective-permute-start = (bf16[48,1024]{1,0:T(8,128)(2,1)}, bf16[48,1024]{1,0:T(8,128)(2,1)S(1)}, u32[]{:S(2)}, u32[]{:S(2)}) collective-permute-start(bf16[48,1024]{1,0:T(8,128)(2,1)} %refs_0_.5), channel_id=1, source_target_pairs={{0,4},{4,0},{8,12},{12,8},{16,20},{20,16},{24,28},{28,24},{1,5},{5... | collective-permute-start | bytes 294920 | tf_op jit(solution)/shard_map/ppermute | solution.py:421
  8.5 5.9 %collective-permute-done.3.refs_4_ = bf16[48,1024]{1,0:T(8,128)(2,1)S(1)} collective-permute-done((bf16[48,1024]{1,0:T(8,128)(2,1)}, bf16[48,1024]{1,0:T(8,128)(2,1)S(1)}, u32[]{:S(2)}, u32[]{:S(2)}) %collective-permute-start.3) | collective-permute-done | bytes 98336 | tf_op jit(solution)/shard_map/ppermute | solution.py:421
  14.4 1.5 collective-permute-start.4
  16.4 3.0 %own_nodes.1.nodes_ref = s32[3,7]{1,0:T(4,128)} custom-call(s32[1]{0:T(128)} %bitcast.1.owner_ref, s32[3,128]{1,0:T(4,128)} %bitcast.7, s32[32]{0:T(128)} %leaf_up.1, s32[16]{0:T(128)} %mid_up.1, s32[8]{0:T(128)} %refs_0_.3, s32[16]{0:T(128)} %refs_1_.1, s32[32]{0:T(128)} %refs_2_.1, s32[8]{0:T(128)} %refs_3_.1, s32[16]{0:T(128)} %refs_4_.1, s32[32]{0:T(128)} %refs_5_.1), custom_call_target="tpu_custom_call" | custom-call | tf_op jit(solution)/shard_map/own_nodes/pallas_call | solution.py:69
  19.5 1.0 collective-permute-done.6.refs_7_
  20.5 2.2 %copy-done = bf16[1,4096,512]{2,1,0:T(8,128)(2,1)S(1)} copy-done((bf16[1,4096,512]{2,1,0:T(8,128)(2,1)S(1)}, bf16[1,4096,512]{2,1,0:T(8,128)(2,1)}, u32[]{:S(2)}) %copy-start) | copy-done | bytes 4194328
  24.3 12.8 %tree_attention.2 = bf16[8,48,640]{2,1,0:T(8,128)(2,1)} custom-call(s32[3,7]{1,0:T(4,128)S(1)} %copy-done.6, s32[1]{0:T(128)} %bitcast.1.owner_ref, bf16[48,1024]{1,0:T(8,128)(2,1)S(1)} %copy-done.4, bf16[48,1024]{1,0:T(8,128)(2,1)S(1)} %collective-permute-done.refs_1_, bf16[48,1024]{1,0:T(8,128)(2,1)S(1)} %collective-permute-done.1.refs_2_, ...), custom_call_target="tpu_custom_call" | custom-call | tf_op jit(solution)/shard_map/tree_attention/pallas_call | solution.py:207
  37.0 9.6 %all-to-all-start = ((bf16[8,48,640]{2,1,0:T(8,128)(2,1)}), bf16[8,48,640]{2,1,0:T(8,128)(2,1)S(1)}, u32[]{:S(2)}, u32[]{:S(2)}) async-start(bf16[8,48,640]{2,1,0:T(8,128)(2,1)} %tree_attention.2), calls=%async_computation | async-start | bytes 983040 | tf_op jit(solution)/shard_map/all_to_all | solution.py:486
  46.6 2.2 %copy-done.1 = bf16[1,4096,512]{2,1,0:T(8,128)(2,1)S(1)} copy-done((bf16[1,4096,512]{2,1,0:T(8,128)(2,1)S(1)}, bf16[1,4096,512]{2,1,0:T(8,128)(2,1)}, u32[]{:S(2)}) %copy-start.1) | copy-done | bytes 4194328
  48.8 12.9 %tree_attention.3 = bf16[8,48,640]{2,1,0:T(8,128)(2,1)} custom-call(s32[3,7]{1,0:T(4,128)S(1)} %copy-done.7, s32[1]{0:T(128)} %bitcast.1.owner_ref, bf16[48,1024]{1,0:T(8,128)(2,1)S(1)} %copy-done.5, bf16[48,1024]{1,0:T(8,128)(2,1)S(1)} %collective-permute-done.refs_1_, bf16[48,1024]{1,0:T(8,128)(2,1)S(1)} %collective-permute-done.1.refs_2_, ...), custom_call_target="tpu_custom_call" | custom-call | tf_op jit(solution)/shard_map/tree_attention/pallas_call | solution.py:207
  61.7 11.3 %all-to-all-start.1 = ((bf16[8,48,640]{2,1,0:T(8,128)(2,1)}), bf16[8,48,640]{2,1,0:T(8,128)(2,1)S(1)}, u32[]{:S(2)}, u32[]{:S(2)}) async-start(bf16[8,48,640]{2,1,0:T(8,128)(2,1)} %tree_attention.3), calls=%async_computation.1 | async-start | bytes 983040 | tf_op jit(solution)/shard_map/all_to_all | solution.py:486
  73.1 4.6 %combine_project.2 = (bf16[48,512]{1,0:T(8,128)(2,1)S(1)}, f32[48,1024]{1,0:T(8,128)S(1)}, f32[48,1024]{1,0:T(8,128)S(1)}, f32[48,1024]{1,0:T(8,128)S(1)}, f32[48,1024]{1,0:T(8,128)S(1)}) custom-call(s32[1]{0:T(128)} %bitcast.place_ref, bf16[8,48,640]{2,1,0:T(8,128)(2,1)S(1)} %all-to-all-done.every_ref, bf16[1024,4096]{1,0:T(8,128)(2,1)} %weight_ref.5), custom_call_target="tpu_custom_call" | custom-call | tf_op jit(solution)/shard_map/combine_project/pallas_call | solution.py:273
  77.7 5.3 %all-to-all-done.1.every_ref = bf16[8,48,640]{2,1,0:T(8,128)(2,1)S(1)} async-done(((bf16[8,48,640]{2,1,0:T(8,128)(2,1)}), bf16[8,48,640]{2,1,0:T(8,128)(2,1)S(1)}, u32[]{:S(2)}, u32[]{:S(2)}) %all-to-all-start.1) | async-done | bytes 491552 | tf_op jit(solution)/shard_map/all_to_all | solution.py:486
  83.0 4.6 %combine_project.3 = (bf16[48,512]{1,0:T(8,128)(2,1)S(1)}, bf16[48,1024]{1,0:T(8,128)(2,1)S(1)}, bf16[48,1024]{1,0:T(8,128)(2,1)S(1)}, bf16[48,1024]{1,0:T(8,128)(2,1)S(1)}, bf16[48,1024]{1,0:T(8,128)(2,1)S(1)}) custom-call(s32[1]{0:T(128)} %bitcast.place_ref, bf16[8,48,640]{2,1,0:T(8,128)(2,1)S(1)} %all-to-all-done.1.every_ref, ...), custom_call_target="tpu_custom_call" | custom-call | tf_op jit(solution)/shard_map/combine_project/pallas_call | solution.py:273
  89.0 1.6 collective-permute-start.8
  90.6 3.3 %collective-permute-done.8 = bf16[48,1024]{1,0:T(8,128)(2,1)S(1)} collective-permute-done((bf16[48,1024]{1,0:T(8,128)(2,1)S(1)}, bf16[48,1024]{1,0:T(8,128)(2,1)S(1)}, u32[]{:S(2)}, u32[]{:S(2)}) %collective-permute-start.8) | collective-permute-done | bytes 98336 | tf_op jit(solution)/shard_map/ppermute | solution.py:421
  94.3 2.1 %collective-permute-start.22 = (bf16[48,1024]{1,0:T(8,128)(2,1)S(1)}, bf16[48,1024]{1,0:T(8,128)(2,1)S(1)}, u32[]{:S(2)}, u32[]{:S(2)}) collective-permute-start(bf16[48,1024]{1,0:T(8,128)(2,1)S(1)} %add_convert_fusion.4.refs_0_), channel_id=1, source_target_pairs={{0,24},{4,28},{8,16},{12,20},{16,8},{20,12},{24,0},{28,4},{1,25},{... | collective-permute-start | bytes 294920 | tf_op jit(solution)/shard_map/ppermute | solution.py:421
  96.4 3.2 %collective-permute-done.20.refs_0_ = bf16[48,1024]{1,0:T(8,128)(2,1)S(1)} collective-permute-done((bf16[48,1024]{1,0:T(8,128)(2,1)S(1)}, bf16[48,1024]{1,0:T(8,128)(2,1)S(1)}, u32[]{:S(2)}, u32[]{:S(2)}) %collective-permute-start.20) | collective-permute-done | bytes 98336 | tf_op jit(solution)/shard_map/ppermute | solution.py:421
  99.6 2.1 %collective-permute-start.21 = (bf16[48,1024]{1,0:T(8,128)(2,1)S(1)}, bf16[48,1024]{1,0:T(8,128)(2,1)S(1)}, u32[]{:S(2)}, u32[]{:S(2)}) collective-permute-start(bf16[48,1024]{1,0:T(8,128)(2,1)S(1)} %collective-permute-done.20.refs_0_), channel_id=1, source_target_pairs={{0,4},{4,0},{8,12},{12,8},{16,20},{20,16},{24,28},{28,24},{1,5},{5... | collective-permute-start | bytes 294920 | tf_op jit(solution)/shard_map/ppermute | solution.py:421
  102.3 1.3 collective-permute-start.11
  104.5 1.8 %collective-permute-done.23.refs_3_ = bf16[48,1024]{1,0:T(8,128)(2,1)S(1)} collective-permute-done((bf16[48,1024]{1,0:T(8,128)(2,1)S(1)}, bf16[48,1024]{1,0:T(8,128)(2,1)S(1)}, u32[]{:S(2)}, u32[]{:S(2)}) %collective-permute-start.23) | collective-permute-done | bytes 98336 | tf_op jit(solution)/shard_map/ppermute | solution.py:421
  106.3 2.0 %copy-done.2 = bf16[1024,1792]{1,0:T(8,128)(2,1)S(1)} copy-done((bf16[1024,1792]{1,0:T(8,128)(2,1)S(1)}, bf16[1024,1792]{1,0:T(8,128)(2,1)}, u32[]{:S(2)}) %copy-start.2) | copy-done | bytes 3670040
  108.3 3.7 %gate_up.3 = (bf16[96,3712]{1,0:T(8,128)(2,1)S(1)}, bf16[96,3712]{1,0:T(8,128)(2,1)S(1)}) custom-call(s32[1]{0:T(128)} %bitcast.3.spot_ref, f32[1,1024]{1,0:T(1,128)S(1)} %bitcast.5, bf16[1024,1792]{1,0:T(8,128)(2,1)S(1)} %copy-done.2, bf16[1024,1792]{1,0:T(8,128)(2,1)} %up_ref.3, bf16[48,1024]{1,0:T(8,128)(2,1)S(1)} %collective-permute-done.20.refs_0_, ...), custom_call_target="tpu_custom_call" | custom-call | tf_op jit(solution)/shard_map/gate_up/pallas_call | solution.py:323
  112.1 1.1 collective-permute-start.10
  113.3 1.0 collective-permute-start.12
  114.2 3.6 %collective-permute-done.10.refs_1_ = bf16[48,1024]{1,0:T(8,128)(2,1)S(1)} collective-permute-done((bf16[48,1024]{1,0:T(8,128)(2,1)S(1)}, bf16[48,1024]{1,0:T(8,128)(2,1)S(1)}, u32[]{:S(2)}, u32[]{:S(2)}) %collective-permute-start.10) | collective-permute-done | bytes 98336 | tf_op jit(solution)/shard_map/ppermute | solution.py:421
  117.8 1.7 collective-permute-done.12.refs_3_
  119.5 3.7 %gate_up.2 = (bf16[96,3712]{1,0:T(8,128)(2,1)S(1)}, bf16[96,3712]{1,0:T(8,128)(2,1)S(1)}) custom-call(s32[1]{0:T(128)} %bitcast.3.spot_ref, f32[1,1024]{1,0:T(1,128)S(1)} %bitcast.6, bf16[1024,1792]{1,0:T(8,128)(2,1)S(1)} %copy-done.2, bf16[1024,1792]{1,0:T(8,128)(2,1)} %up_ref.3, bf16[48,1024]{1,0:T(8,128)(2,1)S(1)} %add_convert_fusion.4.refs_0_, ...), custom_call_target="tpu_custom_call" | custom-call | tf_op jit(solution)/shard_map/gate_up/pallas_call | solution.py:323
  123.6 1.6 collective-permute-start.25
  125.8 1.6 collective-permute-start.14
  127.4 7.5 %collective-permute-done.25.got_ref = bf16[48,3712]{1,0:T(8,128)(2,1)S(1)} collective-permute-done((bf16[48,3712]{1,0:T(8,128)(2,1)S(1)}, bf16[48,3712]{1,0:T(8,128)(2,1)S(1)}, u32[]{:S(2)}, u32[]{:S(2)}) %collective-permute-start.25) | collective-permute-done | bytes 356384 | tf_op jit(solution)/shard_map/ppermute | solution.py:421
  135.1 1.6 collective-permute-start.26
  136.6 5.8 %collective-permute-done.14.got_ref = bf16[48,3712]{1,0:T(8,128)(2,1)S(1)} collective-permute-done((bf16[48,3712]{1,0:T(8,128)(2,1)S(1)}, bf16[48,3712]{1,0:T(8,128)(2,1)S(1)}, u32[]{:S(2)}, u32[]{:S(2)}) %collective-permute-start.14) | collective-permute-done | bytes 356384 | tf_op jit(solution)/shard_map/ppermute | solution.py:421
  142.7 1.6 collective-permute-start.15
  144.3 1.9 %collective-permute-done.26.refs_1_ = bf16[48,1792]{1,0:T(8,128)(2,1)S(1)} collective-permute-done((bf16[48,1792]{1,0:T(8,128)(2,1)S(1)}, bf16[48,1792]{1,0:T(8,128)(2,1)S(1)}, u32[]{:S(2)}, u32[]{:S(2)}) %collective-permute-start.26) | collective-permute-done | bytes 172064 | tf_op jit(solution)/shard_map/ppermute | solution.py:421
  146.3 3.2 %collective-permute-done.15.refs_1_ = bf16[48,1792]{1,0:T(8,128)(2,1)S(1)} collective-permute-done((bf16[48,1792]{1,0:T(8,128)(2,1)S(1)}, bf16[48,1792]{1,0:T(8,128)(2,1)S(1)}, u32[]{:S(2)}, u32[]{:S(2)}) %collective-permute-start.15) | collective-permute-done | bytes 172064 | tf_op jit(solution)/shard_map/ppermute | solution.py:421
  149.6 1.0 down.3
  150.5 1.1 collective-permute-start.30
  151.6 1.0 collective-permute-start.28
  153.6 1.1 collective-permute-start.19
  154.7 1.0 collective-permute-start.17
  156.8 1.5 collective-permute-done.28
  158.3 1.4 collective-permute-start.29
  159.7 2.4 %collective-permute-done.17 = bf16[48,1024]{1,0:T(8,128)(2,1)S(1)} collective-permute-done((bf16[48,1024]{1,0:T(8,128)(2,1)S(1)}, bf16[48,1024]{1,0:T(8,128)(2,1)S(1)}, u32[]{:S(2)}, u32[]{:S(2)}) %collective-permute-start.17) | collective-permute-done | bytes 98336 | tf_op jit(solution)/shard_map/ppermute | solution.py:421
  163.4 1.6 collective-permute-done.29
  164.9 4.6 %collective-permute-done.18 = bf16[48,1024]{1,0:T(8,128)(2,1)S(1)} collective-permute-done((bf16[48,1024]{1,0:T(8,128)(2,1)S(1)}, bf16[48,1024]{1,0:T(8,128)(2,1)S(1)}, u32[]{:S(2)}, u32[]{:S(2)}) %collective-permute-start.18) | collective-permute-done | bytes 98336 | tf_op jit(solution)/shard_map/ppermute | solution.py:421
  (62 shorter events, 11.7 us)
Async XLA Ops:
  0.6 7.4 %collective-permute-start.1 = (bf16[48,1024]{1,0:T(8,128)(2,1)}, bf16[48,1024]{1,0:T(8,128)(2,1)S(1)}, u32[]{:S(2)}, u32[]{:S(2)}) collective-permute-start(bf16[48,1024]{1,0:T(8,128)(2,1)} %refs_0_.5), channel_id=1, source_target_pairs={{0,8},{4,12},{8,0},{12,4},{16,24},{20,28},{24,16},{28,20},{1,9},{5... | collective-permute-start | bytes 294920 | tf_op jit(solution)/shard_map/ppermute | solution.py:421
  3.7 10.6 %collective-permute-start.3 = (bf16[48,1024]{1,0:T(8,128)(2,1)}, bf16[48,1024]{1,0:T(8,128)(2,1)S(1)}, u32[]{:S(2)}, u32[]{:S(2)}) collective-permute-start(bf16[48,1024]{1,0:T(8,128)(2,1)} %refs_0_.5), channel_id=1, source_target_pairs={{0,16},{4,20},{8,24},{12,28},{16,0},{20,4},{24,8},{28,12},{1,17},{... | collective-permute-start | bytes 294920 | tf_op jit(solution)/shard_map/ppermute | solution.py:421
  6.3 9.6 %collective-permute-start.5 = (bf16[48,1024]{1,0:T(8,128)(2,1)}, bf16[48,1024]{1,0:T(8,128)(2,1)S(1)}, u32[]{:S(2)}, u32[]{:S(2)}) collective-permute-start(bf16[48,1024]{1,0:T(8,128)(2,1)} %refs_0_.5), channel_id=1, source_target_pairs={{0,24},{4,28},{8,16},{12,20},{16,8},{20,12},{24,0},{28,4},{1,25},{... | collective-permute-start | bytes 294920 | tf_op jit(solution)/shard_map/ppermute | solution.py:421
  6.3 13.1 %collective-permute-start = (bf16[48,1024]{1,0:T(8,128)(2,1)}, bf16[48,1024]{1,0:T(8,128)(2,1)S(1)}, u32[]{:S(2)}, u32[]{:S(2)}) collective-permute-start(bf16[48,1024]{1,0:T(8,128)(2,1)} %refs_0_.5), channel_id=1, source_target_pairs={{0,4},{4,0},{8,12},{12,8},{16,20},{20,16},{24,28},{28,24},{1,5},{5... | collective-permute-start | bytes 294920 | tf_op jit(solution)/shard_map/ppermute | solution.py:421
  8.0 11.4 %collective-permute-start.2 = (bf16[48,1024]{1,0:T(8,128)(2,1)S(1)}, bf16[48,1024]{1,0:T(8,128)(2,1)S(1)}, u32[]{:S(2)}, u32[]{:S(2)}) collective-permute-start(bf16[48,1024]{1,0:T(8,128)(2,1)S(1)} %collective-permute-done.1.refs_2_), channel_id=1, source_target_pairs={{0,4},{4,0},{8,12},{12,8},{16,20},{20,16},{24,28},{28,24},{1,5},{5... | collective-permute-start | bytes 294920 | tf_op jit(solution)/shard_map/ppermute | solution.py:421
  14.4 5.1 %collective-permute-start.4 = (bf16[48,1024]{1,0:T(8,128)(2,1)S(1)}, bf16[48,1024]{1,0:T(8,128)(2,1)S(1)}, u32[]{:S(2)}, u32[]{:S(2)}) collective-permute-start(bf16[48,1024]{1,0:T(8,128)(2,1)S(1)} %collective-permute-done.3.refs_4_), channel_id=1, source_target_pairs={{0,4},{4,0},{8,12},{12,8},{16,20},{20,16},{24,28},{28,24},{1,5},{5... | collective-permute-start | bytes 294920 | tf_op jit(solution)/shard_map/ppermute | solution.py:421
  15.9 4.6 %collective-permute-start.6 = (bf16[48,1024]{1,0:T(8,128)(2,1)S(1)}, bf16[48,1024]{1,0:T(8,128)(2,1)S(1)}, u32[]{:S(2)}, u32[]{:S(2)}) collective-permute-start(bf16[48,1024]{1,0:T(8,128)(2,1)S(1)} %collective-permute-done.5.refs_6_), channel_id=1, source_target_pairs={{0,4},{4,0},{8,12},{12,8},{16,20},{20,16},{24,28},{28,24},{1,5},{5... | collective-permute-start | bytes 294920 | tf_op jit(solution)/shard_map/ppermute | solution.py:421
  20.5 2.2 %copy-start = (bf16[1,4096,512]{2,1,0:T(8,128)(2,1)S(1)}, bf16[1,4096,512]{2,1,0:T(8,128)(2,1)}, u32[]{:S(2)}) copy-start(bf16[1,4096,512]{2,1,0:T(8,128)(2,1)} %refs_8_.3) | copy-start | bytes 12582916
  22.7 0.9 copy-start.4
  23.6 0.7 copy-start.6
  24.2 22.4 %copy-start.5 = (bf16[48,1024]{1,0:T(8,128)(2,1)S(1)}, bf16[48,1024]{1,0:T(8,128)(2,1)}, u32[]{:S(2)}) copy-start(bf16[48,1024]{1,0:T(8,128)(2,1)} %refs_0_.5) | copy-start | bytes 294916
  24.3 22.4 %copy-start.7 = (s32[3,7]{1,0:T(4,128)S(1)}, s32[3,7]{1,0:T(4,128)}, u32[]{:S(2)}) copy-start(s32[3,7]{1,0:T(4,128)} %own_nodes.1.nodes_ref) | copy-start | bytes 256
  37.0 24.7 %all-to-all-start = ((bf16[8,48,640]{2,1,0:T(8,128)(2,1)}), bf16[8,48,640]{2,1,0:T(8,128)(2,1)S(1)}, u32[]{:S(2)}, u32[]{:S(2)}) async-start(bf16[8,48,640]{2,1,0:T(8,128)(2,1)} %tree_attention.2), calls=%async_computation | async-start | bytes 983040 | tf_op jit(solution)/shard_map/all_to_all | solution.py:486
  46.6 2.2 %copy-start.1 = (bf16[1,4096,512]{2,1,0:T(8,128)(2,1)S(1)}, bf16[1,4096,512]{2,1,0:T(8,128)(2,1)}, u32[]{:S(2)}) copy-start(bf16[1,4096,512]{2,1,0:T(8,128)(2,1)} %refs_8_.3) | copy-start | bytes 12582916
  61.7 21.3 %all-to-all-start.1 = ((bf16[8,48,640]{2,1,0:T(8,128)(2,1)}), bf16[8,48,640]{2,1,0:T(8,128)(2,1)S(1)}, u32[]{:S(2)}, u32[]{:S(2)}) async-start(bf16[8,48,640]{2,1,0:T(8,128)(2,1)} %tree_attention.3), calls=%async_computation.1 | async-start | bytes 983040 | tf_op jit(solution)/shard_map/all_to_all | solution.py:486
  83.0 11.0 %copy-start.9 = (bf16[48,1024]{1,0:T(8,128)(2,1)S(1)}, bf16[48,1024]{1,0:T(8,128)(2,1)}, u32[]{:S(2)}) copy-start(bf16[48,1024]{1,0:T(8,128)(2,1)} %param.32) | copy-start | bytes 294916
  83.0 23.3 %copy-start.8 = (f32[1024]{0:T(1024)S(1)}, f32[1024]{0:T(1024)}, u32[]{:S(2)}) copy-start(f32[1024]{0:T(1024)} %param.34) | copy-start | bytes 12292
  87.6 1.4 collective-permute-start.7
  87.7 2.9 %collective-permute-start.9 = (bf16[48,1024]{1,0:T(8,128)(2,1)S(1)}, bf16[48,1024]{1,0:T(8,128)(2,1)S(1)}, u32[]{:S(2)}, u32[]{:S(2)}) collective-permute-start(bf16[48,1024]{1,0:T(8,128)(2,1)S(1)} %get-tuple-element.37), channel_id=1, source_target_pairs={{0,1},{1,0},{2,3},{3,2},{4,5},{5,4},{6,7},{7,6},{8,9},{9,8},{10,11... | collective-permute-start | bytes 294920 | tf_op jit(solution)/shard_map/ppermute | solution.py:421
  89.0 4.9 %collective-permute-start.8 = (bf16[48,1024]{1,0:T(8,128)(2,1)S(1)}, bf16[48,1024]{1,0:T(8,128)(2,1)S(1)}, u32[]{:S(2)}, u32[]{:S(2)}) collective-permute-start(bf16[48,1024]{1,0:T(8,128)(2,1)S(1)} %add_convert_fusion.5), channel_id=1, source_target_pairs={{0,2},{1,3},{2,0},{3,1},{4,6},{5,7},{6,4},{7,5},{8,10},{9,11},{10,... | collective-permute-start | bytes 294920 | tf_op jit(solution)/shard_map/ppermute | solution.py:421
  94.0 5.5 %collective-permute-start.20 = (bf16[48,1024]{1,0:T(8,128)(2,1)S(1)}, bf16[48,1024]{1,0:T(8,128)(2,1)S(1)}, u32[]{:S(2)}, u32[]{:S(2)}) collective-permute-start(bf16[48,1024]{1,0:T(8,128)(2,1)S(1)} %add_convert_fusion.4.refs_0_), channel_id=1, source_target_pairs={{0,8},{4,12},{8,0},{12,4},{16,24},{20,28},{24,16},{28,20},{1,9},{5... | collective-permute-start | bytes 294920 | tf_op jit(solution)/shard_map/ppermute | solution.py:421
  94.3 7.3 %collective-permute-start.22 = (bf16[48,1024]{1,0:T(8,128)(2,1)S(1)}, bf16[48,1024]{1,0:T(8,128)(2,1)S(1)}, u32[]{:S(2)}, u32[]{:S(2)}) collective-permute-start(bf16[48,1024]{1,0:T(8,128)(2,1)S(1)} %add_convert_fusion.4.refs_0_), channel_id=1, source_target_pairs={{0,24},{4,28},{8,16},{12,20},{16,8},{20,12},{24,0},{28,4},{1,25},{... | collective-permute-start | bytes 294920 | tf_op jit(solution)/shard_map/ppermute | solution.py:421
  99.6 4.9 %collective-permute-start.21 = (bf16[48,1024]{1,0:T(8,128)(2,1)S(1)}, bf16[48,1024]{1,0:T(8,128)(2,1)S(1)}, u32[]{:S(2)}, u32[]{:S(2)}) collective-permute-start(bf16[48,1024]{1,0:T(8,128)(2,1)S(1)} %collective-permute-done.20.refs_0_), channel_id=1, source_target_pairs={{0,4},{4,0},{8,12},{12,8},{16,20},{20,16},{24,28},{28,24},{1,5},{5... | collective-permute-start | bytes 294920 | tf_op jit(solution)/shard_map/ppermute | solution.py:421
  101.7 4.6 %collective-permute-start.23 = (bf16[48,1024]{1,0:T(8,128)(2,1)S(1)}, bf16[48,1024]{1,0:T(8,128)(2,1)S(1)}, u32[]{:S(2)}, u32[]{:S(2)}) collective-permute-start(bf16[48,1024]{1,0:T(8,128)(2,1)S(1)} %collective-permute-done.22.refs_2_), channel_id=1, source_target_pairs={{0,4},{4,0},{8,12},{12,8},{16,20},{20,16},{24,28},{28,24},{1,5},{5... | collective-permute-start | bytes 294920 | tf_op jit(solution)/shard_map/ppermute | solution.py:421
  102.3 11.0 %collective-permute-start.11 = (bf16[48,1024]{1,0:T(8,128)(2,1)S(1)}, bf16[48,1024]{1,0:T(8,128)(2,1)S(1)}, u32[]{:S(2)}, u32[]{:S(2)}) collective-permute-start(bf16[48,1024]{1,0:T(8,128)(2,1)S(1)} %add_convert_fusion.4.refs_0_), channel_id=1, source_target_pairs={{0,16},{4,20},{8,24},{12,28},{16,0},{20,4},{24,8},{28,12},{1,17},{... | collective-permute-start | bytes 294920 | tf_op jit(solution)/shard_map/ppermute | solution.py:421
  106.3 2.0 %copy-start.2 = (bf16[1024,1792]{1,0:T(8,128)(2,1)S(1)}, bf16[1024,1792]{1,0:T(8,128)(2,1)}, u32[]{:S(2)}) copy-start(bf16[1024,1792]{1,0:T(8,128)(2,1)} %gate_ref.3) | copy-start | bytes 11010052
  112.1 11.2 %collective-permute-start.24 = (bf16[96,3712]{1,0:T(8,128)(2,1)S(1)}, bf16[96,3712]{1,0:T(8,128)(2,1)S(1)}, u32[]{:S(2)}, u32[]{:S(2)}) collective-permute-start(bf16[96,3712]{1,0:T(8,128)(2,1)S(1)} %get-tuple-element.47), channel_id=1, source_target_pairs={{0,1},{1,0},{2,3},{3,2},{4,5},{5,4},{6,7},{7,6},{8,9},{9,8},{10,11... | collective-permute-start | bytes 2138120 | tf_op jit(solution)/shard_map/ppermute | solution.py:421
  112.1 5.7 %collective-permute-start.10 = (bf16[48,1024]{1,0:T(8,128)(2,1)S(1)}, bf16[48,1024]{1,0:T(8,128)(2,1)S(1)}, u32[]{:S(2)}, u32[]{:S(2)}) collective-permute-start(bf16[48,1024]{1,0:T(8,128)(2,1)S(1)} %add_convert_fusion.4.refs_0_), channel_id=1, source_target_pairs={{0,4},{4,0},{8,12},{12,8},{16,20},{20,16},{24,28},{28,24},{1,5},{5... | collective-permute-start | bytes 294920 | tf_op jit(solution)/shard_map/ppermute | solution.py:421
  113.3 6.2 %collective-permute-start.12 = (bf16[48,1024]{1,0:T(8,128)(2,1)S(1)}, bf16[48,1024]{1,0:T(8,128)(2,1)S(1)}, u32[]{:S(2)}, u32[]{:S(2)}) collective-permute-start(bf16[48,1024]{1,0:T(8,128)(2,1)S(1)} %collective-permute-done.11.refs_2_), channel_id=1, source_target_pairs={{0,4},{4,0},{8,12},{12,8},{16,20},{20,16},{24,28},{28,24},{1,5},{5... | collective-permute-start | bytes 294920 | tf_op jit(solution)/shard_map/ppermute | solution.py:421
  123.2 26.3 %copy-start.3 = (bf16[1792,1024]{1,0:T(8,128)(2,1)S(1)}, bf16[1792,1024]{1,0:T(8,128)(2,1)}, u32[]{:S(2)}) copy-start(bf16[1792,1024]{1,0:T(8,128)(2,1)} %weight_ref.7) | copy-start | bytes 11010052
  123.2 2.2 %collective-permute-start.13 = (bf16[96,3712]{1,0:T(8,128)(2,1)S(1)}, bf16[96,3712]{1,0:T(8,128)(2,1)S(1)}, u32[]{:S(2)}, u32[]{:S(2)}) collective-permute-start(bf16[96,3712]{1,0:T(8,128)(2,1)S(1)} %get-tuple-element.39), channel_id=1, source_target_pairs={{0,1},{1,0},{2,3},{3,2},{4,5},{5,4},{6,7},{7,6},{8,9},{9,8},{10,11... | collective-permute-start | bytes 2138120 | tf_op jit(solution)/shard_map/ppermute | solution.py:421
  123.6 11.2 %collective-permute-start.25 = (bf16[48,3712]{1,0:T(8,128)(2,1)S(1)}, bf16[48,3712]{1,0:T(8,128)(2,1)S(1)}, u32[]{:S(2)}, u32[]{:S(2)}) collective-permute-start(bf16[48,3712]{1,0:T(8,128)(2,1)S(1)} %get-tuple-element.49), channel_id=1, source_target_pairs={{0,2},{1,3},{2,0},{3,1},{4,6},{5,7},{6,4},{7,5},{8,10},{9,11},{10,... | collective-permute-start | bytes 1069064 | tf_op jit(solution)/shard_map/ppermute | solution.py:421
  125.8 16.7 %collective-permute-start.14 = (bf16[48,3712]{1,0:T(8,128)(2,1)S(1)}, bf16[48,3712]{1,0:T(8,128)(2,1)S(1)}, u32[]{:S(2)}, u32[]{:S(2)}) collective-permute-start(bf16[48,3712]{1,0:T(8,128)(2,1)S(1)} %get-tuple-element.41), channel_id=1, source_target_pairs={{0,2},{1,3},{2,0},{3,1},{4,6},{5,7},{6,4},{7,5},{8,10},{9,11},{10,... | collective-permute-start | bytes 1069064 | tf_op jit(solution)/shard_map/ppermute | solution.py:421
  135.1 11.1 %collective-permute-start.26 = (bf16[48,1792]{1,0:T(8,128)(2,1)S(1)}, bf16[48,1792]{1,0:T(8,128)(2,1)S(1)}, u32[]{:S(2)}, u32[]{:S(2)}) collective-permute-start(bf16[48,1792]{1,0:T(8,128)(2,1)S(1)} %gated.3.refs_0_), channel_id=1, source_target_pairs={{0,2},{1,3},{2,0},{3,1},{4,6},{5,7},{6,4},{7,5},{8,10},{9,11},{10,... | collective-permute-start | bytes 516104 | tf_op jit(solution)/shard_map/ppermute | solution.py:421
  142.7 6.7 %collective-permute-start.15 = (bf16[48,1792]{1,0:T(8,128)(2,1)S(1)}, bf16[48,1792]{1,0:T(8,128)(2,1)S(1)}, u32[]{:S(2)}, u32[]{:S(2)}) collective-permute-start(bf16[48,1792]{1,0:T(8,128)(2,1)S(1)} %gated.2.refs_0_), channel_id=1, source_target_pairs={{0,2},{1,3},{2,0},{3,1},{4,6},{5,7},{6,4},{7,5},{8,10},{9,11},{10,... | collective-permute-start | bytes 516104 | tf_op jit(solution)/shard_map/ppermute | solution.py:421
  146.2 3.4 %collective-permute-start.27 = (bf16[96,1792]{1,0:T(8,128)(2,1)S(1)}, bf16[96,1792]{1,0:T(8,128)(2,1)S(1)}, u32[]{:S(2)}, u32[]{:S(2)}) collective-permute-start(bf16[96,1792]{1,0:T(8,128)(2,1)S(1)} %pad_maximum_fusion.1), channel_id=1, source_target_pairs={{0,1},{1,0},{2,3},{3,2},{4,5},{5,4},{6,7},{7,6},{8,9},{9,8},{10,11... | collective-permute-start | bytes 1032200 | tf_op jit(solution)/shard_map/ppermute | solution.py:421
  149.5 3.2 %collective-permute-start.16 = (bf16[96,1792]{1,0:T(8,128)(2,1)S(1)}, bf16[96,1792]{1,0:T(8,128)(2,1)S(1)}, u32[]{:S(2)}, u32[]{:S(2)}) collective-permute-start(bf16[96,1792]{1,0:T(8,128)(2,1)S(1)} %pad_maximum_fusion), channel_id=1, source_target_pairs={{0,1},{1,0},{2,3},{3,2},{4,5},{5,4},{6,7},{7,6},{8,9},{9,8},{10,11... | collective-permute-start | bytes 1032200 | tf_op jit(solution)/shard_map/ppermute | solution.py:421
  150.5 5.7 %collective-permute-start.30 = (bf16[48,1024]{1,0:T(8,128)(2,1)S(1)}, bf16[48,1024]{1,0:T(8,128)(2,1)S(1)}, u32[]{:S(2)}, u32[]{:S(2)}) collective-permute-start(bf16[48,1024]{1,0:T(8,128)(2,1)S(1)} %get-tuple-element.53), channel_id=1, source_target_pairs={{0,4},{4,0},{8,12},{12,8},{16,20},{20,16},{24,28},{28,24},{1,5},{5... | collective-permute-start | bytes 294920 | tf_op jit(solution)/shard_map/ppermute | solution.py:421
  151.6 6.7 %collective-permute-start.28 = (bf16[48,1024]{1,0:T(8,128)(2,1)S(1)}, bf16[48,1024]{1,0:T(8,128)(2,1)S(1)}, u32[]{:S(2)}, u32[]{:S(2)}) collective-permute-start(bf16[48,1024]{1,0:T(8,128)(2,1)S(1)} %get-tuple-element.51), channel_id=1, source_target_pairs={{0,4},{4,0},{8,12},{12,8},{16,20},{20,16},{24,28},{28,24},{1,5},{5... | collective-permute-start | bytes 294920 | tf_op jit(solution)/shard_map/ppermute | solution.py:421
  153.6 9.8 %collective-permute-start.19 = (bf16[48,1024]{1,0:T(8,128)(2,1)S(1)}, bf16[48,1024]{1,0:T(8,128)(2,1)S(1)}, u32[]{:S(2)}, u32[]{:S(2)}) collective-permute-start(bf16[48,1024]{1,0:T(8,128)(2,1)S(1)} %get-tuple-element.45), channel_id=1, source_target_pairs={{0,4},{4,0},{8,12},{12,8},{16,20},{20,16},{24,28},{28,24},{1,5},{5... | collective-permute-start | bytes 294920 | tf_op jit(solution)/shard_map/ppermute | solution.py:421
  154.7 7.4 %collective-permute-start.17 = (bf16[48,1024]{1,0:T(8,128)(2,1)S(1)}, bf16[48,1024]{1,0:T(8,128)(2,1)S(1)}, u32[]{:S(2)}, u32[]{:S(2)}) collective-permute-start(bf16[48,1024]{1,0:T(8,128)(2,1)S(1)} %get-tuple-element.43), channel_id=1, source_target_pairs={{0,4},{4,0},{8,12},{12,8},{16,20},{20,16},{24,28},{28,24},{1,5},{5... | collective-permute-start | bytes 294920 | tf_op jit(solution)/shard_map/ppermute | solution.py:421
  156.2 7.1 %collective-permute-start.31 = (bf16[48,1024]{1,0:T(8,128)(2,1)S(1)}, bf16[48,1024]{1,0:T(8,128)(2,1)S(1)}, u32[]{:S(2)}, u32[]{:S(2)}) collective-permute-start(bf16[48,1024]{1,0:T(8,128)(2,1)S(1)} %add_convert_fusion.1), channel_id=1, source_target_pairs={{0,8},{4,12},{8,0},{12,4},{16,24},{20,28},{24,16},{28,20},{1,9},{5... | collective-permute-start | bytes 294920 | tf_op jit(solution)/shard_map/ppermute | solution.py:421
  158.3 6.6 %collective-permute-start.29 = (bf16[48,1024]{1,0:T(8,128)(2,1)S(1)}, bf16[48,1024]{1,0:T(8,128)(2,1)S(1)}, u32[]{:S(2)}, u32[]{:S(2)}) collective-permute-start(bf16[48,1024]{1,0:T(8,128)(2,1)S(1)} %add_convert_fusion.2), channel_id=1, source_target_pairs={{0,24},{4,28},{8,16},{12,20},{16,8},{20,12},{24,0},{28,4},{1,25},{... | collective-permute-start | bytes 294920 | tf_op jit(solution)/shard_map/ppermute | solution.py:421
  162.1 7.4 %collective-permute-start.18 = (bf16[48,1024]{1,0:T(8,128)(2,1)S(1)}, bf16[48,1024]{1,0:T(8,128)(2,1)S(1)}, u32[]{:S(2)}, u32[]{:S(2)}) collective-permute-start(bf16[48,1024]{1,0:T(8,128)(2,1)S(1)} %add_convert_fusion.3), channel_id=1, source_target_pairs={{0,16},{4,20},{8,24},{12,28},{16,0},{20,4},{24,8},{28,12},{1,17},{... | collective-permute-start | bytes 294920 | tf_op jit(solution)/shard_map/ppermute | solution.py:421

commit v4 on v3

--- a/solution.py
+++ b/solution.py
@@ -18,6 +18,20 @@
 EPSILON = 1e-05
 ALIGN = 16
 BLOCK = 512
+VMEM_BYTES = 50 << 20
+
+
+def cost(flops, moved, exps):
+    return pl.CostEstimate(flops=flops, bytes_accessed=moved, transcendentals=exps)
+
+
+def streamed(pairs, sems):
+    copies = [
+        pltpu.make_async_copy(source, target, sems.at[k]) for k, (source, target) in enumerate(pairs)
+    ]
+    for copy in copies:
+        copy.start()
+    return copies
 
 
 def own_nodes(owner, local_counts, tree, lengths, slots):
@@ -89,7 +103,31 @@
     def kernel(nodes_ref, owner_ref, *refs):
         query_refs = refs[:part_total]
         cache_refs = refs[part_total : part_total + 3]
-        out_ref, all_rows, run_out, run_lse, acc, peak, total = refs[part_total + 3 :]
+        out_ref, all_rows, run_out, run_lse, acc, peak, total, *rest = refs[part_total + 3 :]
+        kept_refs, sems = rest[:3], rest[3]
+        columns = pl.ds(kv_head * 2 * HEAD, 2 * HEAD)
+
+        def copies(act):
+            node, flag = 0, 0
+            for (slot_total, span, _), cache_ref, kept_ref in zip(levels, cache_refs, kept_refs):
+                block = min(BLOCK, span)
+                for member in range(slot_total):
+                    for index in range(span // block):
+                        here = pl.ds(index * block, block)
+                        copy = pltpu.make_async_copy(
+                            cache_ref.at[member, here, columns],
+                            kept_ref.at[member, here, :],
+                            sems.at[flag + index],
+                        )
+
+                        @pl.when(index * block < nodes_ref[2, node])
+                        def _(copy=copy):
+                            act(copy)
+
+                    node += 1
+                    flag += span // block
+
+        copies(lambda copy: copy.start())
         me = owner_ref[0]
         for part in range(part_total):
             row = pl.multiple_of((me ^ part) * own_rows, ALIGN)
@@ -98,8 +136,8 @@
             ]
         run_out[...] = jnp.zeros_like(run_out)
         run_lse[...] = jnp.full_like(run_lse, LOWEST)
-        node = 0
-        for (slot_total, span, rows), cache_ref in zip(levels, cache_refs):
+        node, flag = 0, 0
+        for (slot_total, span, rows), cache_ref, kept_ref in zip(levels, cache_refs, kept_refs):
             lanes = rows * group_size
             block = min(BLOCK, span)
             for member in range(slot_total):
@@ -107,9 +145,11 @@
                 node += 1
                 window = jnp.minimum(low - lax.rem(low, ALIGN), total_rows - rows)
                 window = pl.multiple_of(window, ALIGN)
-                columns = [h * HEAD for h in range(group_size)]
+                offsets = [h * HEAD for h in range(group_size)]
+                first = flag
+                flag += span // block
                 grouped = jnp.concatenate(
-                    [all_rows[pl.ds(window, rows), c : c + HEAD] for c in columns], axis=0
+                    [all_rows[pl.ds(window, rows), c : c + HEAD] for c in offsets], axis=0
                 )
                 acc[:, :lanes] = jnp.zeros((HEAD, lanes), jnp.float32)
                 peak[:, :lanes] = jnp.full((1, lanes), LOWEST, jnp.float32)
@@ -117,14 +157,13 @@
 
                 def visit(index, carry, masked):
                     at = pl.multiple_of(index * block, block)
-                    keys = cache_ref[
-                        member, pl.ds(at, block), 2 * kv_head * HEAD : (2 * kv_head + 1) * HEAD
-                    ]
-                    values = cache_ref[
-                        member,
-                        pl.ds(at, block),
-                        (2 * kv_head + 1) * HEAD : (2 * kv_head + 2) * HEAD,
-                    ]
+                    pltpu.make_async_copy(
+                        cache_ref.at[member, pl.ds(at, block), columns],
+                        kept_ref.at[member, pl.ds(at, block), :],
+                        sems.at[first + index],
+                    ).wait()
+                    keys = kept_ref[member, pl.ds(at, block), :HEAD]
+                    values = kept_ref[member, pl.ds(at, block), HEAD:]
                     scores = lax.dot_general(
                         keys,
                         grouped,
@@ -164,7 +203,7 @@
                 ).T
                 position = window + lax.broadcasted_iota(jnp.int32, (rows, HEAD), 0)
                 live = (position >= low) & (position < high)
-                for h, c in enumerate(columns):
+                for h, c in enumerate(offsets):
                     here = (pl.ds(window, rows), slice(c, c + HEAD))
                     old_lse, old_out = run_lse[here], run_out[here]
                     add_lse = part_lse[h * rows : (h + 1) * rows]
@@ -201,13 +240,16 @@
             )
             out_ref[part, :, width:] = packed.astype(jnp.bfloat16)
 
+    block_total = sum(count * (span // min(BLOCK, span)) for count, span, _ in levels)
     most = max(rows for _, _, rows in levels) * group_size
     vmem = pl.BlockSpec(memory_space=pltpu.VMEM)
     smem = pl.BlockSpec(memory_space=pltpu.SMEM)
     return pl.pallas_call(
         kernel,
         out_shape=jax.ShapeDtypeStruct((part_total, own_rows, width + HEAD), jnp.bfloat16),
-        in_specs=[smem, smem] + [vmem] * (part_total + 3),
+        in_specs=[smem, smem]
+        + [vmem] * part_total
+        + [pl.BlockSpec(memory_space=pltpu.HBM)] * 3,
         out_specs=vmem,
         scratch_shapes=[
             pltpu.VMEM((total_rows, width), jnp.bfloat16),
@@ -216,8 +258,15 @@
             pltpu.VMEM((HEAD, most), jnp.float32),
             pltpu.VMEM((1, most), jnp.float32),
             pltpu.VMEM((1, most), jnp.float32),
-        ],
-        compiler_params=pltpu.CompilerParams(vmem_limit_bytes=48 << 20),
+        ]
+        + [pltpu.VMEM((count, span, 2 * HEAD), jnp.bfloat16) for count, span, _ in levels]
+        + [pltpu.SemaphoreType.DMA((block_total,))],
+        compiler_params=pltpu.CompilerParams(vmem_limit_bytes=VMEM_BYTES),
+        cost_estimate=cost(
+            4 * HEAD * group_size * sum(c * span * rows for c, span, rows in levels),
+            2 * 2 * HEAD * sum(count * span for count, span, _ in levels),
+            group_size * sum(c * span * rows for c, span, rows in levels),
+        ),
         name="tree_attention",
     )(nodes, owner[None], *query_parts, *caches)
 
@@ -232,7 +281,19 @@
 
     def kernel(place_ref, every_ref, weight_ref, *refs):
         added_refs = refs[:block_total] if added is not None else (None,) * block_total
-        attended_ref, *block_refs = refs[len(refs) - 1 - block_total :]
+        attended_ref, *block_refs = refs[len(refs) - 3 - block_total : -2]
+        kept, sems = refs[-2:]
+        columns = [
+            pl.ds(pl.multiple_of((place_ref[0] ^ block) * own_width, HEAD), own_width)
+            for block in range(block_total)
+        ]
+        copies = streamed(
+            [
+                (weight_ref.at[pl.ds(row_start, width), column], kept.at[block])
+                for block, column in enumerate(columns)
+            ],
+            sems,
+        )
         lse = []
         for part in range(part_total):
             terms = every_ref[part, :, width:].astype(jnp.float32)
@@ -259,11 +320,9 @@
                 jnp.bfloat16
             )
         for block in range(block_total):
-            at = pl.multiple_of((place_ref[0] ^ block) * own_width, HEAD)
+            copies[block].wait()
             product = jnp.dot(
-                attended_ref[...],
-                weight_ref[row_start : row_start + width, pl.ds(at, own_width)],
-                preferred_element_type=jnp.float32,
+                attended_ref[...], kept[block], preferred_element_type=jnp.float32
             )
             if added is not None:
                 product = product + added_refs[block][...]
@@ -274,10 +333,20 @@
         kernel,
         out_shape=[jax.ShapeDtypeStruct((own_rows, width), jnp.bfloat16)]
         + [jax.ShapeDtypeStruct((own_rows, own_width), kind)] * block_total,
-        in_specs=[pl.BlockSpec(memory_space=pltpu.SMEM)]
-        + [vmem] * (2 + (block_total if added is not None else 0)),
+        in_specs=[pl.BlockSpec(memory_space=pltpu.SMEM), vmem]
+        + [pl.BlockSpec(memory_space=pltpu.HBM)]
+        + [vmem] * (block_total if added is not None else 0),
         out_specs=[vmem] * (1 + block_total),
-        compiler_params=pltpu.CompilerParams(vmem_limit_bytes=48 << 20),
+        scratch_shapes=[
+            pltpu.VMEM((block_total, width, own_width), jnp.bfloat16),
+            pltpu.SemaphoreType.DMA((block_total,)),
+        ],
+        compiler_params=pltpu.CompilerParams(vmem_limit_bytes=VMEM_BYTES),
+        cost_estimate=cost(
+            2 * own_rows * width * weight.shape[1],
+            2 * width * weight.shape[1],
+            part_total * own_rows * HEAD,
+        ),
         name="combine_project",
     )(place[None], every, weight, *(added or ()))
     return outs[0], outs[1:]
@@ -295,12 +364,28 @@
     own_rows, features = parts[0].shape
     rows = own_rows * len(parts)
     half = rows // 2
+    piece = half // 2
     each = len(parts) // group_total
     units = gate_weight.shape[1]
+    tile = units // 2 if (units // 2) % HEAD == 0 else units
 
     def kernel(spot_ref, gain_ref, gate_ref, up_ref, *refs):
         part_refs = refs[: len(parts)]
-        keep_ref, send_ref, scaled, squares = refs[len(parts) :]
+        keep_ref, *send_refs, scaled, squares, kept_gate, kept_up, sems = refs[len(parts) :]
+        tiles = [
+            (ref, kept, base, at)
+            for ref, kept, base in ((gate_ref, kept_gate, 0), (up_ref, kept_up, units))
+            for at in range(0, units, tile)
+        ]
+        copies = streamed(
+            [
+                (ref, kept)
+                if tile == units
+                else (ref.at[:, pl.ds(at, tile)], kept.at[:, pl.ds(at, tile)])
+                for ref, kept, _, at in tiles
+            ],
+            sems,
+        )
         for index, part_ref in enumerate(part_refs):
             at = ((index // each) ^ spot_ref[0]) * each + index % each
             here = pl.ds(pl.multiple_of(at * own_rows, ALIGN), own_rows)
@@ -309,43 +394,55 @@
             squares[here, :] = jnp.broadcast_to(
                 jnp.sum(wide * wide, axis=1, keepdims=True), (own_rows, HEAD)
             )
-        for column, weight_ref in ((0, gate_ref), (units, up_ref)):
+        for copy, (_, kept, base, at) in zip(copies, tiles):
+            copy.wait()
+            here = slice(base + at, base + at + tile)
             product = jnp.dot(
-                scaled[...], weight_ref[...], preferred_element_type=jnp.float32
+                scaled[...], kept[:, at : at + tile], preferred_element_type=jnp.float32
             ).astype(jnp.bfloat16)
-            keep_ref[:, column : column + units] = product[:half]
-            send_ref[:, column : column + units] = product[half:]
+            keep_ref[:, here] = product[:half]
+            for k, send_ref in enumerate(send_refs):
+                send_ref[:, here] = product[half + k * piece : half + (k + 1) * piece]
         terms = split_terms(squares[...])
         keep_ref[:, 2 * units :] = terms[:half]
-        send_ref[:, 2 * units :] = terms[half:]
+        for k, send_ref in enumerate(send_refs):
+            send_ref[:, 2 * units :] = terms[half + k * piece : half + (k + 1) * piece]
 
     vmem = pl.BlockSpec(memory_space=pltpu.VMEM)
-    return pl.pallas_call(
+    keep, *send = pl.pallas_call(
         kernel,
-        out_shape=[jax.ShapeDtypeStruct((half, 2 * units + HEAD), jnp.bfloat16)] * 2,
-        in_specs=[pl.BlockSpec(memory_space=pltpu.SMEM)] + [vmem] * (3 + len(parts)),
-        out_specs=[vmem, vmem],
+        out_shape=[jax.ShapeDtypeStruct((half, 2 * units + HEAD), jnp.bfloat16)]
+        + [jax.ShapeDtypeStruct((piece, 2 * units + HEAD), jnp.bfloat16)] * 2,
+        in_specs=[pl.BlockSpec(memory_space=pltpu.SMEM), vmem]
+        + [pl.BlockSpec(memory_space=pltpu.HBM)] * 2
+        + [vmem] * len(parts),
+        out_specs=[vmem] * 3,
         scratch_shapes=[
             pltpu.VMEM((rows, features), jnp.bfloat16),
             pltpu.VMEM((rows, HEAD), jnp.float32),
+            pltpu.VMEM((features, units), jnp.bfloat16),
+            pltpu.VMEM((features, units), jnp.bfloat16),
+            pltpu.SemaphoreType.DMA((2 * units // tile,)),
         ],
-        compiler_params=pltpu.CompilerParams(vmem_limit_bytes=48 << 20),
+        compiler_params=pltpu.CompilerParams(vmem_limit_bytes=VMEM_BYTES),
+        cost_estimate=cost(4 * rows * features * units, 4 * features * units, 0),
         name="gate_up",
     )(spot[None], norm_gain[None, :], gate_weight, up_weight, *parts)
+    return keep, send
 
 
 def add_halves(keep, got, units):
     half = keep.shape[0] // 2
 
-    def kernel(keep_ref, got_ref, next_ref, send_ref):
-        for ref, at in ((next_ref, 0), (send_ref, half)):
+    def kernel(keep_ref, low_ref, high_ref, next_ref, send_ref):
+        for ref, got_ref, at in ((next_ref, low_ref, 0), (send_ref, high_ref, half)):
             here = pl.ds(at, half)
             ref[:, : 2 * units] = (
                 keep_ref[here, : 2 * units].astype(jnp.float32)
-                + got_ref[here, : 2 * units].astype(jnp.float32)
+                + got_ref[:, : 2 * units].astype(jnp.float32)
             ).astype(jnp.bfloat16)
             terms = keep_ref[here, 2 * units :].astype(jnp.float32)
-            terms = terms + got_ref[here, 2 * units :].astype(jnp.float32)
+            terms = terms + got_ref[:, 2 * units :].astype(jnp.float32)
             total = jnp.sum(terms, axis=1, keepdims=True)
             ref[:, 2 * units :] = split_terms(jnp.broadcast_to(total, (half, HEAD)))
 
@@ -353,11 +450,12 @@
     return pl.pallas_call(
         kernel,
         out_shape=[jax.ShapeDtypeStruct((half, keep.shape[1]), jnp.bfloat16)] * 2,
-        in_specs=[vmem, vmem],
+        in_specs=[vmem] * 3,
         out_specs=[vmem, vmem],
-        compiler_params=pltpu.CompilerParams(vmem_limit_bytes=48 << 20),
+        compiler_params=pltpu.CompilerParams(vmem_limit_bytes=VMEM_BYTES),
+        cost_estimate=cost(2 * keep.size, 6 * keep.size, 0),
         name="add_halves",
-    )(keep, got)
+    )(keep, *got)
 
 
 def gated(keep, got, units):
@@ -375,7 +473,8 @@
         out_shape=jax.ShapeDtypeStruct((keep.shape[0], units), jnp.bfloat16),
         in_specs=[vmem, vmem],
         out_specs=vmem,
-        compiler_params=pltpu.CompilerParams(vmem_limit_bytes=48 << 20),
+        compiler_params=pltpu.CompilerParams(vmem_limit_bytes=VMEM_BYTES),
+        cost_estimate=cost(4 * keep.size, 5 * keep.size, keep.size // 2),
         name="gated",
     )(keep, got)
 
@@ -411,7 +510,8 @@
             pltpu.VMEM((rows, units), jnp.bfloat16),
             pltpu.VMEM((rows, features), jnp.float32),
         ],
-        compiler_params=pltpu.CompilerParams(vmem_limit_bytes=48 << 20),
+        compiler_params=pltpu.CompilerParams(vmem_limit_bytes=VMEM_BYTES),
+        cost_estimate=cost(2 * rows * features * units, 2 * features * units, 0),
         name="down",
     )(spot[None], down_weight, *pieces)
 
@@ -421,12 +521,17 @@
     return lax.ppermute(value, axis_name, [(j, j ^ mask) for j in range(axis_total)])
 
 
-def gather_parts(value, axis_name):
+def after(value, token):
+    return lax.optimization_barrier((value, token))[0]
+
+
+def gather_parts(value, axis_name, token=None):
     parts = [value] * lax.axis_size(axis_name)
     for mask in range(len(parts) - 2, 0, -2):
         parts[mask] = swap(value, axis_name, mask)
     for mask in [0] + list(range(len(parts) - 2, 0, -2)):
-        parts[mask + 1] = swap(parts[mask], axis_name, 1)
+        held = parts[mask] if token is None or mask == 0 else after(parts[mask], token)
+        parts[mask + 1] = swap(held, axis_name, 1)
     return parts
 
 
@@ -479,7 +584,7 @@
     mlp_total = lax.axis_size("mlp")
     mlp_place = lax.axis_index("mlp").astype(jnp.int32)
     own_width = stream.shape[1]
-    query_parts = gather_parts(queries, "kv")
+    query_parts = gather_parts(queries, "kv", nodes)
     attended, blocks = [], None
     for k in range(kv_count):
         parts = tree_attention(query_parts, caches, nodes, owner, k)
@@ -496,27 +601,46 @@
         spot = 2 * spot + (mlp_place // step) % 2
     units = gate_weight.shape[1]
     row_parts = gather_parts(residual, "kv")
-    chunks = [
+    first, second = (
         [mask for mask in range(len(row_parts)) if (mask // 2) % 2 == side] for side in range(2)
-    ]
-    mixed = 0.0
-    for masks in chunks:
-        keep, send = gate_up_rows(
-            [row_parts[mask] for mask in masks],
-            norm_gain,
-            gate_weight,
-            up_weight,
-            spot,
-            mlp_total,
-        )
+    )
+    row_parts[0] = after(row_parts[0], [row_parts[mask] for mask in second if mask % 2 == 0])
+
+    def multiply(masks):
+        parts = [row_parts[mask] for mask in masks]
+        return gate_up_rows(parts, norm_gain, gate_weight, up_weight, spot, mlp_total)
+
+    def reduce_once(keep, send, token=None):
         for step in steps[:-1]:
-            keep, send = add_halves(keep, swap(send, "mlp", step), units)
-        pieces = [gated(keep, swap(send, "mlp", steps[-1]), units)]
+            if step > 1:
+                send = jnp.split(send, 2, axis=0)
+            got = [swap(piece, "mlp", step) for piece in send]
+            if token is not None and step == 1:
+                keep = after(keep, token)
+            keep, send = add_halves(keep, got, units)
+        return keep, send
+
+    def regather(hidden):
+        pieces = [hidden]
         for step in reversed(steps):
             held = pieces[0] if len(pieces) == 1 else jnp.concatenate(pieces, axis=0)
             pieces.append(swap(held, "mlp", step))
+        return pieces
+
+    def finish(pieces, masks):
         outs = down_rows(pieces, down_weight, spot, len(masks), own_rows, mlp_total)
-        mixed = mixed + scatter_sum(dict(zip(masks, outs)), "kv")
+        return outs, scatter_sum(dict(zip(masks, outs)), "kv")
+
+    keep, send = reduce_once(*multiply(first))
+    row_parts[second[0]] = after(row_parts[second[0]], send)
+    later = multiply(second)
+    hidden = gated(after(keep, later[0]), swap(send, "mlp", steps[-1]), units)
+    keep, send = reduce_once(*later, hidden)
+    outs, mixed = finish(regather(hidden), first)
+    hidden = gated(after(keep, outs[0]), swap(send, "mlp", steps[-1]), units)
+    pieces = regather(hidden)
+    pieces[0] = after(pieces[0], mixed)
+    mixed = mixed + finish(pieces, second)[1]
     return (jnp.concatenate(attended, axis=1), mixed.astype(jnp.bfloat16))
 
 

time: 169 us -> 165 us (0.976); the launches traced: 170 us -> 164 us
  waiting for transfers between devices: 56.7 us -> 66.1 us
  local copies, waits for them, and re-layouts: 8 us -> 1.59 us
  starting transfers between devices: 54.7 us -> 49.1 us
  Pallas kernels: 48.5 us -> 45.1 us
    unnamed x20 -> x12, local copies, waits for them, and re-layouts: 8 us -> 1.59 us
    all_to_all x2, waiting for transfers between devices: 5.32 us -> 10.1 us  [shards(): every = lax.all_to_all(parts, 'kv', 0, 0)]
    ppermute x32 -> x34, waiting for transfers between devices: 51.3 us -> 56 us  [swap(): lax.ppermute(value, axis_name, [(j, j ^ mask) for j in range(axis_total)])]
    pallas_call x2, Pallas kernels: 9.25 us -> 5.1 us  [combine_project(): pl.pallas_call(kernel, out_shape=[jax.ShapeDtypeStruct((own_rows, width),...]
    pallas_call x2, Pallas kernels: 1.92 us -> 6 us  [down_rows(): pl.pallas_call(kernel, out_shape=[jax.ShapeDtypeStruct((own_rows, feature...]
    pallas_call x2, Pallas kernels: 25.6 us -> 21.9 us  [tree_attention(): pl.pallas_call(kernel, out_shape=jax.ShapeDtypeStruct((part_total, own_ro...]
    ppermute x32 -> x34, starting transfers between devices: 33.7 us -> 30.7 us  [swap(): lax.ppermute(value, axis_name, [(j, j ^ mask) for j in range(axis_total)])]
    all_to_all x2, starting transfers between devices: 20.9 us -> 18.3 us  [shards(): every = lax.all_to_all(parts, 'kv', 0, 0)]
  transfers between devices with their start and end apart: 34 -> 36, of which waited for: 20 -> 23; matrix products, arithmetic and copies ran while one was open for 0% -> 1% of each run, Pallas kernels for 18% -> 15%
where the time goes in v4:
time: 165 us; the launch traced here: 164 us
  waiting for transfers between devices  66.1 us (40%)
  starting transfers between devices  49.1 us (30%)
  Pallas kernels  45.1 us (27%)
    ppermute x34, waiting for transfers between devices, swap(): lax.ppermute(value, axis_name, [(j, j ^ mask) for j in range(axis_total)])  56 us
    ppermute x34, starting transfers between devices, swap(): lax.ppermute(value, axis_name, [(j, j ^ mask) for j in range(axis_total)])  30.7 us
    pallas_call x2, Pallas kernels, tree_attention(): pl.pallas_call(kernel, out_shape=jax.ShapeDtypeStruct((part_total, own_ro...  21.9 us
    all_to_all x2, starting transfers between devices, shards(): every = lax.all_to_all(parts, 'kv', 0, 0)  18.3 us
    all_to_all x2, waiting for transfers between devices, shards(): every = lax.all_to_all(parts, 'kv', 0, 0)  10.1 us
    pallas_call x2, Pallas kernels, gate_up_rows(): pl.pallas_call(kernel, out_shape=[jax.ShapeDtypeStruct((half, 2 * units +...  7.95 us
    pallas_call x2, Pallas kernels, down_rows(): pl.pallas_call(kernel, out_shape=[jax.ShapeDtypeStruct((own_rows, feature...  6 us
    pallas_call x2, Pallas kernels, combine_project(): pl.pallas_call(kernel, out_shape=[jax.ShapeDtypeStruct((own_rows, width),...  5.1 us
  transfers between devices with their start and end apart: 36, of which 23 were waited for; matrix products, arithmetic and copies ran while one was open for 1% of the time, Pallas kernels for 15%

profile of v4, /device:TPU:0, one launch (start us, length us, event | category | flops | bytes accessed | tf_op | source)
XLA Modules:
  0.0 164.3 jit_solution(403722814260275550)
XLA Ops:
  0.6 5.1 %collective-permute-start.5 = (bf16[48,1024]{1,0:T(8,128)(2,1)}, bf16[48,1024]{1,0:T(8,128)(2,1)S(1)}, u32[]{:S(2)}, u32[]{:S(2)}) collective-permute-start(bf16[48,1024]{1,0:T(8,128)(2,1)} %refs_0_.5), channel_id=1, source_target_pairs={{0,24},{4,28},{8,16},{12,20},{16,8},{20,12},{24,0},{28,4},{1,25},{... | collective-permute-start | bytes 294920 | tf_op jit(solution)/shard_map/ppermute | solution.py:521
  6.4 1.6 collective-permute-start
  8.0 3.0 %own_nodes.1.nodes_ref = s32[3,7]{1,0:T(4,128)} custom-call(s32[1]{0:T(128)} %bitcast.1.owner_ref, s32[3,128]{1,0:T(4,128)} %bitcast.7, s32[32]{0:T(128)} %leaf_up.1, s32[16]{0:T(128)} %mid_up.1, s32[8]{0:T(128)} %refs_0_.3, s32[16]{0:T(128)} %refs_1_.1, s32[32]{0:T(128)} %refs_2_.1, s32[8]{0:T(128)} %refs_3_.1, s32[16]{0:T(128)} %refs_4_.1, s32[32]{0:T(128)} %refs_5_.1), custom_call_target="tpu_custom_call" | custom-call | tf_op jit(solution)/shard_map/own_nodes/pallas_call | solution.py:83
  11.5 2.7 %collective-permute-done.3.refs_4_ = bf16[48,1024]{1,0:T(8,128)(2,1)S(1)} collective-permute-done((bf16[48,1024]{1,0:T(8,128)(2,1)}, bf16[48,1024]{1,0:T(8,128)(2,1)S(1)}, u32[]{:S(2)}, u32[]{:S(2)}) %collective-permute-start.3) | collective-permute-done | bytes 98336 | tf_op jit(solution)/shard_map/ppermute | solution.py:521
  14.2 1.5 collective-permute-start.4
  16.3 3.0 %collective-permute-done.4.refs_5_ = bf16[48,1024]{1,0:T(8,128)(2,1)S(1)} collective-permute-done((bf16[48,1024]{1,0:T(8,128)(2,1)S(1)}, bf16[48,1024]{1,0:T(8,128)(2,1)S(1)}, u32[]{:S(2)}, u32[]{:S(2)}) %collective-permute-start.4) | collective-permute-done | bytes 98336 | tf_op jit(solution)/shard_map/ppermute | solution.py:521
  19.3 1.1 collective-permute-done.2.refs_3_
  20.3 0.9 copy-done
  21.2 0.7 copy-done.2
  21.9 10.9 %tree_attention.2 = bf16[8,48,640]{2,1,0:T(8,128)(2,1)} custom-call(s32[3,7]{1,0:T(4,128)S(1)} %copy-done.2, s32[1]{0:T(128)} %bitcast.1.owner_ref, bf16[48,1024]{1,0:T(8,128)(2,1)S(1)} %copy-done, bf16[48,1024]{1,0:T(8,128)(2,1)S(1)} %collective-permute-done.refs_1_, bf16[48,1024]{1,0:T(8,128)(2,1)S(1)} %collective-permute-done.1.refs_2_, ...), custom_call_target="tpu_custom_call" | custom-call | flops 2147483648 | bytes 6291456 | tf_op jit(solution)/shard_map/tree_attention/pallas_call | solution.py:247
  32.8 8.9 %all-to-all-start = ((bf16[8,48,640]{2,1,0:T(8,128)(2,1)}), bf16[8,48,640]{2,1,0:T(8,128)(2,1)S(1)}, u32[]{:S(2)}, u32[]{:S(2)}) async-start(bf16[8,48,640]{2,1,0:T(8,128)(2,1)} %tree_attention.2), calls=%async_computation | async-start | bytes 983040 | tf_op jit(solution)/shard_map/all_to_all | solution.py:591
  41.7 11.0 %tree_attention.3 = bf16[8,48,640]{2,1,0:T(8,128)(2,1)} custom-call(s32[3,7]{1,0:T(4,128)S(1)} %copy-done.3, s32[1]{0:T(128)} %bitcast.1.owner_ref, bf16[48,1024]{1,0:T(8,128)(2,1)S(1)} %copy-done.1, bf16[48,1024]{1,0:T(8,128)(2,1)S(1)} %collective-permute-done.refs_1_, bf16[48,1024]{1,0:T(8,128)(2,1)S(1)} %collective-permute-done.1.refs_2_, ...), custom_call_target="tpu_custom_call" | custom-call | flops 2147483648 | bytes 6291456 | tf_op jit(solution)/shard_map/tree_attention/pallas_call | solution.py:247
  52.8 1.1 all-to-all-done.every_ref
  53.9 9.4 %all-to-all-start.1 = ((bf16[8,48,640]{2,1,0:T(8,128)(2,1)}), bf16[8,48,640]{2,1,0:T(8,128)(2,1)S(1)}, u32[]{:S(2)}, u32[]{:S(2)}) async-start(bf16[8,48,640]{2,1,0:T(8,128)(2,1)} %tree_attention.3), calls=%async_computation.1 | async-start | bytes 983040 | tf_op jit(solution)/shard_map/all_to_all | solution.py:591
  63.2 2.5 %combine_project.2 = (bf16[48,512]{1,0:T(8,128)(2,1)S(1)}, f32[48,1024]{1,0:T(8,128)S(1)}, f32[48,1024]{1,0:T(8,128)S(1)}, f32[48,1024]{1,0:T(8,128)S(1)}, f32[48,1024]{1,0:T(8,128)S(1)}) custom-call(s32[1]{0:T(128)} %bitcast.place_ref, bf16[8,48,640]{2,1,0:T(8,128)(2,1)S(1)} %all-to-all-done.every_ref, bf16[1024,4096]{1,0:T(8,128)(2,1)} %weight_ref.5), custom_call_target="tpu_custom_call" | custom-call | flops 201326592 | bytes 4194304 | tf_op jit(solution)/shard_map/combine_project/pallas_call | solution.py:332
  65.8 9.0 %all-to-all-done.1.every_ref = bf16[8,48,640]{2,1,0:T(8,128)(2,1)S(1)} async-done(((bf16[8,48,640]{2,1,0:T(8,128)(2,1)}), bf16[8,48,640]{2,1,0:T(8,128)(2,1)S(1)}, u32[]{:S(2)}, u32[]{:S(2)}) %all-to-all-start.1) | async-done | bytes 491552 | tf_op jit(solution)/shard_map/all_to_all | solution.py:591
  74.8 2.6 %combine_project.3 = (bf16[48,512]{1,0:T(8,128)(2,1)S(1)}, bf16[48,1024]{1,0:T(8,128)(2,1)S(1)}, bf16[48,1024]{1,0:T(8,128)(2,1)S(1)}, bf16[48,1024]{1,0:T(8,128)(2,1)S(1)}, bf16[48,1024]{1,0:T(8,128)(2,1)S(1)}) custom-call(s32[1]{0:T(128)} %bitcast.place_ref, bf16[8,48,640]{2,1,0:T(8,128)(2,1)S(1)} %all-to-all-done.1.every_ref, ...), custom_call_target="tpu_custom_call" | custom-call | flops 201326592 | bytes 4194304 | tf_op jit(solution)/shard_map/combine_project/pallas_call | solution.py:332
  77.9 0.8 collective-permute-done.7
  78.7 1.6 collective-permute-start.8
  80.3 3.3 %collective-permute-done.8 = bf16[48,1024]{1,0:T(8,128)(2,1)S(1)} collective-permute-done((bf16[48,1024]{1,0:T(8,128)(2,1)S(1)}, bf16[48,1024]{1,0:T(8,128)(2,1)S(1)}, u32[]{:S(2)}, u32[]{:S(2)}) %collective-permute-start.8) | collective-permute-done | bytes 98336 | tf_op jit(solution)/shard_map/ppermute | solution.py:521
  83.7 0.9 collective-permute-start.13
  84.6 2.3 %collective-permute-start.11 = (bf16[48,1024]{1,0:T(8,128)(2,1)S(1)}, bf16[48,1024]{1,0:T(8,128)(2,1)S(1)}, u32[]{:S(2)}, u32[]{:S(2)}) collective-permute-start(bf16[48,1024]{1,0:T(8,128)(2,1)S(1)} %add_convert_fusion.4.refs_0_), channel_id=1, source_target_pairs={{0,24},{4,28},{8,16},{12,20},{16,8},{20,12},{24,0},{28,4},{1,25},{... | collective-permute-start | bytes 294920 | tf_op jit(solution)/shard_map/ppermute | solution.py:521
  87.3 1.5 collective-permute-start.12
  88.7 4.7 %collective-permute-done.13.refs_2_ = bf16[48,1024]{1,0:T(8,128)(2,1)S(1)} collective-permute-done((bf16[48,1024]{1,0:T(8,128)(2,1)S(1)}, bf16[48,1024]{1,0:T(8,128)(2,1)S(1)}, u32[]{:S(2)}, u32[]{:S(2)}) %collective-permute-start.13) | collective-permute-done | bytes 98336 | tf_op jit(solution)/shard_map/ppermute | solution.py:521
  94.0 4.0 %collective-permute-done.14.refs_3_ = bf16[48,1024]{1,0:T(8,128)(2,1)S(1)} collective-permute-done((bf16[48,1024]{1,0:T(8,128)(2,1)S(1)}, bf16[48,1024]{1,0:T(8,128)(2,1)S(1)}, u32[]{:S(2)}, u32[]{:S(2)}) %collective-permute-start.14) | collective-permute-done | bytes 98336 | tf_op jit(solution)/shard_map/ppermute | solution.py:521
  98.0 4.0 %gate_up.2 = (bf16[96,3712]{1,0:T(8,128)(2,1)S(1)}, bf16[48,3712]{1,0:T(8,128)(2,1)S(1)}, bf16[48,3712]{1,0:T(8,128)(2,1)S(1)}) custom-call(s32[1]{0:T(128)} %bitcast.3.spot_ref, f32[1,1024]{1,0:T(1,128)S(1)} %bitcast.5, bf16[1024,1792]{1,0:T(8,128)(2,1)} %gate_ref.3, bf16[1024,1792]{1,0:T(8,128)(2,1)} %up_ref.3, ...), custom_call_target="tpu_custom_call" | custom-call | flops 1409286144 | bytes 7340032 | tf_op jit(solution)/shard_map/gate_up/pallas_call | solution.py:412
  102.6 1.2 collective-permute-done.15.low_ref
  104.6 1.6 collective-permute-start.19
  106.6 1.6 collective-permute-start.17
  108.2 3.6 %collective-permute-done.18.refs_3_ = bf16[48,1024]{1,0:T(8,128)(2,1)S(1)} collective-permute-done((bf16[48,1024]{1,0:T(8,128)(2,1)S(1)}, bf16[48,1024]{1,0:T(8,128)(2,1)S(1)}, u32[]{:S(2)}, u32[]{:S(2)}) %collective-permute-start.18) | collective-permute-done | bytes 98336 | tf_op jit(solution)/shard_map/ppermute | solution.py:521
  111.8 1.1 collective-permute-done.17.refs_1_
  112.8 4.0 %gate_up.3 = (bf16[96,3712]{1,0:T(8,128)(2,1)S(1)}, bf16[48,3712]{1,0:T(8,128)(2,1)S(1)}, bf16[48,3712]{1,0:T(8,128)(2,1)S(1)}) custom-call(s32[1]{0:T(128)} %bitcast.3.spot_ref, f32[1,1024]{1,0:T(1,128)S(1)} %bitcast.6, bf16[1024,1792]{1,0:T(8,128)(2,1)} %gate_ref.3, bf16[1024,1792]{1,0:T(8,128)(2,1)} %up_ref.3, ...), custom_call_target="tpu_custom_call" | custom-call | flops 1409286144 | bytes 7340032 | tf_op jit(solution)/shard_map/gate_up/pallas_call | solution.py:412
  118.2 4.4 %collective-permute-done.20.refs_1_ = bf16[48,1792]{1,0:T(8,128)(2,1)S(1)} collective-permute-done((bf16[48,1792]{1,0:T(8,128)(2,1)S(1)}, bf16[48,1792]{1,0:T(8,128)(2,1)S(1)}, u32[]{:S(2)}, u32[]{:S(2)}) %collective-permute-start.20) | collective-permute-done | bytes 172064 | tf_op jit(solution)/shard_map/ppermute | solution.py:521
  123.6 0.7 collective-permute-done.21.refs_2_
  124.3 3.0 %down.2 = (bf16[48,1024]{1,0:T(8,128)(2,1)S(1)}, bf16[48,1024]{1,0:T(8,128)(2,1)S(1)}, bf16[48,1024]{1,0:T(8,128)(2,1)S(1)}, bf16[48,1024]{1,0:T(8,128)(2,1)S(1)}) custom-call(s32[1]{0:T(128)} %bitcast.3.spot_ref, bf16[1792,1024]{1,0:T(8,128)(2,1)} %weight_ref.7, bf16[48,1792]{1,0:T(8,128)(2,1)S(1)} %gated.2.refs_0_, ...), custom_call_target="tpu_custom_call" | custom-call | flops 704643072 | bytes 3670016 | tf_op jit(solution)/shard_map/down/pallas_call | solution.py:504
  127.3 6.5 %collective-permute-done.27.got_ref = bf16[48,3712]{1,0:T(8,128)(2,1)S(1)} collective-permute-done((bf16[48,3712]{1,0:T(8,128)(2,1)S(1)}, bf16[48,3712]{1,0:T(8,128)(2,1)S(1)}, u32[]{:S(2)}, u32[]{:S(2)}) %collective-permute-start.27) | collective-permute-done | bytes 356384 | tf_op jit(solution)/shard_map/ppermute | solution.py:521
  135.2 1.4 collective-permute-start.24
  136.6 3.4 %collective-permute-done.28.refs_1_ = bf16[48,1792]{1,0:T(8,128)(2,1)S(1)} collective-permute-done((bf16[48,1792]{1,0:T(8,128)(2,1)S(1)}, bf16[48,1792]{1,0:T(8,128)(2,1)S(1)}, u32[]{:S(2)}, u32[]{:S(2)}) %collective-permute-start.28) | collective-permute-done | bytes 172064 | tf_op jit(solution)/shard_map/ppermute | solution.py:521
  140.8 6.5 %collective-permute-done.23 = bf16[48,1024]{1,0:T(8,128)(2,1)S(1)} collective-permute-done((bf16[48,1024]{1,0:T(8,128)(2,1)S(1)}, bf16[48,1024]{1,0:T(8,128)(2,1)S(1)}, u32[]{:S(2)}, u32[]{:S(2)}) %collective-permute-start.23) | collective-permute-done | bytes 98336 | tf_op jit(solution)/shard_map/ppermute | solution.py:521
  147.3 3.0 %down.3 = (bf16[48,1024]{1,0:T(8,128)(2,1)S(1)}, bf16[48,1024]{1,0:T(8,128)(2,1)S(1)}, bf16[48,1024]{1,0:T(8,128)(2,1)S(1)}, bf16[48,1024]{1,0:T(8,128)(2,1)S(1)}) custom-call(s32[1]{0:T(128)} %bitcast.3.spot_ref, bf16[1792,1024]{1,0:T(8,128)(2,1)} %weight_ref.7, bf16[48,1792]{1,0:T(8,128)(2,1)S(1)} %gated.3.refs_0_, ...), custom_call_target="tpu_custom_call" | custom-call | flops 704643072 | bytes 3670016 | tf_op jit(solution)/shard_map/down/pallas_call | solution.py:504
  150.3 1.1 collective-permute-start.30
  151.4 1.0 collective-permute-start.32
  152.4 3.6 %collective-permute-done.30 = bf16[48,1024]{1,0:T(8,128)(2,1)S(1)} collective-permute-done((bf16[48,1024]{1,0:T(8,128)(2,1)S(1)}, bf16[48,1024]{1,0:T(8,128)(2,1)S(1)}, u32[]{:S(2)}, u32[]{:S(2)}) %collective-permute-start.30) | collective-permute-done | bytes 98336 | tf_op jit(solution)/shard_map/ppermute | solution.py:521
  156.1 2.5 %collective-permute-start.31 = (bf16[48,1024]{1,0:T(8,128)(2,1)S(1)}, bf16[48,1024]{1,0:T(8,128)(2,1)S(1)}, u32[]{:S(2)}, u32[]{:S(2)}) collective-permute-start(bf16[48,1024]{1,0:T(8,128)(2,1)S(1)} %add_convert_fusion.2), channel_id=1, source_target_pairs={{0,24},{4,28},{8,16},{12,20},{16,8},{20,12},{24,0},{28,4},{1,25},{... | collective-permute-start | bytes 294920 | tf_op jit(solution)/shard_map/ppermute | solution.py:521
  158.7 0.6 pad_maximum_fusion.2
  159.3 3.3 %collective-permute-done.31 = bf16[48,1024]{1,0:T(8,128)(2,1)S(1)} collective-permute-done((bf16[48,1024]{1,0:T(8,128)(2,1)S(1)}, bf16[48,1024]{1,0:T(8,128)(2,1)S(1)}, u32[]{:S(2)}, u32[]{:S(2)}) %collective-permute-start.31) | collective-permute-done | bytes 98336 | tf_op jit(solution)/shard_map/ppermute | solution.py:521
  162.6 1.0 collective-permute-done.33
  163.6 0.7 add_convert_fusion
  (59 shorter events, 9.7 us)
Async XLA Ops:
  0.6 10.4 %collective-permute-start.5 = (bf16[48,1024]{1,0:T(8,128)(2,1)}, bf16[48,1024]{1,0:T(8,128)(2,1)S(1)}, u32[]{:S(2)}, u32[]{:S(2)}) collective-permute-start(bf16[48,1024]{1,0:T(8,128)(2,1)} %refs_0_.5), channel_id=1, source_target_pairs={{0,24},{4,28},{8,16},{12,20},{16,8},{20,12},{24,0},{28,4},{1,25},{... | collective-permute-start | bytes 294920 | tf_op jit(solution)/shard_map/ppermute | solution.py:521
  5.7 8.5 %collective-permute-start.3 = (bf16[48,1024]{1,0:T(8,128)(2,1)}, bf16[48,1024]{1,0:T(8,128)(2,1)S(1)}, u32[]{:S(2)}, u32[]{:S(2)}) collective-permute-start(bf16[48,1024]{1,0:T(8,128)(2,1)} %refs_0_.5), channel_id=1, source_target_pairs={{0,16},{4,20},{8,24},{12,28},{16,0},{20,4},{24,8},{28,12},{1,17},{... | collective-permute-start | bytes 294920 | tf_op jit(solution)/shard_map/ppermute | solution.py:521
  5.8 10.0 %collective-permute-start.1 = (bf16[48,1024]{1,0:T(8,128)(2,1)}, bf16[48,1024]{1,0:T(8,128)(2,1)S(1)}, u32[]{:S(2)}, u32[]{:S(2)}) collective-permute-start(bf16[48,1024]{1,0:T(8,128)(2,1)} %refs_0_.5), channel_id=1, source_target_pairs={{0,8},{4,12},{8,0},{12,4},{16,24},{20,28},{24,16},{28,20},{1,9},{5... | collective-permute-start | bytes 294920 | tf_op jit(solution)/shard_map/ppermute | solution.py:521
  6.4 9.9 %collective-permute-start = (bf16[48,1024]{1,0:T(8,128)(2,1)}, bf16[48,1024]{1,0:T(8,128)(2,1)S(1)}, u32[]{:S(2)}, u32[]{:S(2)}) collective-permute-start(bf16[48,1024]{1,0:T(8,128)(2,1)} %refs_0_.5), channel_id=1, source_target_pairs={{0,4},{4,0},{8,12},{12,8},{16,20},{20,16},{24,28},{28,24},{1,5},{5... | collective-permute-start | bytes 294920 | tf_op jit(solution)/shard_map/ppermute | solution.py:521
  11.1 5.2 %collective-permute-start.6 = (bf16[48,1024]{1,0:T(8,128)(2,1)S(1)}, bf16[48,1024]{1,0:T(8,128)(2,1)S(1)}, u32[]{:S(2)}, u32[]{:S(2)}) collective-permute-start(bf16[48,1024]{1,0:T(8,128)(2,1)S(1)} %collective-permute-done.5.refs_6_), channel_id=1, source_target_pairs={{0,4},{4,0},{8,12},{12,8},{16,20},{20,16},{24,28},{28,24},{1,5},{5... | collective-permute-start | bytes 294920 | tf_op jit(solution)/shard_map/ppermute | solution.py:521
  14.2 5.1 %collective-permute-start.4 = (bf16[48,1024]{1,0:T(8,128)(2,1)S(1)}, bf16[48,1024]{1,0:T(8,128)(2,1)S(1)}, u32[]{:S(2)}, u32[]{:S(2)}) collective-permute-start(bf16[48,1024]{1,0:T(8,128)(2,1)S(1)} %collective-permute-done.3.refs_4_), channel_id=1, source_target_pairs={{0,4},{4,0},{8,12},{12,8},{16,20},{20,16},{24,28},{28,24},{1,5},{5... | collective-permute-start | bytes 294920 | tf_op jit(solution)/shard_map/ppermute | solution.py:521
  15.7 4.6 %collective-permute-start.2 = (bf16[48,1024]{1,0:T(8,128)(2,1)S(1)}, bf16[48,1024]{1,0:T(8,128)(2,1)S(1)}, u32[]{:S(2)}, u32[]{:S(2)}) collective-permute-start(bf16[48,1024]{1,0:T(8,128)(2,1)S(1)} %collective-permute-done.1.refs_2_), channel_id=1, source_target_pairs={{0,4},{4,0},{8,12},{12,8},{16,20},{20,16},{24,28},{28,24},{1,5},{5... | collective-permute-start | bytes 294920 | tf_op jit(solution)/shard_map/ppermute | solution.py:521
  20.3 0.9 copy-start
  21.2 0.7 copy-start.2
  21.9 19.8 %copy-start.1 = (bf16[48,1024]{1,0:T(8,128)(2,1)S(1)}, bf16[48,1024]{1,0:T(8,128)(2,1)}, u32[]{:S(2)}) copy-start(bf16[48,1024]{1,0:T(8,128)(2,1)} %refs_0_.5) | copy-start | bytes 294916
  21.9 19.8 %copy-start.3 = (s32[3,7]{1,0:T(4,128)S(1)}, s32[3,7]{1,0:T(4,128)}, u32[]{:S(2)}) copy-start(s32[3,7]{1,0:T(4,128)} %own_nodes.1.nodes_ref) | copy-start | bytes 256
  32.8 21.1 %all-to-all-start = ((bf16[8,48,640]{2,1,0:T(8,128)(2,1)}), bf16[8,48,640]{2,1,0:T(8,128)(2,1)S(1)}, u32[]{:S(2)}, u32[]{:S(2)}) async-start(bf16[8,48,640]{2,1,0:T(8,128)(2,1)} %tree_attention.2), calls=%async_computation | async-start | bytes 983040 | tf_op jit(solution)/shard_map/all_to_all | solution.py:591
  53.9 20.9 %all-to-all-start.1 = ((bf16[8,48,640]{2,1,0:T(8,128)(2,1)}), bf16[8,48,640]{2,1,0:T(8,128)(2,1)S(1)}, u32[]{:S(2)}, u32[]{:S(2)}) async-start(bf16[8,48,640]{2,1,0:T(8,128)(2,1)} %tree_attention.3), calls=%async_computation.1 | async-start | bytes 983040 | tf_op jit(solution)/shard_map/all_to_all | solution.py:591
  74.8 8.9 %copy-start.5 = (bf16[48,1024]{1,0:T(8,128)(2,1)S(1)}, bf16[48,1024]{1,0:T(8,128)(2,1)}, u32[]{:S(2)}) copy-start(bf16[48,1024]{1,0:T(8,128)(2,1)} %param.32) | copy-start | bytes 294916
  74.8 23.3 %copy-start.4 = (f32[1024]{0:T(1024)S(1)}, f32[1024]{0:T(1024)}, u32[]{:S(2)}) copy-start(f32[1024]{0:T(1024)} %param.34) | copy-start | bytes 12292
  77.3 1.4 collective-permute-start.7
  77.4 2.9 %collective-permute-start.9 = (bf16[48,1024]{1,0:T(8,128)(2,1)S(1)}, bf16[48,1024]{1,0:T(8,128)(2,1)S(1)}, u32[]{:S(2)}, u32[]{:S(2)}) collective-permute-start(bf16[48,1024]{1,0:T(8,128)(2,1)S(1)} %get-tuple-element.51), channel_id=1, source_target_pairs={{0,1},{1,0},{2,3},{3,2},{4,5},{5,4},{6,7},{7,6},{8,9},{9,8},{10,11... | collective-permute-start | bytes 294920 | tf_op jit(solution)/shard_map/ppermute | solution.py:521
  78.7 4.9 %collective-permute-start.8 = (bf16[48,1024]{1,0:T(8,128)(2,1)S(1)}, bf16[48,1024]{1,0:T(8,128)(2,1)S(1)}, u32[]{:S(2)}, u32[]{:S(2)}) collective-permute-start(bf16[48,1024]{1,0:T(8,128)(2,1)S(1)} %add_convert_fusion.5), channel_id=1, source_target_pairs={{0,2},{1,3},{2,0},{3,1},{4,6},{5,7},{6,4},{7,5},{8,10},{9,11},{10,... | collective-permute-start | bytes 294920 | tf_op jit(solution)/shard_map/ppermute | solution.py:521
  83.7 9.7 %collective-permute-start.13 = (bf16[48,1024]{1,0:T(8,128)(2,1)S(1)}, bf16[48,1024]{1,0:T(8,128)(2,1)S(1)}, u32[]{:S(2)}, u32[]{:S(2)}) collective-permute-start(bf16[48,1024]{1,0:T(8,128)(2,1)S(1)} %add_convert_fusion.4.refs_0_), channel_id=1, source_target_pairs={{0,16},{4,20},{8,24},{12,28},{16,0},{20,4},{24,8},{28,12},{1,17},{... | collective-permute-start | bytes 294920 | tf_op jit(solution)/shard_map/ppermute | solution.py:521
  84.6 9.2 %collective-permute-start.11 = (bf16[48,1024]{1,0:T(8,128)(2,1)S(1)}, bf16[48,1024]{1,0:T(8,128)(2,1)S(1)}, u32[]{:S(2)}, u32[]{:S(2)}) collective-permute-start(bf16[48,1024]{1,0:T(8,128)(2,1)S(1)} %add_convert_fusion.4.refs_0_), channel_id=1, source_target_pairs={{0,24},{4,28},{8,16},{12,20},{16,8},{20,12},{24,0},{28,4},{1,25},{... | collective-permute-start | bytes 294920 | tf_op jit(solution)/shard_map/ppermute | solution.py:521
  87.0 7.0 %collective-permute-start.10 = (bf16[48,1024]{1,0:T(8,128)(2,1)S(1)}, bf16[48,1024]{1,0:T(8,128)(2,1)S(1)}, u32[]{:S(2)}, u32[]{:S(2)}) collective-permute-start(bf16[48,1024]{1,0:T(8,128)(2,1)S(1)} %add_convert_fusion.4.refs_0_), channel_id=1, source_target_pairs={{0,8},{4,12},{8,0},{12,4},{16,24},{20,28},{24,16},{28,20},{1,9},{5... | collective-permute-start | bytes 294920 | tf_op jit(solution)/shard_map/ppermute | solution.py:521
  87.3 6.7 %collective-permute-start.12 = (bf16[48,1024]{1,0:T(8,128)(2,1)S(1)}, bf16[48,1024]{1,0:T(8,128)(2,1)S(1)}, u32[]{:S(2)}, u32[]{:S(2)}) collective-permute-start(bf16[48,1024]{1,0:T(8,128)(2,1)S(1)} %add_convert_fusion.4.refs_0_), channel_id=1, source_target_pairs={{0,4},{4,0},{8,12},{12,8},{16,20},{20,16},{24,28},{28,24},{1,5},{5... | collective-permute-start | bytes 294920 | tf_op jit(solution)/shard_map/ppermute | solution.py:521
  93.4 4.6 %collective-permute-start.14 = (bf16[48,1024]{1,0:T(8,128)(2,1)S(1)}, bf16[48,1024]{1,0:T(8,128)(2,1)S(1)}, u32[]{:S(2)}, u32[]{:S(2)}) collective-permute-start(bf16[48,1024]{1,0:T(8,128)(2,1)S(1)} %collective-permute-done.13.refs_2_), channel_id=1, source_target_pairs={{0,4},{4,0},{8,12},{12,8},{16,20},{20,16},{24,28},{28,24},{1,5},{5... | collective-permute-start | bytes 294920 | tf_op jit(solution)/shard_map/ppermute | solution.py:521
  102.0 1.7 %collective-permute-start.15 = (bf16[48,3712]{1,0:T(8,128)(2,1)S(1)}, bf16[48,3712]{1,0:T(8,128)(2,1)S(1)}, u32[]{:S(2)}, u32[]{:S(2)}) collective-permute-start(bf16[48,3712]{1,0:T(8,128)(2,1)S(1)} %get-tuple-element.54), channel_id=1, source_target_pairs={{0,1},{1,0},{2,3},{3,2},{4,5},{5,4},{6,7},{7,6},{8,9},{9,8},{10,11... | collective-permute-start | bytes 1069064 | tf_op jit(solution)/shard_map/ppermute | solution.py:521
  102.1 2.2 %collective-permute-start.16 = (bf16[48,3712]{1,0:T(8,128)(2,1)S(1)}, bf16[48,3712]{1,0:T(8,128)(2,1)S(1)}, u32[]{:S(2)}, u32[]{:S(2)}) collective-permute-start(bf16[48,3712]{1,0:T(8,128)(2,1)S(1)} %get-tuple-element.55), channel_id=1, source_target_pairs={{0,1},{1,0},{2,3},{3,2},{4,5},{5,4},{6,7},{7,6},{8,9},{9,8},{10,11... | collective-permute-start | bytes 1069064 | tf_op jit(solution)/shard_map/ppermute | solution.py:521
  104.6 12.2 %collective-permute-start.19 = (bf16[48,3712]{1,0:T(8,128)(2,1)S(1)}, bf16[48,3712]{1,0:T(8,128)(2,1)S(1)}, u32[]{:S(2)}, u32[]{:S(2)}) collective-permute-start(bf16[48,3712]{1,0:T(8,128)(2,1)S(1)} %get-tuple-element.57), channel_id=1, source_target_pairs={{0,2},{1,3},{2,0},{3,1},{4,6},{5,7},{6,4},{7,5},{8,10},{9,11},{10,... | collective-permute-start | bytes 1069064 | tf_op jit(solution)/shard_map/ppermute | solution.py:521
  106.2 5.6 %collective-permute-start.18 = (bf16[48,1024]{1,0:T(8,128)(2,1)S(1)}, bf16[48,1024]{1,0:T(8,128)(2,1)S(1)}, u32[]{:S(2)}, u32[]{:S(2)}) collective-permute-start(bf16[48,1024]{1,0:T(8,128)(2,1)S(1)} %collective-permute-done.11.refs_2_), channel_id=1, source_target_pairs={{0,4},{4,0},{8,12},{12,8},{16,20},{20,16},{24,28},{28,24},{1,5},{5... | collective-permute-start | bytes 294920 | tf_op jit(solution)/shard_map/ppermute | solution.py:521
  106.6 6.2 %collective-permute-start.17 = (bf16[48,1024]{1,0:T(8,128)(2,1)S(1)}, bf16[48,1024]{1,0:T(8,128)(2,1)S(1)}, u32[]{:S(2)}, u32[]{:S(2)}) collective-permute-start(bf16[48,1024]{1,0:T(8,128)(2,1)S(1)} %collective-permute-done.10.refs_0_), channel_id=1, source_target_pairs={{0,4},{4,0},{8,12},{12,8},{16,20},{20,16},{24,28},{28,24},{1,5},{5... | collective-permute-start | bytes 294920 | tf_op jit(solution)/shard_map/ppermute | solution.py:521
  117.1 5.5 %collective-permute-start.20 = (bf16[48,1792]{1,0:T(8,128)(2,1)S(1)}, bf16[48,1792]{1,0:T(8,128)(2,1)S(1)}, u32[]{:S(2)}, u32[]{:S(2)}) collective-permute-start(bf16[48,1792]{1,0:T(8,128)(2,1)S(1)} %gated.2.refs_0_), channel_id=1, source_target_pairs={{0,2},{1,3},{2,0},{3,1},{4,6},{5,7},{6,4},{7,5},{8,10},{9,11},{10,... | collective-permute-start | bytes 516104 | tf_op jit(solution)/shard_map/ppermute | solution.py:521
  117.7 5.0 %collective-permute-start.25 = (bf16[48,3712]{1,0:T(8,128)(2,1)S(1)}, bf16[48,3712]{1,0:T(8,128)(2,1)S(1)}, u32[]{:S(2)}, u32[]{:S(2)}) collective-permute-start(bf16[48,3712]{1,0:T(8,128)(2,1)S(1)} %get-tuple-element.66), channel_id=1, source_target_pairs={{0,1},{1,0},{2,3},{3,2},{4,5},{5,4},{6,7},{7,6},{8,9},{9,8},{10,11... | collective-permute-start | bytes 1069064 | tf_op jit(solution)/shard_map/ppermute | solution.py:521
  117.7 5.0 %collective-permute-start.26 = (bf16[48,3712]{1,0:T(8,128)(2,1)S(1)}, bf16[48,3712]{1,0:T(8,128)(2,1)S(1)}, u32[]{:S(2)}, u32[]{:S(2)}) collective-permute-start(bf16[48,3712]{1,0:T(8,128)(2,1)S(1)} %get-tuple-element.67), channel_id=1, source_target_pairs={{0,1},{1,0},{2,3},{3,2},{4,5},{5,4},{6,7},{7,6},{8,9},{9,8},{10,11... | collective-permute-start | bytes 1069064 | tf_op jit(solution)/shard_map/ppermute | solution.py:521
  122.6 1.7 %collective-permute-start.21 = (bf16[96,1792]{1,0:T(8,128)(2,1)S(1)}, bf16[96,1792]{1,0:T(8,128)(2,1)S(1)}, u32[]{:S(2)}, u32[]{:S(2)}) collective-permute-start(bf16[96,1792]{1,0:T(8,128)(2,1)S(1)} %pad_maximum_fusion), channel_id=1, source_target_pairs={{0,1},{1,0},{2,3},{3,2},{4,5},{5,4},{6,7},{7,6},{8,9},{9,8},{10,11... | collective-permute-start | bytes 1032200 | tf_op jit(solution)/shard_map/ppermute | solution.py:521
  123.0 10.8 %collective-permute-start.27 = (bf16[48,3712]{1,0:T(8,128)(2,1)S(1)}, bf16[48,3712]{1,0:T(8,128)(2,1)S(1)}, u32[]{:S(2)}, u32[]{:S(2)}) collective-permute-start(bf16[48,3712]{1,0:T(8,128)(2,1)S(1)} %get-tuple-element.70), channel_id=1, source_target_pairs={{0,2},{1,3},{2,0},{3,1},{4,6},{5,7},{6,4},{7,5},{8,10},{9,11},{10,... | collective-permute-start | bytes 1069064 | tf_op jit(solution)/shard_map/ppermute | solution.py:521
  134.0 6.0 %collective-permute-start.28 = (bf16[48,1792]{1,0:T(8,128)(2,1)S(1)}, bf16[48,1792]{1,0:T(8,128)(2,1)S(1)}, u32[]{:S(2)}, u32[]{:S(2)}) collective-permute-start(bf16[48,1792]{1,0:T(8,128)(2,1)S(1)} %gated.3.refs_0_), channel_id=1, source_target_pairs={{0,2},{1,3},{2,0},{3,1},{4,6},{5,7},{6,4},{7,5},{8,10},{9,11},{10,... | collective-permute-start | bytes 516104 | tf_op jit(solution)/shard_map/ppermute | solution.py:521
  134.6 5.6 %collective-permute-start.22 = (bf16[48,1024]{1,0:T(8,128)(2,1)S(1)}, bf16[48,1024]{1,0:T(8,128)(2,1)S(1)}, u32[]{:S(2)}, u32[]{:S(2)}) collective-permute-start(bf16[48,1024]{1,0:T(8,128)(2,1)S(1)} %get-tuple-element.62), channel_id=1, source_target_pairs={{0,4},{4,0},{8,12},{12,8},{16,20},{20,16},{24,28},{28,24},{1,5},{5... | collective-permute-start | bytes 294920 | tf_op jit(solution)/shard_map/ppermute | solution.py:521
  135.2 5.6 %collective-permute-start.24 = (bf16[48,1024]{1,0:T(8,128)(2,1)S(1)}, bf16[48,1024]{1,0:T(8,128)(2,1)S(1)}, u32[]{:S(2)}, u32[]{:S(2)}) collective-permute-start(bf16[48,1024]{1,0:T(8,128)(2,1)S(1)} %get-tuple-element.64), channel_id=1, source_target_pairs={{0,4},{4,0},{8,12},{12,8},{16,20},{20,16},{24,28},{28,24},{1,5},{5... | collective-permute-start | bytes 294920 | tf_op jit(solution)/shard_map/ppermute | solution.py:521
  140.1 7.2 %collective-permute-start.29 = (bf16[96,1792]{1,0:T(8,128)(2,1)S(1)}, bf16[96,1792]{1,0:T(8,128)(2,1)S(1)}, u32[]{:S(2)}, u32[]{:S(2)}) collective-permute-start(bf16[96,1792]{1,0:T(8,128)(2,1)S(1)} %pad_maximum_fusion.1), channel_id=1, source_target_pairs={{0,1},{1,0},{2,3},{3,2},{4,5},{5,4},{6,7},{7,6},{8,9},{9,8},{10,11... | collective-permute-start | bytes 1032200 | tf_op jit(solution)/shard_map/ppermute | solution.py:521
  140.2 7.1 %collective-permute-start.23 = (bf16[48,1024]{1,0:T(8,128)(2,1)S(1)}, bf16[48,1024]{1,0:T(8,128)(2,1)S(1)}, u32[]{:S(2)}, u32[]{:S(2)}) collective-permute-start(bf16[48,1024]{1,0:T(8,128)(2,1)S(1)} %add_convert_fusion.3), channel_id=1, source_target_pairs={{0,16},{4,20},{8,24},{12,28},{16,0},{20,4},{24,8},{28,12},{1,17},{... | collective-permute-start | bytes 294920 | tf_op jit(solution)/shard_map/ppermute | solution.py:521
  150.3 5.7 %collective-permute-start.30 = (bf16[48,1024]{1,0:T(8,128)(2,1)S(1)}, bf16[48,1024]{1,0:T(8,128)(2,1)S(1)}, u32[]{:S(2)}, u32[]{:S(2)}) collective-permute-start(bf16[48,1024]{1,0:T(8,128)(2,1)S(1)} %get-tuple-element.73), channel_id=1, source_target_pairs={{0,4},{4,0},{8,12},{12,8},{16,20},{20,16},{24,28},{28,24},{1,5},{5... | collective-permute-start | bytes 294920 | tf_op jit(solution)/shard_map/ppermute | solution.py:521
  151.4 7.1 %collective-permute-start.32 = (bf16[48,1024]{1,0:T(8,128)(2,1)S(1)}, bf16[48,1024]{1,0:T(8,128)(2,1)S(1)}, u32[]{:S(2)}, u32[]{:S(2)}) collective-permute-start(bf16[48,1024]{1,0:T(8,128)(2,1)S(1)} %get-tuple-element.75), channel_id=1, source_target_pairs={{0,4},{4,0},{8,12},{12,8},{16,20},{20,16},{24,28},{28,24},{1,5},{5... | collective-permute-start | bytes 294920 | tf_op jit(solution)/shard_map/ppermute | solution.py:521
  156.1 6.5 %collective-permute-start.31 = (bf16[48,1024]{1,0:T(8,128)(2,1)S(1)}, bf16[48,1024]{1,0:T(8,128)(2,1)S(1)}, u32[]{:S(2)}, u32[]{:S(2)}) collective-permute-start(bf16[48,1024]{1,0:T(8,128)(2,1)S(1)} %add_convert_fusion.2), channel_id=1, source_target_pairs={{0,24},{4,28},{8,16},{12,20},{16,8},{20,12},{24,0},{28,4},{1,25},{... | collective-permute-start | bytes 294920 | tf_op jit(solution)/shard_map/ppermute | solution.py:521
  158.6 5.0 %collective-permute-start.33 = (bf16[48,1024]{1,0:T(8,128)(2,1)S(1)}, bf16[48,1024]{1,0:T(8,128)(2,1)S(1)}, u32[]{:S(2)}, u32[]{:S(2)}) collective-permute-start(bf16[48,1024]{1,0:T(8,128)(2,1)S(1)} %add_convert_fusion.1), channel_id=1, source_target_pairs={{0,8},{4,12},{8,0},{12,4},{16,24},{20,28},{24,16},{28,20},{1,9},{5... | collective-permute-start | bytes 294920 | tf_op jit(solution)/shard_map/ppermute | solution.py:521

commit v5 on v4

--- a/solution.py
+++ b/solution.py
@@ -19,6 +19,7 @@
 ALIGN = 16
 BLOCK = 512
 VMEM_BYTES = 50 << 20
+SMALL_BYTES = 24 << 20
 
 
 def cost(flops, moved, exps):
@@ -106,28 +107,42 @@
         out_ref, all_rows, run_out, run_lse, acc, peak, total, *rest = refs[part_total + 3 :]
         kept_refs, sems = rest[:3], rest[3]
         columns = pl.ds(kv_head * 2 * HEAD, 2 * HEAD)
-
-        def copies(act):
-            node, flag = 0, 0
-            for (slot_total, span, _), cache_ref, kept_ref in zip(levels, cache_refs, kept_refs):
-                block = min(BLOCK, span)
-                for member in range(slot_total):
-                    for index in range(span // block):
-                        here = pl.ds(index * block, block)
-                        copy = pltpu.make_async_copy(
-                            cache_ref.at[member, here, columns],
-                            kept_ref.at[member, here, :],
-                            sems.at[flag + index],
-                        )
-
-                        @pl.when(index * block < nodes_ref[2, node])
-                        def _(copy=copy):
-                            act(copy)
-
-                    node += 1
-                    flag += span // block
-
-        copies(lambda copy: copy.start())
+        starts = [0, levels[0][0], levels[0][0] + levels[1][0]]
+        lengths, flag_starts, flag = [], [], 0
+        for start, (slot_total, span, _) in zip(starts, levels):
+            lengths.append([nodes_ref[2, start + member] for member in range(slot_total)])
+            flag_starts.append(flag)
+            flag += slot_total * (span // min(BLOCK, span))
+
+        def block_copy(level, member, index):
+            span = levels[level][1]
+            block = min(BLOCK, span)
+            at = index * block
+            here = pl.ds(at if isinstance(at, int) else pl.multiple_of(at, block), block)
+            return pltpu.make_async_copy(
+                cache_refs[level].at[member, here, columns],
+                kept_refs[level].at[member, here, :],
+                sems.at[flag_starts[level] + member * (span // block) + index],
+            )
+
+        steps = []
+        for level, (slot_total, span, _) in enumerate(levels):
+            block = min(BLOCK, span)
+            pair = min(2 * block, span)
+            longest = lengths[level][0]
+            shortest = lengths[level][0]
+            for length in lengths[level][1:]:
+                longest, shortest = jnp.maximum(longest, length), jnp.minimum(shortest, length)
+            whole, most = lax.div(shortest, pair), lax.div(longest + pair - 1, pair)
+            steps.append((block, pair, whole, most))
+            for index in range(span // pair):
+
+                @pl.when(index < most)
+                def _(level=level, index=index, ratio=pair // block, slot_total=slot_total):
+                    for piece in range(ratio):
+                        for member in range(slot_total):
+                            block_copy(level, member, index * ratio + piece).start()
+
         me = owner_ref[0]
         for part in range(part_total):
             row = pl.multiple_of((me ^ part) * own_rows, ALIGN)
@@ -136,78 +151,98 @@
             ]
         run_out[...] = jnp.zeros_like(run_out)
         run_lse[...] = jnp.full_like(run_lse, LOWEST)
-        node, flag = 0, 0
-        for (slot_total, span, rows), cache_ref, kept_ref in zip(levels, cache_refs, kept_refs):
+        offsets = [h * HEAD for h in range(group_size)]
+        for level, (slot_total, span, rows) in enumerate(levels):
+            block, pair, whole, most = steps[level]
             lanes = rows * group_size
-            block = min(BLOCK, span)
+            every = lanes * slot_total
+            windows, grouped = [], []
             for member in range(slot_total):
-                low, high, length = nodes_ref[0, node], nodes_ref[1, node], nodes_ref[2, node]
-                node += 1
+                low = nodes_ref[0, starts[level] + member]
                 window = jnp.minimum(low - lax.rem(low, ALIGN), total_rows - rows)
                 window = pl.multiple_of(window, ALIGN)
-                offsets = [h * HEAD for h in range(group_size)]
-                first = flag
-                flag += span // block
-                grouped = jnp.concatenate(
-                    [all_rows[pl.ds(window, rows), c : c + HEAD] for c in offsets], axis=0
+                windows.append(window)
+                grouped.append(
+                    jnp.concatenate(
+                        [all_rows[pl.ds(window, rows), c : c + HEAD] for c in offsets], axis=0
+                    )
                 )
-                acc[:, :lanes] = jnp.zeros((HEAD, lanes), jnp.float32)
-                peak[:, :lanes] = jnp.full((1, lanes), LOWEST, jnp.float32)
-                total[:, :lanes] = jnp.zeros((1, lanes), jnp.float32)
-
-                def visit(index, carry, masked):
-                    at = pl.multiple_of(index * block, block)
-                    pltpu.make_async_copy(
-                        cache_ref.at[member, pl.ds(at, block), columns],
-                        kept_ref.at[member, pl.ds(at, block), :],
-                        sems.at[first + index],
-                    ).wait()
-                    keys = kept_ref[member, pl.ds(at, block), :HEAD]
-                    values = kept_ref[member, pl.ds(at, block), HEAD:]
-                    scores = lax.dot_general(
-                        keys,
-                        grouped,
-                        (((1,), (1,)), ((), ())),
-                        preferred_element_type=jnp.float32,
-                    )
+            lane_of = lax.broadcasted_iota(jnp.int32, (1, every), 1)
+            limits = jnp.full((1, every), lengths[level][0], jnp.int32)
+            for member in range(1, slot_total):
+                limits = jnp.where(lane_of >= member * lanes, lengths[level][member], limits)
+            acc[:, :every] = jnp.zeros((HEAD, every), jnp.float32)
+            peak[:, :every] = jnp.full((1, every), LOWEST, jnp.float32)
+            total[:, :every] = jnp.zeros((1, every), jnp.float32)
+
+            def visit(index, carry, masked):
+                ratio = pair // block
+                for piece in range(ratio):
+                    for member in range(slot_total):
+                        block_copy(level, member, index * ratio + piece).wait()
+                scores = []
+                for piece in range(ratio):
+                    at = pl.multiple_of((index * ratio + piece) * block, block)
+                    found = [
+                        lax.dot_general(
+                            kept_refs[level][member, pl.ds(at, block), :HEAD],
+                            grouped[member],
+                            (((1,), (1,)), ((), ())),
+                            preferred_element_type=jnp.float32,
+                        )
+                        for member in range(slot_total)
+                    ]
+                    found = found[0] if slot_total == 1 else jnp.concatenate(found, axis=1)
                     if masked:
-                        position = at + lax.broadcasted_iota(jnp.int32, (block, lanes), 0)
-                        scores = jnp.where(position < length, scores, LOWEST)
-                    old_peak = peak[:, :lanes]
-                    new_peak = jnp.maximum(old_peak, jnp.max(scores, axis=0, keepdims=True))
-                    weights = jnp.exp((scores - new_peak) * score_scale)
+                        position = lax.broadcasted_iota(jnp.int32, (block, every), 0)
+                        found = jnp.where(position < limits - at, found, LOWEST)
+                    scores.append((at, found))
+                for at, found in scores:
+                    old_peak = peak[:, :every]
+                    new_peak = jnp.maximum(old_peak, jnp.max(found, axis=0, keepdims=True))
+                    weights = jnp.exp((found - new_peak) * score_scale)
+                    if masked:
+                        position = lax.broadcasted_iota(jnp.int32, (block, every), 0)
+                        weights = jnp.where(position < limits - at, weights, 0.0)
                     fade = jnp.exp((old_peak - new_peak) * score_scale)
-                    peak[:, :lanes] = new_peak
-                    total[:, :lanes] = total[:, :lanes] * fade + jnp.sum(
+                    peak[:, :every] = new_peak
+                    total[:, :every] = total[:, :every] * fade + jnp.sum(
                         weights, axis=0, keepdims=True
                     )
-                    acc[:, :lanes] = acc[:, :lanes] * fade + lax.dot_general(
-                        values,
-                        weights.astype(jnp.bfloat16),
-                        (((0,), (0,)), ((), ())),
-                        preferred_element_type=jnp.float32,
-                    )
-                    return carry
-
-                whole = lax.div(length, block)
-                lax.fori_loop(0, whole, lambda i, c: visit(i, c, False), 0)
-
-                @pl.when(whole * block < length)
-                def _():
-                    visit(whole, 0, True)
-
-                weight_sum = total[:, :lanes]
-                part_out = (acc[:, :lanes] / weight_sum).T
-                part_lse = jnp.broadcast_to(
-                    peak[:, :lanes] * score_scale + jnp.log(weight_sum), (HEAD, lanes)
-                ).T
+                    rounded = weights.astype(jnp.bfloat16)
+                    for member in range(slot_total):
+                        here = slice(member * lanes, (member + 1) * lanes)
+                        acc[:, here] = acc[:, here] * fade[:, here] + lax.dot_general(
+                            kept_refs[level][member, pl.ds(at, block), HEAD:],
+                            rounded[:, here],
+                            (((0,), (0,)), ((), ())),
+                            preferred_element_type=jnp.float32,
+                        )
+                return carry
+
+            lax.fori_loop(0, whole, lambda i, c: visit(i, c, False), 0)
+            lax.fori_loop(whole, most, lambda i, c: visit(i, c, True), 0)
+
+            weight_sum = total[:, :every]
+            part_out = (acc[:, :every] / weight_sum).T
+            part_lse = jnp.broadcast_to(
+                peak[:, :every] * score_scale + jnp.log(weight_sum), (HEAD, every)
+            ).T
+            for member, window in enumerate(windows):
+                low = nodes_ref[0, starts[level] + member]
+                high = nodes_ref[1, starts[level] + member]
                 position = window + lax.broadcasted_iota(jnp.int32, (rows, HEAD), 0)
                 live = (position >= low) & (position < high)
                 for h, c in enumerate(offsets):
                     here = (pl.ds(window, rows), slice(c, c + HEAD))
                     old_lse, old_out = run_lse[here], run_out[here]
-                    add_lse = part_lse[h * rows : (h + 1) * rows]
-                    add_out = part_out[h * rows : (h + 1) * rows]
+                    at = member * lanes + h * rows
+                    add_lse = part_lse[at : at + rows]
+                    add_out = part_out[at : at + rows]
+                    if level == 0:
+                        run_out[here] = jnp.where(live, add_out, old_out)
+                        run_lse[here] = jnp.where(live, add_lse, old_lse)
+                        continue
                     best = jnp.maximum(old_lse, add_lse)
                     old_share = jnp.exp(old_lse - best)
                     add_share = jnp.exp(add_lse - best)
@@ -241,7 +276,7 @@
             out_ref[part, :, width:] = packed.astype(jnp.bfloat16)
 
     block_total = sum(count * (span // min(BLOCK, span)) for count, span, _ in levels)
-    most = max(rows for _, _, rows in levels) * group_size
+    most = max(count * rows for count, _, rows in levels) * group_size
     vmem = pl.BlockSpec(memory_space=pltpu.VMEM)
     smem = pl.BlockSpec(memory_space=pltpu.SMEM)
     return pl.pallas_call(
@@ -452,7 +487,7 @@
         out_shape=[jax.ShapeDtypeStruct((half, keep.shape[1]), jnp.bfloat16)] * 2,
         in_specs=[vmem] * 3,
         out_specs=[vmem, vmem],
-        compiler_params=pltpu.CompilerParams(vmem_limit_bytes=VMEM_BYTES),
+        compiler_params=pltpu.CompilerParams(vmem_limit_bytes=SMALL_BYTES),
         cost_estimate=cost(2 * keep.size, 6 * keep.size, 0),
         name="add_halves",
     )(keep, *got)
@@ -473,7 +508,7 @@
         out_shape=jax.ShapeDtypeStruct((keep.shape[0], units), jnp.bfloat16),
         in_specs=[vmem, vmem],
         out_specs=vmem,
-        compiler_params=pltpu.CompilerParams(vmem_limit_bytes=VMEM_BYTES),
+        compiler_params=pltpu.CompilerParams(vmem_limit_bytes=SMALL_BYTES),
         cost_estimate=cost(4 * keep.size, 5 * keep.size, keep.size // 2),
         name="gated",
     )(keep, got)
@@ -510,7 +545,7 @@
             pltpu.VMEM((rows, units), jnp.bfloat16),
             pltpu.VMEM((rows, features), jnp.float32),
         ],
-        compiler_params=pltpu.CompilerParams(vmem_limit_bytes=VMEM_BYTES),
+        compiler_params=pltpu.CompilerParams(vmem_limit_bytes=SMALL_BYTES),
         cost_estimate=cost(2 * rows * features * units, 2 * features * units, 0),
         name="down",
     )(spot[None], down_weight, *pieces)
@@ -535,17 +570,24 @@
     return parts
 
 
-def scatter_sum(parts, axis_name):
-    wide = jnp.float32
+def pair_sums(parts, axis_name):
     evens = sorted((mask for mask in parts if mask % 2 == 0), reverse=True)
     got = {mask: swap(parts[mask + 1], axis_name, 1) for mask in evens}
+    pairs = {
+        mask: parts[mask].astype(jnp.float32) + got[mask].astype(jnp.float32) for mask in evens
+    }
+    return {mask: pair.astype(jnp.bfloat16) if mask else pair for mask, pair in pairs.items()}
+
+
+def far_sum(pairs, axis_name):
     summed = 0.0
-    for mask in evens:
-        pair = parts[mask].astype(wide) + got[mask].astype(wide)
-        if mask:
-            pair = swap(pair.astype(jnp.bfloat16), axis_name, mask).astype(wide)
-        summed = summed + pair
+    for mask, pair in pairs.items():
+        summed = summed + (swap(pair, axis_name, mask).astype(jnp.float32) if mask else pair)
     return summed
+
+
+def scatter_sum(parts, axis_name):
+    return far_sum(pair_sums(parts, axis_name), axis_name)
 
 
 def shards(
@@ -629,18 +671,20 @@
 
     def finish(pieces, masks):
         outs = down_rows(pieces, down_weight, spot, len(masks), own_rows, mlp_total)
-        return outs, scatter_sum(dict(zip(masks, outs)), "kv")
+        return pair_sums(dict(zip(masks, outs)), "kv")
 
     keep, send = reduce_once(*multiply(first))
     row_parts[second[0]] = after(row_parts[second[0]], send)
     later = multiply(second)
     hidden = gated(after(keep, later[0]), swap(send, "mlp", steps[-1]), units)
     keep, send = reduce_once(*later, hidden)
-    outs, mixed = finish(regather(hidden), first)
-    hidden = gated(after(keep, outs[0]), swap(send, "mlp", steps[-1]), units)
+    pairs = finish(regather(hidden), first)
+    keep = after(keep, [pair for mask, pair in pairs.items() if mask])
+    hidden = gated(keep, swap(send, "mlp", steps[-1]), units)
+    mixed = far_sum(pairs, "kv")
     pieces = regather(hidden)
     pieces[0] = after(pieces[0], mixed)
-    mixed = mixed + finish(pieces, second)[1]
+    mixed = mixed + far_sum(finish(pieces, second), "kv")
     return (jnp.concatenate(attended, axis=1), mixed.astype(jnp.bfloat16))
 
 

time: 165 us -> 157 us (0.952)
  Pallas kernels: 45.1 us -> 39.6 us
    pallas_call x2, Pallas kernels: 6 us -> 1.9 us  [down_rows(): pl.pallas_call(kernel, out_shape=[jax.ShapeDtypeStruct((own_rows, feature...]
    all_to_all x2, waiting for transfers between devices: 10.1 us -> 7.4 us  [shards(): every = lax.all_to_all(parts, 'kv', 0, 0)]
    ppermute x34, waiting for transfers between devices: 56 us -> 58.4 us  [swap(): lax.ppermute(value, axis_name, [(j, j ^ mask) for j in range(axis_total)])]
  transfers between devices with their start and end apart: 36 -> 36, of which waited for: 23 -> 22; matrix products, arithmetic and copies ran while one was open for 1% -> 1% of each run, Pallas kernels for 15% -> 13%
where the time goes in v5:
time: 157 us; the launch traced here: 158 us
  waiting for transfers between devices  65.8 us (42%)
  starting transfers between devices  48.2 us (31%)
  Pallas kernels  39.6 us (25%)
  local copies, waits for them, and re-layouts  1.59 us (1%)
  other arithmetic  1.58 us (1%)
    ppermute x34, waiting for transfers between devices, swap(): lax.ppermute(value, axis_name, [(j, j ^ mask) for j in range(axis_total)])  58.4 us
    ppermute x34, starting transfers between devices, swap(): lax.ppermute(value, axis_name, [(j, j ^ mask) for j in range(axis_total)])  31.1 us
    pallas_call x2, Pallas kernels, tree_attention(): pl.pallas_call(kernel, out_shape=jax.ShapeDtypeStruct((part_total, own_ro...  20.5 us
    all_to_all x2, starting transfers between devices, shards(): every = lax.all_to_all(parts, 'kv', 0, 0)  17.1 us
    pallas_call x2, Pallas kernels, gate_up_rows(): pl.pallas_call(kernel, out_shape=[jax.ShapeDtypeStruct((half, 2 * units +...  7.95 us
    all_to_all x2, waiting for transfers between devices, shards(): every = lax.all_to_all(parts, 'kv', 0, 0)  7.4 us
    pallas_call x2, Pallas kernels, combine_project(): pl.pallas_call(kernel, out_shape=[jax.ShapeDtypeStruct((own_rows, width),...  5.1 us
  transfers between devices with their start and end apart: 36, of which 22 were waited for; matrix products, arithmetic and copies ran while one was open for 1% of the time, Pallas kernels for 13%

profile of v5, /device:TPU:0, one launch (start us, length us, event | category | flops | bytes accessed | tf_op | source)
XLA Modules:
  0.0 157.7 jit_solution(6129887337576406515)
XLA Ops:
  0.6 5.1 %collective-permute-start.5 = (bf16[48,1024]{1,0:T(8,128)(2,1)}, bf16[48,1024]{1,0:T(8,128)(2,1)S(1)}, u32[]{:S(2)}, u32[]{:S(2)}) collective-permute-start(bf16[48,1024]{1,0:T(8,128)(2,1)} %refs_0_.5), channel_id=1, source_target_pairs={{0,24},{4,28},{8,16},{12,20},{16,8},{20,12},{24,0},{28,4},{1,25},{... | collective-permute-start | bytes 294920 | tf_op jit(solution)/shard_map/ppermute | solution.py:556
  6.4 1.6 %collective-permute-start = (bf16[48,1024]{1,0:T(8,128)(2,1)}, bf16[48,1024]{1,0:T(8,128)(2,1)S(1)}, u32[]{:S(2)}, u32[]{:S(2)}) collective-permute-start(bf16[48,1024]{1,0:T(8,128)(2,1)} %refs_0_.5), channel_id=1, source_target_pairs={{0,4},{4,0},{8,12},{12,8},{16,20},{20,16},{24,28},{28,24},{1,5},{5... | collective-permute-start | bytes 294920 | tf_op jit(solution)/shard_map/ppermute | solution.py:556
  8.0 3.0 %own_nodes.1.nodes_ref = s32[3,7]{1,0:T(4,128)} custom-call(s32[1]{0:T(128)} %bitcast.1.owner_ref, s32[3,128]{1,0:T(4,128)} %bitcast.7, s32[32]{0:T(128)} %leaf_up.1, s32[16]{0:T(128)} %mid_up.1, s32[8]{0:T(128)} %refs_0_.3, s32[16]{0:T(128)} %refs_1_.1, s32[32]{0:T(128)} %refs_2_.1, s32[8]{0:T(128)} %refs_3_.1, s32[16]{0:T(128)} %refs_4_.1, s32[32]{0:T(128)} %refs_5_.1), custom_call_target="tpu_custom_call" | custom-call | tf_op jit(solution)/shard_map/own_nodes/pallas_call | solution.py:84
  11.5 2.7 %collective-permute-done.3.refs_4_ = bf16[48,1024]{1,0:T(8,128)(2,1)S(1)} collective-permute-done((bf16[48,1024]{1,0:T(8,128)(2,1)}, bf16[48,1024]{1,0:T(8,128)(2,1)S(1)}, u32[]{:S(2)}, u32[]{:S(2)}) %collective-permute-start.3) | collective-permute-done | bytes 98336 | tf_op jit(solution)/shard_map/ppermute | solution.py:556
  14.2 1.5 collective-permute-start.4
  16.3 3.0 %collective-permute-done.4.refs_5_ = bf16[48,1024]{1,0:T(8,128)(2,1)S(1)} collective-permute-done((bf16[48,1024]{1,0:T(8,128)(2,1)S(1)}, bf16[48,1024]{1,0:T(8,128)(2,1)S(1)}, u32[]{:S(2)}, u32[]{:S(2)}) %collective-permute-start.4) | collective-permute-done | bytes 98336 | tf_op jit(solution)/shard_map/ppermute | solution.py:556
  19.3 1.1 collective-permute-done.2.refs_3_
  20.3 0.9 copy-done.1
  21.9 10.2 %tree_attention.2 = bf16[8,48,640]{2,1,0:T(8,128)(2,1)} custom-call(s32[3,7]{1,0:T(4,128)S(1)} %copy-done.3, s32[1]{0:T(128)} %bitcast.1.owner_ref, bf16[48,1024]{1,0:T(8,128)(2,1)S(1)} %copy-done.1, bf16[48,1024]{1,0:T(8,128)(2,1)S(1)} %collective-permute-done.refs_1_, bf16[48,1024]{1,0:T(8,128)(2,1)S(1)} %collective-permute-done.1.refs_2_, ...), custom_call_target="tpu_custom_call" | custom-call | flops 2147483648 | bytes 6291456 | tf_op jit(solution)/shard_map/tree_attention/pallas_call | solution.py:282
  32.2 7.6 %all-to-all-start = ((bf16[8,48,640]{2,1,0:T(8,128)(2,1)}), bf16[8,48,640]{2,1,0:T(8,128)(2,1)S(1)}, u32[]{:S(2)}, u32[]{:S(2)}) async-start(bf16[8,48,640]{2,1,0:T(8,128)(2,1)} %tree_attention.2), calls=%async_computation | async-start | bytes 983040 | tf_op jit(solution)/shard_map/all_to_all | solution.py:633
  39.8 10.2 %tree_attention.3 = bf16[8,48,640]{2,1,0:T(8,128)(2,1)} custom-call(s32[3,7]{1,0:T(4,128)S(1)} %copy-done.4, s32[1]{0:T(128)} %bitcast.1.owner_ref, bf16[48,1024]{1,0:T(8,128)(2,1)S(1)} %copy-done.2, bf16[48,1024]{1,0:T(8,128)(2,1)S(1)} %collective-permute-done.refs_1_, bf16[48,1024]{1,0:T(8,128)(2,1)S(1)} %collective-permute-done.1.refs_2_, ...), custom_call_target="tpu_custom_call" | custom-call | flops 2147483648 | bytes 6291456 | tf_op jit(solution)/shard_map/tree_attention/pallas_call | solution.py:282
  50.1 9.5 %all-to-all-start.1 = ((bf16[8,48,640]{2,1,0:T(8,128)(2,1)}), bf16[8,48,640]{2,1,0:T(8,128)(2,1)S(1)}, u32[]{:S(2)}, u32[]{:S(2)}) async-start(bf16[8,48,640]{2,1,0:T(8,128)(2,1)} %tree_attention.3), calls=%async_computation.1 | async-start | bytes 983040 | tf_op jit(solution)/shard_map/all_to_all | solution.py:633
  59.6 2.5 %combine_project.2 = (bf16[48,512]{1,0:T(8,128)(2,1)S(1)}, f32[48,1024]{1,0:T(8,128)S(1)}, f32[48,1024]{1,0:T(8,128)S(1)}, f32[48,1024]{1,0:T(8,128)S(1)}, f32[48,1024]{1,0:T(8,128)S(1)}) custom-call(s32[1]{0:T(128)} %bitcast.place_ref, bf16[8,48,640]{2,1,0:T(8,128)(2,1)S(1)} %all-to-all-done.every_ref, bf16[1024,4096]{1,0:T(8,128)(2,1)} %weight_ref.5), custom_call_target="tpu_custom_call" | custom-call | flops 201326592 | bytes 4194304 | tf_op jit(solution)/shard_map/combine_project/pallas_call | solution.py:367
  62.1 7.4 %all-to-all-done.1.every_ref = bf16[8,48,640]{2,1,0:T(8,128)(2,1)S(1)} async-done(((bf16[8,48,640]{2,1,0:T(8,128)(2,1)}), bf16[8,48,640]{2,1,0:T(8,128)(2,1)S(1)}, u32[]{:S(2)}, u32[]{:S(2)}) %all-to-all-start.1) | async-done | bytes 491552 | tf_op jit(solution)/shard_map/all_to_all | solution.py:633
  69.5 2.6 %combine_project.3 = (bf16[48,512]{1,0:T(8,128)(2,1)S(1)}, bf16[48,1024]{1,0:T(8,128)(2,1)S(1)}, bf16[48,1024]{1,0:T(8,128)(2,1)S(1)}, bf16[48,1024]{1,0:T(8,128)(2,1)S(1)}, bf16[48,1024]{1,0:T(8,128)(2,1)S(1)}) custom-call(s32[1]{0:T(128)} %bitcast.place_ref, bf16[8,48,640]{2,1,0:T(8,128)(2,1)S(1)} %all-to-all-done.1.every_ref, ...), custom_call_target="tpu_custom_call" | custom-call | flops 201326592 | bytes 4194304 | tf_op jit(solution)/shard_map/combine_project/pallas_call | solution.py:367
  73.5 1.6 %collective-permute-start.8 = (bf16[48,1024]{1,0:T(8,128)(2,1)S(1)}, bf16[48,1024]{1,0:T(8,128)(2,1)S(1)}, u32[]{:S(2)}, u32[]{:S(2)}) collective-permute-start(bf16[48,1024]{1,0:T(8,128)(2,1)S(1)} %add_convert_fusion.5), channel_id=1, source_target_pairs={{0,2},{1,3},{2,0},{3,1},{4,6},{5,7},{6,4},{7,5},{8,10},{9,11},{10,... | collective-permute-start | bytes 294920 | tf_op jit(solution)/shard_map/ppermute | solution.py:556
  75.1 3.3 %collective-permute-done.8 = bf16[48,1024]{1,0:T(8,128)(2,1)S(1)} collective-permute-done((bf16[48,1024]{1,0:T(8,128)(2,1)S(1)}, bf16[48,1024]{1,0:T(8,128)(2,1)S(1)}, u32[]{:S(2)}, u32[]{:S(2)}) %collective-permute-start.8) | collective-permute-done | bytes 98336 | tf_op jit(solution)/shard_map/ppermute | solution.py:556
  78.5 0.9 collective-permute-start.13
  79.4 1.8 %collective-permute-start.11 = (bf16[48,1024]{1,0:T(8,128)(2,1)S(1)}, bf16[48,1024]{1,0:T(8,128)(2,1)S(1)}, u32[]{:S(2)}, u32[]{:S(2)}) collective-permute-start(bf16[48,1024]{1,0:T(8,128)(2,1)S(1)} %add_convert_fusion.4.refs_0_), channel_id=1, source_target_pairs={{0,24},{4,28},{8,16},{12,20},{16,8},{20,12},{24,0},{28,4},{1,25},{... | collective-permute-start | bytes 294920 | tf_op jit(solution)/shard_map/ppermute | solution.py:556
  81.1 0.9 collective-permute-start.10
  82.0 1.5 collective-permute-start.12
  83.5 4.6 %collective-permute-done.13.refs_2_ = bf16[48,1024]{1,0:T(8,128)(2,1)S(1)} collective-permute-done((bf16[48,1024]{1,0:T(8,128)(2,1)S(1)}, bf16[48,1024]{1,0:T(8,128)(2,1)S(1)}, u32[]{:S(2)}, u32[]{:S(2)}) %collective-permute-start.13) | collective-permute-done | bytes 98336 | tf_op jit(solution)/shard_map/ppermute | solution.py:556
  88.1 0.9 collective-permute-start.14
  89.1 3.7 %collective-permute-done.14.refs_3_ = bf16[48,1024]{1,0:T(8,128)(2,1)S(1)} collective-permute-done((bf16[48,1024]{1,0:T(8,128)(2,1)S(1)}, bf16[48,1024]{1,0:T(8,128)(2,1)S(1)}, u32[]{:S(2)}, u32[]{:S(2)}) %collective-permute-start.14) | collective-permute-done | bytes 98336 | tf_op jit(solution)/shard_map/ppermute | solution.py:556
  92.7 4.0 %gate_up.2 = (bf16[96,3712]{1,0:T(8,128)(2,1)S(1)}, bf16[48,3712]{1,0:T(8,128)(2,1)S(1)}, bf16[48,3712]{1,0:T(8,128)(2,1)S(1)}) custom-call(s32[1]{0:T(128)} %bitcast.3.spot_ref, f32[1,1024]{1,0:T(1,128)S(1)} %bitcast.5, bf16[1024,1792]{1,0:T(8,128)(2,1)} %gate_ref.3, bf16[1024,1792]{1,0:T(8,128)(2,1)} %up_ref.3, ...), custom_call_target="tpu_custom_call" | custom-call | flops 1409286144 | bytes 7340032 | tf_op jit(solution)/shard_map/gate_up/pallas_call | solution.py:447
  97.3 1.2 collective-permute-done.15.low_ref
  99.3 1.6 %collective-permute-start.19 = (bf16[48,3712]{1,0:T(8,128)(2,1)S(1)}, bf16[48,3712]{1,0:T(8,128)(2,1)S(1)}, u32[]{:S(2)}, u32[]{:S(2)}) collective-permute-start(bf16[48,3712]{1,0:T(8,128)(2,1)S(1)} %get-tuple-element.57), channel_id=1, source_target_pairs={{0,2},{1,3},{2,0},{3,1},{4,6},{5,7},{6,4},{7,5},{8,10},{9,11},{10,... | collective-permute-start | bytes 1069064 | tf_op jit(solution)/shard_map/ppermute | solution.py:556
  100.9 1.0 collective-permute-start.18
  101.8 1.1 collective-permute-start.17
  102.9 3.6 %collective-permute-done.18.refs_3_ = bf16[48,1024]{1,0:T(8,128)(2,1)S(1)} collective-permute-done((bf16[48,1024]{1,0:T(8,128)(2,1)S(1)}, bf16[48,1024]{1,0:T(8,128)(2,1)S(1)}, u32[]{:S(2)}, u32[]{:S(2)}) %collective-permute-start.18) | collective-permute-done | bytes 98336 | tf_op jit(solution)/shard_map/ppermute | solution.py:556
  106.5 1.1 collective-permute-done.17.refs_1_
  107.5 4.0 %gate_up.3 = (bf16[96,3712]{1,0:T(8,128)(2,1)S(1)}, bf16[48,3712]{1,0:T(8,128)(2,1)S(1)}, bf16[48,3712]{1,0:T(8,128)(2,1)S(1)}) custom-call(s32[1]{0:T(128)} %bitcast.3.spot_ref, f32[1,1024]{1,0:T(1,128)S(1)} %bitcast.6, bf16[1024,1792]{1,0:T(8,128)(2,1)} %gate_ref.3, bf16[1024,1792]{1,0:T(8,128)(2,1)} %up_ref.3, ...), custom_call_target="tpu_custom_call" | custom-call | flops 1409286144 | bytes 7340032 | tf_op jit(solution)/shard_map/gate_up/pallas_call | solution.py:447
  112.9 4.4 %collective-permute-done.20.refs_1_ = bf16[48,1792]{1,0:T(8,128)(2,1)S(1)} collective-permute-done((bf16[48,1792]{1,0:T(8,128)(2,1)S(1)}, bf16[48,1792]{1,0:T(8,128)(2,1)S(1)}, u32[]{:S(2)}, u32[]{:S(2)}) %collective-permute-start.20) | collective-permute-done | bytes 172064 | tf_op jit(solution)/shard_map/ppermute | solution.py:556
  119.0 0.9 down.2
  120.0 1.0 collective-permute-start.22
  121.0 3.9 %collective-permute-done.22 = bf16[48,1024]{1,0:T(8,128)(2,1)S(1)} collective-permute-done((bf16[48,1024]{1,0:T(8,128)(2,1)S(1)}, bf16[48,1024]{1,0:T(8,128)(2,1)S(1)}, u32[]{:S(2)}, u32[]{:S(2)}) %collective-permute-start.22) | collective-permute-done | bytes 98336 | tf_op jit(solution)/shard_map/ppermute | solution.py:556
  124.9 3.6 %collective-permute-done.27.got_ref = bf16[48,3712]{1,0:T(8,128)(2,1)S(1)} collective-permute-done((bf16[48,3712]{1,0:T(8,128)(2,1)S(1)}, bf16[48,3712]{1,0:T(8,128)(2,1)S(1)}, u32[]{:S(2)}, u32[]{:S(2)}) %collective-permute-start.27) | collective-permute-done | bytes 356384 | tf_op jit(solution)/shard_map/ppermute | solution.py:556
  129.3 5.5 %collective-permute-done.28.refs_1_ = bf16[48,1792]{1,0:T(8,128)(2,1)S(1)} collective-permute-done((bf16[48,1792]{1,0:T(8,128)(2,1)S(1)}, bf16[48,1792]{1,0:T(8,128)(2,1)S(1)}, u32[]{:S(2)}, u32[]{:S(2)}) %collective-permute-start.28) | collective-permute-done | bytes 172064 | tf_op jit(solution)/shard_map/ppermute | solution.py:556
  134.9 1.0 collective-permute-start.24
  135.9 4.2 %collective-permute-done.24 = bf16[48,1024]{1,0:T(8,128)(2,1)S(1)} collective-permute-done((bf16[48,1024]{1,0:T(8,128)(2,1)S(1)}, bf16[48,1024]{1,0:T(8,128)(2,1)S(1)}, u32[]{:S(2)}, u32[]{:S(2)}) %collective-permute-start.24) | collective-permute-done | bytes 98336 | tf_op jit(solution)/shard_map/ppermute | solution.py:556
  140.1 2.6 %collective-permute-done.23 = bf16[48,1024]{1,0:T(8,128)(2,1)S(1)} collective-permute-done((bf16[48,1024]{1,0:T(8,128)(2,1)S(1)}, bf16[48,1024]{1,0:T(8,128)(2,1)S(1)}, u32[]{:S(2)}, u32[]{:S(2)}) %collective-permute-start.23) | collective-permute-done | bytes 98336 | tf_op jit(solution)/shard_map/ppermute | solution.py:556
  142.8 1.0 down.3
  143.7 1.0 collective-permute-start.30
  144.8 1.0 collective-permute-start.32
  145.8 3.6 %collective-permute-done.30 = bf16[48,1024]{1,0:T(8,128)(2,1)S(1)} collective-permute-done((bf16[48,1024]{1,0:T(8,128)(2,1)S(1)}, bf16[48,1024]{1,0:T(8,128)(2,1)S(1)}, u32[]{:S(2)}, u32[]{:S(2)}) %collective-permute-start.30) | collective-permute-done | bytes 98336 | tf_op jit(solution)/shard_map/ppermute | solution.py:556
  149.5 2.3 %collective-permute-start.31 = (bf16[48,1024]{1,0:T(8,128)(2,1)S(1)}, bf16[48,1024]{1,0:T(8,128)(2,1)S(1)}, u32[]{:S(2)}, u32[]{:S(2)}) collective-permute-start(bf16[48,1024]{1,0:T(8,128)(2,1)S(1)} %add_convert_fusion.2), channel_id=1, source_target_pairs={{0,24},{4,28},{8,16},{12,20},{16,8},{20,12},{24,0},{28,4},{1,25},{... | collective-permute-start | bytes 294920 | tf_op jit(solution)/shard_map/ppermute | solution.py:556
  152.6 3.4 %collective-permute-done.31 = bf16[48,1024]{1,0:T(8,128)(2,1)S(1)} collective-permute-done((bf16[48,1024]{1,0:T(8,128)(2,1)S(1)}, bf16[48,1024]{1,0:T(8,128)(2,1)S(1)}, u32[]{:S(2)}, u32[]{:S(2)}) %collective-permute-start.31) | collective-permute-done | bytes 98336 | tf_op jit(solution)/shard_map/ppermute | solution.py:556
  156.0 1.0 collective-permute-done.33
  (61 shorter events, 10.7 us)
Async XLA Ops:
  0.6 10.4 %collective-permute-start.5 = (bf16[48,1024]{1,0:T(8,128)(2,1)}, bf16[48,1024]{1,0:T(8,128)(2,1)S(1)}, u32[]{:S(2)}, u32[]{:S(2)}) collective-permute-start(bf16[48,1024]{1,0:T(8,128)(2,1)} %refs_0_.5), channel_id=1, source_target_pairs={{0,24},{4,28},{8,16},{12,20},{16,8},{20,12},{24,0},{28,4},{1,25},{... | collective-permute-start | bytes 294920 | tf_op jit(solution)/shard_map/ppermute | solution.py:556
  5.7 8.5 %collective-permute-start.3 = (bf16[48,1024]{1,0:T(8,128)(2,1)}, bf16[48,1024]{1,0:T(8,128)(2,1)S(1)}, u32[]{:S(2)}, u32[]{:S(2)}) collective-permute-start(bf16[48,1024]{1,0:T(8,128)(2,1)} %refs_0_.5), channel_id=1, source_target_pairs={{0,16},{4,20},{8,24},{12,28},{16,0},{20,4},{24,8},{28,12},{1,17},{... | collective-permute-start | bytes 294920 | tf_op jit(solution)/shard_map/ppermute | solution.py:556
  5.8 10.0 %collective-permute-start.1 = (bf16[48,1024]{1,0:T(8,128)(2,1)}, bf16[48,1024]{1,0:T(8,128)(2,1)S(1)}, u32[]{:S(2)}, u32[]{:S(2)}) collective-permute-start(bf16[48,1024]{1,0:T(8,128)(2,1)} %refs_0_.5), channel_id=1, source_target_pairs={{0,8},{4,12},{8,0},{12,4},{16,24},{20,28},{24,16},{28,20},{1,9},{5... | collective-permute-start | bytes 294920 | tf_op jit(solution)/shard_map/ppermute | solution.py:556
  6.4 9.9 %collective-permute-start = (bf16[48,1024]{1,0:T(8,128)(2,1)}, bf16[48,1024]{1,0:T(8,128)(2,1)S(1)}, u32[]{:S(2)}, u32[]{:S(2)}) collective-permute-start(bf16[48,1024]{1,0:T(8,128)(2,1)} %refs_0_.5), channel_id=1, source_target_pairs={{0,4},{4,0},{8,12},{12,8},{16,20},{20,16},{24,28},{28,24},{1,5},{5... | collective-permute-start | bytes 294920 | tf_op jit(solution)/shard_map/ppermute | solution.py:556
  11.1 5.2 %collective-permute-start.6 = (bf16[48,1024]{1,0:T(8,128)(2,1)S(1)}, bf16[48,1024]{1,0:T(8,128)(2,1)S(1)}, u32[]{:S(2)}, u32[]{:S(2)}) collective-permute-start(bf16[48,1024]{1,0:T(8,128)(2,1)S(1)} %collective-permute-done.5.refs_6_), channel_id=1, source_target_pairs={{0,4},{4,0},{8,12},{12,8},{16,20},{20,16},{24,28},{28,24},{1,5},{5... | collective-permute-start | bytes 294920 | tf_op jit(solution)/shard_map/ppermute | solution.py:556
  14.2 5.1 %collective-permute-start.4 = (bf16[48,1024]{1,0:T(8,128)(2,1)S(1)}, bf16[48,1024]{1,0:T(8,128)(2,1)S(1)}, u32[]{:S(2)}, u32[]{:S(2)}) collective-permute-start(bf16[48,1024]{1,0:T(8,128)(2,1)S(1)} %collective-permute-done.3.refs_4_), channel_id=1, source_target_pairs={{0,4},{4,0},{8,12},{12,8},{16,20},{20,16},{24,28},{28,24},{1,5},{5... | collective-permute-start | bytes 294920 | tf_op jit(solution)/shard_map/ppermute | solution.py:556
  15.7 4.6 %collective-permute-start.2 = (bf16[48,1024]{1,0:T(8,128)(2,1)S(1)}, bf16[48,1024]{1,0:T(8,128)(2,1)S(1)}, u32[]{:S(2)}, u32[]{:S(2)}) collective-permute-start(bf16[48,1024]{1,0:T(8,128)(2,1)S(1)} %collective-permute-done.1.refs_2_), channel_id=1, source_target_pairs={{0,4},{4,0},{8,12},{12,8},{16,20},{20,16},{24,28},{28,24},{1,5},{5... | collective-permute-start | bytes 294920 | tf_op jit(solution)/shard_map/ppermute | solution.py:556
  20.3 0.9 copy-start.1
  21.2 0.7 copy-start.3
  21.9 17.9 %copy-start.2 = (bf16[48,1024]{1,0:T(8,128)(2,1)S(1)}, bf16[48,1024]{1,0:T(8,128)(2,1)}, u32[]{:S(2)}) copy-start(bf16[48,1024]{1,0:T(8,128)(2,1)} %refs_0_.5) | copy-start | bytes 294916
  21.9 17.9 %copy-start.4 = (s32[3,7]{1,0:T(4,128)S(1)}, s32[3,7]{1,0:T(4,128)}, u32[]{:S(2)}) copy-start(s32[3,7]{1,0:T(4,128)} %own_nodes.1.nodes_ref) | copy-start | bytes 256
  32.2 17.9 %all-to-all-start = ((bf16[8,48,640]{2,1,0:T(8,128)(2,1)}), bf16[8,48,640]{2,1,0:T(8,128)(2,1)S(1)}, u32[]{:S(2)}, u32[]{:S(2)}) async-start(bf16[8,48,640]{2,1,0:T(8,128)(2,1)} %tree_attention.2), calls=%async_computation | async-start | bytes 983040 | tf_op jit(solution)/shard_map/all_to_all | solution.py:633
  50.1 19.4 %all-to-all-start.1 = ((bf16[8,48,640]{2,1,0:T(8,128)(2,1)}), bf16[8,48,640]{2,1,0:T(8,128)(2,1)S(1)}, u32[]{:S(2)}, u32[]{:S(2)}) async-start(bf16[8,48,640]{2,1,0:T(8,128)(2,1)} %tree_attention.3), calls=%async_computation.1 | async-start | bytes 983040 | tf_op jit(solution)/shard_map/all_to_all | solution.py:633
  69.5 8.9 %copy-start.6 = (bf16[48,1024]{1,0:T(8,128)(2,1)S(1)}, bf16[48,1024]{1,0:T(8,128)(2,1)}, u32[]{:S(2)}) copy-start(bf16[48,1024]{1,0:T(8,128)(2,1)} %param.32) | copy-start | bytes 294916
  69.5 23.2 %copy-start.5 = (f32[1024]{0:T(1024)S(1)}, f32[1024]{0:T(1024)}, u32[]{:S(2)}) copy-start(f32[1024]{0:T(1024)} %param.34) | copy-start | bytes 12292
  72.1 1.4 collective-permute-start.7
  72.2 2.9 %collective-permute-start.9 = (bf16[48,1024]{1,0:T(8,128)(2,1)S(1)}, bf16[48,1024]{1,0:T(8,128)(2,1)S(1)}, u32[]{:S(2)}, u32[]{:S(2)}) collective-permute-start(bf16[48,1024]{1,0:T(8,128)(2,1)S(1)} %get-tuple-element.51), channel_id=1, source_target_pairs={{0,1},{1,0},{2,3},{3,2},{4,5},{5,4},{6,7},{7,6},{8,9},{9,8},{10,11... | collective-permute-start | bytes 294920 | tf_op jit(solution)/shard_map/ppermute | solution.py:556
  73.5 4.9 %collective-permute-start.8 = (bf16[48,1024]{1,0:T(8,128)(2,1)S(1)}, bf16[48,1024]{1,0:T(8,128)(2,1)S(1)}, u32[]{:S(2)}, u32[]{:S(2)}) collective-permute-start(bf16[48,1024]{1,0:T(8,128)(2,1)S(1)} %add_convert_fusion.5), channel_id=1, source_target_pairs={{0,2},{1,3},{2,0},{3,1},{4,6},{5,7},{6,4},{7,5},{8,10},{9,11},{10,... | collective-permute-start | bytes 294920 | tf_op jit(solution)/shard_map/ppermute | solution.py:556
  78.5 9.6 %collective-permute-start.13 = (bf16[48,1024]{1,0:T(8,128)(2,1)S(1)}, bf16[48,1024]{1,0:T(8,128)(2,1)S(1)}, u32[]{:S(2)}, u32[]{:S(2)}) collective-permute-start(bf16[48,1024]{1,0:T(8,128)(2,1)S(1)} %add_convert_fusion.4.refs_0_), channel_id=1, source_target_pairs={{0,16},{4,20},{8,24},{12,28},{16,0},{20,4},{24,8},{28,12},{1,17},{... | collective-permute-start | bytes 294920 | tf_op jit(solution)/shard_map/ppermute | solution.py:556
  79.4 9.7 %collective-permute-start.11 = (bf16[48,1024]{1,0:T(8,128)(2,1)S(1)}, bf16[48,1024]{1,0:T(8,128)(2,1)S(1)}, u32[]{:S(2)}, u32[]{:S(2)}) collective-permute-start(bf16[48,1024]{1,0:T(8,128)(2,1)S(1)} %add_convert_fusion.4.refs_0_), channel_id=1, source_target_pairs={{0,24},{4,28},{8,16},{12,20},{16,8},{20,12},{24,0},{28,4},{1,25},{... | collective-permute-start | bytes 294920 | tf_op jit(solution)/shard_map/ppermute | solution.py:556
  81.1 7.9 %collective-permute-start.10 = (bf16[48,1024]{1,0:T(8,128)(2,1)S(1)}, bf16[48,1024]{1,0:T(8,128)(2,1)S(1)}, u32[]{:S(2)}, u32[]{:S(2)}) collective-permute-start(bf16[48,1024]{1,0:T(8,128)(2,1)S(1)} %add_convert_fusion.4.refs_0_), channel_id=1, source_target_pairs={{0,8},{4,12},{8,0},{12,4},{16,24},{20,28},{24,16},{28,20},{1,9},{5... | collective-permute-start | bytes 294920 | tf_op jit(solution)/shard_map/ppermute | solution.py:556
  82.0 7.0 %collective-permute-start.12 = (bf16[48,1024]{1,0:T(8,128)(2,1)S(1)}, bf16[48,1024]{1,0:T(8,128)(2,1)S(1)}, u32[]{:S(2)}, u32[]{:S(2)}) collective-permute-start(bf16[48,1024]{1,0:T(8,128)(2,1)S(1)} %add_convert_fusion.4.refs_0_), channel_id=1, source_target_pairs={{0,4},{4,0},{8,12},{12,8},{16,20},{20,16},{24,28},{28,24},{1,5},{5... | collective-permute-start | bytes 294920 | tf_op jit(solution)/shard_map/ppermute | solution.py:556
  88.1 4.6 %collective-permute-start.14 = (bf16[48,1024]{1,0:T(8,128)(2,1)S(1)}, bf16[48,1024]{1,0:T(8,128)(2,1)S(1)}, u32[]{:S(2)}, u32[]{:S(2)}) collective-permute-start(bf16[48,1024]{1,0:T(8,128)(2,1)S(1)} %collective-permute-done.13.refs_2_), channel_id=1, source_target_pairs={{0,4},{4,0},{8,12},{12,8},{16,20},{20,16},{24,28},{28,24},{1,5},{5... | collective-permute-start | bytes 294920 | tf_op jit(solution)/shard_map/ppermute | solution.py:556
  96.7 1.7 %collective-permute-start.15 = (bf16[48,3712]{1,0:T(8,128)(2,1)S(1)}, bf16[48,3712]{1,0:T(8,128)(2,1)S(1)}, u32[]{:S(2)}, u32[]{:S(2)}) collective-permute-start(bf16[48,3712]{1,0:T(8,128)(2,1)S(1)} %get-tuple-element.54), channel_id=1, source_target_pairs={{0,1},{1,0},{2,3},{3,2},{4,5},{5,4},{6,7},{7,6},{8,9},{9,8},{10,11... | collective-permute-start | bytes 1069064 | tf_op jit(solution)/shard_map/ppermute | solution.py:556
  96.8 2.2 %collective-permute-start.16 = (bf16[48,3712]{1,0:T(8,128)(2,1)S(1)}, bf16[48,3712]{1,0:T(8,128)(2,1)S(1)}, u32[]{:S(2)}, u32[]{:S(2)}) collective-permute-start(bf16[48,3712]{1,0:T(8,128)(2,1)S(1)} %get-tuple-element.55), channel_id=1, source_target_pairs={{0,1},{1,0},{2,3},{3,2},{4,5},{5,4},{6,7},{7,6},{8,9},{9,8},{10,11... | collective-permute-start | bytes 1069064 | tf_op jit(solution)/shard_map/ppermute | solution.py:556
  99.3 19.7 %copy-start = (bf16[1792,1024]{1,0:T(8,128)(2,1)S(1)}, bf16[1792,1024]{1,0:T(8,128)(2,1)}, u32[]{:S(2)}) copy-start(bf16[1792,1024]{1,0:T(8,128)(2,1)} %weight_ref.7) | copy-start | bytes 11010052
  99.3 12.2 %collective-permute-start.19 = (bf16[48,3712]{1,0:T(8,128)(2,1)S(1)}, bf16[48,3712]{1,0:T(8,128)(2,1)S(1)}, u32[]{:S(2)}, u32[]{:S(2)}) collective-permute-start(bf16[48,3712]{1,0:T(8,128)(2,1)S(1)} %get-tuple-element.57), channel_id=1, source_target_pairs={{0,2},{1,3},{2,0},{3,1},{4,6},{5,7},{6,4},{7,5},{8,10},{9,11},{10,... | collective-permute-start | bytes 1069064 | tf_op jit(solution)/shard_map/ppermute | solution.py:556
  100.9 5.6 %collective-permute-start.18 = (bf16[48,1024]{1,0:T(8,128)(2,1)S(1)}, bf16[48,1024]{1,0:T(8,128)(2,1)S(1)}, u32[]{:S(2)}, u32[]{:S(2)}) collective-permute-start(bf16[48,1024]{1,0:T(8,128)(2,1)S(1)} %collective-permute-done.11.refs_2_), channel_id=1, source_target_pairs={{0,4},{4,0},{8,12},{12,8},{16,20},{20,16},{24,28},{28,24},{1,5},{5... | collective-permute-start | bytes 294920 | tf_op jit(solution)/shard_map/ppermute | solution.py:556
  101.8 5.7 %collective-permute-start.17 = (bf16[48,1024]{1,0:T(8,128)(2,1)S(1)}, bf16[48,1024]{1,0:T(8,128)(2,1)S(1)}, u32[]{:S(2)}, u32[]{:S(2)}) collective-permute-start(bf16[48,1024]{1,0:T(8,128)(2,1)S(1)} %collective-permute-done.10.refs_0_), channel_id=1, source_target_pairs={{0,4},{4,0},{8,12},{12,8},{16,20},{20,16},{24,28},{28,24},{1,5},{5... | collective-permute-start | bytes 294920 | tf_op jit(solution)/shard_map/ppermute | solution.py:556
  111.8 5.5 %collective-permute-start.20 = (bf16[48,1792]{1,0:T(8,128)(2,1)S(1)}, bf16[48,1792]{1,0:T(8,128)(2,1)S(1)}, u32[]{:S(2)}, u32[]{:S(2)}) collective-permute-start(bf16[48,1792]{1,0:T(8,128)(2,1)S(1)} %gated.2.refs_0_), channel_id=1, source_target_pairs={{0,2},{1,3},{2,0},{3,1},{4,6},{5,7},{6,4},{7,5},{8,10},{9,11},{10,... | collective-permute-start | bytes 516104 | tf_op jit(solution)/shard_map/ppermute | solution.py:556
  112.4 5.0 %collective-permute-start.25 = (bf16[48,3712]{1,0:T(8,128)(2,1)S(1)}, bf16[48,3712]{1,0:T(8,128)(2,1)S(1)}, u32[]{:S(2)}, u32[]{:S(2)}) collective-permute-start(bf16[48,3712]{1,0:T(8,128)(2,1)S(1)} %get-tuple-element.66), channel_id=1, source_target_pairs={{0,1},{1,0},{2,3},{3,2},{4,5},{5,4},{6,7},{7,6},{8,9},{9,8},{10,11... | collective-permute-start | bytes 1069064 | tf_op jit(solution)/shard_map/ppermute | solution.py:556
  112.4 5.0 %collective-permute-start.26 = (bf16[48,3712]{1,0:T(8,128)(2,1)S(1)}, bf16[48,3712]{1,0:T(8,128)(2,1)S(1)}, u32[]{:S(2)}, u32[]{:S(2)}) collective-permute-start(bf16[48,3712]{1,0:T(8,128)(2,1)S(1)} %get-tuple-element.67), channel_id=1, source_target_pairs={{0,1},{1,0},{2,3},{3,2},{4,5},{5,4},{6,7},{7,6},{8,9},{9,8},{10,11... | collective-permute-start | bytes 1069064 | tf_op jit(solution)/shard_map/ppermute | solution.py:556
  117.3 1.7 %collective-permute-start.21 = (bf16[96,1792]{1,0:T(8,128)(2,1)S(1)}, bf16[96,1792]{1,0:T(8,128)(2,1)S(1)}, u32[]{:S(2)}, u32[]{:S(2)}) collective-permute-start(bf16[96,1792]{1,0:T(8,128)(2,1)S(1)} %pad_maximum_fusion), channel_id=1, source_target_pairs={{0,1},{1,0},{2,3},{3,2},{4,5},{5,4},{6,7},{7,6},{8,9},{9,8},{10,11... | collective-permute-start | bytes 1032200 | tf_op jit(solution)/shard_map/ppermute | solution.py:556
  117.7 10.8 %collective-permute-start.27 = (bf16[48,3712]{1,0:T(8,128)(2,1)S(1)}, bf16[48,3712]{1,0:T(8,128)(2,1)S(1)}, u32[]{:S(2)}, u32[]{:S(2)}) collective-permute-start(bf16[48,3712]{1,0:T(8,128)(2,1)S(1)} %get-tuple-element.70), channel_id=1, source_target_pairs={{0,2},{1,3},{2,0},{3,1},{4,6},{5,7},{6,4},{7,5},{8,10},{9,11},{10,... | collective-permute-start | bytes 1069064 | tf_op jit(solution)/shard_map/ppermute | solution.py:556
  120.0 4.9 %collective-permute-start.22 = (bf16[48,1024]{1,0:T(8,128)(2,1)S(1)}, bf16[48,1024]{1,0:T(8,128)(2,1)S(1)}, u32[]{:S(2)}, u32[]{:S(2)}) collective-permute-start(bf16[48,1024]{1,0:T(8,128)(2,1)S(1)} %get-tuple-element.62), channel_id=1, source_target_pairs={{0,4},{4,0},{8,12},{12,8},{16,20},{20,16},{24,28},{28,24},{1,5},{5... | collective-permute-start | bytes 294920 | tf_op jit(solution)/shard_map/ppermute | solution.py:556
  128.8 6.0 %collective-permute-start.28 = (bf16[48,1792]{1,0:T(8,128)(2,1)S(1)}, bf16[48,1792]{1,0:T(8,128)(2,1)S(1)}, u32[]{:S(2)}, u32[]{:S(2)}) collective-permute-start(bf16[48,1792]{1,0:T(8,128)(2,1)S(1)} %gated.3.refs_0_), channel_id=1, source_target_pairs={{0,2},{1,3},{2,0},{3,1},{4,6},{5,7},{6,4},{7,5},{8,10},{9,11},{10,... | collective-permute-start | bytes 516104 | tf_op jit(solution)/shard_map/ppermute | solution.py:556
  134.8 7.9 %collective-permute-start.29 = (bf16[96,1792]{1,0:T(8,128)(2,1)S(1)}, bf16[96,1792]{1,0:T(8,128)(2,1)S(1)}, u32[]{:S(2)}, u32[]{:S(2)}) collective-permute-start(bf16[96,1792]{1,0:T(8,128)(2,1)S(1)} %pad_maximum_fusion.1), channel_id=1, source_target_pairs={{0,1},{1,0},{2,3},{3,2},{4,5},{5,4},{6,7},{7,6},{8,9},{9,8},{10,11... | collective-permute-start | bytes 1032200 | tf_op jit(solution)/shard_map/ppermute | solution.py:556
  134.9 5.2 %collective-permute-start.24 = (bf16[48,1024]{1,0:T(8,128)(2,1)S(1)}, bf16[48,1024]{1,0:T(8,128)(2,1)S(1)}, u32[]{:S(2)}, u32[]{:S(2)}) collective-permute-start(bf16[48,1024]{1,0:T(8,128)(2,1)S(1)} %get-tuple-element.64), channel_id=1, source_target_pairs={{0,4},{4,0},{8,12},{12,8},{16,20},{20,16},{24,28},{28,24},{1,5},{5... | collective-permute-start | bytes 294920 | tf_op jit(solution)/shard_map/ppermute | solution.py:556
  135.9 6.8 %collective-permute-start.23 = (bf16[48,1024]{1,0:T(8,128)(2,1)S(1)}, bf16[48,1024]{1,0:T(8,128)(2,1)S(1)}, u32[]{:S(2)}, u32[]{:S(2)}) collective-permute-start(bf16[48,1024]{1,0:T(8,128)(2,1)S(1)} %add_convert_fusion.3), channel_id=1, source_target_pairs={{0,16},{4,20},{8,24},{12,28},{16,0},{20,4},{24,8},{28,12},{1,17},{... | collective-permute-start | bytes 294920 | tf_op jit(solution)/shard_map/ppermute | solution.py:556
  143.7 5.7 %collective-permute-start.30 = (bf16[48,1024]{1,0:T(8,128)(2,1)S(1)}, bf16[48,1024]{1,0:T(8,128)(2,1)S(1)}, u32[]{:S(2)}, u32[]{:S(2)}) collective-permute-start(bf16[48,1024]{1,0:T(8,128)(2,1)S(1)} %get-tuple-element.73), channel_id=1, source_target_pairs={{0,4},{4,0},{8,12},{12,8},{16,20},{20,16},{24,28},{28,24},{1,5},{5... | collective-permute-start | bytes 294920 | tf_op jit(solution)/shard_map/ppermute | solution.py:556
  144.8 7.0 %collective-permute-start.32 = (bf16[48,1024]{1,0:T(8,128)(2,1)S(1)}, bf16[48,1024]{1,0:T(8,128)(2,1)S(1)}, u32[]{:S(2)}, u32[]{:S(2)}) collective-permute-start(bf16[48,1024]{1,0:T(8,128)(2,1)S(1)} %get-tuple-element.75), channel_id=1, source_target_pairs={{0,4},{4,0},{8,12},{12,8},{16,20},{20,16},{24,28},{28,24},{1,5},{5... | collective-permute-start | bytes 294920 | tf_op jit(solution)/shard_map/ppermute | solution.py:556
  149.5 6.5 %collective-permute-start.31 = (bf16[48,1024]{1,0:T(8,128)(2,1)S(1)}, bf16[48,1024]{1,0:T(8,128)(2,1)S(1)}, u32[]{:S(2)}, u32[]{:S(2)}) collective-permute-start(bf16[48,1024]{1,0:T(8,128)(2,1)S(1)} %add_convert_fusion.2), channel_id=1, source_target_pairs={{0,24},{4,28},{8,16},{12,20},{16,8},{20,12},{24,0},{28,4},{1,25},{... | collective-permute-start | bytes 294920 | tf_op jit(solution)/shard_map/ppermute | solution.py:556
  151.8 5.2 %collective-permute-start.33 = (bf16[48,1024]{1,0:T(8,128)(2,1)S(1)}, bf16[48,1024]{1,0:T(8,128)(2,1)S(1)}, u32[]{:S(2)}, u32[]{:S(2)}) collective-permute-start(bf16[48,1024]{1,0:T(8,128)(2,1)S(1)} %add_convert_fusion.1), channel_id=1, source_target_pairs={{0,8},{4,12},{8,0},{12,4},{16,24},{20,28},{24,16},{28,20},{1,9},{5... | collective-permute-start | bytes 294920 | tf_op jit(solution)/shard_map/ppermute | solution.py:556

commit v6 on v5

--- a/solution.py
+++ b/solution.py
@@ -104,7 +104,9 @@
     def kernel(nodes_ref, owner_ref, *refs):
         query_refs = refs[:part_total]
         cache_refs = refs[part_total : part_total + 3]
-        out_ref, all_rows, run_out, run_lse, acc, peak, total, *rest = refs[part_total + 3 :]
+        near_ref, far_ref, all_rows, run_out, run_lse, acc, peak, total, *rest = refs[
+            part_total + 3 :
+        ]
         kept_refs, sems = rest[:3], rest[3]
         columns = pl.ds(kv_head * 2 * HEAD, 2 * HEAD)
         starts = [0, levels[0][0], levels[0][0] + levels[1][0]]
@@ -253,27 +255,14 @@
                     run_lse[here] = jnp.where(live, best + jnp.log(share), old_lse)
         lane = lax.broadcasted_iota(jnp.int32, (own_rows, HEAD), 1)
         for part in range(part_total):
-            at = part * own_rows
-            out_ref[part, :, :width] = run_out[at : at + own_rows, :].astype(jnp.bfloat16)
+            out_ref = far_ref if part % 2 else near_ref
+            here = pl.ds(pl.multiple_of((me ^ part) * own_rows, ALIGN), own_rows)
+            out_ref[part // 2, :, :width] = run_out[here, :].astype(jnp.bfloat16)
             lse = jnp.zeros((own_rows, HEAD), jnp.float32)
             for h in range(group_size):
-                piece = run_lse[at : at + own_rows, h * HEAD : (h + 1) * HEAD]
+                piece = run_lse[here, h * HEAD : (h + 1) * HEAD]
                 lse = jnp.where(lax.rem(lane, group_size) == h, piece, lse)
-            first = lse.astype(jnp.bfloat16)
-            rest = lse - first.astype(jnp.float32)
-            second = rest.astype(jnp.bfloat16)
-            third = rest - second.astype(jnp.float32)
-            field = lax.div(lane, group_size)
-            packed = jnp.where(
-                field == 0,
-                first.astype(jnp.float32),
-                jnp.where(
-                    field == 1,
-                    second.astype(jnp.float32),
-                    jnp.where(field == 2, third, 0.0),
-                ),
-            )
-            out_ref[part, :, width:] = packed.astype(jnp.bfloat16)
+            out_ref[part // 2, :, width:] = lse_terms(lse, lane, group_size)
 
     block_total = sum(count * (span // min(BLOCK, span)) for count, span, _ in levels)
     most = max(count * rows for count, _, rows in levels) * group_size
@@ -281,11 +270,14 @@
     smem = pl.BlockSpec(memory_space=pltpu.SMEM)
     return pl.pallas_call(
         kernel,
-        out_shape=jax.ShapeDtypeStruct((part_total, own_rows, width + HEAD), jnp.bfloat16),
+        out_shape=[
+            jax.ShapeDtypeStruct((part_total // 2, own_rows, width + HEAD), jnp.bfloat16)
+        ]
+        * 2,
         in_specs=[smem, smem]
         + [vmem] * part_total
         + [pl.BlockSpec(memory_space=pltpu.HBM)] * 3,
-        out_specs=vmem,
+        out_specs=[vmem, vmem],
         scratch_shapes=[
             pltpu.VMEM((total_rows, width), jnp.bfloat16),
             pltpu.VMEM((total_rows, width), jnp.float32),
@@ -306,15 +298,72 @@
     )(nodes, owner[None], *query_parts, *caches)
 
 
+def lse_of(packed, group_size):
+    terms = packed.astype(jnp.float32)
+    return (
+        terms
+        + pltpu.roll(terms, HEAD - group_size, 1)
+        + pltpu.roll(terms, HEAD - 2 * group_size, 1)
+    )
+
+
+def lse_terms(lse, lane, group_size):
+    first = lse.astype(jnp.bfloat16).astype(jnp.float32)
+    second = (lse - first).astype(jnp.bfloat16).astype(jnp.float32)
+    third = lse - first - second
+    field = lax.div(lane, group_size)
+    packed = jnp.where(field == 2, third, 0.0)
+    packed = jnp.where(field == 1, second, packed)
+    return jnp.where(field == 0, first, packed).astype(jnp.bfloat16)
+
+
+def merge_pairs(near, got):
+    pair_total, own_rows, wide = near.shape
+    width = wide - HEAD
+    group_size = width // HEAD
+
+    def kernel(near_ref, got_ref, *out_refs):
+        lane = lax.broadcasted_iota(jnp.int32, (own_rows, HEAD), 1)
+        for k, out_ref in enumerate(out_refs):
+            left = lse_of(near_ref[k, :, width:], group_size)
+            right = lse_of(got_ref[k, :, width:], group_size)
+            best = jnp.maximum(left, right)
+            left, right = jnp.exp(left - best), jnp.exp(right - best)
+            whole = left + right
+            left, right = left / whole, right / whole
+            for h in range(group_size):
+                here = slice(h * HEAD, (h + 1) * HEAD)
+                out_ref[:, here] = (
+                    near_ref[k, :, here].astype(jnp.float32) * left[:, h : h + 1]
+                    + got_ref[k, :, here].astype(jnp.float32) * right[:, h : h + 1]
+                ).astype(jnp.bfloat16)
+            lse = jnp.where(lane < group_size, best + jnp.log(whole), 0.0)
+            lse = lse + pltpu.roll(lse, group_size, 1) + pltpu.roll(lse, 2 * group_size, 1)
+            out_ref[:, width:] = lse_terms(lse, lane, group_size)
+
+    vmem = pl.BlockSpec(memory_space=pltpu.VMEM)
+    return pl.pallas_call(
+        kernel,
+        out_shape=[jax.ShapeDtypeStruct((own_rows, wide), jnp.bfloat16)] * pair_total,
+        in_specs=[vmem, vmem],
+        out_specs=[vmem] * pair_total,
+        compiler_params=pltpu.CompilerParams(vmem_limit_bytes=SMALL_BYTES),
+        cost_estimate=cost(4 * near.size, 6 * near.size, pair_total * own_rows * 2 * HEAD),
+        name="merge_pairs",
+    )(near, got)
+
+
 def combine_project(every, weight, row_start, added, place, own_width):
-    part_total, own_rows, wide = every.shape
+    part_total = len(every)
+    own_rows, wide = every[0].shape
     width = wide - HEAD
     group_size = width // HEAD
     block_total = weight.shape[1] // own_width
     last = added is not None or width == weight.shape[0]
     kind = jnp.bfloat16 if last else jnp.float32
 
-    def kernel(place_ref, every_ref, weight_ref, *refs):
+    def kernel(place_ref, weight_ref, *refs):
+        every_refs, refs = refs[:part_total], refs[part_total:]
         added_refs = refs[:block_total] if added is not None else (None,) * block_total
         attended_ref, *block_refs = refs[len(refs) - 3 - block_total : -2]
         kept, sems = refs[-2:]
@@ -329,14 +378,7 @@
             ],
             sems,
         )
-        lse = []
-        for part in range(part_total):
-            terms = every_ref[part, :, width:].astype(jnp.float32)
-            lse.append(
-                terms
-                + pltpu.roll(terms, HEAD - group_size, 1)
-                + pltpu.roll(terms, HEAD - 2 * group_size, 1)
-            )
+        lse = [lse_of(ref[:, width:], group_size) for ref in every_refs]
         best = lse[0]
         for one in lse[1:]:
             best = jnp.maximum(best, one)
@@ -348,7 +390,7 @@
             summed = jnp.zeros((own_rows, HEAD), jnp.float32)
             for part in range(part_total):
                 summed = summed + (
-                    every_ref[part, :, h * HEAD : (h + 1) * HEAD].astype(jnp.float32)
+                    every_refs[part][:, h * HEAD : (h + 1) * HEAD].astype(jnp.float32)
                     * share[part][:, h : h + 1]
                 )
             attended_ref[:, h * HEAD : (h + 1) * HEAD] = (summed / whole[:, h : h + 1]).astype(
@@ -368,9 +410,8 @@
         kernel,
         out_shape=[jax.ShapeDtypeStruct((own_rows, width), jnp.bfloat16)]
         + [jax.ShapeDtypeStruct((own_rows, own_width), kind)] * block_total,
-        in_specs=[pl.BlockSpec(memory_space=pltpu.SMEM), vmem]
-        + [pl.BlockSpec(memory_space=pltpu.HBM)]
-        + [vmem] * (block_total if added is not None else 0),
+        in_specs=[pl.BlockSpec(memory_space=pltpu.SMEM), pl.BlockSpec(memory_space=pltpu.HBM)]
+        + [vmem] * (part_total + (block_total if added is not None else 0)),
         out_specs=[vmem] * (1 + block_total),
         scratch_shapes=[
             pltpu.VMEM((block_total, width, own_width), jnp.bfloat16),
@@ -383,7 +424,7 @@
             part_total * own_rows * HEAD,
         ),
         name="combine_project",
-    )(place[None], every, weight, *(added or ()))
+    )(place[None], weight, *every, *(added or ()))
     return outs[0], outs[1:]
 
 
@@ -629,8 +670,9 @@
     query_parts = gather_parts(queries, "kv", nodes)
     attended, blocks = [], None
     for k in range(kv_count):
-        parts = tree_attention(query_parts, caches, nodes, owner, k)
-        every = lax.all_to_all(parts, "kv", 0, 0)
+        near, far = tree_attention(query_parts, caches, nodes, owner, k)
+        merged = merge_pairs(near, swap(far, "kv", 1))
+        every = [swap(one, "kv", 2 * pair) if pair else one for pair, one in enumerate(merged)]
         one, blocks = combine_project(
             every, out_weight, k * group_width, blocks, mlp_place, own_width
         )
@@ -662,10 +704,12 @@
             keep, send = add_halves(keep, got, units)
         return keep, send
 
-    def regather(hidden):
+    def regather(hidden, token):
         pieces = [hidden]
         for step in reversed(steps):
             held = pieces[0] if len(pieces) == 1 else jnp.concatenate(pieces, axis=0)
+            if step != steps[-1] and token is not None:
+                held = after(held, token)
             pieces.append(swap(held, "mlp", step))
         return pieces
 
@@ -678,13 +722,11 @@
     later = multiply(second)
     hidden = gated(after(keep, later[0]), swap(send, "mlp", steps[-1]), units)
     keep, send = reduce_once(*later, hidden)
-    pairs = finish(regather(hidden), first)
-    keep = after(keep, [pair for mask, pair in pairs.items() if mask])
+    pairs = finish(regather(hidden, None), first)
+    keep = after(keep, pairs[0])
     hidden = gated(keep, swap(send, "mlp", steps[-1]), units)
     mixed = far_sum(pairs, "kv")
-    pieces = regather(hidden)
-    pieces[0] = after(pieces[0], mixed)
-    mixed = mixed + far_sum(finish(pieces, second), "kv")
+    mixed = mixed + far_sum(finish(regather(hidden, mixed), second), "kv")
     return (jnp.concatenate(attended, axis=1), mixed.astype(jnp.bfloat16))
 
 

time: 157 us -> 148 us (0.943); the launches traced: 158 us -> 146 us
  waiting for transfers between devices: 65.8 us -> 58 us
  Pallas kernels: 39.6 us -> 36.7 us
    all_to_all x2 -> x0, starting transfers between devices: 17.1 us -> none  [shards(): every = lax.all_to_all(parts, 'kv', 0, 0)]
    ppermute x34 -> x42, starting transfers between devices: 31.1 us -> 47.6 us  [swap(): lax.ppermute(value, axis_name, [(j, j ^ mask) for j in range(axis_total)])]
    all_to_all x2 -> x0, waiting for transfers between devices: 7.4 us -> none  [shards(): every = lax.all_to_all(parts, 'kv', 0, 0)]
    pallas_call x2 -> x4, Pallas kernels: 20.5 us -> 17.6 us  [the longest x2 16 us: tree_attention(): pl.pallas_call(kernel, out_shape=[jax.ShapeDtypeStruct((part_total // 2,...]
    ppermute x34 -> x42, waiting for transfers between devices: 58.4 us -> 58 us  [swap(): lax.ppermute(value, axis_name, [(j, j ^ mask) for j in range(axis_total)])]
  transfers between devices with their start and end apart: 36 -> 42, of which waited for: 22 -> 22; matrix products, arithmetic and copies ran while one was open for 1% -> 1% of each run, Pallas kernels for 13% -> 14%
where the time goes in v6:
time: 148 us; the launch traced here: 146 us
  waiting for transfers between devices  58 us (39%)
  starting transfers between devices  47.6 us (32%)
  Pallas kernels  36.7 us (25%)
  local copies, waits for them, and re-layouts  1.59 us (1%)
  other arithmetic  1.58 us (1%)
    ppermute x42, waiting for transfers between devices, swap(): lax.ppermute(value, axis_name, [(j, j ^ mask) for j in range(axis_total)])  58 us
    ppermute x42, starting transfers between devices, swap(): lax.ppermute(value, axis_name, [(j, j ^ mask) for j in range(axis_total)])  47.6 us
    pallas_call x2, Pallas kernels, tree_attention(): pl.pallas_call(kernel, out_shape=[jax.ShapeDtypeStruct((part_total // 2,...  16 us
    pallas_call x2, Pallas kernels, gate_up_rows(): pl.pallas_call(kernel, out_shape=[jax.ShapeDtypeStruct((half, 2 * units +...  7.95 us
    pallas_call x2, Pallas kernels, combine_project(): pl.pallas_call(kernel, out_shape=[jax.ShapeDtypeStruct((own_rows, width),...  5.08 us
    pallas_call x1, Pallas kernels, own_nodes(): pl.pallas_call(kernel, out_shape=jax.ShapeDtypeStruct((3, node_total), jn...  3.03 us
  transfers between devices with their start and end apart: 42, of which 22 were waited for; matrix products, arithmetic and copies ran while one was open for 1% of the time, Pallas kernels for 14%

profile of v6, /device:TPU:0, one launch (start us, length us, event | category | flops | bytes accessed | tf_op | source)
XLA Modules:
  0.0 146.4 jit_solution(11799330258901170915)
XLA Ops:
  0.6 5.1 %collective-permute-start.5 = (bf16[48,1024]{1,0:T(8,128)(2,1)}, bf16[48,1024]{1,0:T(8,128)(2,1)S(1)}, u32[]{:S(2)}, u32[]{:S(2)}) collective-permute-start(bf16[48,1024]{1,0:T(8,128)(2,1)} %refs_0_.5), channel_id=1, source_target_pairs={{0,24},{4,28},{8,16},{12,20},{16,8},{20,12},{24,0},{28,4},{1,25},{... | collective-permute-start | bytes 294920 | tf_op jit(solution)/shard_map/ppermute | solution.py:597
  6.4 1.6 %collective-permute-start = (bf16[48,1024]{1,0:T(8,128)(2,1)}, bf16[48,1024]{1,0:T(8,128)(2,1)S(1)}, u32[]{:S(2)}, u32[]{:S(2)}) collective-permute-start(bf16[48,1024]{1,0:T(8,128)(2,1)} %refs_0_.5), channel_id=1, source_target_pairs={{0,4},{4,0},{8,12},{12,8},{16,20},{20,16},{24,28},{28,24},{1,5},{5... | collective-permute-start | bytes 294920 | tf_op jit(solution)/shard_map/ppermute | solution.py:597
  8.0 3.0 %own_nodes.1.nodes_ref = s32[3,7]{1,0:T(4,128)} custom-call(s32[1]{0:T(128)} %bitcast.1.owner_ref, s32[3,128]{1,0:T(4,128)} %bitcast.7, s32[32]{0:T(128)} %leaf_up.1, s32[16]{0:T(128)} %mid_up.1, s32[8]{0:T(128)} %refs_0_.3, s32[16]{0:T(128)} %refs_1_.1, s32[32]{0:T(128)} %refs_2_.1, s32[8]{0:T(128)} %refs_3_.1, s32[16]{0:T(128)} %refs_4_.1, s32[32]{0:T(128)} %refs_5_.1), custom_call_target="tpu_custom_call" | custom-call | tf_op jit(solution)/shard_map/own_nodes/pallas_call | solution.py:84
  11.5 2.7 %collective-permute-done.3.refs_4_ = bf16[48,1024]{1,0:T(8,128)(2,1)S(1)} collective-permute-done((bf16[48,1024]{1,0:T(8,128)(2,1)}, bf16[48,1024]{1,0:T(8,128)(2,1)S(1)}, u32[]{:S(2)}, u32[]{:S(2)}) %collective-permute-start.3) | collective-permute-done | bytes 98336 | tf_op jit(solution)/shard_map/ppermute | solution.py:597
  14.2 1.5 %collective-permute-start.4 = (bf16[48,1024]{1,0:T(8,128)(2,1)S(1)}, bf16[48,1024]{1,0:T(8,128)(2,1)S(1)}, u32[]{:S(2)}, u32[]{:S(2)}) collective-permute-start(bf16[48,1024]{1,0:T(8,128)(2,1)S(1)} %collective-permute-done.3.refs_4_), channel_id=1, source_target_pairs={{0,4},{4,0},{8,12},{12,8},{16,20},{20,16},{24,28},{28,24},{1,5},{5... | collective-permute-start | bytes 294920 | tf_op jit(solution)/shard_map/ppermute | solution.py:597
  16.3 3.0 %collective-permute-done.4.refs_5_ = bf16[48,1024]{1,0:T(8,128)(2,1)S(1)} collective-permute-done((bf16[48,1024]{1,0:T(8,128)(2,1)S(1)}, bf16[48,1024]{1,0:T(8,128)(2,1)S(1)}, u32[]{:S(2)}, u32[]{:S(2)}) %collective-permute-start.4) | collective-permute-done | bytes 98336 | tf_op jit(solution)/shard_map/ppermute | solution.py:597
  19.3 1.1 collective-permute-done.2.refs_3_
  20.3 0.9 copy-done.1
  21.9 7.9 %tree_attention.2 = (bf16[4,48,640]{2,1,0:T(8,128)(2,1)S(1)}, bf16[4,48,640]{2,1,0:T(8,128)(2,1)S(1)}) custom-call(s32[3,7]{1,0:T(4,128)S(1)} %copy-done.2, s32[1]{0:T(128)} %bitcast.1.owner_ref, bf16[48,1024]{1,0:T(8,128)(2,1)S(1)} %copy-done.1, bf16[48,1024]{1,0:T(8,128)(2,1)S(1)} %collective-permute-done.refs_1_, ...), custom_call_target="tpu_custom_call" | custom-call | flops 2147483648 | bytes 6291456 | tf_op jit(solution)/shard_map/tree_attention/pallas_call | solution.py:271
  29.8 4.3 %collective-permute-start.7 = (bf16[4,48,640]{2,1,0:T(8,128)(2,1)S(1)}, bf16[4,48,640]{2,1,0:T(8,128)(2,1)S(1)}, u32[]{:S(2)}, u32[]{:S(2)}) collective-permute-start(bf16[4,48,640]{2,1,0:T(8,128)(2,1)S(1)} %get-tuple-element.55), channel_id=1, source_target_pairs={{0,4},{4,0},{8,12},{12,8},{16,20},{20,16},{24,28},{28,24},{1,5},{5... | collective-permute-start | bytes 737288 | tf_op jit(solution)/shard_map/ppermute | solution.py:597
  34.1 8.1 %tree_attention.3 = (bf16[4,48,640]{2,1,0:T(8,128)(2,1)S(1)}, bf16[4,48,640]{2,1,0:T(8,128)(2,1)S(1)}) custom-call(s32[3,7]{1,0:T(4,128)S(1)} %copy-done.2, s32[1]{0:T(128)} %bitcast.1.owner_ref, bf16[48,1024]{1,0:T(8,128)(2,1)S(1)} %copy-done.1, bf16[48,1024]{1,0:T(8,128)(2,1)S(1)} %collective-permute-done.refs_1_, ...), custom_call_target="tpu_custom_call" | custom-call | flops 2147483648 | bytes 6291456 | tf_op jit(solution)/shard_map/tree_attention/pallas_call | solution.py:271
  42.2 3.2 %collective-permute-start.11 = (bf16[4,48,640]{2,1,0:T(8,128)(2,1)S(1)}, bf16[4,48,640]{2,1,0:T(8,128)(2,1)S(1)}, u32[]{:S(2)}, u32[]{:S(2)}) collective-permute-start(bf16[4,48,640]{2,1,0:T(8,128)(2,1)S(1)} %get-tuple-element.62), channel_id=1, source_target_pairs={{0,4},{4,0},{8,12},{12,8},{16,20},{20,16},{24,28},{28,24},{1,5},{5... | collective-permute-start | bytes 737288 | tf_op jit(solution)/shard_map/ppermute | solution.py:597
  45.5 0.8 merge_pairs.2
  46.4 4.7 %collective-permute-start.9 = (bf16[48,640]{1,0:T(8,128)(2,1)S(1)}, bf16[48,640]{1,0:T(8,128)(2,1)S(1)}, u32[]{:S(2)}, u32[]{:S(2)}) collective-permute-start(bf16[48,640]{1,0:T(8,128)(2,1)S(1)} %get-tuple-element.58), channel_id=1, source_target_pairs={{0,16},{4,20},{8,24},{12,28},{16,0},{20,4},{24,8},{28,12},{1,17},{... | collective-permute-start | bytes 184328 | tf_op jit(solution)/shard_map/ppermute | solution.py:597
  51.0 1.4 collective-permute-start.10
  52.4 0.8 merge_pairs.3
  53.9 3.3 %collective-permute-start.13 = (bf16[48,640]{1,0:T(8,128)(2,1)S(1)}, bf16[48,640]{1,0:T(8,128)(2,1)S(1)}, u32[]{:S(2)}, u32[]{:S(2)}) collective-permute-start(bf16[48,640]{1,0:T(8,128)(2,1)S(1)} %get-tuple-element.65), channel_id=1, source_target_pairs={{0,16},{4,20},{8,24},{12,28},{16,0},{20,4},{24,8},{28,12},{1,17},{... | collective-permute-start | bytes 184328 | tf_op jit(solution)/shard_map/ppermute | solution.py:597
  57.2 1.4 collective-permute-start.14
  58.6 2.5 %combine_project.2 = (bf16[48,512]{1,0:T(8,128)(2,1)S(1)}, f32[48,1024]{1,0:T(8,128)S(1)}, f32[48,1024]{1,0:T(8,128)S(1)}, f32[48,1024]{1,0:T(8,128)S(1)}, f32[48,1024]{1,0:T(8,128)S(1)}) custom-call(s32[1]{0:T(128)} %bitcast.place_ref, bf16[1024,4096]{1,0:T(8,128)(2,1)} %weight_ref.5, bf16[48,640]{1,0:T(8,128)(2,1)S(1)} %get-tuple-element.56.refs_0_, ...), custom_call_target="tpu_custom_call" | custom-call | flops 201326592 | bytes 4194304 | tf_op jit(solution)/shard_map/combine_project/pallas_call | solution.py:409
  61.2 2.2 %collective-permute-done.14.refs_3_ = bf16[48,640]{1,0:T(8,128)(2,1)S(1)} collective-permute-done((bf16[48,640]{1,0:T(8,128)(2,1)S(1)}, bf16[48,640]{1,0:T(8,128)(2,1)S(1)}, u32[]{:S(2)}, u32[]{:S(2)}) %collective-permute-start.14) | collective-permute-done | bytes 61472 | tf_op jit(solution)/shard_map/ppermute | solution.py:597
  63.3 2.6 %combine_project.3 = (bf16[48,512]{1,0:T(8,128)(2,1)S(1)}, bf16[48,1024]{1,0:T(8,128)(2,1)S(1)}, bf16[48,1024]{1,0:T(8,128)(2,1)S(1)}, bf16[48,1024]{1,0:T(8,128)(2,1)S(1)}, bf16[48,1024]{1,0:T(8,128)(2,1)S(1)}) custom-call(s32[1]{0:T(128)} %bitcast.place_ref, bf16[1024,4096]{1,0:T(8,128)(2,1)} %weight_ref.5, bf16[48,640]{1,0:T(8,128)(2,1)S(1)} %get-tuple-element.63.refs_0_, ...), custom_call_target="tpu_custom_call" | custom-call | flops 201326592 | bytes 4194304 | tf_op jit(solution)/shard_map/combine_project/pallas_call | solution.py:409
  66.5 0.8 collective-permute-done.15
  67.3 1.6 %collective-permute-start.16 = (bf16[48,1024]{1,0:T(8,128)(2,1)S(1)}, bf16[48,1024]{1,0:T(8,128)(2,1)S(1)}, u32[]{:S(2)}, u32[]{:S(2)}) collective-permute-start(bf16[48,1024]{1,0:T(8,128)(2,1)S(1)} %add_convert_fusion.5), channel_id=1, source_target_pairs={{0,2},{1,3},{2,0},{3,1},{4,6},{5,7},{6,4},{7,5},{8,10},{9,11},{10,... | collective-permute-start | bytes 294920 | tf_op jit(solution)/shard_map/ppermute | solution.py:597
  68.9 3.3 %collective-permute-done.16 = bf16[48,1024]{1,0:T(8,128)(2,1)S(1)} collective-permute-done((bf16[48,1024]{1,0:T(8,128)(2,1)S(1)}, bf16[48,1024]{1,0:T(8,128)(2,1)S(1)}, u32[]{:S(2)}, u32[]{:S(2)}) %collective-permute-start.16) | collective-permute-done | bytes 98336 | tf_op jit(solution)/shard_map/ppermute | solution.py:597
  72.3 1.0 collective-permute-start.21
  73.3 2.1 %collective-permute-start.19 = (bf16[48,1024]{1,0:T(8,128)(2,1)S(1)}, bf16[48,1024]{1,0:T(8,128)(2,1)S(1)}, u32[]{:S(2)}, u32[]{:S(2)}) collective-permute-start(bf16[48,1024]{1,0:T(8,128)(2,1)S(1)} %add_convert_fusion.4.refs_0_), channel_id=1, source_target_pairs={{0,24},{4,28},{8,16},{12,20},{16,8},{20,12},{24,0},{28,4},{1,25},{... | collective-permute-start | bytes 294920 | tf_op jit(solution)/shard_map/ppermute | solution.py:597
  75.8 1.0 collective-permute-start.20
  76.8 5.2 %collective-permute-done.21.refs_2_ = bf16[48,1024]{1,0:T(8,128)(2,1)S(1)} collective-permute-done((bf16[48,1024]{1,0:T(8,128)(2,1)S(1)}, bf16[48,1024]{1,0:T(8,128)(2,1)S(1)}, u32[]{:S(2)}, u32[]{:S(2)}) %collective-permute-start.21) | collective-permute-done | bytes 98336 | tf_op jit(solution)/shard_map/ppermute | solution.py:597
  82.5 4.2 %collective-permute-done.22.refs_3_ = bf16[48,1024]{1,0:T(8,128)(2,1)S(1)} collective-permute-done((bf16[48,1024]{1,0:T(8,128)(2,1)S(1)}, bf16[48,1024]{1,0:T(8,128)(2,1)S(1)}, u32[]{:S(2)}, u32[]{:S(2)}) %collective-permute-start.22) | collective-permute-done | bytes 98336 | tf_op jit(solution)/shard_map/ppermute | solution.py:597
  86.7 4.0 %gate_up.2 = (bf16[96,3712]{1,0:T(8,128)(2,1)S(1)}, bf16[48,3712]{1,0:T(8,128)(2,1)S(1)}, bf16[48,3712]{1,0:T(8,128)(2,1)S(1)}) custom-call(s32[1]{0:T(128)} %bitcast.3.spot_ref, f32[1,1024]{1,0:T(1,128)S(1)} %bitcast.5, bf16[1024,1792]{1,0:T(8,128)(2,1)} %gate_ref.3, bf16[1024,1792]{1,0:T(8,128)(2,1)} %up_ref.3, ...), custom_call_target="tpu_custom_call" | custom-call | flops 1409286144 | bytes 7340032 | tf_op jit(solution)/shard_map/gate_up/pallas_call | solution.py:488
  91.3 1.2 collective-permute-done.23.low_ref
  93.3 1.6 %collective-permute-start.27 = (bf16[48,3712]{1,0:T(8,128)(2,1)S(1)}, bf16[48,3712]{1,0:T(8,128)(2,1)S(1)}, u32[]{:S(2)}, u32[]{:S(2)}) collective-permute-start(bf16[48,3712]{1,0:T(8,128)(2,1)S(1)} %get-tuple-element.81), channel_id=1, source_target_pairs={{0,2},{1,3},{2,0},{3,1},{4,6},{5,7},{6,4},{7,5},{8,10},{9,11},{10,... | collective-permute-start | bytes 1069064 | tf_op jit(solution)/shard_map/ppermute | solution.py:597
  94.9 2.0 %collective-permute-start.25 = (bf16[48,1024]{1,0:T(8,128)(2,1)S(1)}, bf16[48,1024]{1,0:T(8,128)(2,1)S(1)}, u32[]{:S(2)}, u32[]{:S(2)}) collective-permute-start(bf16[48,1024]{1,0:T(8,128)(2,1)S(1)} %collective-permute-done.18.refs_0_), channel_id=1, source_target_pairs={{0,4},{4,0},{8,12},{12,8},{16,20},{20,16},{24,28},{28,24},{1,5},{5... | collective-permute-start | bytes 294920 | tf_op jit(solution)/shard_map/ppermute | solution.py:597
  96.9 3.6 %collective-permute-done.26.refs_3_ = bf16[48,1024]{1,0:T(8,128)(2,1)S(1)} collective-permute-done((bf16[48,1024]{1,0:T(8,128)(2,1)S(1)}, bf16[48,1024]{1,0:T(8,128)(2,1)S(1)}, u32[]{:S(2)}, u32[]{:S(2)}) %collective-permute-start.26) | collective-permute-done | bytes 98336 | tf_op jit(solution)/shard_map/ppermute | solution.py:597
  100.5 1.1 collective-permute-done.25.refs_1_
  101.5 4.0 %gate_up.3 = (bf16[96,3712]{1,0:T(8,128)(2,1)S(1)}, bf16[48,3712]{1,0:T(8,128)(2,1)S(1)}, bf16[48,3712]{1,0:T(8,128)(2,1)S(1)}) custom-call(s32[1]{0:T(128)} %bitcast.3.spot_ref, f32[1,1024]{1,0:T(1,128)S(1)} %bitcast.6, bf16[1024,1792]{1,0:T(8,128)(2,1)} %gate_ref.3, bf16[1024,1792]{1,0:T(8,128)(2,1)} %up_ref.3, ...), custom_call_target="tpu_custom_call" | custom-call | flops 1409286144 | bytes 7340032 | tf_op jit(solution)/shard_map/gate_up/pallas_call | solution.py:488
  106.8 4.4 %collective-permute-done.28.refs_1_ = bf16[48,1792]{1,0:T(8,128)(2,1)S(1)} collective-permute-done((bf16[48,1792]{1,0:T(8,128)(2,1)S(1)}, bf16[48,1792]{1,0:T(8,128)(2,1)S(1)}, u32[]{:S(2)}, u32[]{:S(2)}) %collective-permute-start.28) | collective-permute-done | bytes 172064 | tf_op jit(solution)/shard_map/ppermute | solution.py:597
  113.0 0.9 down.2
  114.5 8.0 %collective-permute-done.35.got_ref = bf16[48,3712]{1,0:T(8,128)(2,1)S(1)} collective-permute-done((bf16[48,3712]{1,0:T(8,128)(2,1)S(1)}, bf16[48,3712]{1,0:T(8,128)(2,1)S(1)}, u32[]{:S(2)}, u32[]{:S(2)}) %collective-permute-start.35) | collective-permute-done | bytes 356384 | tf_op jit(solution)/shard_map/ppermute | solution.py:597
  123.9 4.9 %collective-permute-done.36.refs_1_ = bf16[48,1792]{1,0:T(8,128)(2,1)S(1)} collective-permute-done((bf16[48,1792]{1,0:T(8,128)(2,1)S(1)}, bf16[48,1792]{1,0:T(8,128)(2,1)S(1)}, u32[]{:S(2)}, u32[]{:S(2)}) %collective-permute-start.36) | collective-permute-done | bytes 172064 | tf_op jit(solution)/shard_map/ppermute | solution.py:597
  128.8 0.9 collective-permute-done.31
  129.8 1.6 %collective-permute-done.37.refs_2_ = bf16[96,1792]{1,0:T(8,128)(2,1)S(1)} collective-permute-done((bf16[96,1792]{1,0:T(8,128)(2,1)S(1)}, bf16[96,1792]{1,0:T(8,128)(2,1)S(1)}, u32[]{:S(2)}, u32[]{:S(2)}) %collective-permute-start.37) | collective-permute-done | bytes 344096 | tf_op jit(solution)/shard_map/ppermute | solution.py:597
  131.5 1.0 down.3
  132.4 1.6 %collective-permute-start.38 = (bf16[48,1024]{1,0:T(8,128)(2,1)S(1)}, bf16[48,1024]{1,0:T(8,128)(2,1)S(1)}, u32[]{:S(2)}, u32[]{:S(2)}) collective-permute-start(bf16[48,1024]{1,0:T(8,128)(2,1)S(1)} %get-tuple-element.97), channel_id=1, source_target_pairs={{0,4},{4,0},{8,12},{12,8},{16,20},{20,16},{24,28},{28,24},{1,5},{5... | collective-permute-start | bytes 294920 | tf_op jit(solution)/shard_map/ppermute | solution.py:597
  134.5 3.6 %collective-permute-done.38 = bf16[48,1024]{1,0:T(8,128)(2,1)S(1)} collective-permute-done((bf16[48,1024]{1,0:T(8,128)(2,1)S(1)}, bf16[48,1024]{1,0:T(8,128)(2,1)S(1)}, u32[]{:S(2)}, u32[]{:S(2)}) %collective-permute-start.38) | collective-permute-done | bytes 98336 | tf_op jit(solution)/shard_map/ppermute | solution.py:597
  138.2 2.2 %collective-permute-start.39 = (bf16[48,1024]{1,0:T(8,128)(2,1)S(1)}, bf16[48,1024]{1,0:T(8,128)(2,1)S(1)}, u32[]{:S(2)}, u32[]{:S(2)}) collective-permute-start(bf16[48,1024]{1,0:T(8,128)(2,1)S(1)} %add_convert_fusion.2), channel_id=1, source_target_pairs={{0,24},{4,28},{8,16},{12,20},{16,8},{20,12},{24,0},{28,4},{1,25},{... | collective-permute-start | bytes 294920 | tf_op jit(solution)/shard_map/ppermute | solution.py:597
  141.2 3.6 %collective-permute-done.39 = bf16[48,1024]{1,0:T(8,128)(2,1)S(1)} collective-permute-done((bf16[48,1024]{1,0:T(8,128)(2,1)S(1)}, bf16[48,1024]{1,0:T(8,128)(2,1)S(1)}, u32[]{:S(2)}, u32[]{:S(2)}) %collective-permute-start.39) | collective-permute-done | bytes 98336 | tf_op jit(solution)/shard_map/ppermute | solution.py:597
  144.7 1.0 collective-permute-done.41
  (71 shorter events, 13.1 us)
Async XLA Ops:
  0.6 10.4 %collective-permute-start.5 = (bf16[48,1024]{1,0:T(8,128)(2,1)}, bf16[48,1024]{1,0:T(8,128)(2,1)S(1)}, u32[]{:S(2)}, u32[]{:S(2)}) collective-permute-start(bf16[48,1024]{1,0:T(8,128)(2,1)} %refs_0_.5), channel_id=1, source_target_pairs={{0,24},{4,28},{8,16},{12,20},{16,8},{20,12},{24,0},{28,4},{1,25},{... | collective-permute-start | bytes 294920 | tf_op jit(solution)/shard_map/ppermute | solution.py:597
  5.7 8.5 %collective-permute-start.3 = (bf16[48,1024]{1,0:T(8,128)(2,1)}, bf16[48,1024]{1,0:T(8,128)(2,1)S(1)}, u32[]{:S(2)}, u32[]{:S(2)}) collective-permute-start(bf16[48,1024]{1,0:T(8,128)(2,1)} %refs_0_.5), channel_id=1, source_target_pairs={{0,16},{4,20},{8,24},{12,28},{16,0},{20,4},{24,8},{28,12},{1,17},{... | collective-permute-start | bytes 294920 | tf_op jit(solution)/shard_map/ppermute | solution.py:597
  5.8 10.0 %collective-permute-start.1 = (bf16[48,1024]{1,0:T(8,128)(2,1)}, bf16[48,1024]{1,0:T(8,128)(2,1)S(1)}, u32[]{:S(2)}, u32[]{:S(2)}) collective-permute-start(bf16[48,1024]{1,0:T(8,128)(2,1)} %refs_0_.5), channel_id=1, source_target_pairs={{0,8},{4,12},{8,0},{12,4},{16,24},{20,28},{24,16},{28,20},{1,9},{5... | collective-permute-start | bytes 294920 | tf_op jit(solution)/shard_map/ppermute | solution.py:597
  6.4 9.9 %collective-permute-start = (bf16[48,1024]{1,0:T(8,128)(2,1)}, bf16[48,1024]{1,0:T(8,128)(2,1)S(1)}, u32[]{:S(2)}, u32[]{:S(2)}) collective-permute-start(bf16[48,1024]{1,0:T(8,128)(2,1)} %refs_0_.5), channel_id=1, source_target_pairs={{0,4},{4,0},{8,12},{12,8},{16,20},{20,16},{24,28},{28,24},{1,5},{5... | collective-permute-start | bytes 294920 | tf_op jit(solution)/shard_map/ppermute | solution.py:597
  11.1 5.2 %collective-permute-start.6 = (bf16[48,1024]{1,0:T(8,128)(2,1)S(1)}, bf16[48,1024]{1,0:T(8,128)(2,1)S(1)}, u32[]{:S(2)}, u32[]{:S(2)}) collective-permute-start(bf16[48,1024]{1,0:T(8,128)(2,1)S(1)} %collective-permute-done.5.refs_6_), channel_id=1, source_target_pairs={{0,4},{4,0},{8,12},{12,8},{16,20},{20,16},{24,28},{28,24},{1,5},{5... | collective-permute-start | bytes 294920 | tf_op jit(solution)/shard_map/ppermute | solution.py:597
  14.2 5.1 %collective-permute-start.4 = (bf16[48,1024]{1,0:T(8,128)(2,1)S(1)}, bf16[48,1024]{1,0:T(8,128)(2,1)S(1)}, u32[]{:S(2)}, u32[]{:S(2)}) collective-permute-start(bf16[48,1024]{1,0:T(8,128)(2,1)S(1)} %collective-permute-done.3.refs_4_), channel_id=1, source_target_pairs={{0,4},{4,0},{8,12},{12,8},{16,20},{20,16},{24,28},{28,24},{1,5},{5... | collective-permute-start | bytes 294920 | tf_op jit(solution)/shard_map/ppermute | solution.py:597
  15.7 4.6 %collective-permute-start.2 = (bf16[48,1024]{1,0:T(8,128)(2,1)S(1)}, bf16[48,1024]{1,0:T(8,128)(2,1)S(1)}, u32[]{:S(2)}, u32[]{:S(2)}) collective-permute-start(bf16[48,1024]{1,0:T(8,128)(2,1)S(1)} %collective-permute-done.1.refs_2_), channel_id=1, source_target_pairs={{0,4},{4,0},{8,12},{12,8},{16,20},{20,16},{24,28},{28,24},{1,5},{5... | collective-permute-start | bytes 294920 | tf_op jit(solution)/shard_map/ppermute | solution.py:597
  20.3 0.9 copy-start.1
  21.2 0.7 copy-start.2
  29.8 15.7 %collective-permute-start.7 = (bf16[4,48,640]{2,1,0:T(8,128)(2,1)S(1)}, bf16[4,48,640]{2,1,0:T(8,128)(2,1)S(1)}, u32[]{:S(2)}, u32[]{:S(2)}) collective-permute-start(bf16[4,48,640]{2,1,0:T(8,128)(2,1)S(1)} %get-tuple-element.55), channel_id=1, source_target_pairs={{0,4},{4,0},{8,12},{12,8},{16,20},{20,16},{24,28},{28,24},{1,5},{5... | collective-permute-start | bytes 737288 | tf_op jit(solution)/shard_map/ppermute | solution.py:597
  42.2 10.2 %collective-permute-start.11 = (bf16[4,48,640]{2,1,0:T(8,128)(2,1)S(1)}, bf16[4,48,640]{2,1,0:T(8,128)(2,1)S(1)}, u32[]{:S(2)}, u32[]{:S(2)}) collective-permute-start(bf16[4,48,640]{2,1,0:T(8,128)(2,1)S(1)} %get-tuple-element.62), channel_id=1, source_target_pairs={{0,4},{4,0},{8,12},{12,8},{16,20},{20,16},{24,28},{28,24},{1,5},{5... | collective-permute-start | bytes 737288 | tf_op jit(solution)/shard_map/ppermute | solution.py:597
  46.3 10.9 %collective-permute-start.8 = (bf16[48,640]{1,0:T(8,128)(2,1)S(1)}, bf16[48,640]{1,0:T(8,128)(2,1)S(1)}, u32[]{:S(2)}, u32[]{:S(2)}) collective-permute-start(bf16[48,640]{1,0:T(8,128)(2,1)S(1)} %get-tuple-element.57), channel_id=1, source_target_pairs={{0,8},{4,12},{8,0},{12,4},{16,24},{20,28},{24,16},{28,20},{1,9},{5... | collective-permute-start | bytes 184328 | tf_op jit(solution)/shard_map/ppermute | solution.py:597
  46.4 12.2 %collective-permute-start.9 = (bf16[48,640]{1,0:T(8,128)(2,1)S(1)}, bf16[48,640]{1,0:T(8,128)(2,1)S(1)}, u32[]{:S(2)}, u32[]{:S(2)}) collective-permute-start(bf16[48,640]{1,0:T(8,128)(2,1)S(1)} %get-tuple-element.58), channel_id=1, source_target_pairs={{0,16},{4,20},{8,24},{12,28},{16,0},{20,4},{24,8},{28,12},{1,17},{... | collective-permute-start | bytes 184328 | tf_op jit(solution)/shard_map/ppermute | solution.py:597
  51.0 7.6 %collective-permute-start.10 = (bf16[48,640]{1,0:T(8,128)(2,1)S(1)}, bf16[48,640]{1,0:T(8,128)(2,1)S(1)}, u32[]{:S(2)}, u32[]{:S(2)}) collective-permute-start(bf16[48,640]{1,0:T(8,128)(2,1)S(1)} %get-tuple-element.59), channel_id=1, source_target_pairs={{0,24},{4,28},{8,16},{12,20},{16,8},{20,12},{24,0},{28,4},{1,25},{... | collective-permute-start | bytes 184328 | tf_op jit(solution)/shard_map/ppermute | solution.py:597
  53.2 7.9 %collective-permute-start.12 = (bf16[48,640]{1,0:T(8,128)(2,1)S(1)}, bf16[48,640]{1,0:T(8,128)(2,1)S(1)}, u32[]{:S(2)}, u32[]{:S(2)}) collective-permute-start(bf16[48,640]{1,0:T(8,128)(2,1)S(1)} %get-tuple-element.64), channel_id=1, source_target_pairs={{0,8},{4,12},{8,0},{12,4},{16,24},{20,28},{24,16},{28,20},{1,9},{5... | collective-permute-start | bytes 184328 | tf_op jit(solution)/shard_map/ppermute | solution.py:597
  53.9 7.3 %collective-permute-start.13 = (bf16[48,640]{1,0:T(8,128)(2,1)S(1)}, bf16[48,640]{1,0:T(8,128)(2,1)S(1)}, u32[]{:S(2)}, u32[]{:S(2)}) collective-permute-start(bf16[48,640]{1,0:T(8,128)(2,1)S(1)} %get-tuple-element.65), channel_id=1, source_target_pairs={{0,16},{4,20},{8,24},{12,28},{16,0},{20,4},{24,8},{28,12},{1,17},{... | collective-permute-start | bytes 184328 | tf_op jit(solution)/shard_map/ppermute | solution.py:597
  57.2 6.1 %collective-permute-start.14 = (bf16[48,640]{1,0:T(8,128)(2,1)S(1)}, bf16[48,640]{1,0:T(8,128)(2,1)S(1)}, u32[]{:S(2)}, u32[]{:S(2)}) collective-permute-start(bf16[48,640]{1,0:T(8,128)(2,1)S(1)} %get-tuple-element.66), channel_id=1, source_target_pairs={{0,24},{4,28},{8,16},{12,20},{16,8},{20,12},{24,0},{28,4},{1,25},{... | collective-permute-start | bytes 184328 | tf_op jit(solution)/shard_map/ppermute | solution.py:597
  63.3 8.9 %copy-start.4 = (bf16[48,1024]{1,0:T(8,128)(2,1)S(1)}, bf16[48,1024]{1,0:T(8,128)(2,1)}, u32[]{:S(2)}) copy-start(bf16[48,1024]{1,0:T(8,128)(2,1)} %param.32) | copy-start | bytes 294916
  63.3 23.4 %copy-start.3 = (f32[1024]{0:T(1024)S(1)}, f32[1024]{0:T(1024)}, u32[]{:S(2)}) copy-start(f32[1024]{0:T(1024)} %param.34) | copy-start | bytes 12292
  65.9 1.4 collective-permute-start.15
  66.0 2.9 %collective-permute-start.17 = (bf16[48,1024]{1,0:T(8,128)(2,1)S(1)}, bf16[48,1024]{1,0:T(8,128)(2,1)S(1)}, u32[]{:S(2)}, u32[]{:S(2)}) collective-permute-start(bf16[48,1024]{1,0:T(8,128)(2,1)S(1)} %get-tuple-element.75), channel_id=1, source_target_pairs={{0,1},{1,0},{2,3},{3,2},{4,5},{5,4},{6,7},{7,6},{8,9},{9,8},{10,11... | collective-permute-start | bytes 294920 | tf_op jit(solution)/shard_map/ppermute | solution.py:597
  67.3 4.9 %collective-permute-start.16 = (bf16[48,1024]{1,0:T(8,128)(2,1)S(1)}, bf16[48,1024]{1,0:T(8,128)(2,1)S(1)}, u32[]{:S(2)}, u32[]{:S(2)}) collective-permute-start(bf16[48,1024]{1,0:T(8,128)(2,1)S(1)} %add_convert_fusion.5), channel_id=1, source_target_pairs={{0,2},{1,3},{2,0},{3,1},{4,6},{5,7},{6,4},{7,5},{8,10},{9,11},{10,... | collective-permute-start | bytes 294920 | tf_op jit(solution)/shard_map/ppermute | solution.py:597
  72.3 9.8 %collective-permute-start.21 = (bf16[48,1024]{1,0:T(8,128)(2,1)S(1)}, bf16[48,1024]{1,0:T(8,128)(2,1)S(1)}, u32[]{:S(2)}, u32[]{:S(2)}) collective-permute-start(bf16[48,1024]{1,0:T(8,128)(2,1)S(1)} %add_convert_fusion.4.refs_0_), channel_id=1, source_target_pairs={{0,16},{4,20},{8,24},{12,28},{16,0},{20,4},{24,8},{28,12},{1,17},{... | collective-permute-start | bytes 294920 | tf_op jit(solution)/shard_map/ppermute | solution.py:597
  73.3 8.8 %collective-permute-start.19 = (bf16[48,1024]{1,0:T(8,128)(2,1)S(1)}, bf16[48,1024]{1,0:T(8,128)(2,1)S(1)}, u32[]{:S(2)}, u32[]{:S(2)}) collective-permute-start(bf16[48,1024]{1,0:T(8,128)(2,1)S(1)} %add_convert_fusion.4.refs_0_), channel_id=1, source_target_pairs={{0,24},{4,28},{8,16},{12,20},{16,8},{20,12},{24,0},{28,4},{1,25},{... | collective-permute-start | bytes 294920 | tf_op jit(solution)/shard_map/ppermute | solution.py:597
  75.4 7.1 %collective-permute-start.18 = (bf16[48,1024]{1,0:T(8,128)(2,1)S(1)}, bf16[48,1024]{1,0:T(8,128)(2,1)S(1)}, u32[]{:S(2)}, u32[]{:S(2)}) collective-permute-start(bf16[48,1024]{1,0:T(8,128)(2,1)S(1)} %add_convert_fusion.4.refs_0_), channel_id=1, source_target_pairs={{0,8},{4,12},{8,0},{12,4},{16,24},{20,28},{24,16},{28,20},{1,9},{5... | collective-permute-start | bytes 294920 | tf_op jit(solution)/shard_map/ppermute | solution.py:597
  75.8 6.7 %collective-permute-start.20 = (bf16[48,1024]{1,0:T(8,128)(2,1)S(1)}, bf16[48,1024]{1,0:T(8,128)(2,1)S(1)}, u32[]{:S(2)}, u32[]{:S(2)}) collective-permute-start(bf16[48,1024]{1,0:T(8,128)(2,1)S(1)} %add_convert_fusion.4.refs_0_), channel_id=1, source_target_pairs={{0,4},{4,0},{8,12},{12,8},{16,20},{20,16},{24,28},{28,24},{1,5},{5... | collective-permute-start | bytes 294920 | tf_op jit(solution)/shard_map/ppermute | solution.py:597
  82.1 4.6 %collective-permute-start.22 = (bf16[48,1024]{1,0:T(8,128)(2,1)S(1)}, bf16[48,1024]{1,0:T(8,128)(2,1)S(1)}, u32[]{:S(2)}, u32[]{:S(2)}) collective-permute-start(bf16[48,1024]{1,0:T(8,128)(2,1)S(1)} %collective-permute-done.21.refs_2_), channel_id=1, source_target_pairs={{0,4},{4,0},{8,12},{12,8},{16,20},{20,16},{24,28},{28,24},{1,5},{5... | collective-permute-start | bytes 294920 | tf_op jit(solution)/shard_map/ppermute | solution.py:597
  90.7 1.7 %collective-permute-start.23 = (bf16[48,3712]{1,0:T(8,128)(2,1)S(1)}, bf16[48,3712]{1,0:T(8,128)(2,1)S(1)}, u32[]{:S(2)}, u32[]{:S(2)}) collective-permute-start(bf16[48,3712]{1,0:T(8,128)(2,1)S(1)} %get-tuple-element.78), channel_id=1, source_target_pairs={{0,1},{1,0},{2,3},{3,2},{4,5},{5,4},{6,7},{7,6},{8,9},{9,8},{10,11... | collective-permute-start | bytes 1069064 | tf_op jit(solution)/shard_map/ppermute | solution.py:597
  90.8 2.2 %collective-permute-start.24 = (bf16[48,3712]{1,0:T(8,128)(2,1)S(1)}, bf16[48,3712]{1,0:T(8,128)(2,1)S(1)}, u32[]{:S(2)}, u32[]{:S(2)}) collective-permute-start(bf16[48,3712]{1,0:T(8,128)(2,1)S(1)} %get-tuple-element.79), channel_id=1, source_target_pairs={{0,1},{1,0},{2,3},{3,2},{4,5},{5,4},{6,7},{7,6},{8,9},{9,8},{10,11... | collective-permute-start | bytes 1069064 | tf_op jit(solution)/shard_map/ppermute | solution.py:597
  93.3 19.7 %copy-start = (bf16[1792,1024]{1,0:T(8,128)(2,1)S(1)}, bf16[1792,1024]{1,0:T(8,128)(2,1)}, u32[]{:S(2)}) copy-start(bf16[1792,1024]{1,0:T(8,128)(2,1)} %weight_ref.7) | copy-start | bytes 11010052
  93.3 12.2 %collective-permute-start.27 = (bf16[48,3712]{1,0:T(8,128)(2,1)S(1)}, bf16[48,3712]{1,0:T(8,128)(2,1)S(1)}, u32[]{:S(2)}, u32[]{:S(2)}) collective-permute-start(bf16[48,3712]{1,0:T(8,128)(2,1)S(1)} %get-tuple-element.81), channel_id=1, source_target_pairs={{0,2},{1,3},{2,0},{3,1},{4,6},{5,7},{6,4},{7,5},{8,10},{9,11},{10,... | collective-permute-start | bytes 1069064 | tf_op jit(solution)/shard_map/ppermute | solution.py:597
  94.9 5.6 %collective-permute-start.26 = (bf16[48,1024]{1,0:T(8,128)(2,1)S(1)}, bf16[48,1024]{1,0:T(8,128)(2,1)S(1)}, u32[]{:S(2)}, u32[]{:S(2)}) collective-permute-start(bf16[48,1024]{1,0:T(8,128)(2,1)S(1)} %collective-permute-done.19.refs_2_), channel_id=1, source_target_pairs={{0,4},{4,0},{8,12},{12,8},{16,20},{20,16},{24,28},{28,24},{1,5},{5... | collective-permute-start | bytes 294920 | tf_op jit(solution)/shard_map/ppermute | solution.py:597
  94.9 6.7 %collective-permute-start.25 = (bf16[48,1024]{1,0:T(8,128)(2,1)S(1)}, bf16[48,1024]{1,0:T(8,128)(2,1)S(1)}, u32[]{:S(2)}, u32[]{:S(2)}) collective-permute-start(bf16[48,1024]{1,0:T(8,128)(2,1)S(1)} %collective-permute-done.18.refs_0_), channel_id=1, source_target_pairs={{0,4},{4,0},{8,12},{12,8},{16,20},{20,16},{24,28},{28,24},{1,5},{5... | collective-permute-start | bytes 294920 | tf_op jit(solution)/shard_map/ppermute | solution.py:597
  105.8 5.5 %collective-permute-start.28 = (bf16[48,1792]{1,0:T(8,128)(2,1)S(1)}, bf16[48,1792]{1,0:T(8,128)(2,1)S(1)}, u32[]{:S(2)}, u32[]{:S(2)}) collective-permute-start(bf16[48,1792]{1,0:T(8,128)(2,1)S(1)} %gated.2.refs_0_), channel_id=1, source_target_pairs={{0,2},{1,3},{2,0},{3,1},{4,6},{5,7},{6,4},{7,5},{8,10},{9,11},{10,... | collective-permute-start | bytes 516104 | tf_op jit(solution)/shard_map/ppermute | solution.py:597
  106.3 5.0 %collective-permute-start.33 = (bf16[48,3712]{1,0:T(8,128)(2,1)S(1)}, bf16[48,3712]{1,0:T(8,128)(2,1)S(1)}, u32[]{:S(2)}, u32[]{:S(2)}) collective-permute-start(bf16[48,3712]{1,0:T(8,128)(2,1)S(1)} %get-tuple-element.90), channel_id=1, source_target_pairs={{0,1},{1,0},{2,3},{3,2},{4,5},{5,4},{6,7},{7,6},{8,9},{9,8},{10,11... | collective-permute-start | bytes 1069064 | tf_op jit(solution)/shard_map/ppermute | solution.py:597
  106.3 5.0 %collective-permute-start.34 = (bf16[48,3712]{1,0:T(8,128)(2,1)S(1)}, bf16[48,3712]{1,0:T(8,128)(2,1)S(1)}, u32[]{:S(2)}, u32[]{:S(2)}) collective-permute-start(bf16[48,3712]{1,0:T(8,128)(2,1)S(1)} %get-tuple-element.91), channel_id=1, source_target_pairs={{0,1},{1,0},{2,3},{3,2},{4,5},{5,4},{6,7},{7,6},{8,9},{9,8},{10,11... | collective-permute-start | bytes 1069064 | tf_op jit(solution)/shard_map/ppermute | solution.py:597
  111.3 1.7 %collective-permute-start.29 = (bf16[96,1792]{1,0:T(8,128)(2,1)S(1)}, bf16[96,1792]{1,0:T(8,128)(2,1)S(1)}, u32[]{:S(2)}, u32[]{:S(2)}) collective-permute-start(bf16[96,1792]{1,0:T(8,128)(2,1)S(1)} %pad_maximum_fusion), channel_id=1, source_target_pairs={{0,1},{1,0},{2,3},{3,2},{4,5},{5,4},{6,7},{7,6},{8,9},{9,8},{10,11... | collective-permute-start | bytes 1032200 | tf_op jit(solution)/shard_map/ppermute | solution.py:597
  111.7 10.8 %collective-permute-start.35 = (bf16[48,3712]{1,0:T(8,128)(2,1)S(1)}, bf16[48,3712]{1,0:T(8,128)(2,1)S(1)}, u32[]{:S(2)}, u32[]{:S(2)}) collective-permute-start(bf16[48,3712]{1,0:T(8,128)(2,1)S(1)} %get-tuple-element.94), channel_id=1, source_target_pairs={{0,2},{1,3},{2,0},{3,1},{4,6},{5,7},{6,4},{7,5},{8,10},{9,11},{10,... | collective-permute-start | bytes 1069064 | tf_op jit(solution)/shard_map/ppermute | solution.py:597
  113.9 9.8 %collective-permute-start.30 = (bf16[48,1024]{1,0:T(8,128)(2,1)S(1)}, bf16[48,1024]{1,0:T(8,128)(2,1)S(1)}, u32[]{:S(2)}, u32[]{:S(2)}) collective-permute-start(bf16[48,1024]{1,0:T(8,128)(2,1)S(1)} %get-tuple-element.86), channel_id=1, source_target_pairs={{0,4},{4,0},{8,12},{12,8},{16,20},{20,16},{24,28},{28,24},{1,5},{5... | collective-permute-start | bytes 294920 | tf_op jit(solution)/shard_map/ppermute | solution.py:597
  122.7 6.0 %collective-permute-start.36 = (bf16[48,1792]{1,0:T(8,128)(2,1)S(1)}, bf16[48,1792]{1,0:T(8,128)(2,1)S(1)}, u32[]{:S(2)}, u32[]{:S(2)}) collective-permute-start(bf16[48,1792]{1,0:T(8,128)(2,1)S(1)} %gated.3.refs_0_), channel_id=1, source_target_pairs={{0,2},{1,3},{2,0},{3,1},{4,6},{5,7},{6,4},{7,5},{8,10},{9,11},{10,... | collective-permute-start | bytes 516104 | tf_op jit(solution)/shard_map/ppermute | solution.py:597
  123.3 5.5 %collective-permute-start.32 = (bf16[48,1024]{1,0:T(8,128)(2,1)S(1)}, bf16[48,1024]{1,0:T(8,128)(2,1)S(1)}, u32[]{:S(2)}, u32[]{:S(2)}) collective-permute-start(bf16[48,1024]{1,0:T(8,128)(2,1)S(1)} %get-tuple-element.88), channel_id=1, source_target_pairs={{0,4},{4,0},{8,12},{12,8},{16,20},{20,16},{24,28},{28,24},{1,5},{5... | collective-permute-start | bytes 294920 | tf_op jit(solution)/shard_map/ppermute | solution.py:597
  123.8 5.9 %collective-permute-start.31 = (bf16[48,1024]{1,0:T(8,128)(2,1)S(1)}, bf16[48,1024]{1,0:T(8,128)(2,1)S(1)}, u32[]{:S(2)}, u32[]{:S(2)}) collective-permute-start(bf16[48,1024]{1,0:T(8,128)(2,1)S(1)} %add_convert_fusion.3), channel_id=1, source_target_pairs={{0,16},{4,20},{8,24},{12,28},{16,0},{20,4},{24,8},{28,12},{1,17},{... | collective-permute-start | bytes 294920 | tf_op jit(solution)/shard_map/ppermute | solution.py:597
  129.8 1.7 %collective-permute-start.37 = (bf16[96,1792]{1,0:T(8,128)(2,1)S(1)}, bf16[96,1792]{1,0:T(8,128)(2,1)S(1)}, u32[]{:S(2)}, u32[]{:S(2)}) collective-permute-start(bf16[96,1792]{1,0:T(8,128)(2,1)S(1)} %pad_maximum_fusion.1), channel_id=1, source_target_pairs={{0,1},{1,0},{2,3},{3,2},{4,5},{5,4},{6,7},{7,6},{8,9},{9,8},{10,11... | collective-permute-start | bytes 1032200 | tf_op jit(solution)/shard_map/ppermute | solution.py:597
  132.4 5.7 %collective-permute-start.38 = (bf16[48,1024]{1,0:T(8,128)(2,1)S(1)}, bf16[48,1024]{1,0:T(8,128)(2,1)S(1)}, u32[]{:S(2)}, u32[]{:S(2)}) collective-permute-start(bf16[48,1024]{1,0:T(8,128)(2,1)S(1)} %get-tuple-element.97), channel_id=1, source_target_pairs={{0,4},{4,0},{8,12},{12,8},{16,20},{20,16},{24,28},{28,24},{1,5},{5... | collective-permute-start | bytes 294920 | tf_op jit(solution)/shard_map/ppermute | solution.py:597
  134.0 6.4 %collective-permute-start.40 = (bf16[48,1024]{1,0:T(8,128)(2,1)S(1)}, bf16[48,1024]{1,0:T(8,128)(2,1)S(1)}, u32[]{:S(2)}, u32[]{:S(2)}) collective-permute-start(bf16[48,1024]{1,0:T(8,128)(2,1)S(1)} %get-tuple-element.99), channel_id=1, source_target_pairs={{0,4},{4,0},{8,12},{12,8},{16,20},{20,16},{24,28},{28,24},{1,5},{5... | collective-permute-start | bytes 294920 | tf_op jit(solution)/shard_map/ppermute | solution.py:597
  138.2 6.5 %collective-permute-start.39 = (bf16[48,1024]{1,0:T(8,128)(2,1)S(1)}, bf16[48,1024]{1,0:T(8,128)(2,1)S(1)}, u32[]{:S(2)}, u32[]{:S(2)}) collective-permute-start(bf16[48,1024]{1,0:T(8,128)(2,1)S(1)} %add_convert_fusion.2), channel_id=1, source_target_pairs={{0,24},{4,28},{8,16},{12,20},{16,8},{20,12},{24,0},{28,4},{1,25},{... | collective-permute-start | bytes 294920 | tf_op jit(solution)/shard_map/ppermute | solution.py:597
  140.4 5.3 %collective-permute-start.41 = (bf16[48,1024]{1,0:T(8,128)(2,1)S(1)}, bf16[48,1024]{1,0:T(8,128)(2,1)S(1)}, u32[]{:S(2)}, u32[]{:S(2)}) collective-permute-start(bf16[48,1024]{1,0:T(8,128)(2,1)S(1)} %add_convert_fusion.1), channel_id=1, source_target_pairs={{0,8},{4,12},{8,0},{12,4},{16,24},{20,28},{24,16},{28,20},{1,9},{5... | collective-permute-start | bytes 294920 | tf_op jit(solution)/shard_map/ppermute | solution.py:597

commit v7 on v6

--- a/solution.py
+++ b/solution.py
@@ -203,9 +203,6 @@
                     old_peak = peak[:, :every]
                     new_peak = jnp.maximum(old_peak, jnp.max(found, axis=0, keepdims=True))
                     weights = jnp.exp((found - new_peak) * score_scale)
-                    if masked:
-                        position = lax.broadcasted_iota(jnp.int32, (block, every), 0)
-                        weights = jnp.where(position < limits - at, weights, 0.0)
                     fade = jnp.exp((old_peak - new_peak) * score_scale)
                     peak[:, :every] = new_peak
                     total[:, :every] = total[:, :every] * fade + jnp.sum(
@@ -667,7 +664,7 @@
     mlp_total = lax.axis_size("mlp")
     mlp_place = lax.axis_index("mlp").astype(jnp.int32)
     own_width = stream.shape[1]
-    query_parts = gather_parts(queries, "kv", nodes)
+    query_parts = gather_parts(queries, "kv")
     attended, blocks = [], None
     for k in range(kv_count):
         near, far = tree_attention(query_parts, caches, nodes, owner, k)
@@ -707,26 +704,28 @@
     def regather(hidden, token):
         pieces = [hidden]
         for step in reversed(steps):
-            held = pieces[0] if len(pieces) == 1 else jnp.concatenate(pieces, axis=0)
-            if step != steps[-1] and token is not None:
-                held = after(held, token)
-            pieces.append(swap(held, "mlp", step))
+            pieces += [
+                swap(piece if k == 0 or step == steps[-1] else after(piece, token), "mlp", step)
+                for k, piece in enumerate(pieces)
+            ]
         return pieces
 
     def finish(pieces, masks):
         outs = down_rows(pieces, down_weight, spot, len(masks), own_rows, mlp_total)
-        return pair_sums(dict(zip(masks, outs)), "kv")
+        return dict(zip(masks, outs))
 
     keep, send = reduce_once(*multiply(first))
     row_parts[second[0]] = after(row_parts[second[0]], send)
     later = multiply(second)
     hidden = gated(after(keep, later[0]), swap(send, "mlp", steps[-1]), units)
     keep, send = reduce_once(*later, hidden)
-    pairs = finish(regather(hidden, None), first)
+    pairs = pair_sums(finish(regather(hidden, send), first), "kv")
     keep = after(keep, pairs[0])
     hidden = gated(keep, swap(send, "mlp", steps[-1]), units)
     mixed = far_sum(pairs, "kv")
-    mixed = mixed + far_sum(finish(regather(hidden, mixed), second), "kv")
+    late = finish(regather(hidden, mixed), second)
+    for mask in sorted(late, reverse=True):
+        mixed = mixed + swap(late[mask], "kv", mask).astype(jnp.float32)
     return (jnp.concatenate(attended, axis=1), mixed.astype(jnp.bfloat16))
 
 

time: 148 us -> 141 us (0.953)
  waiting for transfers between devices: 58 us -> 47.4 us
  Pallas kernels: 36.7 us -> 40.4 us
    ppermute x42 -> x44, waiting for transfers between devices: 58 us -> 47.4 us  [swap(): lax.ppermute(value, axis_name, [(j, j ^ mask) for j in range(axis_total)])]
    pallas_call x2, Pallas kernels: 16 us -> 19.6 us  [tree_attention(): pl.pallas_call(kernel, out_shape=[jax.ShapeDtypeStruct((part_total // 2,...]
    ppermute x42 -> x44, starting transfers between devices: 47.6 us -> 47.6 us  [swap(): lax.ppermute(value, axis_name, [(j, j ^ mask) for j in range(axis_total)])]
  transfers between devices with their start and end apart: 42 -> 44, of which waited for: 22 -> 17; matrix products, arithmetic and copies ran while one was open for 1% -> 1% of each run, Pallas kernels for 14% -> 16%
where the time goes in v7:
time: 141 us; the launch traced here: 139 us
  starting transfers between devices  47.6 us (34%)
  waiting for transfers between devices  47.4 us (34%)
  Pallas kernels  40.4 us (29%)
  local copies, waits for them, and re-layouts  1.59 us (1%)
  other arithmetic  1.51 us (1%)
    ppermute x44, starting transfers between devices, swap(): lax.ppermute(value, axis_name, [(j, j ^ mask) for j in range(axis_total)])  47.6 us
    ppermute x44, waiting for transfers between devices, swap(): lax.ppermute(value, axis_name, [(j, j ^ mask) for j in range(axis_total)])  47.4 us
    pallas_call x2, Pallas kernels, tree_attention(): pl.pallas_call(kernel, out_shape=[jax.ShapeDtypeStruct((part_total // 2,...  19.6 us
    pallas_call x2, Pallas kernels, gate_up_rows(): pl.pallas_call(kernel, out_shape=[jax.ShapeDtypeStruct((half, 2 * units +...  7.95 us
    pallas_call x2, Pallas kernels, combine_project(): pl.pallas_call(kernel, out_shape=[jax.ShapeDtypeStruct((own_rows, width),...  5.08 us
    pallas_call x1, Pallas kernels, own_nodes(): pl.pallas_call(kernel, out_shape=jax.ShapeDtypeStruct((3, node_total), jn...  3.03 us
  transfers between devices with their start and end apart: 44, of which 17 were waited for; matrix products, arithmetic and copies ran while one was open for 1% of the time, Pallas kernels for 16%

profile of v7, /device:TPU:0, one launch (start us, length us, event | category | flops | bytes accessed | tf_op | source)
XLA Modules:
  0.0 139.3 jit_solution(18108952075822589108)
XLA Ops:
  0.6 3.1 %collective-permute-start.1 = (bf16[48,1024]{1,0:T(8,128)(2,1)}, bf16[48,1024]{1,0:T(8,128)(2,1)S(1)}, u32[]{:S(2)}, u32[]{:S(2)}) collective-permute-start(bf16[48,1024]{1,0:T(8,128)(2,1)} %refs_0_.5), channel_id=1, source_target_pairs={{0,8},{4,12},{8,0},{12,4},{16,24},{20,28},{24,16},{28,20},{1,9},{5... | collective-permute-start | bytes 294920 | tf_op jit(solution)/shard_map/ppermute | solution.py:594
  3.7 2.6 %collective-permute-start.3 = (bf16[48,1024]{1,0:T(8,128)(2,1)}, bf16[48,1024]{1,0:T(8,128)(2,1)S(1)}, u32[]{:S(2)}, u32[]{:S(2)}) collective-permute-start(bf16[48,1024]{1,0:T(8,128)(2,1)} %refs_0_.5), channel_id=1, source_target_pairs={{0,16},{4,20},{8,24},{12,28},{16,0},{20,4},{24,8},{28,12},{1,17},{... | collective-permute-start | bytes 294920 | tf_op jit(solution)/shard_map/ppermute | solution.py:594
  6.3 1.7 %collective-permute-start = (bf16[48,1024]{1,0:T(8,128)(2,1)}, bf16[48,1024]{1,0:T(8,128)(2,1)S(1)}, u32[]{:S(2)}, u32[]{:S(2)}) collective-permute-start(bf16[48,1024]{1,0:T(8,128)(2,1)} %refs_0_.5), channel_id=1, source_target_pairs={{0,4},{4,0},{8,12},{12,8},{16,20},{20,16},{24,28},{28,24},{1,5},{5... | collective-permute-start | bytes 294920 | tf_op jit(solution)/shard_map/ppermute | solution.py:594
  8.5 5.9 %collective-permute-done.3.refs_4_ = bf16[48,1024]{1,0:T(8,128)(2,1)S(1)} collective-permute-done((bf16[48,1024]{1,0:T(8,128)(2,1)}, bf16[48,1024]{1,0:T(8,128)(2,1)S(1)}, u32[]{:S(2)}, u32[]{:S(2)}) %collective-permute-start.3) | collective-permute-done | bytes 98336 | tf_op jit(solution)/shard_map/ppermute | solution.py:594
  14.4 1.5 %collective-permute-start.4 = (bf16[48,1024]{1,0:T(8,128)(2,1)S(1)}, bf16[48,1024]{1,0:T(8,128)(2,1)S(1)}, u32[]{:S(2)}, u32[]{:S(2)}) collective-permute-start(bf16[48,1024]{1,0:T(8,128)(2,1)S(1)} %collective-permute-done.3.refs_4_), channel_id=1, source_target_pairs={{0,4},{4,0},{8,12},{12,8},{16,20},{20,16},{24,28},{28,24},{1,5},{5... | collective-permute-start | bytes 294920 | tf_op jit(solution)/shard_map/ppermute | solution.py:594
  16.4 3.0 %own_nodes.1.nodes_ref = s32[3,7]{1,0:T(4,128)} custom-call(s32[1]{0:T(128)} %bitcast.1.owner_ref, s32[3,128]{1,0:T(4,128)} %bitcast.7, s32[32]{0:T(128)} %leaf_up.1, s32[16]{0:T(128)} %mid_up.1, s32[8]{0:T(128)} %refs_0_.3, s32[16]{0:T(128)} %refs_1_.1, s32[32]{0:T(128)} %refs_2_.1, s32[8]{0:T(128)} %refs_3_.1, s32[16]{0:T(128)} %refs_4_.1, s32[32]{0:T(128)} %refs_5_.1), custom_call_target="tpu_custom_call" | custom-call | tf_op jit(solution)/shard_map/own_nodes/pallas_call | solution.py:84
  19.5 1.0 collective-permute-done.6.refs_7_
  22.1 9.7 %tree_attention.2 = (bf16[4,48,640]{2,1,0:T(8,128)(2,1)S(1)}, bf16[4,48,640]{2,1,0:T(8,128)(2,1)S(1)}) custom-call(s32[3,7]{1,0:T(4,128)S(1)} %copy-done.2, s32[1]{0:T(128)} %bitcast.1.owner_ref, bf16[48,1024]{1,0:T(8,128)(2,1)S(1)} %copy-done.1, bf16[48,1024]{1,0:T(8,128)(2,1)S(1)} %collective-permute-done.refs_1_, ...), custom_call_target="tpu_custom_call" | custom-call | flops 2147483648 | bytes 6291456 | tf_op jit(solution)/shard_map/tree_attention/pallas_call | solution.py:268
  31.9 9.9 %tree_attention.3 = (bf16[4,48,640]{2,1,0:T(8,128)(2,1)S(1)}, bf16[4,48,640]{2,1,0:T(8,128)(2,1)S(1)}) custom-call(s32[3,7]{1,0:T(4,128)S(1)} %copy-done.2, s32[1]{0:T(128)} %bitcast.1.owner_ref, bf16[48,1024]{1,0:T(8,128)(2,1)S(1)} %copy-done.1, bf16[48,1024]{1,0:T(8,128)(2,1)S(1)} %collective-permute-done.refs_1_, ...), custom_call_target="tpu_custom_call" | custom-call | flops 2147483648 | bytes 6291456 | tf_op jit(solution)/shard_map/tree_attention/pallas_call | solution.py:268
  43.3 1.8 %collective-permute-start.8 = (bf16[48,640]{1,0:T(8,128)(2,1)S(1)}, bf16[48,640]{1,0:T(8,128)(2,1)S(1)}, u32[]{:S(2)}, u32[]{:S(2)}) collective-permute-start(bf16[48,640]{1,0:T(8,128)(2,1)S(1)} %get-tuple-element.52), channel_id=1, source_target_pairs={{0,8},{4,12},{8,0},{12,4},{16,24},{20,28},{24,16},{28,20},{1,9},{5... | collective-permute-start | bytes 184328 | tf_op jit(solution)/shard_map/ppermute | solution.py:594
  45.1 1.8 %collective-permute-start.9 = (bf16[48,640]{1,0:T(8,128)(2,1)S(1)}, bf16[48,640]{1,0:T(8,128)(2,1)S(1)}, u32[]{:S(2)}, u32[]{:S(2)}) collective-permute-start(bf16[48,640]{1,0:T(8,128)(2,1)S(1)} %get-tuple-element.53), channel_id=1, source_target_pairs={{0,16},{4,20},{8,24},{12,28},{16,0},{20,4},{24,8},{28,12},{1,17},{... | collective-permute-start | bytes 184328 | tf_op jit(solution)/shard_map/ppermute | solution.py:594
  46.9 1.4 collective-permute-start.10
  49.1 1.6 %collective-permute-start.12 = (bf16[48,640]{1,0:T(8,128)(2,1)S(1)}, bf16[48,640]{1,0:T(8,128)(2,1)S(1)}, u32[]{:S(2)}, u32[]{:S(2)}) collective-permute-start(bf16[48,640]{1,0:T(8,128)(2,1)S(1)} %get-tuple-element.59), channel_id=1, source_target_pairs={{0,8},{4,12},{8,0},{12,4},{16,24},{20,28},{24,16},{28,20},{1,9},{5... | collective-permute-start | bytes 184328 | tf_op jit(solution)/shard_map/ppermute | solution.py:594
  50.7 2.3 %collective-permute-start.13 = (bf16[48,640]{1,0:T(8,128)(2,1)S(1)}, bf16[48,640]{1,0:T(8,128)(2,1)S(1)}, u32[]{:S(2)}, u32[]{:S(2)}) collective-permute-start(bf16[48,640]{1,0:T(8,128)(2,1)S(1)} %get-tuple-element.60), channel_id=1, source_target_pairs={{0,16},{4,20},{8,24},{12,28},{16,0},{20,4},{24,8},{28,12},{1,17},{... | collective-permute-start | bytes 184328 | tf_op jit(solution)/shard_map/ppermute | solution.py:594
  53.0 1.4 collective-permute-start.14
  54.4 2.5 %combine_project.2 = (bf16[48,512]{1,0:T(8,128)(2,1)S(1)}, f32[48,1024]{1,0:T(8,128)S(1)}, f32[48,1024]{1,0:T(8,128)S(1)}, f32[48,1024]{1,0:T(8,128)S(1)}, f32[48,1024]{1,0:T(8,128)S(1)}) custom-call(s32[1]{0:T(128)} %bitcast.place_ref, bf16[1024,4096]{1,0:T(8,128)(2,1)} %weight_ref.5, bf16[48,640]{1,0:T(8,128)(2,1)S(1)} %get-tuple-element.51.refs_0_, ...), custom_call_target="tpu_custom_call" | custom-call | flops 201326592 | bytes 4194304 | tf_op jit(solution)/shard_map/combine_project/pallas_call | solution.py:406
  57.0 2.2 %collective-permute-done.14.refs_3_ = bf16[48,640]{1,0:T(8,128)(2,1)S(1)} collective-permute-done((bf16[48,640]{1,0:T(8,128)(2,1)S(1)}, bf16[48,640]{1,0:T(8,128)(2,1)S(1)}, u32[]{:S(2)}, u32[]{:S(2)}) %collective-permute-start.14) | collective-permute-done | bytes 61472 | tf_op jit(solution)/shard_map/ppermute | solution.py:594
  59.2 2.6 %combine_project.3 = (bf16[48,512]{1,0:T(8,128)(2,1)S(1)}, bf16[48,1024]{1,0:T(8,128)(2,1)S(1)}, bf16[48,1024]{1,0:T(8,128)(2,1)S(1)}, bf16[48,1024]{1,0:T(8,128)(2,1)S(1)}, bf16[48,1024]{1,0:T(8,128)(2,1)S(1)}) custom-call(s32[1]{0:T(128)} %bitcast.place_ref, bf16[1024,4096]{1,0:T(8,128)(2,1)} %weight_ref.5, bf16[48,640]{1,0:T(8,128)(2,1)S(1)} %get-tuple-element.58.refs_0_, ...), custom_call_target="tpu_custom_call" | custom-call | flops 201326592 | bytes 4194304 | tf_op jit(solution)/shard_map/combine_project/pallas_call | solution.py:406
  63.1 1.6 %collective-permute-start.16 = (bf16[48,1024]{1,0:T(8,128)(2,1)S(1)}, bf16[48,1024]{1,0:T(8,128)(2,1)S(1)}, u32[]{:S(2)}, u32[]{:S(2)}) collective-permute-start(bf16[48,1024]{1,0:T(8,128)(2,1)S(1)} %add_convert_fusion.3), channel_id=1, source_target_pairs={{0,2},{1,3},{2,0},{3,1},{4,6},{5,7},{6,4},{7,5},{8,10},{9,11},{10,... | collective-permute-start | bytes 294920 | tf_op jit(solution)/shard_map/ppermute | solution.py:594
  64.7 3.3 %collective-permute-done.16 = bf16[48,1024]{1,0:T(8,128)(2,1)S(1)} collective-permute-done((bf16[48,1024]{1,0:T(8,128)(2,1)S(1)}, bf16[48,1024]{1,0:T(8,128)(2,1)S(1)}, u32[]{:S(2)}, u32[]{:S(2)}) %collective-permute-start.16) | collective-permute-done | bytes 98336 | tf_op jit(solution)/shard_map/ppermute | solution.py:594
  68.1 1.0 collective-permute-start.21
  69.1 1.0 collective-permute-start.18
  70.1 2.4 %collective-permute-start.19 = (bf16[48,1024]{1,0:T(8,128)(2,1)S(1)}, bf16[48,1024]{1,0:T(8,128)(2,1)S(1)}, u32[]{:S(2)}, u32[]{:S(2)}) collective-permute-start(bf16[48,1024]{1,0:T(8,128)(2,1)S(1)} %add_convert_fusion.2.refs_0_), channel_id=1, source_target_pairs={{0,24},{4,28},{8,16},{12,20},{16,8},{20,12},{24,0},{28,4},{1,25},{... | collective-permute-start | bytes 294920 | tf_op jit(solution)/shard_map/ppermute | solution.py:594
  72.6 1.0 collective-permute-start.20
  73.6 4.4 %collective-permute-done.21.refs_2_ = bf16[48,1024]{1,0:T(8,128)(2,1)S(1)} collective-permute-done((bf16[48,1024]{1,0:T(8,128)(2,1)S(1)}, bf16[48,1024]{1,0:T(8,128)(2,1)S(1)}, u32[]{:S(2)}, u32[]{:S(2)}) %collective-permute-start.21) | collective-permute-done | bytes 98336 | tf_op jit(solution)/shard_map/ppermute | solution.py:594
  78.6 4.0 %collective-permute-done.22.refs_3_ = bf16[48,1024]{1,0:T(8,128)(2,1)S(1)} collective-permute-done((bf16[48,1024]{1,0:T(8,128)(2,1)S(1)}, bf16[48,1024]{1,0:T(8,128)(2,1)S(1)}, u32[]{:S(2)}, u32[]{:S(2)}) %collective-permute-start.22) | collective-permute-done | bytes 98336 | tf_op jit(solution)/shard_map/ppermute | solution.py:594
  82.6 4.0 %gate_up.2 = (bf16[96,3712]{1,0:T(8,128)(2,1)S(1)}, bf16[48,3712]{1,0:T(8,128)(2,1)S(1)}, bf16[48,3712]{1,0:T(8,128)(2,1)S(1)}) custom-call(s32[1]{0:T(128)} %bitcast.3.spot_ref, f32[1,1024]{1,0:T(1,128)S(1)} %bitcast.5, bf16[1024,1792]{1,0:T(8,128)(2,1)} %gate_ref.3, bf16[1024,1792]{1,0:T(8,128)(2,1)} %up_ref.3, ...), custom_call_target="tpu_custom_call" | custom-call | flops 1409286144 | bytes 7340032 | tf_op jit(solution)/shard_map/gate_up/pallas_call | solution.py:485
  87.8 1.4 collective-permute-start.26
  89.5 1.6 %collective-permute-start.27 = (bf16[48,3712]{1,0:T(8,128)(2,1)S(1)}, bf16[48,3712]{1,0:T(8,128)(2,1)S(1)}, u32[]{:S(2)}, u32[]{:S(2)}) collective-permute-start(bf16[48,3712]{1,0:T(8,128)(2,1)S(1)} %get-tuple-element.76), channel_id=1, source_target_pairs={{0,2},{1,3},{2,0},{3,1},{4,6},{5,7},{6,4},{7,5},{8,10},{9,11},{10,... | collective-permute-start | bytes 1069064 | tf_op jit(solution)/shard_map/ppermute | solution.py:594
  91.1 1.7 %collective-permute-done.25.refs_1_ = bf16[48,1024]{1,0:T(8,128)(2,1)S(1)} collective-permute-done((bf16[48,1024]{1,0:T(8,128)(2,1)S(1)}, bf16[48,1024]{1,0:T(8,128)(2,1)S(1)}, u32[]{:S(2)}, u32[]{:S(2)}) %collective-permute-start.25) | collective-permute-done | bytes 98336 | tf_op jit(solution)/shard_map/ppermute | solution.py:594
  92.8 1.2 collective-permute-done.26.refs_3_
  94.0 4.0 %gate_up.3 = (bf16[96,3712]{1,0:T(8,128)(2,1)S(1)}, bf16[48,3712]{1,0:T(8,128)(2,1)S(1)}, bf16[48,3712]{1,0:T(8,128)(2,1)S(1)}) custom-call(s32[1]{0:T(128)} %bitcast.3.spot_ref, f32[1,1024]{1,0:T(1,128)S(1)} %bitcast.6, bf16[1024,1792]{1,0:T(8,128)(2,1)} %gate_ref.3, bf16[1024,1792]{1,0:T(8,128)(2,1)} %up_ref.3, ...), custom_call_target="tpu_custom_call" | custom-call | flops 1409286144 | bytes 7340032 | tf_op jit(solution)/shard_map/gate_up/pallas_call | solution.py:485
  98.6 1.0 collective-permute-done.27.got_ref
  99.8 1.6 %collective-permute-start.28 = (bf16[48,1792]{1,0:T(8,128)(2,1)S(1)}, bf16[48,1792]{1,0:T(8,128)(2,1)S(1)}, u32[]{:S(2)}, u32[]{:S(2)}) collective-permute-start(bf16[48,1792]{1,0:T(8,128)(2,1)S(1)} %gated.2.refs_0_), channel_id=1, source_target_pairs={{0,2},{1,3},{2,0},{3,1},{4,6},{5,7},{6,4},{7,5},{8,10},{9,11},{10,... | collective-permute-start | bytes 516104 | tf_op jit(solution)/shard_map/ppermute | solution.py:594
  101.8 3.5 %collective-permute-done.28.refs_1_ = bf16[48,1792]{1,0:T(8,128)(2,1)S(1)} collective-permute-done((bf16[48,1792]{1,0:T(8,128)(2,1)S(1)}, bf16[48,1792]{1,0:T(8,128)(2,1)S(1)}, u32[]{:S(2)}, u32[]{:S(2)}) %collective-permute-start.28) | collective-permute-done | bytes 172064 | tf_op jit(solution)/shard_map/ppermute | solution.py:594
  105.3 1.4 %collective-permute-done.32.refs_3_ = bf16[48,1792]{1,0:T(8,128)(2,1)S(1)} collective-permute-done((bf16[48,1792]{1,0:T(8,128)(2,1)S(1)}, bf16[48,1792]{1,0:T(8,128)(2,1)S(1)}, u32[]{:S(2)}, u32[]{:S(2)}) %collective-permute-start.32) | collective-permute-done | bytes 172064 | tf_op jit(solution)/shard_map/ppermute | solution.py:594
  106.7 1.0 down.2
  108.4 1.5 %collective-permute-start.36 = (bf16[48,3712]{1,0:T(8,128)(2,1)S(1)}, bf16[48,3712]{1,0:T(8,128)(2,1)S(1)}, u32[]{:S(2)}, u32[]{:S(2)}) collective-permute-start(bf16[48,3712]{1,0:T(8,128)(2,1)S(1)} %get-tuple-element.83), channel_id=1, source_target_pairs={{0,2},{1,3},{2,0},{3,1},{4,6},{5,7},{6,4},{7,5},{8,10},{9,11},{10,... | collective-permute-start | bytes 1069064 | tf_op jit(solution)/shard_map/ppermute | solution.py:594
  109.9 1.4 collective-permute-start.35
  111.3 1.8 %collective-permute-done.33 = bf16[48,1024]{1,0:T(8,128)(2,1)S(1)} collective-permute-done((bf16[48,1024]{1,0:T(8,128)(2,1)S(1)}, bf16[48,1024]{1,0:T(8,128)(2,1)S(1)}, u32[]{:S(2)}, u32[]{:S(2)}) %collective-permute-start.33) | collective-permute-done | bytes 98336 | tf_op jit(solution)/shard_map/ppermute | solution.py:594
  113.2 5.3 %collective-permute-done.36.got_ref = bf16[48,3712]{1,0:T(8,128)(2,1)S(1)} collective-permute-done((bf16[48,3712]{1,0:T(8,128)(2,1)S(1)}, bf16[48,3712]{1,0:T(8,128)(2,1)S(1)}, u32[]{:S(2)}, u32[]{:S(2)}) %collective-permute-start.36) | collective-permute-done | bytes 356384 | tf_op jit(solution)/shard_map/ppermute | solution.py:594
  118.8 1.6 %collective-permute-start.37 = (bf16[48,1792]{1,0:T(8,128)(2,1)S(1)}, bf16[48,1792]{1,0:T(8,128)(2,1)S(1)}, u32[]{:S(2)}, u32[]{:S(2)}) collective-permute-start(bf16[48,1792]{1,0:T(8,128)(2,1)S(1)} %gated.3.refs_0_), channel_id=1, source_target_pairs={{0,2},{1,3},{2,0},{3,1},{4,6},{5,7},{6,4},{7,5},{8,10},{9,11},{10,... | collective-permute-start | bytes 516104 | tf_op jit(solution)/shard_map/ppermute | solution.py:594
  120.4 3.8 %collective-permute-done.37.refs_1_ = bf16[48,1792]{1,0:T(8,128)(2,1)S(1)} collective-permute-done((bf16[48,1792]{1,0:T(8,128)(2,1)S(1)}, bf16[48,1792]{1,0:T(8,128)(2,1)S(1)}, u32[]{:S(2)}, u32[]{:S(2)}) %collective-permute-start.37) | collective-permute-done | bytes 172064 | tf_op jit(solution)/shard_map/ppermute | solution.py:594
  124.2 1.4 %collective-permute-done.39.refs_3_ = bf16[48,1792]{1,0:T(8,128)(2,1)S(1)} collective-permute-done((bf16[48,1792]{1,0:T(8,128)(2,1)S(1)}, bf16[48,1792]{1,0:T(8,128)(2,1)S(1)}, u32[]{:S(2)}, u32[]{:S(2)}) %collective-permute-start.39) | collective-permute-done | bytes 172064 | tf_op jit(solution)/shard_map/ppermute | solution.py:594
  126.7 2.8 %collective-permute-start.42 = (bf16[48,1024]{1,0:T(8,128)(2,1)S(1)}, bf16[48,1024]{1,0:T(8,128)(2,1)S(1)}, u32[]{:S(2)}, u32[]{:S(2)}) collective-permute-start(bf16[48,1024]{1,0:T(8,128)(2,1)S(1)} %get-tuple-element.94), channel_id=1, source_target_pairs={{0,12},{4,8},{8,4},{12,0},{16,28},{20,24},{24,20},{28,16},{1,13},{... | collective-permute-start | bytes 294920 | tf_op jit(solution)/shard_map/ppermute | solution.py:594
  129.5 1.4 collective-permute-start.41
  130.9 2.5 %collective-permute-start.40 = (bf16[48,1024]{1,0:T(8,128)(2,1)S(1)}, bf16[48,1024]{1,0:T(8,128)(2,1)S(1)}, u32[]{:S(2)}, u32[]{:S(2)}) collective-permute-start(bf16[48,1024]{1,0:T(8,128)(2,1)S(1)} %get-tuple-element.92), channel_id=1, source_target_pairs={{0,28},{4,24},{8,20},{12,16},{16,12},{20,8},{24,4},{28,0},{1,29},{... | collective-permute-start | bytes 294920 | tf_op jit(solution)/shard_map/ppermute | solution.py:594
  134.1 4.6 %collective-permute-done.42 = bf16[48,1024]{1,0:T(8,128)(2,1)S(1)} collective-permute-done((bf16[48,1024]{1,0:T(8,128)(2,1)S(1)}, bf16[48,1024]{1,0:T(8,128)(2,1)S(1)}, u32[]{:S(2)}, u32[]{:S(2)}) %collective-permute-start.42) | collective-permute-done | bytes 98336 | tf_op jit(solution)/shard_map/ppermute | solution.py:594
  (71 shorter events, 13.3 us)
Async XLA Ops:
  0.6 7.4 %collective-permute-start.1 = (bf16[48,1024]{1,0:T(8,128)(2,1)}, bf16[48,1024]{1,0:T(8,128)(2,1)S(1)}, u32[]{:S(2)}, u32[]{:S(2)}) collective-permute-start(bf16[48,1024]{1,0:T(8,128)(2,1)} %refs_0_.5), channel_id=1, source_target_pairs={{0,8},{4,12},{8,0},{12,4},{16,24},{20,28},{24,16},{28,20},{1,9},{5... | collective-permute-start | bytes 294920 | tf_op jit(solution)/shard_map/ppermute | solution.py:594
  3.7 10.6 %collective-permute-start.3 = (bf16[48,1024]{1,0:T(8,128)(2,1)}, bf16[48,1024]{1,0:T(8,128)(2,1)S(1)}, u32[]{:S(2)}, u32[]{:S(2)}) collective-permute-start(bf16[48,1024]{1,0:T(8,128)(2,1)} %refs_0_.5), channel_id=1, source_target_pairs={{0,16},{4,20},{8,24},{12,28},{16,0},{20,4},{24,8},{28,12},{1,17},{... | collective-permute-start | bytes 294920 | tf_op jit(solution)/shard_map/ppermute | solution.py:594
  6.3 9.6 %collective-permute-start.5 = (bf16[48,1024]{1,0:T(8,128)(2,1)}, bf16[48,1024]{1,0:T(8,128)(2,1)S(1)}, u32[]{:S(2)}, u32[]{:S(2)}) collective-permute-start(bf16[48,1024]{1,0:T(8,128)(2,1)} %refs_0_.5), channel_id=1, source_target_pairs={{0,24},{4,28},{8,16},{12,20},{16,8},{20,12},{24,0},{28,4},{1,25},{... | collective-permute-start | bytes 294920 | tf_op jit(solution)/shard_map/ppermute | solution.py:594
  6.3 13.1 %collective-permute-start = (bf16[48,1024]{1,0:T(8,128)(2,1)}, bf16[48,1024]{1,0:T(8,128)(2,1)S(1)}, u32[]{:S(2)}, u32[]{:S(2)}) collective-permute-start(bf16[48,1024]{1,0:T(8,128)(2,1)} %refs_0_.5), channel_id=1, source_target_pairs={{0,4},{4,0},{8,12},{12,8},{16,20},{20,16},{24,28},{28,24},{1,5},{5... | collective-permute-start | bytes 294920 | tf_op jit(solution)/shard_map/ppermute | solution.py:594
  8.0 11.4 %collective-permute-start.2 = (bf16[48,1024]{1,0:T(8,128)(2,1)S(1)}, bf16[48,1024]{1,0:T(8,128)(2,1)S(1)}, u32[]{:S(2)}, u32[]{:S(2)}) collective-permute-start(bf16[48,1024]{1,0:T(8,128)(2,1)S(1)} %collective-permute-done.1.refs_2_), channel_id=1, source_target_pairs={{0,4},{4,0},{8,12},{12,8},{16,20},{20,16},{24,28},{28,24},{1,5},{5... | collective-permute-start | bytes 294920 | tf_op jit(solution)/shard_map/ppermute | solution.py:594
  14.4 5.1 %collective-permute-start.4 = (bf16[48,1024]{1,0:T(8,128)(2,1)S(1)}, bf16[48,1024]{1,0:T(8,128)(2,1)S(1)}, u32[]{:S(2)}, u32[]{:S(2)}) collective-permute-start(bf16[48,1024]{1,0:T(8,128)(2,1)S(1)} %collective-permute-done.3.refs_4_), channel_id=1, source_target_pairs={{0,4},{4,0},{8,12},{12,8},{16,20},{20,16},{24,28},{28,24},{1,5},{5... | collective-permute-start | bytes 294920 | tf_op jit(solution)/shard_map/ppermute | solution.py:594
  15.9 4.6 %collective-permute-start.6 = (bf16[48,1024]{1,0:T(8,128)(2,1)S(1)}, bf16[48,1024]{1,0:T(8,128)(2,1)S(1)}, u32[]{:S(2)}, u32[]{:S(2)}) collective-permute-start(bf16[48,1024]{1,0:T(8,128)(2,1)S(1)} %collective-permute-done.5.refs_6_), channel_id=1, source_target_pairs={{0,4},{4,0},{8,12},{12,8},{16,20},{20,16},{24,28},{28,24},{1,5},{5... | collective-permute-start | bytes 294920 | tf_op jit(solution)/shard_map/ppermute | solution.py:594
  20.5 0.9 copy-start.1
  31.8 10.7 %collective-permute-start.7 = (bf16[4,48,640]{2,1,0:T(8,128)(2,1)S(1)}, bf16[4,48,640]{2,1,0:T(8,128)(2,1)S(1)}, u32[]{:S(2)}, u32[]{:S(2)}) collective-permute-start(bf16[4,48,640]{2,1,0:T(8,128)(2,1)S(1)} %get-tuple-element.50), channel_id=1, source_target_pairs={{0,4},{4,0},{8,12},{12,8},{16,20},{20,16},{24,28},{28,24},{1,5},{5... | collective-permute-start | bytes 737288 | tf_op jit(solution)/shard_map/ppermute | solution.py:594
  41.8 6.5 %collective-permute-start.11 = (bf16[4,48,640]{2,1,0:T(8,128)(2,1)S(1)}, bf16[4,48,640]{2,1,0:T(8,128)(2,1)S(1)}, u32[]{:S(2)}, u32[]{:S(2)}) collective-permute-start(bf16[4,48,640]{2,1,0:T(8,128)(2,1)S(1)} %get-tuple-element.57), channel_id=1, source_target_pairs={{0,4},{4,0},{8,12},{12,8},{16,20},{20,16},{24,28},{28,24},{1,5},{5... | collective-permute-start | bytes 737288 | tf_op jit(solution)/shard_map/ppermute | solution.py:594
  43.3 9.8 %collective-permute-start.8 = (bf16[48,640]{1,0:T(8,128)(2,1)S(1)}, bf16[48,640]{1,0:T(8,128)(2,1)S(1)}, u32[]{:S(2)}, u32[]{:S(2)}) collective-permute-start(bf16[48,640]{1,0:T(8,128)(2,1)S(1)} %get-tuple-element.52), channel_id=1, source_target_pairs={{0,8},{4,12},{8,0},{12,4},{16,24},{20,28},{24,16},{28,20},{1,9},{5... | collective-permute-start | bytes 184328 | tf_op jit(solution)/shard_map/ppermute | solution.py:594
  45.1 9.4 %collective-permute-start.9 = (bf16[48,640]{1,0:T(8,128)(2,1)S(1)}, bf16[48,640]{1,0:T(8,128)(2,1)S(1)}, u32[]{:S(2)}, u32[]{:S(2)}) collective-permute-start(bf16[48,640]{1,0:T(8,128)(2,1)S(1)} %get-tuple-element.53), channel_id=1, source_target_pairs={{0,16},{4,20},{8,24},{12,28},{16,0},{20,4},{24,8},{28,12},{1,17},{... | collective-permute-start | bytes 184328 | tf_op jit(solution)/shard_map/ppermute | solution.py:594
  46.9 7.6 %collective-permute-start.10 = (bf16[48,640]{1,0:T(8,128)(2,1)S(1)}, bf16[48,640]{1,0:T(8,128)(2,1)S(1)}, u32[]{:S(2)}, u32[]{:S(2)}) collective-permute-start(bf16[48,640]{1,0:T(8,128)(2,1)S(1)} %get-tuple-element.54), channel_id=1, source_target_pairs={{0,24},{4,28},{8,16},{12,20},{16,8},{20,12},{24,0},{28,4},{1,25},{... | collective-permute-start | bytes 184328 | tf_op jit(solution)/shard_map/ppermute | solution.py:594
  49.1 7.9 %collective-permute-start.12 = (bf16[48,640]{1,0:T(8,128)(2,1)S(1)}, bf16[48,640]{1,0:T(8,128)(2,1)S(1)}, u32[]{:S(2)}, u32[]{:S(2)}) collective-permute-start(bf16[48,640]{1,0:T(8,128)(2,1)S(1)} %get-tuple-element.59), channel_id=1, source_target_pairs={{0,8},{4,12},{8,0},{12,4},{16,24},{20,28},{24,16},{28,20},{1,9},{5... | collective-permute-start | bytes 184328 | tf_op jit(solution)/shard_map/ppermute | solution.py:594
  50.7 6.3 %collective-permute-start.13 = (bf16[48,640]{1,0:T(8,128)(2,1)S(1)}, bf16[48,640]{1,0:T(8,128)(2,1)S(1)}, u32[]{:S(2)}, u32[]{:S(2)}) collective-permute-start(bf16[48,640]{1,0:T(8,128)(2,1)S(1)} %get-tuple-element.60), channel_id=1, source_target_pairs={{0,16},{4,20},{8,24},{12,28},{16,0},{20,4},{24,8},{28,12},{1,17},{... | collective-permute-start | bytes 184328 | tf_op jit(solution)/shard_map/ppermute | solution.py:594
  53.0 6.1 %collective-permute-start.14 = (bf16[48,640]{1,0:T(8,128)(2,1)S(1)}, bf16[48,640]{1,0:T(8,128)(2,1)S(1)}, u32[]{:S(2)}, u32[]{:S(2)}) collective-permute-start(bf16[48,640]{1,0:T(8,128)(2,1)S(1)} %get-tuple-element.61), channel_id=1, source_target_pairs={{0,24},{4,28},{8,16},{12,20},{16,8},{20,12},{24,0},{28,4},{1,25},{... | collective-permute-start | bytes 184328 | tf_op jit(solution)/shard_map/ppermute | solution.py:594
  59.2 8.9 %copy-start.4 = (bf16[48,1024]{1,0:T(8,128)(2,1)S(1)}, bf16[48,1024]{1,0:T(8,128)(2,1)}, u32[]{:S(2)}) copy-start(bf16[48,1024]{1,0:T(8,128)(2,1)} %param.32) | copy-start | bytes 294916
  59.2 23.4 %copy-start.3 = (f32[1024]{0:T(1024)S(1)}, f32[1024]{0:T(1024)}, u32[]{:S(2)}) copy-start(f32[1024]{0:T(1024)} %param.34) | copy-start | bytes 12292
  61.7 1.4 collective-permute-start.15
  61.8 2.9 %collective-permute-start.17 = (bf16[48,1024]{1,0:T(8,128)(2,1)S(1)}, bf16[48,1024]{1,0:T(8,128)(2,1)S(1)}, u32[]{:S(2)}, u32[]{:S(2)}) collective-permute-start(bf16[48,1024]{1,0:T(8,128)(2,1)S(1)} %get-tuple-element.70), channel_id=1, source_target_pairs={{0,1},{1,0},{2,3},{3,2},{4,5},{5,4},{6,7},{7,6},{8,9},{9,8},{10,11... | collective-permute-start | bytes 294920 | tf_op jit(solution)/shard_map/ppermute | solution.py:594
  63.1 4.9 %collective-permute-start.16 = (bf16[48,1024]{1,0:T(8,128)(2,1)S(1)}, bf16[48,1024]{1,0:T(8,128)(2,1)S(1)}, u32[]{:S(2)}, u32[]{:S(2)}) collective-permute-start(bf16[48,1024]{1,0:T(8,128)(2,1)S(1)} %add_convert_fusion.3), channel_id=1, source_target_pairs={{0,2},{1,3},{2,0},{3,1},{4,6},{5,7},{6,4},{7,5},{8,10},{9,11},{10,... | collective-permute-start | bytes 294920 | tf_op jit(solution)/shard_map/ppermute | solution.py:594
  68.1 9.9 %collective-permute-start.21 = (bf16[48,1024]{1,0:T(8,128)(2,1)S(1)}, bf16[48,1024]{1,0:T(8,128)(2,1)S(1)}, u32[]{:S(2)}, u32[]{:S(2)}) collective-permute-start(bf16[48,1024]{1,0:T(8,128)(2,1)S(1)} %add_convert_fusion.2.refs_0_), channel_id=1, source_target_pairs={{0,16},{4,20},{8,24},{12,28},{16,0},{20,4},{24,8},{28,12},{1,17},{... | collective-permute-start | bytes 294920 | tf_op jit(solution)/shard_map/ppermute | solution.py:594
  69.1 9.5 %collective-permute-start.18 = (bf16[48,1024]{1,0:T(8,128)(2,1)S(1)}, bf16[48,1024]{1,0:T(8,128)(2,1)S(1)}, u32[]{:S(2)}, u32[]{:S(2)}) collective-permute-start(bf16[48,1024]{1,0:T(8,128)(2,1)S(1)} %add_convert_fusion.2.refs_0_), channel_id=1, source_target_pairs={{0,8},{4,12},{8,0},{12,4},{16,24},{20,28},{24,16},{28,20},{1,9},{5... | collective-permute-start | bytes 294920 | tf_op jit(solution)/shard_map/ppermute | solution.py:594
  70.1 8.5 %collective-permute-start.19 = (bf16[48,1024]{1,0:T(8,128)(2,1)S(1)}, bf16[48,1024]{1,0:T(8,128)(2,1)S(1)}, u32[]{:S(2)}, u32[]{:S(2)}) collective-permute-start(bf16[48,1024]{1,0:T(8,128)(2,1)S(1)} %add_convert_fusion.2.refs_0_), channel_id=1, source_target_pairs={{0,24},{4,28},{8,16},{12,20},{16,8},{20,12},{24,0},{28,4},{1,25},{... | collective-permute-start | bytes 294920 | tf_op jit(solution)/shard_map/ppermute | solution.py:594
  72.6 6.1 %collective-permute-start.20 = (bf16[48,1024]{1,0:T(8,128)(2,1)S(1)}, bf16[48,1024]{1,0:T(8,128)(2,1)S(1)}, u32[]{:S(2)}, u32[]{:S(2)}) collective-permute-start(bf16[48,1024]{1,0:T(8,128)(2,1)S(1)} %add_convert_fusion.2.refs_0_), channel_id=1, source_target_pairs={{0,4},{4,0},{8,12},{12,8},{16,20},{20,16},{24,28},{28,24},{1,5},{5... | collective-permute-start | bytes 294920 | tf_op jit(solution)/shard_map/ppermute | solution.py:594
  78.0 4.6 %collective-permute-start.22 = (bf16[48,1024]{1,0:T(8,128)(2,1)S(1)}, bf16[48,1024]{1,0:T(8,128)(2,1)S(1)}, u32[]{:S(2)}, u32[]{:S(2)}) collective-permute-start(bf16[48,1024]{1,0:T(8,128)(2,1)S(1)} %collective-permute-done.21.refs_2_), channel_id=1, source_target_pairs={{0,4},{4,0},{8,12},{12,8},{16,20},{20,16},{24,28},{28,24},{1,5},{5... | collective-permute-start | bytes 294920 | tf_op jit(solution)/shard_map/ppermute | solution.py:594
  86.6 2.6 %collective-permute-start.23 = (bf16[48,3712]{1,0:T(8,128)(2,1)S(1)}, bf16[48,3712]{1,0:T(8,128)(2,1)S(1)}, u32[]{:S(2)}, u32[]{:S(2)}) collective-permute-start(bf16[48,3712]{1,0:T(8,128)(2,1)S(1)} %get-tuple-element.73), channel_id=1, source_target_pairs={{0,1},{1,0},{2,3},{3,2},{4,5},{5,4},{6,7},{7,6},{8,9},{9,8},{10,11... | collective-permute-start | bytes 1069064 | tf_op jit(solution)/shard_map/ppermute | solution.py:594
  86.7 2.5 %collective-permute-start.24 = (bf16[48,3712]{1,0:T(8,128)(2,1)S(1)}, bf16[48,3712]{1,0:T(8,128)(2,1)S(1)}, u32[]{:S(2)}, u32[]{:S(2)}) collective-permute-start(bf16[48,3712]{1,0:T(8,128)(2,1)S(1)} %get-tuple-element.74), channel_id=1, source_target_pairs={{0,1},{1,0},{2,3},{3,2},{4,5},{5,4},{6,7},{7,6},{8,9},{9,8},{10,11... | collective-permute-start | bytes 1069064 | tf_op jit(solution)/shard_map/ppermute | solution.py:594
  87.2 5.7 %collective-permute-start.25 = (bf16[48,1024]{1,0:T(8,128)(2,1)S(1)}, bf16[48,1024]{1,0:T(8,128)(2,1)S(1)}, u32[]{:S(2)}, u32[]{:S(2)}) collective-permute-start(bf16[48,1024]{1,0:T(8,128)(2,1)S(1)} %collective-permute-done.18.refs_0_), channel_id=1, source_target_pairs={{0,4},{4,0},{8,12},{12,8},{16,20},{20,16},{24,28},{28,24},{1,5},{5... | collective-permute-start | bytes 294920 | tf_op jit(solution)/shard_map/ppermute | solution.py:594
  87.8 6.2 %collective-permute-start.26 = (bf16[48,1024]{1,0:T(8,128)(2,1)S(1)}, bf16[48,1024]{1,0:T(8,128)(2,1)S(1)}, u32[]{:S(2)}, u32[]{:S(2)}) collective-permute-start(bf16[48,1024]{1,0:T(8,128)(2,1)S(1)} %collective-permute-done.19.refs_2_), channel_id=1, source_target_pairs={{0,4},{4,0},{8,12},{12,8},{16,20},{20,16},{24,28},{28,24},{1,5},{5... | collective-permute-start | bytes 294920 | tf_op jit(solution)/shard_map/ppermute | solution.py:594
  89.5 17.2 %copy-start = (bf16[1792,1024]{1,0:T(8,128)(2,1)S(1)}, bf16[1792,1024]{1,0:T(8,128)(2,1)}, u32[]{:S(2)}) copy-start(bf16[1792,1024]{1,0:T(8,128)(2,1)} %weight_ref.7) | copy-start | bytes 11010052
  89.5 10.1 %collective-permute-start.27 = (bf16[48,3712]{1,0:T(8,128)(2,1)S(1)}, bf16[48,3712]{1,0:T(8,128)(2,1)S(1)}, u32[]{:S(2)}, u32[]{:S(2)}) collective-permute-start(bf16[48,3712]{1,0:T(8,128)(2,1)S(1)} %get-tuple-element.76), channel_id=1, source_target_pairs={{0,2},{1,3},{2,0},{3,1},{4,6},{5,7},{6,4},{7,5},{8,10},{9,11},{10,... | collective-permute-start | bytes 1069064 | tf_op jit(solution)/shard_map/ppermute | solution.py:594
  98.0 3.4 %collective-permute-start.30 = (bf16[48,3712]{1,0:T(8,128)(2,1)S(1)}, bf16[48,3712]{1,0:T(8,128)(2,1)S(1)}, u32[]{:S(2)}, u32[]{:S(2)}) collective-permute-start(bf16[48,3712]{1,0:T(8,128)(2,1)S(1)} %get-tuple-element.81), channel_id=1, source_target_pairs={{0,1},{1,0},{2,3},{3,2},{4,5},{5,4},{6,7},{7,6},{8,9},{9,8},{10,11... | collective-permute-start | bytes 1069064 | tf_op jit(solution)/shard_map/ppermute | solution.py:594
  98.1 3.3 %collective-permute-start.31 = (bf16[48,3712]{1,0:T(8,128)(2,1)S(1)}, bf16[48,3712]{1,0:T(8,128)(2,1)S(1)}, u32[]{:S(2)}, u32[]{:S(2)}) collective-permute-start(bf16[48,3712]{1,0:T(8,128)(2,1)S(1)} %get-tuple-element.82), channel_id=1, source_target_pairs={{0,1},{1,0},{2,3},{3,2},{4,5},{5,4},{6,7},{7,6},{8,9},{9,8},{10,11... | collective-permute-start | bytes 1069064 | tf_op jit(solution)/shard_map/ppermute | solution.py:594
  99.8 5.5 %collective-permute-start.28 = (bf16[48,1792]{1,0:T(8,128)(2,1)S(1)}, bf16[48,1792]{1,0:T(8,128)(2,1)S(1)}, u32[]{:S(2)}, u32[]{:S(2)}) collective-permute-start(bf16[48,1792]{1,0:T(8,128)(2,1)S(1)} %gated.2.refs_0_), channel_id=1, source_target_pairs={{0,2},{1,3},{2,0},{3,1},{4,6},{5,7},{6,4},{7,5},{8,10},{9,11},{10,... | collective-permute-start | bytes 516104 | tf_op jit(solution)/shard_map/ppermute | solution.py:594
  101.4 3.9 %collective-permute-start.29 = (bf16[48,1792]{1,0:T(8,128)(2,1)S(1)}, bf16[48,1792]{1,0:T(8,128)(2,1)S(1)}, u32[]{:S(2)}, u32[]{:S(2)}) collective-permute-start(bf16[48,1792]{1,0:T(8,128)(2,1)S(1)} %gated.2.refs_0_), channel_id=1, source_target_pairs={{0,1},{1,0},{2,3},{3,2},{4,5},{5,4},{6,7},{7,6},{8,9},{9,8},{10,11... | collective-permute-start | bytes 516104 | tf_op jit(solution)/shard_map/ppermute | solution.py:594
  105.3 1.4 %collective-permute-start.32 = (bf16[48,1792]{1,0:T(8,128)(2,1)S(1)}, bf16[48,1792]{1,0:T(8,128)(2,1)S(1)}, u32[]{:S(2)}, u32[]{:S(2)}) collective-permute-start(bf16[48,1792]{1,0:T(8,128)(2,1)S(1)} %collective-permute-done.28.refs_1_), channel_id=1, source_target_pairs={{0,1},{1,0},{2,3},{3,2},{4,5},{5,4},{6,7},{7,6},{8,9},{9,8},{10,11... | collective-permute-start | bytes 516104 | tf_op jit(solution)/shard_map/ppermute | solution.py:594
  107.7 5.4 %collective-permute-start.33 = (bf16[48,1024]{1,0:T(8,128)(2,1)S(1)}, bf16[48,1024]{1,0:T(8,128)(2,1)S(1)}, u32[]{:S(2)}, u32[]{:S(2)}) collective-permute-start(bf16[48,1024]{1,0:T(8,128)(2,1)S(1)} %get-tuple-element.86), channel_id=1, source_target_pairs={{0,4},{4,0},{8,12},{12,8},{16,20},{20,16},{24,28},{28,24},{1,5},{5... | collective-permute-start | bytes 294920 | tf_op jit(solution)/shard_map/ppermute | solution.py:594
  108.4 10.1 %collective-permute-start.36 = (bf16[48,3712]{1,0:T(8,128)(2,1)S(1)}, bf16[48,3712]{1,0:T(8,128)(2,1)S(1)}, u32[]{:S(2)}, u32[]{:S(2)}) collective-permute-start(bf16[48,3712]{1,0:T(8,128)(2,1)S(1)} %get-tuple-element.83), channel_id=1, source_target_pairs={{0,2},{1,3},{2,0},{3,1},{4,6},{5,7},{6,4},{7,5},{8,10},{9,11},{10,... | collective-permute-start | bytes 1069064 | tf_op jit(solution)/shard_map/ppermute | solution.py:594
  109.9 10.4 %collective-permute-start.35 = (bf16[48,1024]{1,0:T(8,128)(2,1)S(1)}, bf16[48,1024]{1,0:T(8,128)(2,1)S(1)}, u32[]{:S(2)}, u32[]{:S(2)}) collective-permute-start(bf16[48,1024]{1,0:T(8,128)(2,1)S(1)} %get-tuple-element.88), channel_id=1, source_target_pairs={{0,4},{4,0},{8,12},{12,8},{16,20},{20,16},{24,28},{28,24},{1,5},{5... | collective-permute-start | bytes 294920 | tf_op jit(solution)/shard_map/ppermute | solution.py:594
  113.2 7.2 %collective-permute-start.34 = (bf16[48,1024]{1,0:T(8,128)(2,1)S(1)}, bf16[48,1024]{1,0:T(8,128)(2,1)S(1)}, u32[]{:S(2)}, u32[]{:S(2)}) collective-permute-start(bf16[48,1024]{1,0:T(8,128)(2,1)S(1)} %add_convert_fusion.1), channel_id=1, source_target_pairs={{0,16},{4,20},{8,24},{12,28},{16,0},{20,4},{24,8},{28,12},{1,17},{... | collective-permute-start | bytes 294920 | tf_op jit(solution)/shard_map/ppermute | solution.py:594
  118.8 5.5 %collective-permute-start.37 = (bf16[48,1792]{1,0:T(8,128)(2,1)S(1)}, bf16[48,1792]{1,0:T(8,128)(2,1)S(1)}, u32[]{:S(2)}, u32[]{:S(2)}) collective-permute-start(bf16[48,1792]{1,0:T(8,128)(2,1)S(1)} %gated.3.refs_0_), channel_id=1, source_target_pairs={{0,2},{1,3},{2,0},{3,1},{4,6},{5,7},{6,4},{7,5},{8,10},{9,11},{10,... | collective-permute-start | bytes 516104 | tf_op jit(solution)/shard_map/ppermute | solution.py:594
  120.3 3.9 %collective-permute-start.38 = (bf16[48,1792]{1,0:T(8,128)(2,1)S(1)}, bf16[48,1792]{1,0:T(8,128)(2,1)S(1)}, u32[]{:S(2)}, u32[]{:S(2)}) collective-permute-start(bf16[48,1792]{1,0:T(8,128)(2,1)S(1)} %gated.3.refs_0_), channel_id=1, source_target_pairs={{0,1},{1,0},{2,3},{3,2},{4,5},{5,4},{6,7},{7,6},{8,9},{9,8},{10,11... | collective-permute-start | bytes 516104 | tf_op jit(solution)/shard_map/ppermute | solution.py:594
  124.2 1.4 %collective-permute-start.39 = (bf16[48,1792]{1,0:T(8,128)(2,1)S(1)}, bf16[48,1792]{1,0:T(8,128)(2,1)S(1)}, u32[]{:S(2)}, u32[]{:S(2)}) collective-permute-start(bf16[48,1792]{1,0:T(8,128)(2,1)S(1)} %collective-permute-done.37.refs_1_), channel_id=1, source_target_pairs={{0,1},{1,0},{2,3},{3,2},{4,5},{5,4},{6,7},{7,6},{8,9},{9,8},{10,11... | collective-permute-start | bytes 516104 | tf_op jit(solution)/shard_map/ppermute | solution.py:594
  126.6 7.5 %collective-permute-start.43 = (bf16[48,1024]{1,0:T(8,128)(2,1)S(1)}, bf16[48,1024]{1,0:T(8,128)(2,1)S(1)}, u32[]{:S(2)}, u32[]{:S(2)}) collective-permute-start(bf16[48,1024]{1,0:T(8,128)(2,1)S(1)} %get-tuple-element.95), channel_id=1, source_target_pairs={{0,8},{4,12},{8,0},{12,4},{16,24},{20,28},{24,16},{28,20},{1,9},{5... | collective-permute-start | bytes 294920 | tf_op jit(solution)/shard_map/ppermute | solution.py:594
  126.7 12.0 %collective-permute-start.42 = (bf16[48,1024]{1,0:T(8,128)(2,1)S(1)}, bf16[48,1024]{1,0:T(8,128)(2,1)S(1)}, u32[]{:S(2)}, u32[]{:S(2)}) collective-permute-start(bf16[48,1024]{1,0:T(8,128)(2,1)S(1)} %get-tuple-element.94), channel_id=1, source_target_pairs={{0,12},{4,8},{8,4},{12,0},{16,28},{20,24},{24,20},{28,16},{1,13},{... | collective-permute-start | bytes 294920 | tf_op jit(solution)/shard_map/ppermute | solution.py:594
  129.5 9.1 %collective-permute-start.41 = (bf16[48,1024]{1,0:T(8,128)(2,1)S(1)}, bf16[48,1024]{1,0:T(8,128)(2,1)S(1)}, u32[]{:S(2)}, u32[]{:S(2)}) collective-permute-start(bf16[48,1024]{1,0:T(8,128)(2,1)S(1)} %get-tuple-element.93), channel_id=1, source_target_pairs={{0,24},{4,28},{8,16},{12,20},{16,8},{20,12},{24,0},{28,4},{1,25},{... | collective-permute-start | bytes 294920 | tf_op jit(solution)/shard_map/ppermute | solution.py:594
  130.9 7.8 %collective-permute-start.40 = (bf16[48,1024]{1,0:T(8,128)(2,1)S(1)}, bf16[48,1024]{1,0:T(8,128)(2,1)S(1)}, u32[]{:S(2)}, u32[]{:S(2)}) collective-permute-start(bf16[48,1024]{1,0:T(8,128)(2,1)S(1)} %get-tuple-element.92), channel_id=1, source_target_pairs={{0,28},{4,24},{8,20},{12,16},{16,12},{20,8},{24,4},{28,0},{1,29},{... | collective-permute-start | bytes 294920 | tf_op jit(solution)/shard_map/ppermute | solution.py:594
  (1 other events, 0.7 us)

commit v8 on v7

--- a/solution.py
+++ b/solution.py
@@ -606,26 +606,6 @@
         held = parts[mask] if token is None or mask == 0 else after(parts[mask], token)
         parts[mask + 1] = swap(held, axis_name, 1)
     return parts
-
-
-def pair_sums(parts, axis_name):
-    evens = sorted((mask for mask in parts if mask % 2 == 0), reverse=True)
-    got = {mask: swap(parts[mask + 1], axis_name, 1) for mask in evens}
-    pairs = {
-        mask: parts[mask].astype(jnp.float32) + got[mask].astype(jnp.float32) for mask in evens
-    }
-    return {mask: pair.astype(jnp.bfloat16) if mask else pair for mask, pair in pairs.items()}
-
-
-def far_sum(pairs, axis_name):
-    summed = 0.0
-    for mask, pair in pairs.items():
-        summed = summed + (swap(pair, axis_name, mask).astype(jnp.float32) if mask else pair)
-    return summed
-
-
-def scatter_sum(parts, axis_name):
-    return far_sum(pair_sums(parts, axis_name), axis_name)
 
 
 def shards(
@@ -674,7 +654,9 @@
             every, out_weight, k * group_width, blocks, mlp_place, own_width
         )
         attended.append(one)
-    projected = scatter_sum(dict(enumerate(blocks)), "mlp")
+    projected = blocks[0].astype(jnp.float32)
+    for mask in range(mlp_total - 1, 0, -1):
+        projected = projected + swap(blocks[mask], "mlp", mask).astype(jnp.float32)
     residual = (stream.astype(jnp.float32) + projected).astype(jnp.bfloat16)
     steps = [1 << bit for bit in range(mlp_total.bit_length() - 1)]
     spot = jnp.int32(0)
@@ -719,10 +701,12 @@
     later = multiply(second)
     hidden = gated(after(keep, later[0]), swap(send, "mlp", steps[-1]), units)
     keep, send = reduce_once(*later, hidden)
-    pairs = pair_sums(finish(regather(hidden, send), first), "kv")
-    keep = after(keep, pairs[0])
+    early = finish(regather(hidden, send), first)
+    keep = after(keep, early[0])
     hidden = gated(keep, swap(send, "mlp", steps[-1]), units)
-    mixed = far_sum(pairs, "kv")
+    mixed = early[0].astype(jnp.float32)
+    for mask in first[:0:-1]:
+        mixed = mixed + swap(early[mask], "kv", mask).astype(jnp.float32)
     late = finish(regather(hidden, mixed), second)
     for mask in sorted(late, reverse=True):
         mixed = mixed + swap(late[mask], "kv", mask).astype(jnp.float32)

time: 141 us -> 139 us (0.986); the launches traced: 139 us -> 140 us
  starting transfers between devices: 47.6 us -> 55.3 us
  waiting for transfers between devices: 47.4 us -> 43.3 us
  Pallas kernels: 40.4 us -> 37.4 us
    ppermute x44, starting transfers between devices: 47.6 us -> 55.3 us  [swap(): lax.ppermute(value, axis_name, [(j, j ^ mask) for j in range(axis_total)])]
    ppermute x44, waiting for transfers between devices: 47.4 us -> 43.3 us  [swap(): lax.ppermute(value, axis_name, [(j, j ^ mask) for j in range(axis_total)])]
    pallas_call x2, Pallas kernels: 19.6 us -> 16.6 us  [tree_attention(): pl.pallas_call(kernel, out_shape=[jax.ShapeDtypeStruct((part_total // 2,...]
  transfers between devices with their start and end apart: 44 -> 44, of which waited for: 17 -> 19; matrix products, arithmetic and copies ran while one was open for 1% -> 0% of each run, Pallas kernels for 16% -> 16%
where the time goes in v8:
time: 139 us; the launch traced here: 140 us
  starting transfers between devices  55.3 us (40%)
  waiting for transfers between devices  43.3 us (31%)
  Pallas kernels  37.4 us (27%)
  local copies, waits for them, and re-layouts  1.59 us (1%)
  other arithmetic  1.48 us (1%)
    ppermute x44, starting transfers between devices, swap(): lax.ppermute(value, axis_name, [(j, j ^ mask) for j in range(axis_total)])  55.3 us
    ppermute x44, waiting for transfers between devices, swap(): lax.ppermute(value, axis_name, [(j, j ^ mask) for j in range(axis_total)])  43.3 us
    pallas_call x2, Pallas kernels, tree_attention(): pl.pallas_call(kernel, out_shape=[jax.ShapeDtypeStruct((part_total // 2,...  16.6 us
    pallas_call x2, Pallas kernels, gate_up_rows(): pl.pallas_call(kernel, out_shape=[jax.ShapeDtypeStruct((half, 2 * units +...  7.95 us
    pallas_call x2, Pallas kernels, combine_project(): pl.pallas_call(kernel, out_shape=[jax.ShapeDtypeStruct((own_rows, width),...  5.08 us
    pallas_call x1, Pallas kernels, own_nodes(): pl.pallas_call(kernel, out_shape=jax.ShapeDtypeStruct((3, node_total), jn...  3.03 us
  transfers between devices with their start and end apart: 44, of which 19 were waited for; matrix products, arithmetic and copies ran while one was open for 0% of the time, Pallas kernels for 16%

profile of v8, /device:TPU:0, one launch (start us, length us, event | category | flops | bytes accessed | tf_op | source)
XLA Modules:
  0.0 139.9 jit_solution(4157756605712281609)
XLA Ops:
  0.6 3.1 %collective-permute-start.1 = (bf16[48,1024]{1,0:T(8,128)(2,1)}, bf16[48,1024]{1,0:T(8,128)(2,1)S(1)}, u32[]{:S(2)}, u32[]{:S(2)}) collective-permute-start(bf16[48,1024]{1,0:T(8,128)(2,1)} %refs_0_.5), channel_id=1, source_target_pairs={{0,8},{4,12},{8,0},{12,4},{16,24},{20,28},{24,16},{28,20},{1,9},{5... | collective-permute-start | bytes 294920 | tf_op jit(solution)/shard_map/ppermute | solution.py:594
  3.7 2.6 %collective-permute-start.3 = (bf16[48,1024]{1,0:T(8,128)(2,1)}, bf16[48,1024]{1,0:T(8,128)(2,1)S(1)}, u32[]{:S(2)}, u32[]{:S(2)}) collective-permute-start(bf16[48,1024]{1,0:T(8,128)(2,1)} %refs_0_.5), channel_id=1, source_target_pairs={{0,16},{4,20},{8,24},{12,28},{16,0},{20,4},{24,8},{28,12},{1,17},{... | collective-permute-start | bytes 294920 | tf_op jit(solution)/shard_map/ppermute | solution.py:594
  6.3 1.7 %collective-permute-start = (bf16[48,1024]{1,0:T(8,128)(2,1)}, bf16[48,1024]{1,0:T(8,128)(2,1)S(1)}, u32[]{:S(2)}, u32[]{:S(2)}) collective-permute-start(bf16[48,1024]{1,0:T(8,128)(2,1)} %refs_0_.5), channel_id=1, source_target_pairs={{0,4},{4,0},{8,12},{12,8},{16,20},{20,16},{24,28},{28,24},{1,5},{5... | collective-permute-start | bytes 294920 | tf_op jit(solution)/shard_map/ppermute | solution.py:594
  8.5 5.9 %collective-permute-done.3.refs_4_ = bf16[48,1024]{1,0:T(8,128)(2,1)S(1)} collective-permute-done((bf16[48,1024]{1,0:T(8,128)(2,1)}, bf16[48,1024]{1,0:T(8,128)(2,1)S(1)}, u32[]{:S(2)}, u32[]{:S(2)}) %collective-permute-start.3) | collective-permute-done | bytes 98336 | tf_op jit(solution)/shard_map/ppermute | solution.py:594
  14.4 1.5 %collective-permute-start.4 = (bf16[48,1024]{1,0:T(8,128)(2,1)S(1)}, bf16[48,1024]{1,0:T(8,128)(2,1)S(1)}, u32[]{:S(2)}, u32[]{:S(2)}) collective-permute-start(bf16[48,1024]{1,0:T(8,128)(2,1)S(1)} %collective-permute-done.3.refs_4_), channel_id=1, source_target_pairs={{0,4},{4,0},{8,12},{12,8},{16,20},{20,16},{24,28},{28,24},{1,5},{5... | collective-permute-start | bytes 294920 | tf_op jit(solution)/shard_map/ppermute | solution.py:594
  16.4 3.0 %own_nodes.1.nodes_ref = s32[3,7]{1,0:T(4,128)} custom-call(s32[1]{0:T(128)} %bitcast.1.owner_ref, s32[3,128]{1,0:T(4,128)} %bitcast.7, s32[32]{0:T(128)} %leaf_up.1, s32[16]{0:T(128)} %mid_up.1, s32[8]{0:T(128)} %refs_0_.3, s32[16]{0:T(128)} %refs_1_.1, s32[32]{0:T(128)} %refs_2_.1, s32[8]{0:T(128)} %refs_3_.1, s32[16]{0:T(128)} %refs_4_.1, s32[32]{0:T(128)} %refs_5_.1), custom_call_target="tpu_custom_call" | custom-call | tf_op jit(solution)/shard_map/own_nodes/pallas_call | solution.py:84
  19.5 1.0 collective-permute-done.6.refs_7_
  22.1 8.2 %tree_attention.2 = (bf16[4,48,640]{2,1,0:T(8,128)(2,1)S(1)}, bf16[4,48,640]{2,1,0:T(8,128)(2,1)S(1)}) custom-call(s32[3,7]{1,0:T(4,128)S(1)} %copy-done.2, s32[1]{0:T(128)} %bitcast.1.owner_ref, bf16[48,1024]{1,0:T(8,128)(2,1)S(1)} %copy-done.1, bf16[48,1024]{1,0:T(8,128)(2,1)S(1)} %collective-permute-done.refs_1_, ...), custom_call_target="tpu_custom_call" | custom-call | flops 2147483648 | bytes 6291456 | tf_op jit(solution)/shard_map/tree_attention/pallas_call | solution.py:268
  30.3 1.2 collective-permute-start.7
  31.5 8.4 %tree_attention.3 = (bf16[4,48,640]{2,1,0:T(8,128)(2,1)S(1)}, bf16[4,48,640]{2,1,0:T(8,128)(2,1)S(1)}) custom-call(s32[3,7]{1,0:T(4,128)S(1)} %copy-done.2, s32[1]{0:T(128)} %bitcast.1.owner_ref, bf16[48,1024]{1,0:T(8,128)(2,1)S(1)} %copy-done.1, bf16[48,1024]{1,0:T(8,128)(2,1)S(1)} %collective-permute-done.refs_1_, ...), custom_call_target="tpu_custom_call" | custom-call | flops 2147483648 | bytes 6291456 | tf_op jit(solution)/shard_map/tree_attention/pallas_call | solution.py:268
  39.9 1.0 collective-permute-start.11
  42.2 9.0 %collective-permute-start.9 = (bf16[48,640]{1,0:T(8,128)(2,1)S(1)}, bf16[48,640]{1,0:T(8,128)(2,1)S(1)}, u32[]{:S(2)}, u32[]{:S(2)}) collective-permute-start(bf16[48,640]{1,0:T(8,128)(2,1)S(1)} %get-tuple-element.53), channel_id=1, source_target_pairs={{0,16},{4,20},{8,24},{12,28},{16,0},{20,4},{24,8},{28,12},{1,17},{... | collective-permute-start | bytes 184328 | tf_op jit(solution)/shard_map/ppermute | solution.py:594
  52.7 4.7 %collective-permute-start.13 = (bf16[48,640]{1,0:T(8,128)(2,1)S(1)}, bf16[48,640]{1,0:T(8,128)(2,1)S(1)}, u32[]{:S(2)}, u32[]{:S(2)}) collective-permute-start(bf16[48,640]{1,0:T(8,128)(2,1)S(1)} %get-tuple-element.60), channel_id=1, source_target_pairs={{0,16},{4,20},{8,24},{12,28},{16,0},{20,4},{24,8},{28,12},{1,17},{... | collective-permute-start | bytes 184328 | tf_op jit(solution)/shard_map/ppermute | solution.py:594
  57.4 2.5 %combine_project.2 = (bf16[48,512]{1,0:T(8,128)(2,1)S(1)}, f32[48,1024]{1,0:T(8,128)S(1)}, f32[48,1024]{1,0:T(8,128)S(1)}, f32[48,1024]{1,0:T(8,128)S(1)}, f32[48,1024]{1,0:T(8,128)S(1)}) custom-call(s32[1]{0:T(128)} %bitcast.place_ref, bf16[1024,4096]{1,0:T(8,128)(2,1)} %weight_ref.5, bf16[48,640]{1,0:T(8,128)(2,1)S(1)} %get-tuple-element.51.refs_0_, ...), custom_call_target="tpu_custom_call" | custom-call | flops 201326592 | bytes 4194304 | tf_op jit(solution)/shard_map/combine_project/pallas_call | solution.py:406
  60.2 3.2 %collective-permute-done.14.refs_3_ = bf16[48,640]{1,0:T(8,128)(2,1)S(1)} collective-permute-done((bf16[48,640]{1,0:T(8,128)(2,1)S(1)}, bf16[48,640]{1,0:T(8,128)(2,1)S(1)}, u32[]{:S(2)}, u32[]{:S(2)}) %collective-permute-start.14) | collective-permute-done | bytes 61472 | tf_op jit(solution)/shard_map/ppermute | solution.py:594
  63.4 2.6 %combine_project.3 = (bf16[48,512]{1,0:T(8,128)(2,1)S(1)}, bf16[48,1024]{1,0:T(8,128)(2,1)S(1)}, bf16[48,1024]{1,0:T(8,128)(2,1)S(1)}, bf16[48,1024]{1,0:T(8,128)(2,1)S(1)}, bf16[48,1024]{1,0:T(8,128)(2,1)S(1)}) custom-call(s32[1]{0:T(128)} %bitcast.place_ref, bf16[1024,4096]{1,0:T(8,128)(2,1)} %weight_ref.5, bf16[48,640]{1,0:T(8,128)(2,1)S(1)} %get-tuple-element.58.refs_0_, ...), custom_call_target="tpu_custom_call" | custom-call | flops 201326592 | bytes 4194304 | tf_op jit(solution)/shard_map/combine_project/pallas_call | solution.py:406
  66.0 1.6 %collective-permute-start.16 = (bf16[48,1024]{1,0:T(8,128)(2,1)S(1)}, bf16[48,1024]{1,0:T(8,128)(2,1)S(1)}, u32[]{:S(2)}, u32[]{:S(2)}) collective-permute-start(bf16[48,1024]{1,0:T(8,128)(2,1)S(1)} %get-tuple-element.69), channel_id=1, source_target_pairs={{0,2},{1,3},{2,0},{3,1},{4,6},{5,7},{6,4},{7,5},{8,10},{9,11},{10,... | collective-permute-start | bytes 294920 | tf_op jit(solution)/shard_map/ppermute | solution.py:594
  67.9 3.8 %collective-permute-done.16 = bf16[48,1024]{1,0:T(8,128)(2,1)S(1)} collective-permute-done((bf16[48,1024]{1,0:T(8,128)(2,1)S(1)}, bf16[48,1024]{1,0:T(8,128)(2,1)S(1)}, u32[]{:S(2)}, u32[]{:S(2)}) %collective-permute-start.16) | collective-permute-done | bytes 98336 | tf_op jit(solution)/shard_map/ppermute | solution.py:594
  71.7 1.2 collective-permute-done.15
  73.0 1.2 collective-permute-start.18
  74.2 3.2 %collective-permute-start.19 = (bf16[48,1024]{1,0:T(8,128)(2,1)S(1)}, bf16[48,1024]{1,0:T(8,128)(2,1)S(1)}, u32[]{:S(2)}, u32[]{:S(2)}) collective-permute-start(bf16[48,1024]{1,0:T(8,128)(2,1)S(1)} %add_convert_fusion.1.refs_0_), channel_id=1, source_target_pairs={{0,24},{4,28},{8,16},{12,20},{16,8},{20,12},{24,0},{28,4},{1,25},{... | collective-permute-start | bytes 294920 | tf_op jit(solution)/shard_map/ppermute | solution.py:594
  77.4 1.1 collective-permute-start.20
  78.5 1.5 %collective-permute-done.21.refs_2_ = bf16[48,1024]{1,0:T(8,128)(2,1)S(1)} collective-permute-done((bf16[48,1024]{1,0:T(8,128)(2,1)S(1)}, bf16[48,1024]{1,0:T(8,128)(2,1)S(1)}, u32[]{:S(2)}, u32[]{:S(2)}) %collective-permute-start.21) | collective-permute-done | bytes 98336 | tf_op jit(solution)/shard_map/ppermute | solution.py:594
  80.1 1.1 collective-permute-start.22
  81.2 1.1 collective-permute-done.19.refs_2_
  82.8 1.9 %collective-permute-done.22.refs_3_ = bf16[48,1024]{1,0:T(8,128)(2,1)S(1)} collective-permute-done((bf16[48,1024]{1,0:T(8,128)(2,1)S(1)}, bf16[48,1024]{1,0:T(8,128)(2,1)S(1)}, u32[]{:S(2)}, u32[]{:S(2)}) %collective-permute-start.22) | collective-permute-done | bytes 98336 | tf_op jit(solution)/shard_map/ppermute | solution.py:594
  84.7 4.0 %gate_up.2 = (bf16[96,3712]{1,0:T(8,128)(2,1)S(1)}, bf16[48,3712]{1,0:T(8,128)(2,1)S(1)}, bf16[48,3712]{1,0:T(8,128)(2,1)S(1)}) custom-call(s32[1]{0:T(128)} %bitcast.3.spot_ref, f32[1,1024]{1,0:T(1,128)S(1)} %bitcast.5, bf16[1024,1792]{1,0:T(8,128)(2,1)} %gate_ref.3, bf16[1024,1792]{1,0:T(8,128)(2,1)} %up_ref.3, ...), custom_call_target="tpu_custom_call" | custom-call | flops 1409286144 | bytes 7340032 | tf_op jit(solution)/shard_map/gate_up/pallas_call | solution.py:485
  89.2 1.1 collective-permute-start.25
  91.6 1.6 %collective-permute-start.27 = (bf16[48,3712]{1,0:T(8,128)(2,1)S(1)}, bf16[48,3712]{1,0:T(8,128)(2,1)S(1)}, u32[]{:S(2)}, u32[]{:S(2)}) collective-permute-start(bf16[48,3712]{1,0:T(8,128)(2,1)S(1)} %get-tuple-element.76), channel_id=1, source_target_pairs={{0,2},{1,3},{2,0},{3,1},{4,6},{5,7},{6,4},{7,5},{8,10},{9,11},{10,... | collective-permute-start | bytes 1069064 | tf_op jit(solution)/shard_map/ppermute | solution.py:594
  93.2 1.7 %collective-permute-done.25.refs_1_ = bf16[48,1024]{1,0:T(8,128)(2,1)S(1)} collective-permute-done((bf16[48,1024]{1,0:T(8,128)(2,1)S(1)}, bf16[48,1024]{1,0:T(8,128)(2,1)S(1)}, u32[]{:S(2)}, u32[]{:S(2)}) %collective-permute-start.25) | collective-permute-done | bytes 98336 | tf_op jit(solution)/shard_map/ppermute | solution.py:594
  94.9 1.2 collective-permute-done.26.refs_3_
  96.1 4.0 %gate_up.3 = (bf16[96,3712]{1,0:T(8,128)(2,1)S(1)}, bf16[48,3712]{1,0:T(8,128)(2,1)S(1)}, bf16[48,3712]{1,0:T(8,128)(2,1)S(1)}) custom-call(s32[1]{0:T(128)} %bitcast.3.spot_ref, f32[1,1024]{1,0:T(1,128)S(1)} %bitcast.6, bf16[1024,1792]{1,0:T(8,128)(2,1)} %gate_ref.3, bf16[1024,1792]{1,0:T(8,128)(2,1)} %up_ref.3, ...), custom_call_target="tpu_custom_call" | custom-call | flops 1409286144 | bytes 7340032 | tf_op jit(solution)/shard_map/gate_up/pallas_call | solution.py:485
  100.7 1.0 collective-permute-done.27.got_ref
  101.9 1.6 %collective-permute-start.28 = (bf16[48,1792]{1,0:T(8,128)(2,1)S(1)}, bf16[48,1792]{1,0:T(8,128)(2,1)S(1)}, u32[]{:S(2)}, u32[]{:S(2)}) collective-permute-start(bf16[48,1792]{1,0:T(8,128)(2,1)S(1)} %gated.2.refs_0_), channel_id=1, source_target_pairs={{0,2},{1,3},{2,0},{3,1},{4,6},{5,7},{6,4},{7,5},{8,10},{9,11},{10,... | collective-permute-start | bytes 516104 | tf_op jit(solution)/shard_map/ppermute | solution.py:594
  104.4 4.9 %collective-permute-done.28.refs_1_ = bf16[48,1792]{1,0:T(8,128)(2,1)S(1)} collective-permute-done((bf16[48,1792]{1,0:T(8,128)(2,1)S(1)}, bf16[48,1792]{1,0:T(8,128)(2,1)S(1)}, u32[]{:S(2)}, u32[]{:S(2)}) %collective-permute-start.28) | collective-permute-done | bytes 172064 | tf_op jit(solution)/shard_map/ppermute | solution.py:594
  109.3 1.4 %collective-permute-done.32.refs_3_ = bf16[48,1792]{1,0:T(8,128)(2,1)S(1)} collective-permute-done((bf16[48,1792]{1,0:T(8,128)(2,1)S(1)}, bf16[48,1792]{1,0:T(8,128)(2,1)S(1)}, u32[]{:S(2)}, u32[]{:S(2)}) %collective-permute-start.32) | collective-permute-done | bytes 172064 | tf_op jit(solution)/shard_map/ppermute | solution.py:594
  110.7 1.0 down.2
  111.7 1.2 collective-permute-start.35
  113.2 3.0 %collective-permute-start.33 = (bf16[48,1024]{1,0:T(8,128)(2,1)S(1)}, bf16[48,1024]{1,0:T(8,128)(2,1)S(1)}, u32[]{:S(2)}, u32[]{:S(2)}) collective-permute-start(bf16[48,1024]{1,0:T(8,128)(2,1)S(1)} %get-tuple-element.86), channel_id=1, source_target_pairs={{0,20},{4,16},{8,28},{12,24},{16,4},{20,0},{24,12},{28,8},{1,21},{... | collective-permute-start | bytes 294920 | tf_op jit(solution)/shard_map/ppermute | solution.py:594
  116.4 1.6 %collective-permute-start.37 = (bf16[48,1792]{1,0:T(8,128)(2,1)S(1)}, bf16[48,1792]{1,0:T(8,128)(2,1)S(1)}, u32[]{:S(2)}, u32[]{:S(2)}) collective-permute-start(bf16[48,1792]{1,0:T(8,128)(2,1)S(1)} %gated.3.refs_0_), channel_id=1, source_target_pairs={{0,2},{1,3},{2,0},{3,1},{4,6},{5,7},{6,4},{7,5},{8,10},{9,11},{10,... | collective-permute-start | bytes 516104 | tf_op jit(solution)/shard_map/ppermute | solution.py:594
  118.0 4.5 %collective-permute-done.34 = bf16[48,1024]{1,0:T(8,128)(2,1)S(1)} collective-permute-done((bf16[48,1024]{1,0:T(8,128)(2,1)S(1)}, bf16[48,1024]{1,0:T(8,128)(2,1)S(1)}, u32[]{:S(2)}, u32[]{:S(2)}) %collective-permute-start.34) | collective-permute-done | bytes 98336 | tf_op jit(solution)/shard_map/ppermute | solution.py:594
  122.5 2.4 %collective-permute-done.33 = bf16[48,1024]{1,0:T(8,128)(2,1)S(1)} collective-permute-done((bf16[48,1024]{1,0:T(8,128)(2,1)S(1)}, bf16[48,1024]{1,0:T(8,128)(2,1)S(1)}, u32[]{:S(2)}, u32[]{:S(2)}) %collective-permute-start.33) | collective-permute-done | bytes 98336 | tf_op jit(solution)/shard_map/ppermute | solution.py:594
  125.0 1.4 collective-permute-done.39.refs_3_
  126.4 1.0 down.3
  127.4 2.6 %collective-permute-start.42 = (bf16[48,1024]{1,0:T(8,128)(2,1)S(1)}, bf16[48,1024]{1,0:T(8,128)(2,1)S(1)}, u32[]{:S(2)}, u32[]{:S(2)}) collective-permute-start(bf16[48,1024]{1,0:T(8,128)(2,1)S(1)} %get-tuple-element.94), channel_id=1, source_target_pairs={{0,12},{4,8},{8,4},{12,0},{16,28},{20,24},{24,20},{28,16},{1,13},{... | collective-permute-start | bytes 294920 | tf_op jit(solution)/shard_map/ppermute | solution.py:594
  130.0 1.4 collective-permute-start.41
  131.4 2.8 %collective-permute-start.40 = (bf16[48,1024]{1,0:T(8,128)(2,1)S(1)}, bf16[48,1024]{1,0:T(8,128)(2,1)S(1)}, u32[]{:S(2)}, u32[]{:S(2)}) collective-permute-start(bf16[48,1024]{1,0:T(8,128)(2,1)S(1)} %get-tuple-element.92), channel_id=1, source_target_pairs={{0,28},{4,24},{8,20},{12,16},{16,12},{20,8},{24,4},{28,0},{1,29},{... | collective-permute-start | bytes 294920 | tf_op jit(solution)/shard_map/ppermute | solution.py:594
  134.8 4.3 %collective-permute-done.42 = bf16[48,1024]{1,0:T(8,128)(2,1)S(1)} collective-permute-done((bf16[48,1024]{1,0:T(8,128)(2,1)S(1)}, bf16[48,1024]{1,0:T(8,128)(2,1)S(1)}, u32[]{:S(2)}, u32[]{:S(2)}) %collective-permute-start.42) | collective-permute-done | bytes 98336 | tf_op jit(solution)/shard_map/ppermute | solution.py:594
  (69 shorter events, 12.3 us)
Async XLA Ops:
  0.6 7.4 %collective-permute-start.1 = (bf16[48,1024]{1,0:T(8,128)(2,1)}, bf16[48,1024]{1,0:T(8,128)(2,1)S(1)}, u32[]{:S(2)}, u32[]{:S(2)}) collective-permute-start(bf16[48,1024]{1,0:T(8,128)(2,1)} %refs_0_.5), channel_id=1, source_target_pairs={{0,8},{4,12},{8,0},{12,4},{16,24},{20,28},{24,16},{28,20},{1,9},{5... | collective-permute-start | bytes 294920 | tf_op jit(solution)/shard_map/ppermute | solution.py:594
  3.7 10.6 %collective-permute-start.3 = (bf16[48,1024]{1,0:T(8,128)(2,1)}, bf16[48,1024]{1,0:T(8,128)(2,1)S(1)}, u32[]{:S(2)}, u32[]{:S(2)}) collective-permute-start(bf16[48,1024]{1,0:T(8,128)(2,1)} %refs_0_.5), channel_id=1, source_target_pairs={{0,16},{4,20},{8,24},{12,28},{16,0},{20,4},{24,8},{28,12},{1,17},{... | collective-permute-start | bytes 294920 | tf_op jit(solution)/shard_map/ppermute | solution.py:594
  6.3 9.6 %collective-permute-start.5 = (bf16[48,1024]{1,0:T(8,128)(2,1)}, bf16[48,1024]{1,0:T(8,128)(2,1)S(1)}, u32[]{:S(2)}, u32[]{:S(2)}) collective-permute-start(bf16[48,1024]{1,0:T(8,128)(2,1)} %refs_0_.5), channel_id=1, source_target_pairs={{0,24},{4,28},{8,16},{12,20},{16,8},{20,12},{24,0},{28,4},{1,25},{... | collective-permute-start | bytes 294920 | tf_op jit(solution)/shard_map/ppermute | solution.py:594
  6.3 13.1 %collective-permute-start = (bf16[48,1024]{1,0:T(8,128)(2,1)}, bf16[48,1024]{1,0:T(8,128)(2,1)S(1)}, u32[]{:S(2)}, u32[]{:S(2)}) collective-permute-start(bf16[48,1024]{1,0:T(8,128)(2,1)} %refs_0_.5), channel_id=1, source_target_pairs={{0,4},{4,0},{8,12},{12,8},{16,20},{20,16},{24,28},{28,24},{1,5},{5... | collective-permute-start | bytes 294920 | tf_op jit(solution)/shard_map/ppermute | solution.py:594
  8.0 11.4 %collective-permute-start.2 = (bf16[48,1024]{1,0:T(8,128)(2,1)S(1)}, bf16[48,1024]{1,0:T(8,128)(2,1)S(1)}, u32[]{:S(2)}, u32[]{:S(2)}) collective-permute-start(bf16[48,1024]{1,0:T(8,128)(2,1)S(1)} %collective-permute-done.1.refs_2_), channel_id=1, source_target_pairs={{0,4},{4,0},{8,12},{12,8},{16,20},{20,16},{24,28},{28,24},{1,5},{5... | collective-permute-start | bytes 294920 | tf_op jit(solution)/shard_map/ppermute | solution.py:594
  14.4 5.1 %collective-permute-start.4 = (bf16[48,1024]{1,0:T(8,128)(2,1)S(1)}, bf16[48,1024]{1,0:T(8,128)(2,1)S(1)}, u32[]{:S(2)}, u32[]{:S(2)}) collective-permute-start(bf16[48,1024]{1,0:T(8,128)(2,1)S(1)} %collective-permute-done.3.refs_4_), channel_id=1, source_target_pairs={{0,4},{4,0},{8,12},{12,8},{16,20},{20,16},{24,28},{28,24},{1,5},{5... | collective-permute-start | bytes 294920 | tf_op jit(solution)/shard_map/ppermute | solution.py:594
  15.9 4.6 %collective-permute-start.6 = (bf16[48,1024]{1,0:T(8,128)(2,1)S(1)}, bf16[48,1024]{1,0:T(8,128)(2,1)S(1)}, u32[]{:S(2)}, u32[]{:S(2)}) collective-permute-start(bf16[48,1024]{1,0:T(8,128)(2,1)S(1)} %collective-permute-done.5.refs_6_), channel_id=1, source_target_pairs={{0,4},{4,0},{8,12},{12,8},{16,20},{20,16},{24,28},{28,24},{1,5},{5... | collective-permute-start | bytes 294920 | tf_op jit(solution)/shard_map/ppermute | solution.py:594
  20.5 0.9 copy-start.1
  30.3 10.7 %collective-permute-start.7 = (bf16[4,48,640]{2,1,0:T(8,128)(2,1)S(1)}, bf16[4,48,640]{2,1,0:T(8,128)(2,1)S(1)}, u32[]{:S(2)}, u32[]{:S(2)}) collective-permute-start(bf16[4,48,640]{2,1,0:T(8,128)(2,1)S(1)} %get-tuple-element.50), channel_id=1, source_target_pairs={{0,4},{4,0},{8,12},{12,8},{16,20},{20,16},{24,28},{28,24},{1,5},{5... | collective-permute-start | bytes 737288 | tf_op jit(solution)/shard_map/ppermute | solution.py:594
  39.9 11.3 %collective-permute-start.11 = (bf16[4,48,640]{2,1,0:T(8,128)(2,1)S(1)}, bf16[4,48,640]{2,1,0:T(8,128)(2,1)S(1)}, u32[]{:S(2)}, u32[]{:S(2)}) collective-permute-start(bf16[4,48,640]{2,1,0:T(8,128)(2,1)S(1)} %get-tuple-element.57), channel_id=1, source_target_pairs={{0,4},{4,0},{8,12},{12,8},{16,20},{20,16},{24,28},{28,24},{1,5},{5... | collective-permute-start | bytes 737288 | tf_op jit(solution)/shard_map/ppermute | solution.py:594
  41.8 15.6 %collective-permute-start.8 = (bf16[48,640]{1,0:T(8,128)(2,1)S(1)}, bf16[48,640]{1,0:T(8,128)(2,1)S(1)}, u32[]{:S(2)}, u32[]{:S(2)}) collective-permute-start(bf16[48,640]{1,0:T(8,128)(2,1)S(1)} %get-tuple-element.52), channel_id=1, source_target_pairs={{0,8},{4,12},{8,0},{12,4},{16,24},{20,28},{24,16},{28,20},{1,9},{5... | collective-permute-start | bytes 184328 | tf_op jit(solution)/shard_map/ppermute | solution.py:594
  42.2 15.1 %collective-permute-start.9 = (bf16[48,640]{1,0:T(8,128)(2,1)S(1)}, bf16[48,640]{1,0:T(8,128)(2,1)S(1)}, u32[]{:S(2)}, u32[]{:S(2)}) collective-permute-start(bf16[48,640]{1,0:T(8,128)(2,1)S(1)} %get-tuple-element.53), channel_id=1, source_target_pairs={{0,16},{4,20},{8,24},{12,28},{16,0},{20,4},{24,8},{28,12},{1,17},{... | collective-permute-start | bytes 184328 | tf_op jit(solution)/shard_map/ppermute | solution.py:594
  51.2 6.2 %collective-permute-start.10 = (bf16[48,640]{1,0:T(8,128)(2,1)S(1)}, bf16[48,640]{1,0:T(8,128)(2,1)S(1)}, u32[]{:S(2)}, u32[]{:S(2)}) collective-permute-start(bf16[48,640]{1,0:T(8,128)(2,1)S(1)} %get-tuple-element.54), channel_id=1, source_target_pairs={{0,24},{4,28},{8,16},{12,20},{16,8},{20,12},{24,0},{28,4},{1,25},{... | collective-permute-start | bytes 184328 | tf_op jit(solution)/shard_map/ppermute | solution.py:594
  52.0 7.9 %collective-permute-start.12 = (bf16[48,640]{1,0:T(8,128)(2,1)S(1)}, bf16[48,640]{1,0:T(8,128)(2,1)S(1)}, u32[]{:S(2)}, u32[]{:S(2)}) collective-permute-start(bf16[48,640]{1,0:T(8,128)(2,1)S(1)} %get-tuple-element.59), channel_id=1, source_target_pairs={{0,8},{4,12},{8,0},{12,4},{16,24},{20,28},{24,16},{28,20},{1,9},{5... | collective-permute-start | bytes 184328 | tf_op jit(solution)/shard_map/ppermute | solution.py:594
  52.7 7.5 %collective-permute-start.13 = (bf16[48,640]{1,0:T(8,128)(2,1)S(1)}, bf16[48,640]{1,0:T(8,128)(2,1)S(1)}, u32[]{:S(2)}, u32[]{:S(2)}) collective-permute-start(bf16[48,640]{1,0:T(8,128)(2,1)S(1)} %get-tuple-element.60), channel_id=1, source_target_pairs={{0,16},{4,20},{8,24},{12,28},{16,0},{20,4},{24,8},{28,12},{1,17},{... | collective-permute-start | bytes 184328 | tf_op jit(solution)/shard_map/ppermute | solution.py:594
  57.3 6.0 %collective-permute-start.14 = (bf16[48,640]{1,0:T(8,128)(2,1)S(1)}, bf16[48,640]{1,0:T(8,128)(2,1)S(1)}, u32[]{:S(2)}, u32[]{:S(2)}) collective-permute-start(bf16[48,640]{1,0:T(8,128)(2,1)S(1)} %get-tuple-element.61), channel_id=1, source_target_pairs={{0,24},{4,28},{8,16},{12,20},{16,8},{20,12},{24,0},{28,4},{1,25},{... | collective-permute-start | bytes 184328 | tf_op jit(solution)/shard_map/ppermute | solution.py:594
  63.4 9.5 %copy-start.4 = (bf16[48,1024]{1,0:T(8,128)(2,1)S(1)}, bf16[48,1024]{1,0:T(8,128)(2,1)}, u32[]{:S(2)}) copy-start(bf16[48,1024]{1,0:T(8,128)(2,1)} %param.32) | copy-start | bytes 294916
  63.4 21.3 %copy-start.3 = (f32[1024]{0:T(1024)S(1)}, f32[1024]{0:T(1024)}, u32[]{:S(2)}) copy-start(f32[1024]{0:T(1024)} %param.34) | copy-start | bytes 12292
  65.9 1.9 %collective-permute-start.17 = (bf16[48,1024]{1,0:T(8,128)(2,1)S(1)}, bf16[48,1024]{1,0:T(8,128)(2,1)S(1)}, u32[]{:S(2)}, u32[]{:S(2)}) collective-permute-start(bf16[48,1024]{1,0:T(8,128)(2,1)S(1)} %get-tuple-element.70), channel_id=1, source_target_pairs={{0,1},{1,0},{2,3},{3,2},{4,5},{5,4},{6,7},{7,6},{8,9},{9,8},{10,11... | collective-permute-start | bytes 294920 | tf_op jit(solution)/shard_map/ppermute | solution.py:594
  66.0 5.7 %collective-permute-start.16 = (bf16[48,1024]{1,0:T(8,128)(2,1)S(1)}, bf16[48,1024]{1,0:T(8,128)(2,1)S(1)}, u32[]{:S(2)}, u32[]{:S(2)}) collective-permute-start(bf16[48,1024]{1,0:T(8,128)(2,1)S(1)} %get-tuple-element.69), channel_id=1, source_target_pairs={{0,2},{1,3},{2,0},{3,1},{4,6},{5,7},{6,4},{7,5},{8,10},{9,11},{10,... | collective-permute-start | bytes 294920 | tf_op jit(solution)/shard_map/ppermute | solution.py:594
  67.6 5.3 %collective-permute-start.15 = (bf16[48,1024]{1,0:T(8,128)(2,1)S(1)}, bf16[48,1024]{1,0:T(8,128)(2,1)S(1)}, u32[]{:S(2)}, u32[]{:S(2)}) collective-permute-start(bf16[48,1024]{1,0:T(8,128)(2,1)S(1)} %get-tuple-element.68), channel_id=1, source_target_pairs={{0,3},{1,2},{2,1},{3,0},{4,7},{5,6},{6,5},{7,4},{8,11},{9,10},{10,... | collective-permute-start | bytes 294920 | tf_op jit(solution)/shard_map/ppermute | solution.py:594
  72.9 7.1 %collective-permute-start.21 = (bf16[48,1024]{1,0:T(8,128)(2,1)S(1)}, bf16[48,1024]{1,0:T(8,128)(2,1)S(1)}, u32[]{:S(2)}, u32[]{:S(2)}) collective-permute-start(bf16[48,1024]{1,0:T(8,128)(2,1)S(1)} %add_convert_fusion.1.refs_0_), channel_id=1, source_target_pairs={{0,16},{4,20},{8,24},{12,28},{16,0},{20,4},{24,8},{28,12},{1,17},{... | collective-permute-start | bytes 294920 | tf_op jit(solution)/shard_map/ppermute | solution.py:594
  73.0 8.1 %collective-permute-start.18 = (bf16[48,1024]{1,0:T(8,128)(2,1)S(1)}, bf16[48,1024]{1,0:T(8,128)(2,1)S(1)}, u32[]{:S(2)}, u32[]{:S(2)}) collective-permute-start(bf16[48,1024]{1,0:T(8,128)(2,1)S(1)} %add_convert_fusion.1.refs_0_), channel_id=1, source_target_pairs={{0,8},{4,12},{8,0},{12,4},{16,24},{20,28},{24,16},{28,20},{1,9},{5... | collective-permute-start | bytes 294920 | tf_op jit(solution)/shard_map/ppermute | solution.py:594
  74.2 8.1 %collective-permute-start.19 = (bf16[48,1024]{1,0:T(8,128)(2,1)S(1)}, bf16[48,1024]{1,0:T(8,128)(2,1)S(1)}, u32[]{:S(2)}, u32[]{:S(2)}) collective-permute-start(bf16[48,1024]{1,0:T(8,128)(2,1)S(1)} %add_convert_fusion.1.refs_0_), channel_id=1, source_target_pairs={{0,24},{4,28},{8,16},{12,20},{16,8},{20,12},{24,0},{28,4},{1,25},{... | collective-permute-start | bytes 294920 | tf_op jit(solution)/shard_map/ppermute | solution.py:594
  77.4 5.4 %collective-permute-start.20 = (bf16[48,1024]{1,0:T(8,128)(2,1)S(1)}, bf16[48,1024]{1,0:T(8,128)(2,1)S(1)}, u32[]{:S(2)}, u32[]{:S(2)}) collective-permute-start(bf16[48,1024]{1,0:T(8,128)(2,1)S(1)} %add_convert_fusion.1.refs_0_), channel_id=1, source_target_pairs={{0,4},{4,0},{8,12},{12,8},{16,20},{20,16},{24,28},{28,24},{1,5},{5... | collective-permute-start | bytes 294920 | tf_op jit(solution)/shard_map/ppermute | solution.py:594
  80.1 4.6 %collective-permute-start.22 = (bf16[48,1024]{1,0:T(8,128)(2,1)S(1)}, bf16[48,1024]{1,0:T(8,128)(2,1)S(1)}, u32[]{:S(2)}, u32[]{:S(2)}) collective-permute-start(bf16[48,1024]{1,0:T(8,128)(2,1)S(1)} %collective-permute-done.21.refs_2_), channel_id=1, source_target_pairs={{0,4},{4,0},{8,12},{12,8},{16,20},{20,16},{24,28},{28,24},{1,5},{5... | collective-permute-start | bytes 294920 | tf_op jit(solution)/shard_map/ppermute | solution.py:594
  88.7 2.6 %collective-permute-start.23 = (bf16[48,3712]{1,0:T(8,128)(2,1)S(1)}, bf16[48,3712]{1,0:T(8,128)(2,1)S(1)}, u32[]{:S(2)}, u32[]{:S(2)}) collective-permute-start(bf16[48,3712]{1,0:T(8,128)(2,1)S(1)} %get-tuple-element.73), channel_id=1, source_target_pairs={{0,1},{1,0},{2,3},{3,2},{4,5},{5,4},{6,7},{7,6},{8,9},{9,8},{10,11... | collective-permute-start | bytes 1069064 | tf_op jit(solution)/shard_map/ppermute | solution.py:594
  88.7 2.5 %collective-permute-start.24 = (bf16[48,3712]{1,0:T(8,128)(2,1)S(1)}, bf16[48,3712]{1,0:T(8,128)(2,1)S(1)}, u32[]{:S(2)}, u32[]{:S(2)}) collective-permute-start(bf16[48,3712]{1,0:T(8,128)(2,1)S(1)} %get-tuple-element.74), channel_id=1, source_target_pairs={{0,1},{1,0},{2,3},{3,2},{4,5},{5,4},{6,7},{7,6},{8,9},{9,8},{10,11... | collective-permute-start | bytes 1069064 | tf_op jit(solution)/shard_map/ppermute | solution.py:594
  89.2 5.7 %collective-permute-start.25 = (bf16[48,1024]{1,0:T(8,128)(2,1)S(1)}, bf16[48,1024]{1,0:T(8,128)(2,1)S(1)}, u32[]{:S(2)}, u32[]{:S(2)}) collective-permute-start(bf16[48,1024]{1,0:T(8,128)(2,1)S(1)} %collective-permute-done.18.refs_0_), channel_id=1, source_target_pairs={{0,4},{4,0},{8,12},{12,8},{16,20},{20,16},{24,28},{28,24},{1,5},{5... | collective-permute-start | bytes 294920 | tf_op jit(solution)/shard_map/ppermute | solution.py:594
  90.3 5.8 %collective-permute-start.26 = (bf16[48,1024]{1,0:T(8,128)(2,1)S(1)}, bf16[48,1024]{1,0:T(8,128)(2,1)S(1)}, u32[]{:S(2)}, u32[]{:S(2)}) collective-permute-start(bf16[48,1024]{1,0:T(8,128)(2,1)S(1)} %collective-permute-done.19.refs_2_), channel_id=1, source_target_pairs={{0,4},{4,0},{8,12},{12,8},{16,20},{20,16},{24,28},{28,24},{1,5},{5... | collective-permute-start | bytes 294920 | tf_op jit(solution)/shard_map/ppermute | solution.py:594
  91.6 19.1 %copy-start = (bf16[1792,1024]{1,0:T(8,128)(2,1)S(1)}, bf16[1792,1024]{1,0:T(8,128)(2,1)}, u32[]{:S(2)}) copy-start(bf16[1792,1024]{1,0:T(8,128)(2,1)} %weight_ref.7) | copy-start | bytes 11010052
  91.6 10.1 %collective-permute-start.27 = (bf16[48,3712]{1,0:T(8,128)(2,1)S(1)}, bf16[48,3712]{1,0:T(8,128)(2,1)S(1)}, u32[]{:S(2)}, u32[]{:S(2)}) collective-permute-start(bf16[48,3712]{1,0:T(8,128)(2,1)S(1)} %get-tuple-element.76), channel_id=1, source_target_pairs={{0,2},{1,3},{2,0},{3,1},{4,6},{5,7},{6,4},{7,5},{8,10},{9,11},{10,... | collective-permute-start | bytes 1069064 | tf_op jit(solution)/shard_map/ppermute | solution.py:594
  100.1 3.4 %collective-permute-start.30 = (bf16[48,3712]{1,0:T(8,128)(2,1)S(1)}, bf16[48,3712]{1,0:T(8,128)(2,1)S(1)}, u32[]{:S(2)}, u32[]{:S(2)}) collective-permute-start(bf16[48,3712]{1,0:T(8,128)(2,1)S(1)} %get-tuple-element.81), channel_id=1, source_target_pairs={{0,1},{1,0},{2,3},{3,2},{4,5},{5,4},{6,7},{7,6},{8,9},{9,8},{10,11... | collective-permute-start | bytes 1069064 | tf_op jit(solution)/shard_map/ppermute | solution.py:594
  100.2 3.3 %collective-permute-start.31 = (bf16[48,3712]{1,0:T(8,128)(2,1)S(1)}, bf16[48,3712]{1,0:T(8,128)(2,1)S(1)}, u32[]{:S(2)}, u32[]{:S(2)}) collective-permute-start(bf16[48,3712]{1,0:T(8,128)(2,1)S(1)} %get-tuple-element.82), channel_id=1, source_target_pairs={{0,1},{1,0},{2,3},{3,2},{4,5},{5,4},{6,7},{7,6},{8,9},{9,8},{10,11... | collective-permute-start | bytes 1069064 | tf_op jit(solution)/shard_map/ppermute | solution.py:594
  101.9 7.4 %collective-permute-start.28 = (bf16[48,1792]{1,0:T(8,128)(2,1)S(1)}, bf16[48,1792]{1,0:T(8,128)(2,1)S(1)}, u32[]{:S(2)}, u32[]{:S(2)}) collective-permute-start(bf16[48,1792]{1,0:T(8,128)(2,1)S(1)} %gated.2.refs_0_), channel_id=1, source_target_pairs={{0,2},{1,3},{2,0},{3,1},{4,6},{5,7},{6,4},{7,5},{8,10},{9,11},{10,... | collective-permute-start | bytes 516104 | tf_op jit(solution)/shard_map/ppermute | solution.py:594
  103.9 12.3 %collective-permute-start.36 = (bf16[48,3712]{1,0:T(8,128)(2,1)S(1)}, bf16[48,3712]{1,0:T(8,128)(2,1)S(1)}, u32[]{:S(2)}, u32[]{:S(2)}) collective-permute-start(bf16[48,3712]{1,0:T(8,128)(2,1)S(1)} %get-tuple-element.83), channel_id=1, source_target_pairs={{0,2},{1,3},{2,0},{3,1},{4,6},{5,7},{6,4},{7,5},{8,10},{9,11},{10,... | collective-permute-start | bytes 1069064 | tf_op jit(solution)/shard_map/ppermute | solution.py:594
  104.4 4.9 %collective-permute-start.29 = (bf16[48,1792]{1,0:T(8,128)(2,1)S(1)}, bf16[48,1792]{1,0:T(8,128)(2,1)S(1)}, u32[]{:S(2)}, u32[]{:S(2)}) collective-permute-start(bf16[48,1792]{1,0:T(8,128)(2,1)S(1)} %gated.2.refs_0_), channel_id=1, source_target_pairs={{0,1},{1,0},{2,3},{3,2},{4,5},{5,4},{6,7},{7,6},{8,9},{9,8},{10,11... | collective-permute-start | bytes 516104 | tf_op jit(solution)/shard_map/ppermute | solution.py:594
  109.3 1.4 %collective-permute-start.32 = (bf16[48,1792]{1,0:T(8,128)(2,1)S(1)}, bf16[48,1792]{1,0:T(8,128)(2,1)S(1)}, u32[]{:S(2)}, u32[]{:S(2)}) collective-permute-start(bf16[48,1792]{1,0:T(8,128)(2,1)S(1)} %collective-permute-done.28.refs_1_), channel_id=1, source_target_pairs={{0,1},{1,0},{2,3},{3,2},{4,5},{5,4},{6,7},{7,6},{8,9},{9,8},{10,11... | collective-permute-start | bytes 516104 | tf_op jit(solution)/shard_map/ppermute | solution.py:594
  111.7 6.3 %collective-permute-start.35 = (bf16[48,1024]{1,0:T(8,128)(2,1)S(1)}, bf16[48,1024]{1,0:T(8,128)(2,1)S(1)}, u32[]{:S(2)}, u32[]{:S(2)}) collective-permute-start(bf16[48,1024]{1,0:T(8,128)(2,1)S(1)} %get-tuple-element.88), channel_id=1, source_target_pairs={{0,4},{4,0},{8,12},{12,8},{16,20},{20,16},{24,28},{28,24},{1,5},{5... | collective-permute-start | bytes 294920 | tf_op jit(solution)/shard_map/ppermute | solution.py:594
  112.9 9.6 %collective-permute-start.34 = (bf16[48,1024]{1,0:T(8,128)(2,1)S(1)}, bf16[48,1024]{1,0:T(8,128)(2,1)S(1)}, u32[]{:S(2)}, u32[]{:S(2)}) collective-permute-start(bf16[48,1024]{1,0:T(8,128)(2,1)S(1)} %get-tuple-element.87), channel_id=1, source_target_pairs={{0,16},{4,20},{8,24},{12,28},{16,0},{20,4},{24,8},{28,12},{1,17},{... | collective-permute-start | bytes 294920 | tf_op jit(solution)/shard_map/ppermute | solution.py:594
  113.2 11.7 %collective-permute-start.33 = (bf16[48,1024]{1,0:T(8,128)(2,1)S(1)}, bf16[48,1024]{1,0:T(8,128)(2,1)S(1)}, u32[]{:S(2)}, u32[]{:S(2)}) collective-permute-start(bf16[48,1024]{1,0:T(8,128)(2,1)S(1)} %get-tuple-element.86), channel_id=1, source_target_pairs={{0,20},{4,16},{8,28},{12,24},{16,4},{20,0},{24,12},{28,8},{1,21},{... | collective-permute-start | bytes 294920 | tf_op jit(solution)/shard_map/ppermute | solution.py:594
  116.4 8.5 %collective-permute-start.37 = (bf16[48,1792]{1,0:T(8,128)(2,1)S(1)}, bf16[48,1792]{1,0:T(8,128)(2,1)S(1)}, u32[]{:S(2)}, u32[]{:S(2)}) collective-permute-start(bf16[48,1792]{1,0:T(8,128)(2,1)S(1)} %gated.3.refs_0_), channel_id=1, source_target_pairs={{0,2},{1,3},{2,0},{3,1},{4,6},{5,7},{6,4},{7,5},{8,10},{9,11},{10,... | collective-permute-start | bytes 516104 | tf_op jit(solution)/shard_map/ppermute | solution.py:594
  118.0 7.0 %collective-permute-start.38 = (bf16[48,1792]{1,0:T(8,128)(2,1)S(1)}, bf16[48,1792]{1,0:T(8,128)(2,1)S(1)}, u32[]{:S(2)}, u32[]{:S(2)}) collective-permute-start(bf16[48,1792]{1,0:T(8,128)(2,1)S(1)} %gated.3.refs_0_), channel_id=1, source_target_pairs={{0,1},{1,0},{2,3},{3,2},{4,5},{5,4},{6,7},{7,6},{8,9},{9,8},{10,11... | collective-permute-start | bytes 516104 | tf_op jit(solution)/shard_map/ppermute | solution.py:594
  124.9 1.5 %collective-permute-start.39 = (bf16[48,1792]{1,0:T(8,128)(2,1)S(1)}, bf16[48,1792]{1,0:T(8,128)(2,1)S(1)}, u32[]{:S(2)}, u32[]{:S(2)}) collective-permute-start(bf16[48,1792]{1,0:T(8,128)(2,1)S(1)} %collective-permute-done.37.refs_1_), channel_id=1, source_target_pairs={{0,1},{1,0},{2,3},{3,2},{4,5},{5,4},{6,7},{7,6},{8,9},{9,8},{10,11... | collective-permute-start | bytes 516104 | tf_op jit(solution)/shard_map/ppermute | solution.py:594
  127.4 7.5 %collective-permute-start.43 = (bf16[48,1024]{1,0:T(8,128)(2,1)S(1)}, bf16[48,1024]{1,0:T(8,128)(2,1)S(1)}, u32[]{:S(2)}, u32[]{:S(2)}) collective-permute-start(bf16[48,1024]{1,0:T(8,128)(2,1)S(1)} %get-tuple-element.95), channel_id=1, source_target_pairs={{0,8},{4,12},{8,0},{12,4},{16,24},{20,28},{24,16},{28,20},{1,9},{5... | collective-permute-start | bytes 294920 | tf_op jit(solution)/shard_map/ppermute | solution.py:594
  127.4 11.7 %collective-permute-start.42 = (bf16[48,1024]{1,0:T(8,128)(2,1)S(1)}, bf16[48,1024]{1,0:T(8,128)(2,1)S(1)}, u32[]{:S(2)}, u32[]{:S(2)}) collective-permute-start(bf16[48,1024]{1,0:T(8,128)(2,1)S(1)} %get-tuple-element.94), channel_id=1, source_target_pairs={{0,12},{4,8},{8,4},{12,0},{16,28},{20,24},{24,20},{28,16},{1,13},{... | collective-permute-start | bytes 294920 | tf_op jit(solution)/shard_map/ppermute | solution.py:594
  130.0 9.1 %collective-permute-start.41 = (bf16[48,1024]{1,0:T(8,128)(2,1)S(1)}, bf16[48,1024]{1,0:T(8,128)(2,1)S(1)}, u32[]{:S(2)}, u32[]{:S(2)}) collective-permute-start(bf16[48,1024]{1,0:T(8,128)(2,1)S(1)} %get-tuple-element.93), channel_id=1, source_target_pairs={{0,24},{4,28},{8,16},{12,20},{16,8},{20,12},{24,0},{28,4},{1,25},{... | collective-permute-start | bytes 294920 | tf_op jit(solution)/shard_map/ppermute | solution.py:594
  131.4 7.7 %collective-permute-start.40 = (bf16[48,1024]{1,0:T(8,128)(2,1)S(1)}, bf16[48,1024]{1,0:T(8,128)(2,1)S(1)}, u32[]{:S(2)}, u32[]{:S(2)}) collective-permute-start(bf16[48,1024]{1,0:T(8,128)(2,1)S(1)} %get-tuple-element.92), channel_id=1, source_target_pairs={{0,28},{4,24},{8,20},{12,16},{16,12},{20,8},{24,4},{28,0},{1,29},{... | collective-permute-start | bytes 294920 | tf_op jit(solution)/shard_map/ppermute | solution.py:594
  (1 other events, 0.7 us)

commit v9 on v8

--- a/solution.py
+++ b/solution.py
@@ -702,7 +702,6 @@
     hidden = gated(after(keep, later[0]), swap(send, "mlp", steps[-1]), units)
     keep, send = reduce_once(*later, hidden)
     early = finish(regather(hidden, send), first)
-    keep = after(keep, early[0])
     hidden = gated(keep, swap(send, "mlp", steps[-1]), units)
     mixed = early[0].astype(jnp.float32)
     for mask in first[:0:-1]:

time: 139 us -> 140 us (level)
  transfers between devices with their start and end apart: 44 -> 44, of which waited for: 19 -> 21; matrix products, arithmetic and copies ran while one was open for 0% -> 0% of each run, Pallas kernels for 16% -> 16%
where the time goes in v9:
time: 140 us
  starting transfers between devices  55.6 us (40%)
  waiting for transfers between devices  43 us (31%)
  Pallas kernels  37.4 us (27%)
  local copies, waits for them, and re-layouts  1.59 us (1%)
  other arithmetic  1.48 us (1%)
    ppermute x44, starting transfers between devices, swap(): lax.ppermute(value, axis_name, [(j, j ^ mask) for j in range(axis_total)])  55.6 us
    ppermute x44, waiting for transfers between devices, swap(): lax.ppermute(value, axis_name, [(j, j ^ mask) for j in range(axis_total)])  43 us
    pallas_call x2, Pallas kernels, tree_attention(): pl.pallas_call(kernel, out_shape=[jax.ShapeDtypeStruct((part_total // 2,...  16.7 us
    pallas_call x2, Pallas kernels, gate_up_rows(): pl.pallas_call(kernel, out_shape=[jax.ShapeDtypeStruct((half, 2 * units +...  7.95 us
    pallas_call x2, Pallas kernels, combine_project(): pl.pallas_call(kernel, out_shape=[jax.ShapeDtypeStruct((own_rows, width),...  5.08 us
    pallas_call x1, Pallas kernels, own_nodes(): pl.pallas_call(kernel, out_shape=jax.ShapeDtypeStruct((3, node_total), jn...  3.03 us
  transfers between devices with their start and end apart: 44, of which 21 were waited for; matrix products, arithmetic and copies ran while one was open for 0% of the time, Pallas kernels for 16%

profile of v9, /device:TPU:0, one launch (start us, length us, event | category | flops | bytes accessed | tf_op | source)
XLA Modules:
  0.0 139.9 jit_solution(4157756605712281609)
XLA Ops:
  0.6 3.1 %collective-permute-start.1 = (bf16[48,1024]{1,0:T(8,128)(2,1)}, bf16[48,1024]{1,0:T(8,128)(2,1)S(1)}, u32[]{:S(2)}, u32[]{:S(2)}) collective-permute-start(bf16[48,1024]{1,0:T(8,128)(2,1)} %refs_0_.5), channel_id=1, source_target_pairs={{0,8},{4,12},{8,0},{12,4},{16,24},{20,28},{24,16},{28,20},{1,9},{5... | collective-permute-start | bytes 294920 | tf_op jit(solution)/shard_map/ppermute | solution.py:594
  3.7 2.6 %collective-permute-start.3 = (bf16[48,1024]{1,0:T(8,128)(2,1)}, bf16[48,1024]{1,0:T(8,128)(2,1)S(1)}, u32[]{:S(2)}, u32[]{:S(2)}) collective-permute-start(bf16[48,1024]{1,0:T(8,128)(2,1)} %refs_0_.5), channel_id=1, source_target_pairs={{0,16},{4,20},{8,24},{12,28},{16,0},{20,4},{24,8},{28,12},{1,17},{... | collective-permute-start | bytes 294920 | tf_op jit(solution)/shard_map/ppermute | solution.py:594
  6.3 1.7 %collective-permute-start = (bf16[48,1024]{1,0:T(8,128)(2,1)}, bf16[48,1024]{1,0:T(8,128)(2,1)S(1)}, u32[]{:S(2)}, u32[]{:S(2)}) collective-permute-start(bf16[48,1024]{1,0:T(8,128)(2,1)} %refs_0_.5), channel_id=1, source_target_pairs={{0,4},{4,0},{8,12},{12,8},{16,20},{20,16},{24,28},{28,24},{1,5},{5... | collective-permute-start | bytes 294920 | tf_op jit(solution)/shard_map/ppermute | solution.py:594
  8.5 5.9 %collective-permute-done.3.refs_4_ = bf16[48,1024]{1,0:T(8,128)(2,1)S(1)} collective-permute-done((bf16[48,1024]{1,0:T(8,128)(2,1)}, bf16[48,1024]{1,0:T(8,128)(2,1)S(1)}, u32[]{:S(2)}, u32[]{:S(2)}) %collective-permute-start.3) | collective-permute-done | bytes 98336 | tf_op jit(solution)/shard_map/ppermute | solution.py:594
  14.4 1.5 %collective-permute-start.4 = (bf16[48,1024]{1,0:T(8,128)(2,1)S(1)}, bf16[48,1024]{1,0:T(8,128)(2,1)S(1)}, u32[]{:S(2)}, u32[]{:S(2)}) collective-permute-start(bf16[48,1024]{1,0:T(8,128)(2,1)S(1)} %collective-permute-done.3.refs_4_), channel_id=1, source_target_pairs={{0,4},{4,0},{8,12},{12,8},{16,20},{20,16},{24,28},{28,24},{1,5},{5... | collective-permute-start | bytes 294920 | tf_op jit(solution)/shard_map/ppermute | solution.py:594
  16.4 3.0 %own_nodes.1.nodes_ref = s32[3,7]{1,0:T(4,128)} custom-call(s32[1]{0:T(128)} %bitcast.1.owner_ref, s32[3,128]{1,0:T(4,128)} %bitcast.7, s32[32]{0:T(128)} %leaf_up.1, s32[16]{0:T(128)} %mid_up.1, s32[8]{0:T(128)} %refs_0_.3, s32[16]{0:T(128)} %refs_1_.1, s32[32]{0:T(128)} %refs_2_.1, s32[8]{0:T(128)} %refs_3_.1, s32[16]{0:T(128)} %refs_4_.1, s32[32]{0:T(128)} %refs_5_.1), custom_call_target="tpu_custom_call" | custom-call | tf_op jit(solution)/shard_map/own_nodes/pallas_call | solution.py:84
  19.5 1.0 collective-permute-done.6.refs_7_
  22.1 8.2 %tree_attention.2 = (bf16[4,48,640]{2,1,0:T(8,128)(2,1)S(1)}, bf16[4,48,640]{2,1,0:T(8,128)(2,1)S(1)}) custom-call(s32[3,7]{1,0:T(4,128)S(1)} %copy-done.2, s32[1]{0:T(128)} %bitcast.1.owner_ref, bf16[48,1024]{1,0:T(8,128)(2,1)S(1)} %copy-done.1, bf16[48,1024]{1,0:T(8,128)(2,1)S(1)} %collective-permute-done.refs_1_, ...), custom_call_target="tpu_custom_call" | custom-call | flops 2147483648 | bytes 6291456 | tf_op jit(solution)/shard_map/tree_attention/pallas_call | solution.py:268
  30.4 8.4 %tree_attention.3 = (bf16[4,48,640]{2,1,0:T(8,128)(2,1)S(1)}, bf16[4,48,640]{2,1,0:T(8,128)(2,1)S(1)}) custom-call(s32[3,7]{1,0:T(4,128)S(1)} %copy-done.2, s32[1]{0:T(128)} %bitcast.1.owner_ref, bf16[48,1024]{1,0:T(8,128)(2,1)S(1)} %copy-done.1, bf16[48,1024]{1,0:T(8,128)(2,1)S(1)} %collective-permute-done.refs_1_, ...), custom_call_target="tpu_custom_call" | custom-call | flops 2147483648 | bytes 6291456 | tf_op jit(solution)/shard_map/tree_attention/pallas_call | solution.py:268
  38.8 0.9 collective-permute-start.11
  40.5 9.5 %collective-permute-start.8 = (bf16[48,640]{1,0:T(8,128)(2,1)S(1)}, bf16[48,640]{1,0:T(8,128)(2,1)S(1)}, u32[]{:S(2)}, u32[]{:S(2)}) collective-permute-start(bf16[48,640]{1,0:T(8,128)(2,1)S(1)} %get-tuple-element.51), channel_id=1, source_target_pairs={{0,8},{4,12},{8,0},{12,4},{16,24},{20,28},{24,16},{28,20},{1,9},{5... | collective-permute-start | bytes 184328 | tf_op jit(solution)/shard_map/ppermute | solution.py:594
  50.0 2.2 %collective-permute-start.9 = (bf16[48,640]{1,0:T(8,128)(2,1)S(1)}, bf16[48,640]{1,0:T(8,128)(2,1)S(1)}, u32[]{:S(2)}, u32[]{:S(2)}) collective-permute-start(bf16[48,640]{1,0:T(8,128)(2,1)S(1)} %get-tuple-element.52), channel_id=1, source_target_pairs={{0,16},{4,20},{8,24},{12,28},{16,0},{20,4},{24,8},{28,12},{1,17},{... | collective-permute-start | bytes 184328 | tf_op jit(solution)/shard_map/ppermute | solution.py:594
  53.3 1.4 collective-permute-start.12
  54.7 2.8 %collective-permute-start.13 = (bf16[48,640]{1,0:T(8,128)(2,1)S(1)}, bf16[48,640]{1,0:T(8,128)(2,1)S(1)}, u32[]{:S(2)}, u32[]{:S(2)}) collective-permute-start(bf16[48,640]{1,0:T(8,128)(2,1)S(1)} %get-tuple-element.59), channel_id=1, source_target_pairs={{0,16},{4,20},{8,24},{12,28},{16,0},{20,4},{24,8},{28,12},{1,17},{... | collective-permute-start | bytes 184328 | tf_op jit(solution)/shard_map/ppermute | solution.py:594
  58.3 2.5 %combine_project.2 = (bf16[48,512]{1,0:T(8,128)(2,1)S(1)}, f32[48,1024]{1,0:T(8,128)S(1)}, f32[48,1024]{1,0:T(8,128)S(1)}, f32[48,1024]{1,0:T(8,128)S(1)}, f32[48,1024]{1,0:T(8,128)S(1)}) custom-call(s32[1]{0:T(128)} %bitcast.place_ref, bf16[1024,4096]{1,0:T(8,128)(2,1)} %weight_ref.5, bf16[48,640]{1,0:T(8,128)(2,1)S(1)} %get-tuple-element.50.refs_0_, ...), custom_call_target="tpu_custom_call" | custom-call | flops 201326592 | bytes 4194304 | tf_op jit(solution)/shard_map/combine_project/pallas_call | solution.py:406
  60.9 2.6 %collective-permute-done.14.refs_3_ = bf16[48,640]{1,0:T(8,128)(2,1)S(1)} collective-permute-done((bf16[48,640]{1,0:T(8,128)(2,1)S(1)}, bf16[48,640]{1,0:T(8,128)(2,1)S(1)}, u32[]{:S(2)}, u32[]{:S(2)}) %collective-permute-start.14) | collective-permute-done | bytes 61472 | tf_op jit(solution)/shard_map/ppermute | solution.py:594
  63.5 2.6 %combine_project.3 = (bf16[48,512]{1,0:T(8,128)(2,1)S(1)}, bf16[48,1024]{1,0:T(8,128)(2,1)S(1)}, bf16[48,1024]{1,0:T(8,128)(2,1)S(1)}, bf16[48,1024]{1,0:T(8,128)(2,1)S(1)}, bf16[48,1024]{1,0:T(8,128)(2,1)S(1)}) custom-call(s32[1]{0:T(128)} %bitcast.place_ref, bf16[1024,4096]{1,0:T(8,128)(2,1)} %weight_ref.5, bf16[48,640]{1,0:T(8,128)(2,1)S(1)} %get-tuple-element.57.refs_0_, ...), custom_call_target="tpu_custom_call" | custom-call | flops 201326592 | bytes 4194304 | tf_op jit(solution)/shard_map/combine_project/pallas_call | solution.py:406
  66.1 1.6 %collective-permute-start.16 = (bf16[48,1024]{1,0:T(8,128)(2,1)S(1)}, bf16[48,1024]{1,0:T(8,128)(2,1)S(1)}, u32[]{:S(2)}, u32[]{:S(2)}) collective-permute-start(bf16[48,1024]{1,0:T(8,128)(2,1)S(1)} %get-tuple-element.68), channel_id=1, source_target_pairs={{0,2},{1,3},{2,0},{3,1},{4,6},{5,7},{6,4},{7,5},{8,10},{9,11},{10,... | collective-permute-start | bytes 294920 | tf_op jit(solution)/shard_map/ppermute | solution.py:594
  68.0 3.8 %collective-permute-done.16 = bf16[48,1024]{1,0:T(8,128)(2,1)S(1)} collective-permute-done((bf16[48,1024]{1,0:T(8,128)(2,1)S(1)}, bf16[48,1024]{1,0:T(8,128)(2,1)S(1)}, u32[]{:S(2)}, u32[]{:S(2)}) %collective-permute-start.16) | collective-permute-done | bytes 98336 | tf_op jit(solution)/shard_map/ppermute | solution.py:594
  71.8 1.2 collective-permute-done.15
  73.2 1.2 collective-permute-start.18
  74.4 3.2 %collective-permute-start.19 = (bf16[48,1024]{1,0:T(8,128)(2,1)S(1)}, bf16[48,1024]{1,0:T(8,128)(2,1)S(1)}, u32[]{:S(2)}, u32[]{:S(2)}) collective-permute-start(bf16[48,1024]{1,0:T(8,128)(2,1)S(1)} %add_convert_fusion.1.refs_0_), channel_id=1, source_target_pairs={{0,24},{4,28},{8,16},{12,20},{16,8},{20,12},{24,0},{28,4},{1,25},{... | collective-permute-start | bytes 294920 | tf_op jit(solution)/shard_map/ppermute | solution.py:594
  78.4 1.7 %collective-permute-done.21.refs_2_ = bf16[48,1024]{1,0:T(8,128)(2,1)S(1)} collective-permute-done((bf16[48,1024]{1,0:T(8,128)(2,1)S(1)}, bf16[48,1024]{1,0:T(8,128)(2,1)S(1)}, u32[]{:S(2)}, u32[]{:S(2)}) %collective-permute-start.21) | collective-permute-done | bytes 98336 | tf_op jit(solution)/shard_map/ppermute | solution.py:594
  80.2 0.9 collective-permute-start.22
  81.3 1.1 collective-permute-done.19.refs_2_
  82.9 1.9 %collective-permute-done.22.refs_3_ = bf16[48,1024]{1,0:T(8,128)(2,1)S(1)} collective-permute-done((bf16[48,1024]{1,0:T(8,128)(2,1)S(1)}, bf16[48,1024]{1,0:T(8,128)(2,1)S(1)}, u32[]{:S(2)}, u32[]{:S(2)}) %collective-permute-start.22) | collective-permute-done | bytes 98336 | tf_op jit(solution)/shard_map/ppermute | solution.py:594
  84.8 4.0 %gate_up.2 = (bf16[96,3712]{1,0:T(8,128)(2,1)S(1)}, bf16[48,3712]{1,0:T(8,128)(2,1)S(1)}, bf16[48,3712]{1,0:T(8,128)(2,1)S(1)}) custom-call(s32[1]{0:T(128)} %bitcast.3.spot_ref, f32[1,1024]{1,0:T(1,128)S(1)} %bitcast.5, bf16[1024,1792]{1,0:T(8,128)(2,1)} %gate_ref.3, bf16[1024,1792]{1,0:T(8,128)(2,1)} %up_ref.3, ...), custom_call_target="tpu_custom_call" | custom-call | flops 1409286144 | bytes 7340032 | tf_op jit(solution)/shard_map/gate_up/pallas_call | solution.py:485
  90.3 1.1 collective-permute-start.26
  91.8 1.6 %collective-permute-start.27 = (bf16[48,3712]{1,0:T(8,128)(2,1)S(1)}, bf16[48,3712]{1,0:T(8,128)(2,1)S(1)}, u32[]{:S(2)}, u32[]{:S(2)}) collective-permute-start(bf16[48,3712]{1,0:T(8,128)(2,1)S(1)} %get-tuple-element.75), channel_id=1, source_target_pairs={{0,2},{1,3},{2,0},{3,1},{4,6},{5,7},{6,4},{7,5},{8,10},{9,11},{10,... | collective-permute-start | bytes 1069064 | tf_op jit(solution)/shard_map/ppermute | solution.py:594
  93.3 1.7 %collective-permute-done.25.refs_1_ = bf16[48,1024]{1,0:T(8,128)(2,1)S(1)} collective-permute-done((bf16[48,1024]{1,0:T(8,128)(2,1)S(1)}, bf16[48,1024]{1,0:T(8,128)(2,1)S(1)}, u32[]{:S(2)}, u32[]{:S(2)}) %collective-permute-start.25) | collective-permute-done | bytes 98336 | tf_op jit(solution)/shard_map/ppermute | solution.py:594
  95.0 1.2 collective-permute-done.26.refs_3_
  96.3 4.0 %gate_up.3 = (bf16[96,3712]{1,0:T(8,128)(2,1)S(1)}, bf16[48,3712]{1,0:T(8,128)(2,1)S(1)}, bf16[48,3712]{1,0:T(8,128)(2,1)S(1)}) custom-call(s32[1]{0:T(128)} %bitcast.3.spot_ref, f32[1,1024]{1,0:T(1,128)S(1)} %bitcast.6, bf16[1024,1792]{1,0:T(8,128)(2,1)} %gate_ref.3, bf16[1024,1792]{1,0:T(8,128)(2,1)} %up_ref.3, ...), custom_call_target="tpu_custom_call" | custom-call | flops 1409286144 | bytes 7340032 | tf_op jit(solution)/shard_map/gate_up/pallas_call | solution.py:485
  100.8 1.0 collective-permute-done.27.got_ref
  102.1 1.6 %collective-permute-start.28 = (bf16[48,1792]{1,0:T(8,128)(2,1)S(1)}, bf16[48,1792]{1,0:T(8,128)(2,1)S(1)}, u32[]{:S(2)}, u32[]{:S(2)}) collective-permute-start(bf16[48,1792]{1,0:T(8,128)(2,1)S(1)} %gated.2.refs_0_), channel_id=1, source_target_pairs={{0,2},{1,3},{2,0},{3,1},{4,6},{5,7},{6,4},{7,5},{8,10},{9,11},{10,... | collective-permute-start | bytes 516104 | tf_op jit(solution)/shard_map/ppermute | solution.py:594
  104.6 4.9 %collective-permute-done.28.refs_1_ = bf16[48,1792]{1,0:T(8,128)(2,1)S(1)} collective-permute-done((bf16[48,1792]{1,0:T(8,128)(2,1)S(1)}, bf16[48,1792]{1,0:T(8,128)(2,1)S(1)}, u32[]{:S(2)}, u32[]{:S(2)}) %collective-permute-start.28) | collective-permute-done | bytes 172064 | tf_op jit(solution)/shard_map/ppermute | solution.py:594
  109.5 1.4 %collective-permute-done.32.refs_3_ = bf16[48,1792]{1,0:T(8,128)(2,1)S(1)} collective-permute-done((bf16[48,1792]{1,0:T(8,128)(2,1)S(1)}, bf16[48,1792]{1,0:T(8,128)(2,1)S(1)}, u32[]{:S(2)}, u32[]{:S(2)}) %collective-permute-start.32) | collective-permute-done | bytes 172064 | tf_op jit(solution)/shard_map/ppermute | solution.py:594
  110.9 1.0 down.2
  111.8 1.0 collective-permute-start.35
  113.2 3.1 %collective-permute-start.33 = (bf16[48,1024]{1,0:T(8,128)(2,1)S(1)}, bf16[48,1024]{1,0:T(8,128)(2,1)S(1)}, u32[]{:S(2)}, u32[]{:S(2)}) collective-permute-start(bf16[48,1024]{1,0:T(8,128)(2,1)S(1)} %get-tuple-element.85), channel_id=1, source_target_pairs={{0,20},{4,16},{8,28},{12,24},{16,4},{20,0},{24,12},{28,8},{1,21},{... | collective-permute-start | bytes 294920 | tf_op jit(solution)/shard_map/ppermute | solution.py:594
  116.5 1.6 %collective-permute-start.37 = (bf16[48,1792]{1,0:T(8,128)(2,1)S(1)}, bf16[48,1792]{1,0:T(8,128)(2,1)S(1)}, u32[]{:S(2)}, u32[]{:S(2)}) collective-permute-start(bf16[48,1792]{1,0:T(8,128)(2,1)S(1)} %gated.3.refs_0_), channel_id=1, source_target_pairs={{0,2},{1,3},{2,0},{3,1},{4,6},{5,7},{6,4},{7,5},{8,10},{9,11},{10,... | collective-permute-start | bytes 516104 | tf_op jit(solution)/shard_map/ppermute | solution.py:594
  118.1 4.8 %collective-permute-done.34 = bf16[48,1024]{1,0:T(8,128)(2,1)S(1)} collective-permute-done((bf16[48,1024]{1,0:T(8,128)(2,1)S(1)}, bf16[48,1024]{1,0:T(8,128)(2,1)S(1)}, u32[]{:S(2)}, u32[]{:S(2)}) %collective-permute-start.34) | collective-permute-done | bytes 98336 | tf_op jit(solution)/shard_map/ppermute | solution.py:594
  122.9 2.1 %collective-permute-done.33 = bf16[48,1024]{1,0:T(8,128)(2,1)S(1)} collective-permute-done((bf16[48,1024]{1,0:T(8,128)(2,1)S(1)}, bf16[48,1024]{1,0:T(8,128)(2,1)S(1)}, u32[]{:S(2)}, u32[]{:S(2)}) %collective-permute-start.33) | collective-permute-done | bytes 98336 | tf_op jit(solution)/shard_map/ppermute | solution.py:594
  125.2 1.4 collective-permute-done.39.refs_3_
  126.5 0.9 down.3
  127.6 2.5 %collective-permute-start.42 = (bf16[48,1024]{1,0:T(8,128)(2,1)S(1)}, bf16[48,1024]{1,0:T(8,128)(2,1)S(1)}, u32[]{:S(2)}, u32[]{:S(2)}) collective-permute-start(bf16[48,1024]{1,0:T(8,128)(2,1)S(1)} %get-tuple-element.92), channel_id=1, source_target_pairs={{0,12},{4,8},{8,4},{12,0},{16,28},{20,24},{24,20},{28,16},{1,13},{... | collective-permute-start | bytes 294920 | tf_op jit(solution)/shard_map/ppermute | solution.py:594
  130.1 1.4 collective-permute-start.41
  131.4 2.9 %collective-permute-start.40 = (bf16[48,1024]{1,0:T(8,128)(2,1)S(1)}, bf16[48,1024]{1,0:T(8,128)(2,1)S(1)}, u32[]{:S(2)}, u32[]{:S(2)}) collective-permute-start(bf16[48,1024]{1,0:T(8,128)(2,1)S(1)} %get-tuple-element.90), channel_id=1, source_target_pairs={{0,28},{4,24},{8,20},{12,16},{16,12},{20,8},{24,4},{28,0},{1,29},{... | collective-permute-start | bytes 294920 | tf_op jit(solution)/shard_map/ppermute | solution.py:594
  135.0 4.2 %collective-permute-done.42 = bf16[48,1024]{1,0:T(8,128)(2,1)S(1)} collective-permute-done((bf16[48,1024]{1,0:T(8,128)(2,1)S(1)}, bf16[48,1024]{1,0:T(8,128)(2,1)S(1)}, u32[]{:S(2)}, u32[]{:S(2)}) %collective-permute-start.42) | collective-permute-done | bytes 98336 | tf_op jit(solution)/shard_map/ppermute | solution.py:594
  (69 shorter events, 13.4 us)
Async XLA Ops:
  0.6 7.4 %collective-permute-start.1 = (bf16[48,1024]{1,0:T(8,128)(2,1)}, bf16[48,1024]{1,0:T(8,128)(2,1)S(1)}, u32[]{:S(2)}, u32[]{:S(2)}) collective-permute-start(bf16[48,1024]{1,0:T(8,128)(2,1)} %refs_0_.5), channel_id=1, source_target_pairs={{0,8},{4,12},{8,0},{12,4},{16,24},{20,28},{24,16},{28,20},{1,9},{5... | collective-permute-start | bytes 294920 | tf_op jit(solution)/shard_map/ppermute | solution.py:594
  3.7 10.6 %collective-permute-start.3 = (bf16[48,1024]{1,0:T(8,128)(2,1)}, bf16[48,1024]{1,0:T(8,128)(2,1)S(1)}, u32[]{:S(2)}, u32[]{:S(2)}) collective-permute-start(bf16[48,1024]{1,0:T(8,128)(2,1)} %refs_0_.5), channel_id=1, source_target_pairs={{0,16},{4,20},{8,24},{12,28},{16,0},{20,4},{24,8},{28,12},{1,17},{... | collective-permute-start | bytes 294920 | tf_op jit(solution)/shard_map/ppermute | solution.py:594
  6.3 9.6 %collective-permute-start.5 = (bf16[48,1024]{1,0:T(8,128)(2,1)}, bf16[48,1024]{1,0:T(8,128)(2,1)S(1)}, u32[]{:S(2)}, u32[]{:S(2)}) collective-permute-start(bf16[48,1024]{1,0:T(8,128)(2,1)} %refs_0_.5), channel_id=1, source_target_pairs={{0,24},{4,28},{8,16},{12,20},{16,8},{20,12},{24,0},{28,4},{1,25},{... | collective-permute-start | bytes 294920 | tf_op jit(solution)/shard_map/ppermute | solution.py:594
  6.3 13.1 %collective-permute-start = (bf16[48,1024]{1,0:T(8,128)(2,1)}, bf16[48,1024]{1,0:T(8,128)(2,1)S(1)}, u32[]{:S(2)}, u32[]{:S(2)}) collective-permute-start(bf16[48,1024]{1,0:T(8,128)(2,1)} %refs_0_.5), channel_id=1, source_target_pairs={{0,4},{4,0},{8,12},{12,8},{16,20},{20,16},{24,28},{28,24},{1,5},{5... | collective-permute-start | bytes 294920 | tf_op jit(solution)/shard_map/ppermute | solution.py:594
  8.0 11.4 %collective-permute-start.2 = (bf16[48,1024]{1,0:T(8,128)(2,1)S(1)}, bf16[48,1024]{1,0:T(8,128)(2,1)S(1)}, u32[]{:S(2)}, u32[]{:S(2)}) collective-permute-start(bf16[48,1024]{1,0:T(8,128)(2,1)S(1)} %collective-permute-done.1.refs_2_), channel_id=1, source_target_pairs={{0,4},{4,0},{8,12},{12,8},{16,20},{20,16},{24,28},{28,24},{1,5},{5... | collective-permute-start | bytes 294920 | tf_op jit(solution)/shard_map/ppermute | solution.py:594
  14.4 5.1 %collective-permute-start.4 = (bf16[48,1024]{1,0:T(8,128)(2,1)S(1)}, bf16[48,1024]{1,0:T(8,128)(2,1)S(1)}, u32[]{:S(2)}, u32[]{:S(2)}) collective-permute-start(bf16[48,1024]{1,0:T(8,128)(2,1)S(1)} %collective-permute-done.3.refs_4_), channel_id=1, source_target_pairs={{0,4},{4,0},{8,12},{12,8},{16,20},{20,16},{24,28},{28,24},{1,5},{5... | collective-permute-start | bytes 294920 | tf_op jit(solution)/shard_map/ppermute | solution.py:594
  15.9 4.6 %collective-permute-start.6 = (bf16[48,1024]{1,0:T(8,128)(2,1)S(1)}, bf16[48,1024]{1,0:T(8,128)(2,1)S(1)}, u32[]{:S(2)}, u32[]{:S(2)}) collective-permute-start(bf16[48,1024]{1,0:T(8,128)(2,1)S(1)} %collective-permute-done.5.refs_6_), channel_id=1, source_target_pairs={{0,4},{4,0},{8,12},{12,8},{16,20},{20,16},{24,28},{28,24},{1,5},{5... | collective-permute-start | bytes 294920 | tf_op jit(solution)/shard_map/ppermute | solution.py:594
  20.5 0.9 copy-start.1
  30.3 9.4 %collective-permute-start.7 = (bf16[4,48,640]{2,1,0:T(8,128)(2,1)S(1)}, bf16[4,48,640]{2,1,0:T(8,128)(2,1)S(1)}, u32[]{:S(2)}, u32[]{:S(2)}) collective-permute-start(bf16[4,48,640]{2,1,0:T(8,128)(2,1)S(1)} %get-tuple-element.49), channel_id=1, source_target_pairs={{0,4},{4,0},{8,12},{12,8},{16,20},{20,16},{24,28},{28,24},{1,5},{5... | collective-permute-start | bytes 737288 | tf_op jit(solution)/shard_map/ppermute | solution.py:594
  38.8 13.7 %collective-permute-start.11 = (bf16[4,48,640]{2,1,0:T(8,128)(2,1)S(1)}, bf16[4,48,640]{2,1,0:T(8,128)(2,1)S(1)}, u32[]{:S(2)}, u32[]{:S(2)}) collective-permute-start(bf16[4,48,640]{2,1,0:T(8,128)(2,1)S(1)} %get-tuple-element.56), channel_id=1, source_target_pairs={{0,4},{4,0},{8,12},{12,8},{16,20},{20,16},{24,28},{28,24},{1,5},{5... | collective-permute-start | bytes 737288 | tf_op jit(solution)/shard_map/ppermute | solution.py:594
  40.5 16.9 %collective-permute-start.8 = (bf16[48,640]{1,0:T(8,128)(2,1)S(1)}, bf16[48,640]{1,0:T(8,128)(2,1)S(1)}, u32[]{:S(2)}, u32[]{:S(2)}) collective-permute-start(bf16[48,640]{1,0:T(8,128)(2,1)S(1)} %get-tuple-element.51), channel_id=1, source_target_pairs={{0,8},{4,12},{8,0},{12,4},{16,24},{20,28},{24,16},{28,20},{1,9},{5... | collective-permute-start | bytes 184328 | tf_op jit(solution)/shard_map/ppermute | solution.py:594
  50.0 8.1 %collective-permute-start.9 = (bf16[48,640]{1,0:T(8,128)(2,1)S(1)}, bf16[48,640]{1,0:T(8,128)(2,1)S(1)}, u32[]{:S(2)}, u32[]{:S(2)}) collective-permute-start(bf16[48,640]{1,0:T(8,128)(2,1)S(1)} %get-tuple-element.52), channel_id=1, source_target_pairs={{0,16},{4,20},{8,24},{12,28},{16,0},{20,4},{24,8},{28,12},{1,17},{... | collective-permute-start | bytes 184328 | tf_op jit(solution)/shard_map/ppermute | solution.py:594
  52.2 6.1 %collective-permute-start.10 = (bf16[48,640]{1,0:T(8,128)(2,1)S(1)}, bf16[48,640]{1,0:T(8,128)(2,1)S(1)}, u32[]{:S(2)}, u32[]{:S(2)}) collective-permute-start(bf16[48,640]{1,0:T(8,128)(2,1)S(1)} %get-tuple-element.53), channel_id=1, source_target_pairs={{0,24},{4,28},{8,16},{12,20},{16,8},{20,12},{24,0},{28,4},{1,25},{... | collective-permute-start | bytes 184328 | tf_op jit(solution)/shard_map/ppermute | solution.py:594
  53.3 7.5 %collective-permute-start.12 = (bf16[48,640]{1,0:T(8,128)(2,1)S(1)}, bf16[48,640]{1,0:T(8,128)(2,1)S(1)}, u32[]{:S(2)}, u32[]{:S(2)}) collective-permute-start(bf16[48,640]{1,0:T(8,128)(2,1)S(1)} %get-tuple-element.58), channel_id=1, source_target_pairs={{0,8},{4,12},{8,0},{12,4},{16,24},{20,28},{24,16},{28,20},{1,9},{5... | collective-permute-start | bytes 184328 | tf_op jit(solution)/shard_map/ppermute | solution.py:594
  54.7 6.2 %collective-permute-start.13 = (bf16[48,640]{1,0:T(8,128)(2,1)S(1)}, bf16[48,640]{1,0:T(8,128)(2,1)S(1)}, u32[]{:S(2)}, u32[]{:S(2)}) collective-permute-start(bf16[48,640]{1,0:T(8,128)(2,1)S(1)} %get-tuple-element.59), channel_id=1, source_target_pairs={{0,16},{4,20},{8,24},{12,28},{16,0},{20,4},{24,8},{28,12},{1,17},{... | collective-permute-start | bytes 184328 | tf_op jit(solution)/shard_map/ppermute | solution.py:594
  57.5 6.0 %collective-permute-start.14 = (bf16[48,640]{1,0:T(8,128)(2,1)S(1)}, bf16[48,640]{1,0:T(8,128)(2,1)S(1)}, u32[]{:S(2)}, u32[]{:S(2)}) collective-permute-start(bf16[48,640]{1,0:T(8,128)(2,1)S(1)} %get-tuple-element.60), channel_id=1, source_target_pairs={{0,24},{4,28},{8,16},{12,20},{16,8},{20,12},{24,0},{28,4},{1,25},{... | collective-permute-start | bytes 184328 | tf_op jit(solution)/shard_map/ppermute | solution.py:594
  63.5 9.5 %copy-start.4 = (bf16[48,1024]{1,0:T(8,128)(2,1)S(1)}, bf16[48,1024]{1,0:T(8,128)(2,1)}, u32[]{:S(2)}) copy-start(bf16[48,1024]{1,0:T(8,128)(2,1)} %param.32) | copy-start | bytes 294916
  63.5 21.3 %copy-start.3 = (f32[1024]{0:T(1024)S(1)}, f32[1024]{0:T(1024)}, u32[]{:S(2)}) copy-start(f32[1024]{0:T(1024)} %param.34) | copy-start | bytes 12292
  66.1 1.9 %collective-permute-start.17 = (bf16[48,1024]{1,0:T(8,128)(2,1)S(1)}, bf16[48,1024]{1,0:T(8,128)(2,1)S(1)}, u32[]{:S(2)}, u32[]{:S(2)}) collective-permute-start(bf16[48,1024]{1,0:T(8,128)(2,1)S(1)} %get-tuple-element.69), channel_id=1, source_target_pairs={{0,1},{1,0},{2,3},{3,2},{4,5},{5,4},{6,7},{7,6},{8,9},{9,8},{10,11... | collective-permute-start | bytes 294920 | tf_op jit(solution)/shard_map/ppermute | solution.py:594
  66.1 5.7 %collective-permute-start.16 = (bf16[48,1024]{1,0:T(8,128)(2,1)S(1)}, bf16[48,1024]{1,0:T(8,128)(2,1)S(1)}, u32[]{:S(2)}, u32[]{:S(2)}) collective-permute-start(bf16[48,1024]{1,0:T(8,128)(2,1)S(1)} %get-tuple-element.68), channel_id=1, source_target_pairs={{0,2},{1,3},{2,0},{3,1},{4,6},{5,7},{6,4},{7,5},{8,10},{9,11},{10,... | collective-permute-start | bytes 294920 | tf_op jit(solution)/shard_map/ppermute | solution.py:594
  67.7 5.3 %collective-permute-start.15 = (bf16[48,1024]{1,0:T(8,128)(2,1)S(1)}, bf16[48,1024]{1,0:T(8,128)(2,1)S(1)}, u32[]{:S(2)}, u32[]{:S(2)}) collective-permute-start(bf16[48,1024]{1,0:T(8,128)(2,1)S(1)} %get-tuple-element.67), channel_id=1, source_target_pairs={{0,3},{1,2},{2,1},{3,0},{4,7},{5,6},{6,5},{7,4},{8,11},{9,10},{10,... | collective-permute-start | bytes 294920 | tf_op jit(solution)/shard_map/ppermute | solution.py:594
  73.1 7.1 %collective-permute-start.21 = (bf16[48,1024]{1,0:T(8,128)(2,1)S(1)}, bf16[48,1024]{1,0:T(8,128)(2,1)S(1)}, u32[]{:S(2)}, u32[]{:S(2)}) collective-permute-start(bf16[48,1024]{1,0:T(8,128)(2,1)S(1)} %add_convert_fusion.1.refs_0_), channel_id=1, source_target_pairs={{0,16},{4,20},{8,24},{12,28},{16,0},{20,4},{24,8},{28,12},{1,17},{... | collective-permute-start | bytes 294920 | tf_op jit(solution)/shard_map/ppermute | solution.py:594
  73.2 8.1 %collective-permute-start.18 = (bf16[48,1024]{1,0:T(8,128)(2,1)S(1)}, bf16[48,1024]{1,0:T(8,128)(2,1)S(1)}, u32[]{:S(2)}, u32[]{:S(2)}) collective-permute-start(bf16[48,1024]{1,0:T(8,128)(2,1)S(1)} %add_convert_fusion.1.refs_0_), channel_id=1, source_target_pairs={{0,8},{4,12},{8,0},{12,4},{16,24},{20,28},{24,16},{28,20},{1,9},{5... | collective-permute-start | bytes 294920 | tf_op jit(solution)/shard_map/ppermute | solution.py:594
  74.4 8.0 %collective-permute-start.19 = (bf16[48,1024]{1,0:T(8,128)(2,1)S(1)}, bf16[48,1024]{1,0:T(8,128)(2,1)S(1)}, u32[]{:S(2)}, u32[]{:S(2)}) collective-permute-start(bf16[48,1024]{1,0:T(8,128)(2,1)S(1)} %add_convert_fusion.1.refs_0_), channel_id=1, source_target_pairs={{0,24},{4,28},{8,16},{12,20},{16,8},{20,12},{24,0},{28,4},{1,25},{... | collective-permute-start | bytes 294920 | tf_op jit(solution)/shard_map/ppermute | solution.py:594
  77.5 5.4 %collective-permute-start.20 = (bf16[48,1024]{1,0:T(8,128)(2,1)S(1)}, bf16[48,1024]{1,0:T(8,128)(2,1)S(1)}, u32[]{:S(2)}, u32[]{:S(2)}) collective-permute-start(bf16[48,1024]{1,0:T(8,128)(2,1)S(1)} %add_convert_fusion.1.refs_0_), channel_id=1, source_target_pairs={{0,4},{4,0},{8,12},{12,8},{16,20},{20,16},{24,28},{28,24},{1,5},{5... | collective-permute-start | bytes 294920 | tf_op jit(solution)/shard_map/ppermute | solution.py:594
  80.2 4.6 %collective-permute-start.22 = (bf16[48,1024]{1,0:T(8,128)(2,1)S(1)}, bf16[48,1024]{1,0:T(8,128)(2,1)S(1)}, u32[]{:S(2)}, u32[]{:S(2)}) collective-permute-start(bf16[48,1024]{1,0:T(8,128)(2,1)S(1)} %collective-permute-done.21.refs_2_), channel_id=1, source_target_pairs={{0,4},{4,0},{8,12},{12,8},{16,20},{20,16},{24,28},{28,24},{1,5},{5... | collective-permute-start | bytes 294920 | tf_op jit(solution)/shard_map/ppermute | solution.py:594
  88.8 2.6 %collective-permute-start.23 = (bf16[48,3712]{1,0:T(8,128)(2,1)S(1)}, bf16[48,3712]{1,0:T(8,128)(2,1)S(1)}, u32[]{:S(2)}, u32[]{:S(2)}) collective-permute-start(bf16[48,3712]{1,0:T(8,128)(2,1)S(1)} %get-tuple-element.72), channel_id=1, source_target_pairs={{0,1},{1,0},{2,3},{3,2},{4,5},{5,4},{6,7},{7,6},{8,9},{9,8},{10,11... | collective-permute-start | bytes 1069064 | tf_op jit(solution)/shard_map/ppermute | solution.py:594
  88.9 2.5 %collective-permute-start.24 = (bf16[48,3712]{1,0:T(8,128)(2,1)S(1)}, bf16[48,3712]{1,0:T(8,128)(2,1)S(1)}, u32[]{:S(2)}, u32[]{:S(2)}) collective-permute-start(bf16[48,3712]{1,0:T(8,128)(2,1)S(1)} %get-tuple-element.73), channel_id=1, source_target_pairs={{0,1},{1,0},{2,3},{3,2},{4,5},{5,4},{6,7},{7,6},{8,9},{9,8},{10,11... | collective-permute-start | bytes 1069064 | tf_op jit(solution)/shard_map/ppermute | solution.py:594
  89.4 5.7 %collective-permute-start.25 = (bf16[48,1024]{1,0:T(8,128)(2,1)S(1)}, bf16[48,1024]{1,0:T(8,128)(2,1)S(1)}, u32[]{:S(2)}, u32[]{:S(2)}) collective-permute-start(bf16[48,1024]{1,0:T(8,128)(2,1)S(1)} %collective-permute-done.18.refs_0_), channel_id=1, source_target_pairs={{0,4},{4,0},{8,12},{12,8},{16,20},{20,16},{24,28},{28,24},{1,5},{5... | collective-permute-start | bytes 294920 | tf_op jit(solution)/shard_map/ppermute | solution.py:594
  90.3 6.0 %collective-permute-start.26 = (bf16[48,1024]{1,0:T(8,128)(2,1)S(1)}, bf16[48,1024]{1,0:T(8,128)(2,1)S(1)}, u32[]{:S(2)}, u32[]{:S(2)}) collective-permute-start(bf16[48,1024]{1,0:T(8,128)(2,1)S(1)} %collective-permute-done.19.refs_2_), channel_id=1, source_target_pairs={{0,4},{4,0},{8,12},{12,8},{16,20},{20,16},{24,28},{28,24},{1,5},{5... | collective-permute-start | bytes 294920 | tf_op jit(solution)/shard_map/ppermute | solution.py:594
  91.7 19.1 %copy-start = (bf16[1792,1024]{1,0:T(8,128)(2,1)S(1)}, bf16[1792,1024]{1,0:T(8,128)(2,1)}, u32[]{:S(2)}) copy-start(bf16[1792,1024]{1,0:T(8,128)(2,1)} %weight_ref.7) | copy-start | bytes 11010052
  91.8 10.1 %collective-permute-start.27 = (bf16[48,3712]{1,0:T(8,128)(2,1)S(1)}, bf16[48,3712]{1,0:T(8,128)(2,1)S(1)}, u32[]{:S(2)}, u32[]{:S(2)}) collective-permute-start(bf16[48,3712]{1,0:T(8,128)(2,1)S(1)} %get-tuple-element.75), channel_id=1, source_target_pairs={{0,2},{1,3},{2,0},{3,1},{4,6},{5,7},{6,4},{7,5},{8,10},{9,11},{10,... | collective-permute-start | bytes 1069064 | tf_op jit(solution)/shard_map/ppermute | solution.py:594
  100.2 3.4 %collective-permute-start.30 = (bf16[48,3712]{1,0:T(8,128)(2,1)S(1)}, bf16[48,3712]{1,0:T(8,128)(2,1)S(1)}, u32[]{:S(2)}, u32[]{:S(2)}) collective-permute-start(bf16[48,3712]{1,0:T(8,128)(2,1)S(1)} %get-tuple-element.80), channel_id=1, source_target_pairs={{0,1},{1,0},{2,3},{3,2},{4,5},{5,4},{6,7},{7,6},{8,9},{9,8},{10,11... | collective-permute-start | bytes 1069064 | tf_op jit(solution)/shard_map/ppermute | solution.py:594
  100.3 3.3 %collective-permute-start.31 = (bf16[48,3712]{1,0:T(8,128)(2,1)S(1)}, bf16[48,3712]{1,0:T(8,128)(2,1)S(1)}, u32[]{:S(2)}, u32[]{:S(2)}) collective-permute-start(bf16[48,3712]{1,0:T(8,128)(2,1)S(1)} %get-tuple-element.81), channel_id=1, source_target_pairs={{0,1},{1,0},{2,3},{3,2},{4,5},{5,4},{6,7},{7,6},{8,9},{9,8},{10,11... | collective-permute-start | bytes 1069064 | tf_op jit(solution)/shard_map/ppermute | solution.py:594
  102.1 7.4 %collective-permute-start.28 = (bf16[48,1792]{1,0:T(8,128)(2,1)S(1)}, bf16[48,1792]{1,0:T(8,128)(2,1)S(1)}, u32[]{:S(2)}, u32[]{:S(2)}) collective-permute-start(bf16[48,1792]{1,0:T(8,128)(2,1)S(1)} %gated.2.refs_0_), channel_id=1, source_target_pairs={{0,2},{1,3},{2,0},{3,1},{4,6},{5,7},{6,4},{7,5},{8,10},{9,11},{10,... | collective-permute-start | bytes 516104 | tf_op jit(solution)/shard_map/ppermute | solution.py:594
  104.0 12.3 %collective-permute-start.36 = (bf16[48,3712]{1,0:T(8,128)(2,1)S(1)}, bf16[48,3712]{1,0:T(8,128)(2,1)S(1)}, u32[]{:S(2)}, u32[]{:S(2)}) collective-permute-start(bf16[48,3712]{1,0:T(8,128)(2,1)S(1)} %get-tuple-element.82), channel_id=1, source_target_pairs={{0,2},{1,3},{2,0},{3,1},{4,6},{5,7},{6,4},{7,5},{8,10},{9,11},{10,... | collective-permute-start | bytes 1069064 | tf_op jit(solution)/shard_map/ppermute | solution.py:594
  104.6 4.9 %collective-permute-start.29 = (bf16[48,1792]{1,0:T(8,128)(2,1)S(1)}, bf16[48,1792]{1,0:T(8,128)(2,1)S(1)}, u32[]{:S(2)}, u32[]{:S(2)}) collective-permute-start(bf16[48,1792]{1,0:T(8,128)(2,1)S(1)} %gated.2.refs_0_), channel_id=1, source_target_pairs={{0,1},{1,0},{2,3},{3,2},{4,5},{5,4},{6,7},{7,6},{8,9},{9,8},{10,11... | collective-permute-start | bytes 516104 | tf_op jit(solution)/shard_map/ppermute | solution.py:594
  109.4 1.4 %collective-permute-start.32 = (bf16[48,1792]{1,0:T(8,128)(2,1)S(1)}, bf16[48,1792]{1,0:T(8,128)(2,1)S(1)}, u32[]{:S(2)}, u32[]{:S(2)}) collective-permute-start(bf16[48,1792]{1,0:T(8,128)(2,1)S(1)} %collective-permute-done.28.refs_1_), channel_id=1, source_target_pairs={{0,1},{1,0},{2,3},{3,2},{4,5},{5,4},{6,7},{7,6},{8,9},{9,8},{10,11... | collective-permute-start | bytes 516104 | tf_op jit(solution)/shard_map/ppermute | solution.py:594
  111.8 6.3 %collective-permute-start.35 = (bf16[48,1024]{1,0:T(8,128)(2,1)S(1)}, bf16[48,1024]{1,0:T(8,128)(2,1)S(1)}, u32[]{:S(2)}, u32[]{:S(2)}) collective-permute-start(bf16[48,1024]{1,0:T(8,128)(2,1)S(1)} %get-tuple-element.87), channel_id=1, source_target_pairs={{0,4},{4,0},{8,12},{12,8},{16,20},{20,16},{24,28},{28,24},{1,5},{5... | collective-permute-start | bytes 294920 | tf_op jit(solution)/shard_map/ppermute | solution.py:594
  112.8 10.1 %collective-permute-start.34 = (bf16[48,1024]{1,0:T(8,128)(2,1)S(1)}, bf16[48,1024]{1,0:T(8,128)(2,1)S(1)}, u32[]{:S(2)}, u32[]{:S(2)}) collective-permute-start(bf16[48,1024]{1,0:T(8,128)(2,1)S(1)} %get-tuple-element.86), channel_id=1, source_target_pairs={{0,16},{4,20},{8,24},{12,28},{16,0},{20,4},{24,8},{28,12},{1,17},{... | collective-permute-start | bytes 294920 | tf_op jit(solution)/shard_map/ppermute | solution.py:594
  113.2 11.8 %collective-permute-start.33 = (bf16[48,1024]{1,0:T(8,128)(2,1)S(1)}, bf16[48,1024]{1,0:T(8,128)(2,1)S(1)}, u32[]{:S(2)}, u32[]{:S(2)}) collective-permute-start(bf16[48,1024]{1,0:T(8,128)(2,1)S(1)} %get-tuple-element.85), channel_id=1, source_target_pairs={{0,20},{4,16},{8,28},{12,24},{16,4},{20,0},{24,12},{28,8},{1,21},{... | collective-permute-start | bytes 294920 | tf_op jit(solution)/shard_map/ppermute | solution.py:594
  116.5 8.5 %collective-permute-start.37 = (bf16[48,1792]{1,0:T(8,128)(2,1)S(1)}, bf16[48,1792]{1,0:T(8,128)(2,1)S(1)}, u32[]{:S(2)}, u32[]{:S(2)}) collective-permute-start(bf16[48,1792]{1,0:T(8,128)(2,1)S(1)} %gated.3.refs_0_), channel_id=1, source_target_pairs={{0,2},{1,3},{2,0},{3,1},{4,6},{5,7},{6,4},{7,5},{8,10},{9,11},{10,... | collective-permute-start | bytes 516104 | tf_op jit(solution)/shard_map/ppermute | solution.py:594
  118.1 7.0 %collective-permute-start.38 = (bf16[48,1792]{1,0:T(8,128)(2,1)S(1)}, bf16[48,1792]{1,0:T(8,128)(2,1)S(1)}, u32[]{:S(2)}, u32[]{:S(2)}) collective-permute-start(bf16[48,1792]{1,0:T(8,128)(2,1)S(1)} %gated.3.refs_0_), channel_id=1, source_target_pairs={{0,1},{1,0},{2,3},{3,2},{4,5},{5,4},{6,7},{7,6},{8,9},{9,8},{10,11... | collective-permute-start | bytes 516104 | tf_op jit(solution)/shard_map/ppermute | solution.py:594
  125.1 1.5 %collective-permute-start.39 = (bf16[48,1792]{1,0:T(8,128)(2,1)S(1)}, bf16[48,1792]{1,0:T(8,128)(2,1)S(1)}, u32[]{:S(2)}, u32[]{:S(2)}) collective-permute-start(bf16[48,1792]{1,0:T(8,128)(2,1)S(1)} %collective-permute-done.37.refs_1_), channel_id=1, source_target_pairs={{0,1},{1,0},{2,3},{3,2},{4,5},{5,4},{6,7},{7,6},{8,9},{9,8},{10,11... | collective-permute-start | bytes 516104 | tf_op jit(solution)/shard_map/ppermute | solution.py:594
  127.5 7.5 %collective-permute-start.43 = (bf16[48,1024]{1,0:T(8,128)(2,1)S(1)}, bf16[48,1024]{1,0:T(8,128)(2,1)S(1)}, u32[]{:S(2)}, u32[]{:S(2)}) collective-permute-start(bf16[48,1024]{1,0:T(8,128)(2,1)S(1)} %get-tuple-element.93), channel_id=1, source_target_pairs={{0,8},{4,12},{8,0},{12,4},{16,24},{20,28},{24,16},{28,20},{1,9},{5... | collective-permute-start | bytes 294920 | tf_op jit(solution)/shard_map/ppermute | solution.py:594
  127.6 11.6 %collective-permute-start.42 = (bf16[48,1024]{1,0:T(8,128)(2,1)S(1)}, bf16[48,1024]{1,0:T(8,128)(2,1)S(1)}, u32[]{:S(2)}, u32[]{:S(2)}) collective-permute-start(bf16[48,1024]{1,0:T(8,128)(2,1)S(1)} %get-tuple-element.92), channel_id=1, source_target_pairs={{0,12},{4,8},{8,4},{12,0},{16,28},{20,24},{24,20},{28,16},{1,13},{... | collective-permute-start | bytes 294920 | tf_op jit(solution)/shard_map/ppermute | solution.py:594
  130.1 9.1 %collective-permute-start.41 = (bf16[48,1024]{1,0:T(8,128)(2,1)S(1)}, bf16[48,1024]{1,0:T(8,128)(2,1)S(1)}, u32[]{:S(2)}, u32[]{:S(2)}) collective-permute-start(bf16[48,1024]{1,0:T(8,128)(2,1)S(1)} %get-tuple-element.91), channel_id=1, source_target_pairs={{0,24},{4,28},{8,16},{12,20},{16,8},{20,12},{24,0},{28,4},{1,25},{... | collective-permute-start | bytes 294920 | tf_op jit(solution)/shard_map/ppermute | solution.py:594
  131.4 7.8 %collective-permute-start.40 = (bf16[48,1024]{1,0:T(8,128)(2,1)S(1)}, bf16[48,1024]{1,0:T(8,128)(2,1)S(1)}, u32[]{:S(2)}, u32[]{:S(2)}) collective-permute-start(bf16[48,1024]{1,0:T(8,128)(2,1)S(1)} %get-tuple-element.90), channel_id=1, source_target_pairs={{0,28},{4,24},{8,20},{12,16},{16,12},{20,8},{24,4},{28,0},{1,29},{... | collective-permute-start | bytes 294920 | tf_op jit(solution)/shard_map/ppermute | solution.py:594
  (1 other events, 0.7 us)
